TPU v7x, 128 devices: a whole 4x4x4 slice. The times are simulated.
128 devices in a mesh: comp: 2 (over x_lo), tile: 64 (over y, z, x_hi, core).
Axes of the slice: x: 4 (x_hi: 2, x_lo: 2; x = x_hi * 2 + x_lo), y: 4, z: 4, core: 2. Of those that a mesh axis runs over, the one named last changes fastest.
Arguments:
- starting_perturbation: float32 [2, 128, 512, 512], P('comp', None, 'tile'), may hold values from -6 to 6
- measured_discrepancy: float32 [2, 128, 512, 512], P('comp', None, 'tile'), may hold values from -6 to 6
- diffusion: float32 [2, 128, 512, 512], P('comp', None, 'tile'), may hold values from 0.02 to 0.24
- vert_mix: float32 [2, 128, 128], P('comp'), may hold values from -0.03125 to 0.03125
- ocean_mask: int32 [512, 512], P('tile'), may hold values 0 or 1
- pair_tile: int32 [2, 64, 8], replicated, may hold values from 0 to 63, as said below
- pair_patch: int32 [2, 64, 64], replicated, may hold values from 0 to 31
- dest_patch: int32 [2, 64, 64], P('comp', 'tile'), may hold values from 0 to 31
- pair_blocks: int32 [2, 64, 8], P('comp', 'tile'), may hold values from 1 to 8, 48 in all within a row
- remap_weight: float32 [2, 4096, 128, 128], P('comp', 'tile'), may hold values from -0.5 to 0.5
Outputs:
- final_perturbation: float32 [2, 128, 512, 512], P('comp', None, 'tile')
- gradient: float32 [2, 128, 512, 512], P('comp', None, 'tile')
Inputs may be any that keep to these rules, and one draw needn't show every extreme that they name: `pair_tile`: the 8 source tiles listed for destination tile t are distinct; exactly one of them is (t + 32) mod 64, and each other is (t + o) mod 64 for some o from 1 - 8 to 7. A pair's live blocks are its first pair_blocks ones.
All inputs are finite; a program needn't handle non-finite values. No bound on the sum of `ocean_mask` on one device may be relied on, other than what follows from the above.
Results may differ from a plain program's by a relative error of at most 0.0001.
Values sent between devices are 32-bit elements; how exact they have to be, the bound alone decides.
No kernel may reach another device: no remote copies, remote signals or barrier semaphores. Data moves between devices by JAX's collectives and lax.ppermute only.
A program may use at most 128 MiB of HBM per device.

v0:
```python
import jax
import jax.numpy as jnp
from jax import lax
from jax.experimental import pallas as pl
from jax.experimental.pallas import tpu as pltpu
from jax.sharding import PartitionSpec as P

F32 = jnp.float32
BF = jnp.bfloat16
LON, LEV = 512, 128
OFF, PAD = 8, 528
NR = 18
VM = pl.BlockSpec(memory_space=pltpu.VMEM)
SM = pl.BlockSpec(memory_space=pltpu.SMEM)
OFFSETS = tuple(range(-7, 8)) + (32,)


def sds(*shape, dtype=F32):
    return jax.ShapeDtypeStruct(shape, dtype)


def cost(us):
    return pl.CostEstimate(flops=int(us * 5e8), bytes_accessed=1 << 20, transcendentals=0)


def params(**kw):
    return pltpu.CompilerParams(vmem_limit_bytes=60 * 2**20, **kw)


def halves(x):
    hi = x.astype(BF)
    return hi, (x - hi.astype(F32)).astype(BF)


def start_in_kernel(x, top, bot):
    for r in range(8):
        dst = top if r < 4 else bot
        dst[r % 4] = x[pl.ds(r, 128, stride=8), :].T


def start_in(x):
    blk = pl.BlockSpec((4, 128, 128), lambda j: (0, j, 0))
    return pl.pallas_call(
        start_in_kernel,
        grid=(4,),
        out_shape=(sds(4, LON, LEV), sds(4, LON, LEV)),
        in_specs=[pl.BlockSpec((1024, 128), lambda j: (0, j))],
        out_specs=(blk, blk),
        compiler_params=params(),
        cost_estimate=cost(4),
        name="start_in",
    )(x)


def diff_in_kernel(x, sea, full, top, bot):
    for r in range(8):
        y = (x[pl.ds(r, 128, stride=8), :] * sea[r : r + 1, :]).T
        full[r] = y
        if r < 3:
            top[r] = y
        if r > 4:
            bot[r - 5] = y


def diff_in(x, sea):
    blk = pl.BlockSpec((3, 128, 128), lambda j: (0, j, 0))
    return pl.pallas_call(
        diff_in_kernel,
        grid=(4,),
        out_shape=(sds(8, LON, LEV), sds(3, LON, LEV), sds(3, LON, LEV)),
        in_specs=[
            pl.BlockSpec((1024, 128), lambda j: (0, j)),
            pl.BlockSpec((8, 128), lambda j: (0, j)),
        ],
        out_specs=(pl.BlockSpec((8, 128, 128), lambda j: (0, j, 0)), blk, blk),
        compiler_params=params(),
        cost_estimate=cost(4),
        name="diff_in",
    )(x, sea)


def to_rows_kernel(x, o):
    for r in range(8):
        o[r] = x[pl.ds(r, 128, stride=8), :].T


def to_rows(x):
    return pl.pallas_call(
        to_rows_kernel,
        grid=(4,),
        out_shape=sds(8, LON, LEV),
        in_specs=[pl.BlockSpec((1024, 128), lambda j: (0, j))],
        out_specs=pl.BlockSpec((8, 128, 128), lambda j: (0, j, 0)),
        compiler_params=params(),
        cost_estimate=cost(4),
        name="to_rows",
    )(x)


def to_raw_kernel(x, o):
    for r in range(8):
        o[pl.ds(r, 128, stride=8), :] = x[r].T


def to_raw(x):
    return pl.pallas_call(
        to_raw_kernel,
        grid=(4,),
        out_shape=sds(1024, LON),
        in_specs=[pl.BlockSpec((8, 128, 128), lambda j: (0, j, 0))],
        out_specs=pl.BlockSpec((1024, 128), lambda j: (0, j)),
        compiler_params=params(),
        cost_estimate=cost(4),
        name="to_raw",
    )(x)


def grad_out_kernel(x, up, dn, o):
    for r in range(8):
        add = up[r] if r < 4 else dn[r - 4]
        o[pl.ds(r, 128, stride=8), :] = (x[r] + add).T


def grad_out(x, up, dn):
    blk = pl.BlockSpec((4, 128, 128), lambda j: (0, j, 0))
    return pl.pallas_call(
        grad_out_kernel,
        grid=(4,),
        out_shape=sds(1024, LON),
        in_specs=[pl.BlockSpec((8, 128, 128), lambda j: (0, j, 0)), blk, blk],
        out_specs=pl.BlockSpec((1024, 128), lambda j: (0, j)),
        compiler_params=params(),
        cost_estimate=cost(4),
        name="grad_out",
    )(x, up, dn)


def mix_kernel(w, fwd, bwd):
    for dst, x in ((fwd, w[...].T), (bwd, w[...])):
        hi, lo = halves(x)
        dst[0:128, 0:128] = hi
        dst[128:256, 0:128] = hi
        dst[0:128, 128:256] = lo
        dst[128:256, 128:256] = jnp.zeros((128, 128), BF)


def mixes(w):
    return pl.pallas_call(
        mix_kernel,
        out_shape=(sds(256, 256, dtype=BF), sds(256, 256, dtype=BF)),
        in_specs=[VM],
        out_specs=(VM, VM),
        name="mixes",
    )(w)


def put(v, r, j, new):
    v[r, pl.ds(OFF + 128 * j, 128), :] = new
    if j == 0:
        v[r, pl.ds(OFF + LON, 1), :] = new[0:1]
    if j == 3:
        v[r, pl.ds(OFF - 1, 1), :] = new[127:128]


def put_halves(h, r, j, new):
    hi, lo = halves(new)
    h[r, pl.ds(128 * j, 128), 0:128] = hi
    h[r, pl.ds(128 * j, 128), 128:256] = lo


def around(v, r, j):
    at = OFF + 128 * j
    n = v[r - 1, pl.ds(at, 128), :] + v[r + 1, pl.ds(at, 128), :]
    return n + (v[r, pl.ds(at - 1, 128), :] + v[r, pl.ds(at + 1, 128), :])


def mixed(h, w2, r, j):
    y = jnp.dot(h[r, pl.ds(128 * j, 128), :], w2[...], preferred_element_type=F32)
    return y[:, 0:128] + y[:, 128:256]


def rows(lo, hi, body):
    def step(r, carry):
        for j in range(4):
            body(r, j)
        return carry

    lax.fori_loop(lo, hi, step, 0)


def forward_step(va, vb, h, d, w2, lo, hi, first=False, last=False):
    def body(r, j):
        y = mixed(h, w2, r, j)
        c = va[r, pl.ds(OFF + 128 * j, 128), :]
        dd = d[r, pl.ds(128 * j, 128), :]
        n = dd * (around(va, r, j) - 4.0 * c)
        if first:
            c = jnp.where(dd > 0.0, c, 0.0)
        new = (c + n) + y
        put(vb, r, j, new)
        if not last:
            put_halves(h, r, j, new)

    rows(lo, hi, body)


def push_step(ga, gb, u, h, d, w2, s, last=False):
    def body(r, j):
        y = mixed(h, w2, r, j)
        at = pl.ds(128 * j, 128)
        n = around(ga, r, j) - 4.0 * ga[r, pl.ds(OFF + 128 * j, 128), :]
        c = u[r, at, :]
        if last:
            u[r, at, :] = (c + n) + y
        else:
            dd = d[r, at, :]
            new = (c + jnp.where(dd > 0.0, n, 0.0)) + y
            u[r, at, :] = new
            put(gb, r, j, dd * new)
            put_halves(h, r, j, new)

    rows(5 - s, 13 + s, body)


def load_diffusion(d, full, up, dn):
    for src, r0, n in ((up, 2, 3), (full, 5, 8), (dn, 13, 3)):

        def cp(i, carry, src=src, r0=r0):
            d[r0 + i] = src[i]
            return carry

        lax.fori_loop(0, n, cp, 0)


def clear_outside(ga, gb, u, h):
    def clear(i, carry):
        r = jnp.where(i < 5, i, i + 8)
        ga[r] = jnp.zeros((PAD, 128), F32)
        gb[r] = jnp.zeros((PAD, 128), F32)
        u[r] = jnp.zeros((LON, 128), F32)
        h[r] = jnp.zeros((LON, 256), BF)
        return carry

    lax.fori_loop(0, 10, clear, 0)


def lanes():
    return lax.broadcasted_iota(jnp.int32, (128, 128), 1)


def gather_surface(read, count):
    def step(r, acc):
        for j in range(4):
            p = 4 * r + j
            acc = jnp.where(lanes() == p, pltpu.roll(read(r, j), p, 1), acc)
        return acc

    return lax.fori_loop(0, count, step, jnp.zeros((128, 128), F32)).T


def spread_column(cols, p):
    return jnp.where(lanes() == 0, pltpu.roll(cols, (128 - p) % 128, 1), 0.0)


BLOCK_SCRATCH = [
    pltpu.VMEM((NR, PAD, 128), F32),
    pltpu.VMEM((NR, PAD, 128), F32),
    pltpu.VMEM((NR, LON, 256), BF),
    pltpu.VMEM((NR, LON, 128), F32),
]


def first_kernel(top, bot, hu, hd, dt, du, dn, w2, o_top, o_bot, o_surf, va, vb, h, d):
    load_diffusion(d, dt, du, dn)
    for src, r0 in ((hu, 1), (top, 5), (bot, 9), (hd, 13)):

        def cp(i, carry, src=src, r0=r0):
            for j in range(4):
                x = src[i, pl.ds(128 * j, 128), :]
                put(va, r0 + i, j, x)
                keep = d[r0 + i, pl.ds(128 * j, 128), :] > 0.0
                put_halves(h, r0 + i, j, jnp.where(keep, x, 0.0))
            return carry

        lax.fori_loop(0, 4, cp, 0)
    forward_step(va, vb, h, d, w2, 2, 16, first=True)
    forward_step(vb, va, h, d, w2, 3, 15)
    forward_step(va, vb, h, d, w2, 4, 14)
    forward_step(vb, va, h, d, w2, 5, 13, last=True)

    def out(i, carry):
        o_top[i] = va[5 + i, pl.ds(OFF, LON), :]
        o_bot[i] = va[9 + i, pl.ds(OFF, LON), :]
        return carry

    lax.fori_loop(0, 4, out, 0)
    o_surf[...] = gather_surface(lambda r, j: va[r + 5, pl.ds(OFF + 128 * j, 128), :], 8)[0:32]


def first_block(*args):
    return pl.pallas_call(
        first_kernel,
        out_shape=(sds(4, LON, LEV), sds(4, LON, LEV), sds(32, 128)),
        in_specs=[VM] * 8,
        out_specs=(VM,) * 3,
        scratch_shapes=BLOCK_SCRATCH,
        compiler_params=params(),
        cost_estimate=cost(15),
        name="first_block",
    )(*args)


def middle_kernel(
    top, bot, hu, hd, s, su, sd, dt, du, dn, m, w2f, w2b,
    o_final, o_adj, o_up, o_dn, o_s, o_su, o_sd, va, vb, h, d, u, cols,
):
    load_diffusion(d, dt, du, dn)
    cols[0:16] = su[...]
    cols[16:48] = s[...]
    cols[48:64] = sd[...]
    cols[64:128] = jnp.zeros((64, 128), F32)
    cols[...] = cols[...].T
    for src, r0 in ((hu, 1), (top, 5), (bot, 9), (hd, 13)):

        def cp(i, carry, src=src, r0=r0):
            for j in range(4):
                x = src[i, pl.ds(128 * j, 128), :]
                x = x + spread_column(cols[...], 4 * (r0 - 1 + i) + j)
                put(va, r0 + i, j, x)
                put_halves(h, r0 + i, j, x)
            return carry

        lax.fori_loop(0, 4, cp, 0)
    forward_step(va, vb, h, d, w2f, 2, 16)
    forward_step(vb, va, h, d, w2f, 3, 15)
    forward_step(va, vb, h, d, w2f, 4, 14)
    forward_step(vb, va, h, d, w2f, 5, 13, last=True)
    clear_outside(va, vb, u, h)

    def body(r, j):
        at = pl.ds(128 * j, 128)
        x = va[r, pl.ds(OFF + 128 * j, 128), :]
        o_final[r - 5, at, :] = x
        x = x - m[r - 5, at, :]
        dd = d[r, at, :]
        x = jnp.where(dd > 0.0, x, 0.0)
        u[r, at, :] = x
        put(vb, r, j, dd * x)
        put_halves(h, r, j, x)

    rows(5, 13, body)
    push_step(vb, va, u, h, d, w2b, 1)
    push_step(va, vb, u, h, d, w2b, 2)
    push_step(vb, va, u, h, d, w2b, 3)
    push_step(va, vb, u, h, d, w2b, 4, last=True)

    def out(i, carry):
        o_up[i] = u[1 + i]
        o_adj[i] = u[5 + i]
        o_adj[4 + i] = u[9 + i]
        o_dn[i] = u[13 + i]
        return carry

    lax.fori_loop(0, 4, out, 0)
    g = gather_surface(lambda r, j: u[r + 1, pl.ds(128 * j, 128), :], 16)
    o_su[...] = g[0:16]
    o_s[...] = g[16:48]
    o_sd[...] = g[48:64]


def middle_block(*args):
    return pl.pallas_call(
        middle_kernel,
        out_shape=(
            sds(8, LON, LEV), sds(8, LON, LEV), sds(4, LON, LEV), sds(4, LON, LEV),
            sds(32, 128), sds(16, 128), sds(16, 128),
        ),
        in_specs=[VM] * 13,
        out_specs=(VM,) * 7,
        scratch_shapes=BLOCK_SCRATCH
        + [pltpu.VMEM((NR, LON, 128), F32), pltpu.VMEM((128, 128), F32)],
        compiler_params=params(),
        cost_estimate=cost(30),
        name="middle_block",
    )(*args)


def last_kernel(
    adj, ru, rd, s, top, bot, dt, du, dn, w2b, o_base, o_up, o_dn, va, vb, h, d, u, cols
):
    load_diffusion(d, dt, du, dn)
    clear_outside(va, vb, u, h)
    cols[0:32] = s[...]
    cols[32:128] = jnp.zeros((96, 128), F32)
    cols[...] = cols[...].T
    for src, r0 in ((ru, 5), (rd, 9)):

        def cp(i, carry, src=src, r0=r0):
            r = r0 + i
            for j in range(4):
                at = pl.ds(128 * j, 128)
                x = adj[r - 5, at, :] + src[i, at, :]
                x = x + spread_column(cols[...], 4 * (r - 5) + j)
                dd = d[r, at, :]
                x = jnp.where(dd > 0.0, x, 0.0)
                u[r, at, :] = x
                put(vb, r, j, dd * x)
                put_halves(h, r, j, x)
            return carry

        lax.fori_loop(0, 4, cp, 0)
    push_step(vb, va, u, h, d, w2b, 1)
    push_step(va, vb, u, h, d, w2b, 2)
    push_step(vb, va, u, h, d, w2b, 3)
    push_step(va, vb, u, h, d, w2b, 4, last=True)

    def out(i, carry):
        o_up[i] = u[1 + i]
        o_base[i] = u[5 + i] + top[i]
        o_base[4 + i] = u[9 + i] + bot[i]
        o_dn[i] = u[13 + i]
        return carry

    lax.fori_loop(0, 4, out, 0)


def last_block(*args):
    return pl.pallas_call(
        last_kernel,
        out_shape=(sds(8, LON, LEV), sds(4, LON, LEV), sds(4, LON, LEV)),
        in_specs=[VM] * 10,
        out_specs=(VM,) * 3,
        scratch_shapes=BLOCK_SCRATCH
        + [pltpu.VMEM((NR, LON, 128), F32), pltpu.VMEM((128, 128), F32)],
        compiler_params=params(),
        cost_estimate=cost(15),
        name="last_block",
    )(*args)


def offer_kernel(me, send_rows, surf, o):
    o[...] = jnp.zeros((512, 128), F32)
    for off in OFFSETS:
        t = lax.rem(me[0] + (off + 64), 64) * 8
        for q in range(8):
            o[pl.ds(t + q, 1), :] = surf[pl.ds(send_rows[t + q], 1), :]


def offer(me, send_rows, surf):
    return pl.pallas_call(
        offer_kernel,
        out_shape=sds(512, 128),
        in_specs=[SM, SM, VM],
        out_specs=VM,
        name="offer",
    )(me, send_rows, surf)


def remap_kernel(pick, live, dest, arrived, w, sea, o):
    def step(i, acc):
        for k in range(4):
            b = 4 * i + k
            x = arrived[pl.ds(pick[b], 1), :]
            red = jnp.sum(w[b] * x, axis=1, keepdims=True)
            where = jnp.where(live[b] > 0, dest[b], -1)
            acc = acc + jnp.where(lanes() == where, red, 0.0)
        return acc

    acc = lax.fori_loop(0, 16, step, jnp.zeros((128, 128), F32))
    o[...] = acc.T[0:32] * sea[...]


def remap(pick, live, dest, arrived, w, sea):
    return pl.pallas_call(
        remap_kernel,
        out_shape=sds(32, 128),
        in_specs=[SM, SM, SM, VM, VM, VM],
        out_specs=VM,
        compiler_params=params(),
        cost_estimate=cost(3),
        name="remap",
    )(pick, live, dest, arrived, w, sea)


def remap_back_kernel(pick, live, dest, s, ru, rd, w, sea, o, cols, wide):
    cols[0:16] = (s[0:16] + ru[...]) * sea[0:16]
    cols[16:32] = (s[16:32] + rd[...]) * sea[16:32]
    cols[32:128] = jnp.zeros((96, 128), F32)
    cols[...] = cols[...].T
    for p in range(32):
        wide[p] = jnp.broadcast_to(cols[:, p : p + 1], (128, 128))
    o[...] = jnp.zeros((512, 128), F32)

    def step(i, carry):
        for k in range(4):
            b = 4 * i + k
            red = jnp.sum(w[b] * wide[dest[b]], axis=0, keepdims=True)
            o[pl.ds(pick[b], 1), :] = jnp.where(live[b] > 0, red, 0.0)
        return carry

    lax.fori_loop(0, 16, step, 0)


def remap_back(pick, live, dest, s, ru, rd, w, sea):
    return pl.pallas_call(
        remap_back_kernel,
        out_shape=sds(512, 128),
        in_specs=[SM, SM, SM, VM, VM, VM, VM, VM],
        out_specs=VM,
        scratch_shapes=[pltpu.VMEM((128, 128), F32), pltpu.VMEM((32, 128, 128), F32)],
        compiler_params=params(),
        cost_estimate=cost(3),
        name="remap_back",
    )(pick, live, dest, s, ru, rd, w, sea)


def collect_kernel(me, send_rows, got, o):
    o[...] = jnp.zeros((32, 128), F32)
    for off in OFFSETS:
        t = lax.rem(me[0] + (off + 64), 64) * 8
        for q in range(8):
            at = pl.ds(send_rows[t + q], 1)
            o[at, :] = o[at, :] + got[pl.ds(t + q, 1), :]


def collect(me, send_rows, got):
    return pl.pallas_call(
        collect_kernel,
        out_shape=sds(32, 128),
        in_specs=[SM, SM, VM],
        out_specs=VM,
        name="collect",
    )(me, send_rows, got)


def shards(
    starting_perturbation,
    measured_discrepancy,
    diffusion,
    vert_mix,
    ocean_mask,
    pair_tile,
    pair_patch,
    dest_patch,
    pair_blocks,
    remap_weight,
):
    component = lax.axis_index("comp")
    own_tile = lax.axis_index("tile")
    down_pairs = [(i, i + 1) for i in range(63)]
    up_pairs = [(i + 1, i) for i in range(63)]

    def to_next(x):
        return lax.ppermute(x, "tile", down_pairs)

    def to_prev(x):
        return lax.ppermute(x, "tile", up_pairs)

    def swap(x):
        return lax.ppermute(x, "comp", [(0, 1), (1, 0)])

    def exchange(x):
        x = x.reshape(64, 8, 128)
        x = lax.all_to_all(x, "tile", split_axis=0, concat_axis=0, tiled=True)
        return x.reshape(512, 128)

    start = starting_perturbation.reshape(1024, LON)
    s_top, s_bot = start_in(start)
    s_hu, s_hd = to_next(s_bot), to_prev(s_top)
    sea = jnp.where(component == 1, ocean_mask.astype(F32), 1.0)
    sea32 = sea.reshape(32, 128)
    dt, d_top, d_bot = diff_in(diffusion.reshape(1024, LON), sea)
    du, dd = to_next(d_bot), to_prev(d_top)
    w2f, w2b = mixes(vert_mix[0])

    slots = jnp.arange(64, dtype=jnp.int32)
    pick = jnp.repeat(pair_tile[component, own_tile], 8) * 8 + slots % 8
    live = (slots % 8 < jnp.repeat(pair_blocks[0, 0], 8)).astype(jnp.int32)
    dest = dest_patch[0, 0]
    hits = (pair_tile[component] == own_tile).astype(jnp.int32)
    sources = pair_patch[component].reshape(64, 8, 8)
    send_rows = jnp.sum(hits[:, :, None] * sources, axis=1).reshape(512)
    me = own_tile.reshape(1)
    weights = remap_weight[0]
    measured = to_rows(measured_discrepancy.reshape(1024, LON))

    v_top, v_bot, surf = first_block(s_top, s_bot, s_hu, s_hd, dt, du, dd, w2f)
    other = swap(surf)
    v_hu, v_hd = to_next(v_bot), to_prev(v_top)
    arrived = exchange(offer(me, send_rows, other))
    fix = remap(pick, live, dest, arrived, weights, sea32)
    f_hu, f_hd = to_next(fix[16:32]), to_prev(fix[0:16])
    final, adj, a_up, a_dn, a0, a0_up, a0_dn = middle_block(
        v_top, v_bot, v_hu, v_hd, fix, f_hu, f_hd, dt, du, dd, measured, w2f, w2b
    )
    r0u, r0d = to_next(a0_dn), to_prev(a0_up)
    ru, rd = to_next(a_dn), to_prev(a_up)
    final_raw = to_raw(final)
    back = exchange(remap_back(pick, live, dest, a0, r0u, r0d, weights, sea32))
    back = swap(collect(me, send_rows, back))
    base, g_up, g_dn = last_block(adj, ru, rd, back, s_top, s_bot, dt, du, dd, w2b)
    gu, gd = to_next(g_dn), to_prev(g_up)
    gradient = grad_out(base, gu, gd)
    shape = starting_perturbation.shape
    return final_raw.reshape(shape), gradient.reshape(shape)


def solution(mesh):
    field = P("comp", None, "tile", None)
    placed = (
        field,
        field,
        field,
        P("comp", None, None),
        P("tile", None),
        P(),
        P(),
        P("comp", "tile", None),
        P("comp", "tile", None),
        P("comp", "tile", None, None),
    )
    return jax.shard_map(
        shards,
        mesh=mesh,
        in_specs=placed,
        out_specs=(field, field),
        check_vma=False,
    )
```

profile of v0, /device:TPU:8, one launch (start us, length us, event | category | flops | bytes accessed | tf_op | source)
XLA Modules:
  0.0 291.5 jit_solution(9299112996111320233)
XLA Ops:
  0.7 4.2 %start_in.1 = (f32[4,512,128]{2,1,0:T(8,128)}, f32[4,512,128]{2,1,0:T(8,128)}) custom-call(f32[1024,512]{1,0:T(8,128)} %bitcast.28), custom_call_target="tpu_custom_call" | custom-call | flops 2000000000 | bytes 1048576 | tf_op jit(solution)/shard_map/start_in/pallas_call | solution.py:43
  4.9 7.7 %collective-permute-start.1 = (f32[4,512,128]{2,1,0:T(8,128)}, f32[4,512,128]{2,1,0:T(8,128)S(1)}, u32[]{:S(2)}, u32[]{:S(2)}) collective-permute-start(f32[4,512,128]{2,1,0:T(8,128)} %get-tuple-element.22.top), channel_id=1, source_target_pairs={{1,0},{2,1},{3,2},{4,3},{5,4},{6,5},{7,6},{8,7},{9,8},{10,9},{11,1... | collective-permute-start | bytes 3145736 | tf_op jit(solution)/shard_map/ppermute | solution.py:557
  12.6 1.9 collective-permute-start
  14.6 0.6 convert_select_fusion.sea
  15.2 4.4 %diff_in.1 = (f32[8,512,128]{2,1,0:T(8,128)}, f32[3,512,128]{2,1,0:T(8,128)}, f32[3,512,128]{2,1,0:T(8,128)}) custom-call(f32[1024,512]{1,0:T(8,128)} %bitcast.29, f32[8,512]{1,0:T(8,128)} %convert_select_fusion.sea), custom_call_target="tpu_custom_call" | custom-call | flops 2000000000 | bytes 1048576 | tf_op jit(solution)/shard_map/diff_in/pallas_call | solution.py:67
  19.6 1.9 collective-permute-start.2
  21.5 8.2 %collective-permute-start.3 = (f32[3,512,128]{2,1,0:T(8,128)}, f32[3,512,128]{2,1,0:T(8,128)}, u32[]{:S(2)}, u32[]{:S(2)}) collective-permute-start(f32[3,512,128]{2,1,0:T(8,128)} %get-tuple-element.26), channel_id=1, source_target_pairs={{1,0},{2,1},{3,2},{4,3},{5,4},{6,5},{7,6},{8,7},{9,8},{10,9},{11,1... | collective-permute-start | bytes 2359304 | tf_op jit(solution)/shard_map/ppermute | solution.py:557
  29.7 0.1 copy.16
  29.8 1.6 mixes.1
  31.4 22.9 %collective-permute-done.2.du = f32[3,512,128]{2,1,0:T(8,128)S(1)} collective-permute-done((f32[3,512,128]{2,1,0:T(8,128)}, f32[3,512,128]{2,1,0:T(8,128)S(1)}, u32[]{:S(2)}, u32[]{:S(2)}) %collective-permute-start.2) | collective-permute-done | bytes 786464 | tf_op jit(solution)/shard_map/ppermute | solution.py:554
  54.3 0.9 copy-done.15
  55.1 0.3 copy-done.9
  55.5 0.3 copy-done.10
  55.8 18.9 %first_block.1 = (f32[4,512,128]{2,1,0:T(8,128)}, f32[4,512,128]{2,1,0:T(8,128)}, f32[32,128]{1,0:T(8,128)}) custom-call(f32[4,512,128]{2,1,0:T(8,128)} %get-tuple-element.22.top, f32[4,512,128]{2,1,0:T(8,128)} %get-tuple-element.23.bot, f32[4,512,128]{2,1,0:T(8,128)} %copy-done.10, f32[4,512,128]{2,1,0:T(8,128)} %copy-done.9, ...), custom_call_target="tpu_custom_call" | custom-call | flops 7500000256 | bytes 1048576 | tf_op jit(solution)/shard_map/first_block/pallas_call | solution.py:301
  74.7 1.4 collective-permute-start.6
  76.2 6.0 %collective-permute-start.5 = (f32[4,512,128]{2,1,0:T(8,128)}, f32[4,512,128]{2,1,0:T(8,128)S(1)}, u32[]{:S(2)}, u32[]{:S(2)}) collective-permute-start(f32[4,512,128]{2,1,0:T(8,128)} %get-tuple-element.28.top), channel_id=1, source_target_pairs={{1,0},{2,1},{3,2},{4,3},{5,4},{6,5},{7,6},{8,7},{9,8},{10,9},{11,1... | collective-permute-start | bytes 3145736 | tf_op jit(solution)/shard_map/ppermute | solution.py:557
  82.2 1.9 collective-permute-start.4
  84.1 0.2 multiply_reduce_fusion
  84.3 0.1 broadcast_in_dim.12
  84.4 0.1 mul.30
  84.5 0.1 copy.15
  84.6 0.7 reshape.66.send_rows
  85.3 0.6 copy-done.3
  85.9 1.6 offer.1
  87.4 11.0 %all-to-all-start = ((f32[64,8,128]{2,1,0:T(8,128)}), f32[64,8,128]{2,1,0:T(8,128)S(1)}, u32[]{:S(2)}, u32[]{:S(2)}) async-start(f32[64,8,128]{2,1,0:T(8,128)} %bitcast.20), calls=%async_computation | async-start | bytes 524288 | tf_op jit(solution)/shard_map/all_to_all | solution.py:564
  98.4 0.5 fusion.1.pick
  99.0 0.6 reshape.69.sea
  99.6 0.1 broadcast_in_dim.13
  99.6 0.1 reshape.64
  99.7 0.5 compare_convert_fusion.live
  100.2 8.6 %all-to-all-done = f32[64,8,128]{2,1,0:T(8,128)S(1)} async-done(((f32[64,8,128]{2,1,0:T(8,128)}), f32[64,8,128]{2,1,0:T(8,128)S(1)}, u32[]{:S(2)}, u32[]{:S(2)}) %all-to-all-start) | async-done | bytes 262176 | tf_op jit(solution)/shard_map/all_to_all | solution.py:564
  108.8 0.7 copy-done.1
  109.5 5.2 %remap.1.s = f32[32,128]{1,0:T(8,128)} custom-call(s32[64]{0:T(128)} %fusion.1.pick, s32[64]{0:T(128)} %compare_convert_fusion.live, s32[64]{0:T(128)} %bitcast.31, f32[512,128]{1,0:T(8,128)} %bitcast.22, f32[64,128,128]{2,1,0:T(8,128)} %bitcast.26, f32[32,128]{1,0:T(8,128)} %reshape.69.sea), custom_call_target="tpu_custom_call" | custom-call | flops 1500000000 | bytes 1048576 | tf_op jit(solution)/shard_map/remap/pallas_call | solution.py:474
  114.7 0.7 fusion.2
  115.4 8.2 %collective-permute-start.8 = (f32[16,128]{1,0:T(8,128)S(1)}, f32[16,128]{1,0:T(8,128)S(1)}, u32[]{:S(2)}, u32[]{:S(2)}) collective-permute-start(f32[16,128]{1,0:T(8,128)S(1)} %get-tuple-element.42), channel_id=1, source_target_pairs={{1,0},{2,1},{3,2},{4,3},{5,4},{6,5},{7,6},{8,7},{9,8},{10,9},{11,1... | collective-permute-start | bytes 24584 | tf_op jit(solution)/shard_map/ppermute | solution.py:557
  123.7 1.9 collective-permute-start.7
  125.6 4.1 %to_rows.1.m = f32[8,512,128]{2,1,0:T(8,128)} custom-call(f32[1024,512]{1,0:T(8,128)} %bitcast.30), custom_call_target="tpu_custom_call" | custom-call | flops 2000000000 | bytes 1048576 | tf_op jit(solution)/shard_map/to_rows/pallas_call | solution.py:88
  129.7 3.4 %collective-permute-done.7.su = f32[16,128]{1,0:T(8,128)S(1)} collective-permute-done((f32[16,128]{1,0:T(8,128)S(1)}, f32[16,128]{1,0:T(8,128)S(1)}, u32[]{:S(2)}, u32[]{:S(2)}) %collective-permute-start.7) | collective-permute-done | bytes 8224 | tf_op jit(solution)/shard_map/ppermute | solution.py:554
  133.2 0.6 copy-done.18
  133.7 0.4 copy-done.7
  134.2 0.4 copy-done.8
  134.6 39.2 %middle_block.1 = (f32[8,512,128]{2,1,0:T(8,128)}, f32[8,512,128]{2,1,0:T(8,128)}, f32[4,512,128]{2,1,0:T(8,128)}, f32[4,512,128]{2,1,0:T(8,128)}, f32[32,128]{1...) custom-call(f32[4,512,128]{2,1,0:T(8,128)} %get-tuple-element.28.top, f32[4,512,128]{2,1,0:T(8,128)} %get-tuple-element.29.bot, ...), custom_call_target="tpu_custom_call" | custom-call | flops 15000000512 | bytes 1048576 | tf_op jit(solution)/shard_map/middle_block/pallas_call | solution.py:372
  173.8 1.9 collective-permute-start.9
  175.7 8.2 %collective-permute-start.10 = (f32[4,512,128]{2,1,0:T(8,128)}, f32[4,512,128]{2,1,0:T(8,128)S(1)}, u32[]{:S(2)}, u32[]{:S(2)}) collective-permute-start(f32[4,512,128]{2,1,0:T(8,128)} %get-tuple-element.35), channel_id=1, source_target_pairs={{1,0},{2,1},{3,2},{4,3},{5,4},{6,5},{7,6},{8,7},{9,8},{10,9},{11,1... | collective-permute-start | bytes 3145736 | tf_op jit(solution)/shard_map/ppermute | solution.py:557
  183.8 1.9 collective-permute-start.11
  185.8 8.2 %collective-permute-start.12 = (f32[16,128]{1,0:T(8,128)}, f32[16,128]{1,0:T(8,128)S(1)}, u32[]{:S(2)}, u32[]{:S(2)}) collective-permute-start(f32[16,128]{1,0:T(8,128)} %get-tuple-element.38), channel_id=1, source_target_pairs={{1,0},{2,1},{3,2},{4,3},{5,4},{6,5},{7,6},{8,7},{9,8},{10,9},{11,1... | collective-permute-start | bytes 24584 | tf_op jit(solution)/shard_map/ppermute | solution.py:557
  193.9 11.3 %collective-permute-done.11.ru = f32[16,128]{1,0:T(8,128)S(1)} collective-permute-done((f32[16,128]{1,0:T(8,128)}, f32[16,128]{1,0:T(8,128)S(1)}, u32[]{:S(2)}, u32[]{:S(2)}) %collective-permute-start.11) | collective-permute-done | bytes 8224 | tf_op jit(solution)/shard_map/ppermute | solution.py:554
  205.2 0.6 copy-done.19
  205.8 4.3 %remap_back.1 = f32[512,128]{1,0:T(8,128)} custom-call(s32[64]{0:T(128)} %fusion.1.pick, s32[64]{0:T(128)} %compare_convert_fusion.live, s32[64]{0:T(128)} %bitcast.32, f32[32,128]{1,0:T(8,128)} %get-tuple-element.36.s, f32[16,128]{1,0:T(8,128)} %copy-done.19, f32[16,128]{1,0:T(8,128)} %copy-done.20, f32[64,128,128]{2,1,0:T(8,128)} %bitcast.27, ...), custom_call_target="tpu_custom_call" | custom-call | flops 1500000000 | bytes 1048576 | tf_op jit(solution)/shard_map/remap_back/pallas_call | solution.py:505
  210.2 14.3 %all_to_all.10 = f32[64,8,128]{2,1,0:T(8,128)} all-to-all(f32[64,8,128]{2,1,0:T(8,128)} %bitcast.23), channel_id=1, replica_groups=mesh['comp'=2,'tile'=64] {'tile'}, dimensions={0} | all-to-all | bytes 524288 | tf_op jit(solution)/shard_map/all_to_all | solution.py:564
  224.5 2.2 collect.1
  226.7 0.0 collective-permute-start.13
  226.7 3.9 %collective-permute-done.13.s = f32[32,128]{1,0:T(8,128)S(1)} collective-permute-done((f32[32,128]{1,0:T(8,128)}, f32[32,128]{1,0:T(8,128)S(1)}, u32[]{:S(2)}, u32[]{:S(2)}) %collective-permute-start.13) | collective-permute-done | bytes 16416 | tf_op jit(solution)/shard_map/ppermute | solution.py:560
  230.7 0.6 copy-done.16
  231.2 0.4 copy-done.11
  231.6 0.4 copy-done.12
  232.0 22.9 %last_block.1 = (f32[8,512,128]{2,1,0:T(8,128)}, f32[4,512,128]{2,1,0:T(8,128)}, f32[4,512,128]{2,1,0:T(8,128)}) custom-call(f32[8,512,128]{2,1,0:T(8,128)} %get-tuple-element.33.adj, f32[4,512,128]{2,1,0:T(8,128)} %copy-done.11, f32[4,512,128]{2,1,0:T(8,128)} %copy-done.12, f32[32,128]{1,0:T(8,128)} %copy-done.16, f32[4,512,128]{2,1,0:T(8,128)} %get-tuple-element.22.top, ...), custom_call_target="tpu_custom_call" | custom-call | flops 7500000256 | bytes 1048576 | tf_op jit(solution)/shard_map/last_block/pallas_call | solution.py:428
  254.8 1.9 collective-permute-start.14
  256.8 8.2 %collective-permute-start.15 = (f32[4,512,128]{2,1,0:T(8,128)}, f32[4,512,128]{2,1,0:T(8,128)S(1)}, u32[]{:S(2)}, u32[]{:S(2)}) collective-permute-start(f32[4,512,128]{2,1,0:T(8,128)} %get-tuple-element.41), channel_id=1, source_target_pairs={{1,0},{2,1},{3,2},{4,3},{5,4},{6,5},{7,6},{8,7},{9,8},{10,9},{11,1... | collective-permute-start | bytes 3145736 | tf_op jit(solution)/shard_map/ppermute | solution.py:557
  264.9 4.1 %to_raw.1 = f32[1024,512]{1,0:T(8,128)} custom-call(f32[8,512,128]{2,1,0:T(8,128)} %get-tuple-element.32.x), custom_call_target="tpu_custom_call" | custom-call | flops 2000000000 | bytes 1048576 | tf_op jit(solution)/shard_map/to_raw/pallas_call | solution.py:106
  269.0 16.7 %collective-permute-done.14.up = f32[4,512,128]{2,1,0:T(8,128)S(1)} collective-permute-done((f32[4,512,128]{2,1,0:T(8,128)}, f32[4,512,128]{2,1,0:T(8,128)S(1)}, u32[]{:S(2)}, u32[]{:S(2)}) %collective-permute-start.14) | collective-permute-done | bytes 1048608 | tf_op jit(solution)/shard_map/ppermute | solution.py:554
  285.7 1.0 copy-done.13
  286.7 0.4 copy-done.14
  287.1 4.4 %grad_out.1 = f32[1024,512]{1,0:T(8,128)} custom-call(f32[8,512,128]{2,1,0:T(8,128)} %get-tuple-element.39.x, f32[4,512,128]{2,1,0:T(8,128)} %copy-done.13, f32[4,512,128]{2,1,0:T(8,128)} %copy-done.14), custom_call_target="tpu_custom_call" | custom-call | flops 2000000000 | bytes 1048576 | tf_op jit(solution)/shard_map/grad_out/pallas_call | solution.py:126
  (42 shorter events, 0.1 us)
Async XLA Ops:
  0.6 29.0 %copy-start = (s32[2,64,64]{2,1,0:T(8,128)S(1)}, s32[2,64,64]{2,1,0:T(8,128)}, u32[]{:S(2)}) copy-start(s32[2,64,64]{2,1,0:T(8,128)} %param.16) | copy-start | bytes 98308
  0.6 13.9 %copy-start.4 = (s32[8,512]{1,0:T(8,128)S(1)}, s32[8,512]{1,0:T(8,128)}, u32[]{:S(2)}) copy-start(s32[8,512]{1,0:T(8,128)} %param.14) | copy-start | bytes 49156
  4.9 49.4 %collective-permute-start.1 = (f32[4,512,128]{2,1,0:T(8,128)}, f32[4,512,128]{2,1,0:T(8,128)S(1)}, u32[]{:S(2)}, u32[]{:S(2)}) collective-permute-start(f32[4,512,128]{2,1,0:T(8,128)} %get-tuple-element.22.top), channel_id=1, source_target_pairs={{1,0},{2,1},{3,2},{4,3},{5,4},{6,5},{7,6},{8,7},{9,8},{10,9},{11,1... | collective-permute-start | bytes 3145736 | tf_op jit(solution)/shard_map/ppermute | solution.py:557
  12.6 41.6 %collective-permute-start = (f32[4,512,128]{2,1,0:T(8,128)}, f32[4,512,128]{2,1,0:T(8,128)S(1)}, u32[]{:S(2)}, u32[]{:S(2)}) collective-permute-start(f32[4,512,128]{2,1,0:T(8,128)} %get-tuple-element.23.bot), channel_id=1, source_target_pairs={{0,1},{1,2},{2,3},{3,4},{4,5},{5,6},{6,7},{7,8},{8,9},{9,10},{10,1... | collective-permute-start | bytes 3145736 | tf_op jit(solution)/shard_map/ppermute | solution.py:554
  15.2 16.2 %copy-start.5 = (s32[2,64,8]{1,2,0:T(8,128)S(1)}, s32[2,64,8]{1,2,0:T(8,128)}, u32[]{:S(2)}) copy-start(s32[2,64,8]{1,2,0:T(8,128)} %param.15) | copy-start | bytes 12292
  19.6 34.7 %collective-permute-start.2 = (f32[3,512,128]{2,1,0:T(8,128)}, f32[3,512,128]{2,1,0:T(8,128)S(1)}, u32[]{:S(2)}, u32[]{:S(2)}) collective-permute-start(f32[3,512,128]{2,1,0:T(8,128)} %get-tuple-element.25), channel_id=1, source_target_pairs={{0,1},{1,2},{2,3},{3,4},{4,5},{5,6},{6,7},{7,8},{8,9},{9,10},{10,1... | collective-permute-start | bytes 2359304 | tf_op jit(solution)/shard_map/ppermute | solution.py:554
  21.5 32.8 %collective-permute-start.3 = (f32[3,512,128]{2,1,0:T(8,128)}, f32[3,512,128]{2,1,0:T(8,128)}, u32[]{:S(2)}, u32[]{:S(2)}) collective-permute-start(f32[3,512,128]{2,1,0:T(8,128)} %get-tuple-element.26), channel_id=1, source_target_pairs={{1,0},{2,1},{3,2},{4,3},{5,4},{6,5},{7,6},{8,7},{9,8},{10,9},{11,1... | collective-permute-start | bytes 2359304 | tf_op jit(solution)/shard_map/ppermute | solution.py:557
  54.2 0.9 copy-start.15
  54.3 1.2 copy-start.9
  54.3 1.5 copy-start.10
  55.8 43.1 %copy-start.2 = (f32[8,512]{1,0:T(8,128)S(1)}, f32[8,512]{1,0:T(8,128)}, u32[]{:S(2)}) copy-start(f32[8,512]{1,0:T(8,128)} %convert_select_fusion.sea) | copy-start | bytes 49156
  55.8 43.7 %copy-start.6 = (s32[1,1,8]{2,1,0:T(1,128)S(1)}, s32[1,1,8]{2,1,0:T(1,128)}, u32[]{:S(2)}) copy-start(s32[1,1,8]{2,1,0:T(1,128)} %param.18) | copy-start | bytes 100
  74.7 10.5 %collective-permute-start.6 = (f32[32,128]{1,0:T(8,128)}, f32[32,128]{1,0:T(8,128)S(1)}, u32[]{:S(2)}, u32[]{:S(2)}) collective-permute-start(f32[32,128]{1,0:T(8,128)} %get-tuple-element.30), channel_id=1, source_target_pairs={{0,64},{64,0},{1,65},{65,1},{2,66},{66,2},{3,67},{67,3},{4,68},{68... | collective-permute-start | bytes 49160 | tf_op jit(solution)/shard_map/ppermute | solution.py:560
  76.2 57.0 %collective-permute-start.5 = (f32[4,512,128]{2,1,0:T(8,128)}, f32[4,512,128]{2,1,0:T(8,128)S(1)}, u32[]{:S(2)}, u32[]{:S(2)}) collective-permute-start(f32[4,512,128]{2,1,0:T(8,128)} %get-tuple-element.28.top), channel_id=1, source_target_pairs={{1,0},{2,1},{3,2},{4,3},{5,4},{6,5},{7,6},{8,7},{9,8},{10,9},{11,1... | collective-permute-start | bytes 3145736 | tf_op jit(solution)/shard_map/ppermute | solution.py:557
  82.2 51.0 %collective-permute-start.4 = (f32[4,512,128]{2,1,0:T(8,128)}, f32[4,512,128]{2,1,0:T(8,128)S(1)}, u32[]{:S(2)}, u32[]{:S(2)}) collective-permute-start(f32[4,512,128]{2,1,0:T(8,128)} %get-tuple-element.29.bot), channel_id=1, source_target_pairs={{0,1},{1,2},{2,3},{3,4},{4,5},{5,6},{6,7},{7,8},{8,9},{9,10},{10,1... | collective-permute-start | bytes 3145736 | tf_op jit(solution)/shard_map/ppermute | solution.py:554
  85.3 0.6 copy-start.3
  87.4 21.4 %all-to-all-start = ((f32[64,8,128]{2,1,0:T(8,128)}), f32[64,8,128]{2,1,0:T(8,128)S(1)}, u32[]{:S(2)}, u32[]{:S(2)}) async-start(f32[64,8,128]{2,1,0:T(8,128)} %bitcast.20), calls=%async_computation | async-start | bytes 524288 | tf_op jit(solution)/shard_map/all_to_all | solution.py:564
  108.8 0.7 copy-start.1
  115.4 14.3 %collective-permute-start.8 = (f32[16,128]{1,0:T(8,128)S(1)}, f32[16,128]{1,0:T(8,128)S(1)}, u32[]{:S(2)}, u32[]{:S(2)}) collective-permute-start(f32[16,128]{1,0:T(8,128)S(1)} %get-tuple-element.42), channel_id=1, source_target_pairs={{1,0},{2,1},{3,2},{4,3},{5,4},{6,5},{7,6},{8,7},{9,8},{10,9},{11,1... | collective-permute-start | bytes 24584 | tf_op jit(solution)/shard_map/ppermute | solution.py:557
  123.7 9.5 %collective-permute-start.7 = (f32[16,128]{1,0:T(8,128)S(1)}, f32[16,128]{1,0:T(8,128)S(1)}, u32[]{:S(2)}, u32[]{:S(2)}) collective-permute-start(f32[16,128]{1,0:T(8,128)S(1)} %get-tuple-element.43), channel_id=1, source_target_pairs={{0,1},{1,2},{2,3},{3,4},{4,5},{5,6},{6,7},{7,8},{8,9},{9,10},{10,1... | collective-permute-start | bytes 24584 | tf_op jit(solution)/shard_map/ppermute | solution.py:554
  129.7 3.5 %copy-start.17 = (f32[16,128]{1,0:T(8,128)}, f32[16,128]{1,0:T(8,128)S(1)}, u32[]{:S(2)}) copy-start(f32[16,128]{1,0:T(8,128)S(1)} %collective-permute-done.8.sd) | copy-start | bytes 24580
  133.1 0.6 copy-start.18
  133.2 1.0 copy-start.7
  133.2 1.4 copy-start.8
  173.8 56.9 %collective-permute-start.9 = (f32[4,512,128]{2,1,0:T(8,128)}, f32[4,512,128]{2,1,0:T(8,128)S(1)}, u32[]{:S(2)}, u32[]{:S(2)}) collective-permute-start(f32[4,512,128]{2,1,0:T(8,128)} %get-tuple-element.34), channel_id=1, source_target_pairs={{0,1},{1,2},{2,3},{3,4},{4,5},{5,6},{6,7},{7,8},{8,9},{9,10},{10,1... | collective-permute-start | bytes 3145736 | tf_op jit(solution)/shard_map/ppermute | solution.py:554
  175.7 55.0 %collective-permute-start.10 = (f32[4,512,128]{2,1,0:T(8,128)}, f32[4,512,128]{2,1,0:T(8,128)S(1)}, u32[]{:S(2)}, u32[]{:S(2)}) collective-permute-start(f32[4,512,128]{2,1,0:T(8,128)} %get-tuple-element.35), channel_id=1, source_target_pairs={{1,0},{2,1},{3,2},{4,3},{5,4},{6,5},{7,6},{8,7},{9,8},{10,9},{11,1... | collective-permute-start | bytes 3145736 | tf_op jit(solution)/shard_map/ppermute | solution.py:557
  183.8 21.4 %collective-permute-start.11 = (f32[16,128]{1,0:T(8,128)}, f32[16,128]{1,0:T(8,128)S(1)}, u32[]{:S(2)}, u32[]{:S(2)}) collective-permute-start(f32[16,128]{1,0:T(8,128)} %get-tuple-element.37), channel_id=1, source_target_pairs={{0,1},{1,2},{2,3},{3,4},{4,5},{5,6},{6,7},{7,8},{8,9},{9,10},{10,1... | collective-permute-start | bytes 24584 | tf_op jit(solution)/shard_map/ppermute | solution.py:554
  185.8 19.4 %collective-permute-start.12 = (f32[16,128]{1,0:T(8,128)}, f32[16,128]{1,0:T(8,128)S(1)}, u32[]{:S(2)}, u32[]{:S(2)}) collective-permute-start(f32[16,128]{1,0:T(8,128)} %get-tuple-element.38), channel_id=1, source_target_pairs={{1,0},{2,1},{3,2},{4,3},{5,4},{6,5},{7,6},{8,7},{9,8},{10,9},{11,1... | collective-permute-start | bytes 24584 | tf_op jit(solution)/shard_map/ppermute | solution.py:557
  205.2 0.6 copy-start.19
  205.2 0.6 copy-start.20
  226.7 3.9 %collective-permute-start.13 = (f32[32,128]{1,0:T(8,128)}, f32[32,128]{1,0:T(8,128)S(1)}, u32[]{:S(2)}, u32[]{:S(2)}) collective-permute-start(f32[32,128]{1,0:T(8,128)} %collect.1), channel_id=1, source_target_pairs={{0,64},{64,0},{1,65},{65,1},{2,66},{66,2},{3,67},{67,3},{4,68},{68... | collective-permute-start | bytes 49160 | tf_op jit(solution)/shard_map/ppermute | solution.py:560
  230.6 0.6 copy-start.16
  230.6 1.0 copy-start.11
  230.6 1.3 copy-start.12
  254.8 30.9 %collective-permute-start.14 = (f32[4,512,128]{2,1,0:T(8,128)}, f32[4,512,128]{2,1,0:T(8,128)S(1)}, u32[]{:S(2)}, u32[]{:S(2)}) collective-permute-start(f32[4,512,128]{2,1,0:T(8,128)} %get-tuple-element.40), channel_id=1, source_target_pairs={{0,1},{1,2},{2,3},{3,4},{4,5},{5,6},{6,7},{7,8},{8,9},{9,10},{10,1... | collective-permute-start | bytes 3145736 | tf_op jit(solution)/shard_map/ppermute | solution.py:554
  256.8 29.0 %collective-permute-start.15 = (f32[4,512,128]{2,1,0:T(8,128)}, f32[4,512,128]{2,1,0:T(8,128)S(1)}, u32[]{:S(2)}, u32[]{:S(2)}) collective-permute-start(f32[4,512,128]{2,1,0:T(8,128)} %get-tuple-element.41), channel_id=1, source_target_pairs={{1,0},{2,1},{3,2},{4,3},{5,4},{6,5},{7,6},{8,7},{9,8},{10,9},{11,1... | collective-permute-start | bytes 3145736 | tf_op jit(solution)/shard_map/ppermute | solution.py:557
  285.7 1.0 copy-start.13
  285.7 1.3 copy-start.14
where the time goes:
time: 293 us; the launch traced here: 292 us
  Pallas kernels  117 us (40%)
  starting transfers between devices  80.4 us (27%)
  waiting for transfers between devices  66.8 us (23%)
  blocking collectives  14.3 us (5%)
  local copies, waits for them, and re-layouts  9.99 us (3%)
    ppermute x7, starting transfers between devices, to_prev(): return lax.ppermute(x, 'tile', up_pairs)  54.6 us
    ppermute x7, waiting for transfers between devices, to_next(): return lax.ppermute(x, 'tile', down_pairs)  54.2 us
    pallas_call x1, Pallas kernels, middle_block(): pl.pallas_call(middle_kernel, out_shape=(sds(8, LON, LEV), sds(8, LON, LE...  39.2 us
    pallas_call x1, Pallas kernels, last_block(): pl.pallas_call(last_kernel, out_shape=(sds(8, LON, LEV), sds(4, LON, LEV)...  22.9 us
    pallas_call x1, Pallas kernels, first_block(): pl.pallas_call(first_kernel, out_shape=(sds(4, LON, LEV), sds(4, LON, LEV...  18.9 us
    all_to_all x1, blocking collectives, exchange(): x = lax.all_to_all(x, 'tile', split_axis=0, concat_axis=0, tiled=True)  14.3 us
    ppermute x7, starting transfers between devices, to_next(): return lax.ppermute(x, 'tile', down_pairs)  13.4 us
    all_to_all x1, starting transfers between devices, exchange(): x = lax.all_to_all(x, 'tile', split_axis=0, concat_axis=0, tiled=True)  11 us
  transfers between devices with their start and end apart: 17, of which 6 were waited for; matrix products, arithmetic and copies ran while one was open for 1% of the time, Pallas kernels for 9%

commit v1 on v0

v1 whole, which is shorter than its diff:
```python
import jax
import jax.numpy as jnp
from jax import lax
from jax.experimental import pallas as pl
from jax.experimental.pallas import tpu as pltpu
from jax.sharding import PartitionSpec as P

F32 = jnp.float32
BF = jnp.bfloat16
LON, LEV = 512, 128
OFF, PAD = 8, 528
NR = 18
VM = pl.BlockSpec(memory_space=pltpu.VMEM)
SM = pl.BlockSpec(memory_space=pltpu.SMEM)
OFFSETS = tuple(range(-7, 8)) + (32,)


def sds(*shape, dtype=F32):
    return jax.ShapeDtypeStruct(shape, dtype)


def cost(us):
    return pl.CostEstimate(flops=int(us * 5e8), bytes_accessed=1 << 20, transcendentals=0)


def params(**kw):
    return pltpu.CompilerParams(vmem_limit_bytes=44 * 2**20, **kw)


def halves(x):
    hi = x.astype(BF)
    return hi, (x - hi.astype(F32)).astype(BF)


def start_in_kernel(x, top, bot):
    for r in range(8):
        dst = top if r < 4 else bot
        dst[r % 4] = x[pl.ds(r, 128, stride=8), :].T


def start_in(x):
    blk = pl.BlockSpec((4, 128, 128), lambda j: (0, j, 0))
    return pl.pallas_call(
        start_in_kernel,
        grid=(4,),
        out_shape=(sds(4, LON, LEV), sds(4, LON, LEV)),
        in_specs=[pl.BlockSpec((1024, 128), lambda j: (0, j))],
        out_specs=(blk, blk),
        compiler_params=params(),
        cost_estimate=cost(4),
        name="start_in",
    )(x)


def diff_in_kernel(x, sea, full, top, bot):
    for r in range(8):
        y = (x[pl.ds(r, 128, stride=8), :] * sea[r : r + 1, :]).T
        full[r] = y
        if r < 3:
            top[r] = y
        if r > 4:
            bot[r - 5] = y


def diff_in(x, sea):
    blk = pl.BlockSpec((3, 128, 128), lambda j: (0, j, 0))
    return pl.pallas_call(
        diff_in_kernel,
        grid=(4,),
        out_shape=(sds(8, LON, LEV), sds(3, LON, LEV), sds(3, LON, LEV)),
        in_specs=[
            pl.BlockSpec((1024, 128), lambda j: (0, j)),
            pl.BlockSpec((8, 128), lambda j: (0, j)),
        ],
        out_specs=(pl.BlockSpec((8, 128, 128), lambda j: (0, j, 0)), blk, blk),
        compiler_params=params(),
        cost_estimate=cost(4),
        name="diff_in",
    )(x, sea)


def to_rows_kernel(x, o):
    for r in range(8):
        o[r] = x[pl.ds(r, 128, stride=8), :].T


def to_rows(x):
    return pl.pallas_call(
        to_rows_kernel,
        grid=(4,),
        out_shape=sds(8, LON, LEV),
        in_specs=[pl.BlockSpec((1024, 128), lambda j: (0, j))],
        out_specs=pl.BlockSpec((8, 128, 128), lambda j: (0, j, 0)),
        compiler_params=params(),
        cost_estimate=cost(4),
        name="to_rows",
    )(x)


def to_raw_kernel(x, o):
    for r in range(8):
        o[pl.ds(r, 128, stride=8), :] = x[r].T


def to_raw(x):
    return pl.pallas_call(
        to_raw_kernel,
        grid=(4,),
        out_shape=sds(1024, LON),
        in_specs=[pl.BlockSpec((8, 128, 128), lambda j: (0, j, 0))],
        out_specs=pl.BlockSpec((1024, 128), lambda j: (0, j)),
        compiler_params=params(),
        cost_estimate=cost(4),
        name="to_raw",
    )(x)


def grad_out_kernel(me, x, up, dn, o):
    for r in range(8):
        add = up[r] if r < 4 else dn[r - 4]
        o[pl.ds(r, 128, stride=8), :] = (x[r] + add).T
    for edge, r0 in ((0, 0), (63, 4)):

        @pl.when(me[0] == edge)
        def _(r0=r0):
            for r in range(r0, r0 + 4):
                o[pl.ds(r, 128, stride=8), :] = x[r].T


def grad_out(me, x, up, dn):
    blk = pl.BlockSpec((4, 128, 128), lambda j: (0, j, 0))
    return pl.pallas_call(
        grad_out_kernel,
        grid=(4,),
        out_shape=sds(1024, LON),
        in_specs=[SM, pl.BlockSpec((8, 128, 128), lambda j: (0, j, 0)), blk, blk],
        out_specs=pl.BlockSpec((1024, 128), lambda j: (0, j)),
        compiler_params=params(),
        cost_estimate=cost(4),
        name="grad_out",
    )(me, x, up, dn)


def mix_kernel(w, fwd, bwd):
    for dst, x in ((fwd, w[...].T), (bwd, w[...])):
        hi, lo = halves(x)
        dst[0:128, 0:128] = hi
        dst[128:256, 0:128] = hi
        dst[0:128, 128:256] = lo
        dst[128:256, 128:256] = jnp.zeros((128, 128), BF)


def mixes(w):
    return pl.pallas_call(
        mix_kernel,
        out_shape=(sds(256, 256, dtype=BF), sds(256, 256, dtype=BF)),
        in_specs=[VM],
        out_specs=(VM, VM),
        name="mixes",
    )(w)


def put(v, r, j, new):
    v[r, pl.ds(OFF + 128 * j, 128), :] = new
    if j == 0:
        v[r, pl.ds(OFF + LON, 1), :] = new[0:1]
    if j == 3:
        v[r, pl.ds(OFF - 1, 1), :] = new[127:128]


def put_halves(h, r, j, new):
    hi, lo = halves(new)
    h[r, pl.ds(128 * j, 128), 0:128] = hi
    h[r, pl.ds(128 * j, 128), 128:256] = lo


def around(v, r, j):
    at = OFF + 128 * j
    n = v[r - 1, pl.ds(at, 128), :] + v[r + 1, pl.ds(at, 128), :]
    return n + (v[r, pl.ds(at - 1, 128), :] + v[r, pl.ds(at + 1, 128), :])


GROUP = {14: 7, 12: 6, 10: 5, 8: 4}


def mixed_rows(h, w2, lo, n, body):
    k = GROUP[n]

    def step(i, carry):
        r0 = lo + k * i
        y = jnp.dot(h[pl.ds(r0, k)].reshape(LON * k, 256), w2[...], preferred_element_type=F32)
        for q in range(k):
            for j in range(4):
                part = y[LON * q + 128 * j : LON * q + 128 * j + 128]
                body(r0 + q, j, part[:, 0:128] + part[:, 128:256])
        return carry

    lax.fori_loop(0, n // k, step, 0)


def forward_step(va, vb, h, d, w2, s, first=False, last=False):
    def body(r, j, y):
        c = va[r, pl.ds(OFF + 128 * j, 128), :]
        dd = d[r, pl.ds(128 * j, 128), :]
        n = dd * (around(va, r, j) - 4.0 * c)
        if first:
            c = jnp.where(dd > 0.0, c, 0.0)
        new = (c + n) + y
        put(vb, r, j, new)
        if not last:
            put_halves(h, r, j, new)

    mixed_rows(h, w2, 1 + s, 16 - 2 * s, body)


def push_step(ga, gb, u, h, d, w2, s, last=False):
    def finish(r, j, new, dd):
        u[r, pl.ds(128 * j, 128), :] = new
        put(gb, r, j, dd * new)
        put_halves(h, r, j, new)

    def body(r, j, y):
        at = pl.ds(128 * j, 128)
        n = around(ga, r, j) - 4.0 * ga[r, pl.ds(OFF + 128 * j, 128), :]
        c = u[r, at, :]
        if last:
            u[r, at, :] = (c + n) + y
        else:
            dd = d[r, at, :]
            finish(r, j, (c + jnp.where(dd > 0.0, n, 0.0)) + y, dd)

    mixed_rows(h, w2, 6 - s, 6 + 2 * s, body)
    for r, near in ((5 - s, 6 - s), (12 + s, 11 + s)):
        for j in range(4):
            at = pl.ds(128 * j, 128)
            n = ga[near, pl.ds(OFF + 128 * j, 128), :]
            if last:
                u[r, at, :] = n
            else:
                dd = d[r, at, :]
                finish(r, j, jnp.where(dd > 0.0, n, 0.0), dd)


def push_block(ga, gb, u, h, d, w2):
    for s, g in ((1, ga), (2, gb), (3, ga), (4, gb)):
        g[5 - s] = jnp.zeros((PAD, 128), F32)
        g[12 + s] = jnp.zeros((PAD, 128), F32)
    push_step(ga, gb, u, h, d, w2, 1)
    push_step(gb, ga, u, h, d, w2, 2)
    push_step(ga, gb, u, h, d, w2, 3)
    push_step(gb, ga, u, h, d, w2, 4, last=True)


def forward_block(va, vb, h, d, w2, first=False):
    forward_step(va, vb, h, d, w2, 1, first=first)
    forward_step(vb, va, h, d, w2, 2)
    forward_step(va, vb, h, d, w2, 3)
    forward_step(vb, va, h, d, w2, 4, last=True)


def copies(sems, pairs):
    out = [pltpu.make_async_copy(a, b, sems.at[i]) for i, (a, b) in enumerate(pairs)]
    for c in out:
        c.start()
    return out


def wait(*todo):
    for c in todo:
        c.wait()


def tile_rows(v, r0, n):
    return v.at[pl.ds(r0, n), pl.ds(OFF, LON), :]


def clear_ends(me, up, dn):
    for edge, todo in ((0, up), (63, dn)):

        @pl.when(me[0] == edge)
        def _(todo=todo):
            for ref, r0, n in todo:
                ref[pl.ds(r0, n)] = jnp.zeros((n,) + ref.shape[1:], F32)


def lanes():
    return lax.broadcasted_iota(jnp.int32, (128, 128), 1)


def gather_surface(read, count):
    def step(r, acc):
        for j in range(4):
            p = 4 * r + j
            acc = jnp.where(lanes() == p, pltpu.roll(read(r, j), p, 1), acc)
        return acc

    return lax.fori_loop(0, count, step, jnp.zeros((128, 128), F32)).T


def spread_column(cols, p):
    return jnp.where(lanes() == 0, pltpu.roll(cols, (128 - p) % 128, 1), 0.0)


BLOCK_SCRATCH = [
    pltpu.VMEM((NR, PAD, 128), F32),
    pltpu.VMEM((NR, PAD, 128), F32),
    pltpu.VMEM((NR, LON, 256), BF),
    pltpu.VMEM((NR, LON, 128), F32),
]
U_SCRATCH = pltpu.VMEM((NR, LON, 128), F32)
COLS = pltpu.VMEM((128, 128), F32)
ANY = pl.BlockSpec(memory_space=pl.ANY)


def dma_sems(n):
    return pltpu.SemaphoreType.DMA((n,))


def first_kernel(me, top, bot, hu, hd, dt, du, dn, w2, o_top, o_bot, o_surf, va, vb, h, d, sems):
    c = copies(
        sems,
        [
            (dt, d.at[pl.ds(5, 8)]),
            (top, tile_rows(va, 5, 4)),
            (bot, tile_rows(va, 9, 4)),
            (du, d.at[pl.ds(2, 3)]),
            (hu, tile_rows(va, 1, 4)),
            (dn, d.at[pl.ds(13, 3)]),
            (hd, tile_rows(va, 13, 4)),
        ],
    )

    def prepare(r0, n):
        def cp(i, carry):
            r = r0 + i
            for j in range(4):
                x = va[r, pl.ds(OFF + 128 * j, 128), :]
                if j == 0:
                    va[r, pl.ds(OFF + LON, 1), :] = x[0:1]
                if j == 3:
                    va[r, pl.ds(OFF - 1, 1), :] = x[127:128]
                keep = d[r, pl.ds(128 * j, 128), :] > 0.0
                put_halves(h, r, j, jnp.where(keep, x, 0.0))
            return carry

        lax.fori_loop(0, n, cp, 0)

    wait(c[0], c[1])
    prepare(5, 4)
    wait(c[2])
    prepare(9, 4)
    wait(*c[3:])
    clear_ends(me, ((va, 1, 4), (d, 2, 3)), ((va, 13, 4), (d, 13, 3)))
    prepare(2, 3)
    prepare(13, 3)
    forward_block(va, vb, h, d, w2, first=True)
    c = copies(sems, [(tile_rows(va, 5, 4), o_top), (tile_rows(va, 9, 4), o_bot)])
    o_surf[...] = gather_surface(lambda r, j: va[r + 5, pl.ds(OFF + 128 * j, 128), :], 8)[0:32]
    wait(*c)


def first_block(*args):
    return pl.pallas_call(
        first_kernel,
        out_shape=(sds(4, LON, LEV), sds(4, LON, LEV), sds(32, 128)),
        in_specs=[SM] + [ANY] * 7 + [VM],
        out_specs=(ANY, ANY, VM),
        scratch_shapes=BLOCK_SCRATCH + [dma_sems(7)],
        compiler_params=params(),
        cost_estimate=cost(15),
        name="first_block",
    )(*args)


def middle_kernel(
    me, top, bot, hu, hd, s, su, sd, dt, du, dn, m, w2f, w2b,
    o_final, o_adj, o_up, o_dn, o_s, o_su, o_sd, va, vb, h, d, u, mm, cols, sems,
):
    c = copies(
        sems,
        [
            (top, tile_rows(va, 5, 4)),
            (bot, tile_rows(va, 9, 4)),
            (hu, tile_rows(va, 1, 4)),
            (hd, tile_rows(va, 13, 4)),
            (dt, d.at[pl.ds(5, 8)]),
            (du, d.at[pl.ds(2, 3)]),
            (dn, d.at[pl.ds(13, 3)]),
            (m, mm),
        ],
    )
    cols[0:16] = su[...]
    cols[16:48] = s[...]
    cols[48:64] = sd[...]
    cols[64:128] = jnp.zeros((64, 128), F32)
    clear_ends(me, ((cols, 0, 16),), ((cols, 48, 16),))
    cols[...] = cols[...].T

    def prepare(r0):
        def cp(i, carry):
            r = r0 + i
            for j in range(4):
                x = va[r, pl.ds(OFF + 128 * j, 128), :]
                x = x + spread_column(cols[...], 4 * (r - 1) + j)
                put(va, r, j, x)
                put_halves(h, r, j, x)
            return carry

        lax.fori_loop(0, 4, cp, 0)

    for i, r0 in ((0, 5), (1, 9)):
        wait(c[i])
        prepare(r0)
    wait(*c[2:7])
    clear_ends(me, ((va, 1, 4), (d, 2, 3)), ((va, 13, 4), (d, 13, 3)))
    prepare(1)
    prepare(13)
    forward_block(va, vb, h, d, w2f)
    out = copies(sems, [(tile_rows(va, 5, 8), o_final)])
    wait(c[7])

    def body(i, carry):
        r = 5 + i
        for j in range(4):
            at = pl.ds(128 * j, 128)
            x = va[r, pl.ds(OFF + 128 * j, 128), :] - mm[i, at, :]
            dd = d[r, at, :]
            x = jnp.where(dd > 0.0, x, 0.0)
            u[r, at, :] = x
            put(vb, r, j, dd * x)
            put_halves(h, r, j, x)
        return carry

    lax.fori_loop(0, 8, body, 0)
    wait(*out)
    push_block(vb, va, u, h, d, w2b)
    out = copies(
        sems,
        [
            (u.at[pl.ds(1, 4)], o_up),
            (u.at[pl.ds(13, 4)], o_dn),
            (u.at[pl.ds(5, 8)], o_adj),
        ],
    )
    g = gather_surface(lambda r, j: u[r + 1, pl.ds(128 * j, 128), :], 16)
    o_su[...] = g[0:16]
    o_s[...] = g[16:48]
    o_sd[...] = g[48:64]
    wait(*out)


def middle_block(*args):
    return pl.pallas_call(
        middle_kernel,
        out_shape=(
            sds(8, LON, LEV), sds(8, LON, LEV), sds(4, LON, LEV), sds(4, LON, LEV),
            sds(32, 128), sds(16, 128), sds(16, 128),
        ),
        in_specs=[SM] + [ANY] * 4 + [VM] * 3 + [ANY] * 4 + [VM] * 2,
        out_specs=(ANY,) * 4 + (VM,) * 3,
        scratch_shapes=BLOCK_SCRATCH
        + [U_SCRATCH, pltpu.VMEM((8, LON, 128), F32), COLS, dma_sems(8)],
        compiler_params=params(),
        cost_estimate=cost(30),
        name="middle_block",
    )(*args)


def last_kernel(
    me, adj, ru, rd, s, top, bot, dt, du, dn, w2b, o_base, o_up, o_dn,
    va, vb, h, d, u, got, base, cols, sems,
):
    c = copies(
        sems,
        [
            (adj, u.at[pl.ds(5, 8)]),
            (dt, d.at[pl.ds(5, 8)]),
            (ru, got.at[pl.ds(0, 4)]),
            (rd, got.at[pl.ds(4, 4)]),
            (du, d.at[pl.ds(2, 3)]),
            (dn, d.at[pl.ds(13, 3)]),
            (top, base.at[pl.ds(0, 4)]),
            (bot, base.at[pl.ds(4, 4)]),
        ],
    )
    cols[0:32] = s[...]
    cols[32:128] = jnp.zeros((96, 128), F32)
    cols[...] = cols[...].T
    wait(*c[0:4])
    clear_ends(me, ((got, 0, 4),), ((got, 4, 4),))

    def cp(i, carry):
        r = 5 + i
        for j in range(4):
            at = pl.ds(128 * j, 128)
            x = u[r, at, :] + got[i, at, :]
            x = x + spread_column(cols[...], 4 * i + j)
            dd = d[r, at, :]
            x = jnp.where(dd > 0.0, x, 0.0)
            u[r, at, :] = x
            put(vb, r, j, dd * x)
            put_halves(h, r, j, x)
        return carry

    lax.fori_loop(0, 8, cp, 0)
    wait(*c[4:8])
    clear_ends(me, ((d, 2, 3),), ((d, 13, 3),))
    push_block(vb, va, u, h, d, w2b)
    out = copies(sems, [(u.at[pl.ds(1, 4)], o_up), (u.at[pl.ds(13, 4)], o_dn)])

    def add(i, carry):
        base[i] = base[i] + u[5 + i]
        return carry

    lax.fori_loop(0, 8, add, 0)
    end = pltpu.make_async_copy(base, o_base, sems.at[2])
    end.start()
    wait(*out)
    end.wait()


def last_block(*args):
    return pl.pallas_call(
        last_kernel,
        out_shape=(sds(8, LON, LEV), sds(4, LON, LEV), sds(4, LON, LEV)),
        in_specs=[SM] + [ANY] * 3 + [VM] + [ANY] * 5 + [VM],
        out_specs=(ANY,) * 3,
        scratch_shapes=BLOCK_SCRATCH
        + [
            U_SCRATCH,
            pltpu.VMEM((8, LON, 128), F32),
            pltpu.VMEM((8, LON, 128), F32),
            COLS,
            dma_sems(8),
        ],
        compiler_params=params(),
        cost_estimate=cost(15),
        name="last_block",
    )(*args)


def offer_kernel(me, send_rows, surf, o):
    o[...] = jnp.zeros((512, 128), F32)
    for off in OFFSETS:
        t = lax.rem(me[0] + (off + 64), 64) * 8
        for q in range(8):
            o[pl.ds(t + q, 1), :] = surf[pl.ds(send_rows[t + q], 1), :]


def offer(me, send_rows, surf):
    return pl.pallas_call(
        offer_kernel,
        out_shape=sds(512, 128),
        in_specs=[SM, SM, VM],
        out_specs=VM,
        name="offer",
    )(me, send_rows, surf)


def fetch_blocks(ids, w, buf, sems):
    for k in range(LIVE):
        pltpu.make_async_copy(w.at[ids[k]], buf.at[k], sems.at[k // 12]).start()


def fetched(w, buf, sems, part):
    pltpu.make_async_copy(w.at[pl.ds(0, 12)], buf.at[pl.ds(12 * part, 12)], sems.at[part]).wait()


LIVE = 48
WEIGHTS = [pltpu.VMEM((LIVE, 128, 128), F32), pltpu.SemaphoreType.DMA((4,))]


def remap_kernel(ids, pick, dest, arrived, w, sea, o, buf, sems):
    fetch_blocks(ids, w, buf, sems)
    acc = jnp.zeros((128, 128), F32)
    for part in range(4):
        fetched(w, buf, sems, part)

        def step(i, acc, part=part):
            for q in range(4):
                k = 12 * part + 4 * i + q
                x = arrived[pl.ds(pick[k], 1), :]
                red = jnp.sum(buf[k] * x, axis=1, keepdims=True)
                acc = acc + jnp.where(lanes() == dest[k], red, 0.0)
            return acc

        acc = lax.fori_loop(0, 3, step, acc)
    o[...] = acc.T[0:32] * sea[...]


def remap(ids, pick, dest, arrived, w, sea):
    return pl.pallas_call(
        remap_kernel,
        out_shape=sds(32, 128),
        in_specs=[SM, SM, SM, VM, ANY, VM],
        out_specs=VM,
        scratch_shapes=WEIGHTS,
        compiler_params=params(),
        cost_estimate=cost(3),
        name="remap",
    )(ids, pick, dest, arrived, w, sea)


def remap_back_kernel(me, ids, pick, dest, s, ru, rd, w, sea, o, cols, wide, buf, sems):
    fetch_blocks(ids, w, buf, sems)
    cols[0:16] = ru[...]
    cols[16:32] = rd[...]
    clear_ends(me, ((cols, 0, 16),), ((cols, 16, 16),))
    cols[0:32] = (cols[0:32] + s[...]) * sea[...]
    cols[32:128] = jnp.zeros((96, 128), F32)
    cols[...] = cols[...].T
    for p in range(32):
        wide[p] = jnp.broadcast_to(cols[:, p : p + 1], (128, 128))
    o[...] = jnp.zeros((512, 128), F32)
    for part in range(4):
        fetched(w, buf, sems, part)

        def step(i, carry, part=part):
            for q in range(4):
                k = 12 * part + 4 * i + q
                red = jnp.sum(buf[k] * wide[dest[k]], axis=0, keepdims=True)
                o[pl.ds(pick[k], 1), :] = red
            return carry

        lax.fori_loop(0, 3, step, 0)


def remap_back(me, ids, pick, dest, s, ru, rd, w, sea):
    return pl.pallas_call(
        remap_back_kernel,
        out_shape=sds(512, 128),
        in_specs=[SM, SM, SM, SM, VM, VM, VM, ANY, VM],
        out_specs=VM,
        scratch_shapes=[COLS, pltpu.VMEM((32, 128, 128), F32)] + WEIGHTS,
        compiler_params=params(),
        cost_estimate=cost(3),
        name="remap_back",
    )(me, ids, pick, dest, s, ru, rd, w, sea)


def collect_kernel(me, send_rows, got, o):
    o[...] = jnp.zeros((32, 128), F32)
    for off in OFFSETS:
        t = lax.rem(me[0] + (off + 64), 64) * 8
        for q in range(8):
            at = pl.ds(send_rows[t + q], 1)
            o[at, :] = o[at, :] + got[pl.ds(t + q, 1), :]


def collect(me, send_rows, got):
    return pl.pallas_call(
        collect_kernel,
        out_shape=sds(32, 128),
        in_specs=[SM, SM, VM],
        out_specs=VM,
        name="collect",
    )(me, send_rows, got)


def shards(
    starting_perturbation,
    measured_discrepancy,
    diffusion,
    vert_mix,
    ocean_mask,
    pair_tile,
    pair_patch,
    dest_patch,
    pair_blocks,
    remap_weight,
):
    component = lax.axis_index("comp")
    own_tile = lax.axis_index("tile")
    down_pairs = [(i, (i + 1) % 64) for i in range(64)]
    up_pairs = [((i + 1) % 64, i) for i in range(64)]

    def to_next(x):
        return lax.ppermute(x, "tile", down_pairs)

    def to_prev(x):
        return lax.ppermute(x, "tile", up_pairs)

    def swap(x):
        return lax.ppermute(x, "comp", [(0, 1), (1, 0)])

    def exchange(x):
        x = x.reshape(64, 8, 128)
        x = lax.all_to_all(x, "tile", split_axis=0, concat_axis=0, tiled=True)
        return x.reshape(512, 128)

    start = starting_perturbation.reshape(1024, LON)
    s_top, s_bot = start_in(start)
    s_hu, s_hd = to_next(s_bot), to_prev(s_top)
    sea = jnp.where(component == 1, ocean_mask.astype(F32), 1.0)
    sea32 = sea.reshape(32, 128)
    dt, d_top, d_bot = diff_in(diffusion.reshape(1024, LON), sea)
    du, dd = to_next(d_bot), to_prev(d_top)
    w2f, w2b = mixes(vert_mix[0])

    slots = jnp.arange(64, dtype=jnp.int32)
    live = slots % 8 < jnp.repeat(pair_blocks[0, 0], 8)
    place = jnp.sum((slots[None, :] < slots[:, None]) & live[None, :], axis=1)
    chosen = ((place[None, :] == slots[:LIVE, None]) & live[None, :]).astype(jnp.int32)
    ids = jnp.sum(chosen * slots[None, :], axis=1)
    pick = jnp.repeat(pair_tile[component, own_tile], 8) * 8 + slots % 8
    pick = jnp.sum(chosen * pick[None, :], axis=1)
    dest = jnp.sum(chosen * dest_patch[0, 0][None, :], axis=1)
    hits = (pair_tile[component] == own_tile).astype(jnp.int32)
    sources = pair_patch[component].reshape(64, 8, 8)
    send_rows = jnp.sum(hits[:, :, None] * sources, axis=1).reshape(512)
    me = own_tile.reshape(1)
    weights = remap_weight[0]
    measured = to_rows(measured_discrepancy.reshape(1024, LON))
    s_hu, s_hd, du, dd, w2f, w2b, ids, pick, dest, send_rows, measured, sea32 = (
        lax.optimization_barrier(
            (s_hu, s_hd, du, dd, w2f, w2b, ids, pick, dest, send_rows, measured, sea32)
        )
    )

    v_top, v_bot, surf = first_block(me, s_top, s_bot, s_hu, s_hd, dt, du, dd, w2f)
    other = swap(surf)
    v_top, v_bot, other = lax.optimization_barrier((v_top, v_bot, other))
    v_hu, v_hd = to_next(v_bot), to_prev(v_top)
    arrived = exchange(offer(me, send_rows, other))
    fix = remap(ids, pick, dest, arrived, weights, sea32)
    f_hu, f_hd = to_next(fix[16:32]), to_prev(fix[0:16])
    final, adj, a_up, a_dn, a0, a0_up, a0_dn = middle_block(
        me, v_top, v_bot, v_hu, v_hd, fix, f_hu, f_hd, dt, du, dd, measured, w2f, w2b
    )
    r0u, r0d = to_next(a0_dn), to_prev(a0_up)
    a_up, a_dn, r0u, r0d = lax.optimization_barrier((a_up, a_dn, r0u, r0d))
    ru, rd = to_next(a_dn), to_prev(a_up)
    back = exchange(remap_back(me, ids, pick, dest, a0, r0u, r0d, weights, sea32))
    back = swap(collect(me, send_rows, back))
    base, g_up, g_dn = last_block(me, adj, ru, rd, back, s_top, s_bot, dt, du, dd, w2b)
    gu, gd = to_next(g_dn), to_prev(g_up)
    final_raw = to_raw(final)
    gradient = grad_out(me, base, gu, gd)
    shape = starting_perturbation.shape
    return final_raw.reshape(shape), gradient.reshape(shape)


def solution(mesh):
    field = P("comp", None, "tile", None)
    placed = (
        field,
        field,
        field,
        P("comp", None, None),
        P("tile", None),
        P(),
        P(),
        P("comp", "tile", None),
        P("comp", "tile", None),
        P("comp", "tile", None, None),
    )
    return jax.shard_map(
        shards,
        mesh=mesh,
        in_specs=placed,
        out_specs=(field, field),
        check_vma=False,
    )
```

time: 293 us -> 236 us (0.81)
  Pallas kernels: 117 us -> 72.8 us
  starting transfers between devices: 80.4 us -> 38.7 us
  blocking collectives: 14.3 us -> 52.8 us
  waiting for transfers between devices: 66.8 us -> 55.3 us
    all_to_all x1 -> x2, blocking collectives: 14.3 us -> 52.8 us  [exchange(): x = lax.all_to_all(x, 'tile', split_axis=0, concat_axis=0, tiled=True)]
    ppermute x7, starting transfers between devices: 54.6 us -> 35.6 us  [to_prev(): return lax.ppermute(x, 'tile', up_pairs)]
    pallas_call x1, Pallas kernels: 39.2 us -> 21.1 us  [middle_block(): pl.pallas_call(middle_kernel, out_shape=(sds(8, LON, LEV), sds(8, LON, LE...]
    ppermute x7, starting transfers between devices: 13.4 us -> 0.16 us  [to_next(): return lax.ppermute(x, 'tile', down_pairs)]
    all_to_all x1 -> x0, starting transfers between devices: 11 us -> none  [exchange(): x = lax.all_to_all(x, 'tile', split_axis=0, concat_axis=0, tiled=True)]
    pallas_call x1, Pallas kernels: 22.9 us -> 12.3 us  [last_block(): pl.pallas_call(last_kernel, out_shape=(sds(8, LON, LEV), sds(4, LON, LEV)...]
    all_to_all x1 -> x0, waiting for transfers between devices: 8.58 us -> none  [exchange(): x = lax.all_to_all(x, 'tile', split_axis=0, concat_axis=0, tiled=True)]
    pallas_call x1, Pallas kernels: 18.9 us -> 10.5 us  [first_block(): pl.pallas_call(first_kernel, out_shape=(sds(4, LON, LEV), sds(4, LON, LEV...]
  transfers between devices with their start and end apart: 17 -> 16, of which waited for: 6 -> 7; matrix products, arithmetic and copies ran while one was open for 1% -> 1% of each run, Pallas kernels for 9% -> 10%
where the time goes in v1:
time: 236 us; the launch traced here: 234 us
  Pallas kernels  72.8 us (31%)
  waiting for transfers between devices  55.3 us (23%)
  blocking collectives  52.8 us (22%)
  starting transfers between devices  38.7 us (16%)
  local copies, waits for them, and re-layouts  12.5 us (5%)
    all_to_all x2, blocking collectives, exchange(): x = lax.all_to_all(x, 'tile', split_axis=0, concat_axis=0, tiled=True)  52.8 us
    ppermute x7, waiting for transfers between devices, to_next(): return lax.ppermute(x, 'tile', down_pairs)  49 us
    ppermute x7, starting transfers between devices, to_prev(): return lax.ppermute(x, 'tile', up_pairs)  35.6 us
    pallas_call x1, Pallas kernels, middle_block(): pl.pallas_call(middle_kernel, out_shape=(sds(8, LON, LEV), sds(8, LON, LE...  21.1 us
    pallas_call x1, Pallas kernels, last_block(): pl.pallas_call(last_kernel, out_shape=(sds(8, LON, LEV), sds(4, LON, LEV)...  12.3 us
    unnamed x45, local copies, waits for them, and re-layouts  11.4 us
    pallas_call x1, Pallas kernels, first_block(): pl.pallas_call(first_kernel, out_shape=(sds(4, LON, LEV), sds(4, LON, LEV...  10.5 us
    pallas_call x1, Pallas kernels, remap(): pl.pallas_call(remap_kernel, out_shape=sds(32, 128), in_specs=[SM, SM, SM...  6.63 us
  transfers between devices with their start and end apart: 16, of which 7 were waited for; matrix products, arithmetic and copies ran while one was open for 1% of the time, Pallas kernels for 10%

profile of v1, /device:TPU:8, one launch (start us, length us, event | category | flops | bytes accessed | tf_op | source)
XLA Modules:
  0.0 233.5 jit_solution(6834101594038049798)
XLA Ops:
  0.6 0.0 copy-start
  0.7 1.6 copy-done.3
  2.3 2.3 start_in.1
  4.6 5.8 %collective-permute-start.1 = (f32[4,512,128]{2,1,0:T(8,128)S(1)}, f32[4,512,128]{2,1,0:T(8,128)}, u32[]{:S(2)}, u32[]{:S(2)}) collective-permute-start(f32[4,512,128]{2,1,0:T(8,128)S(1)} %get-tuple-element.41.top), channel_id=1, source_target_pairs={{1,0},{2,1},{3,2},{4,3},{5,4},{6,5},{7,6},{8,7},{9,8},{10,9},{11,1... | collective-permute-start | bytes 3145736 | tf_op jit(solution)/shard_map/ppermute | solution.py:681
  10.4 0.0 copy-start.19
  10.4 0.0 copy-start.20
  10.4 0.0 copy-start.21
  10.4 2.5 %diff_in.1 = (f32[8,512,128]{2,1,0:T(8,128)S(1)}, f32[3,512,128]{2,1,0:T(8,128)}, f32[3,512,128]{2,1,0:T(8,128)}) custom-call(f32[1024,512]{1,0:T(8,128)S(1)} %bitcast.26, f32[8,512]{1,0:T(8,128)S(1)} %convert_select_fusion.sea), custom_call_target="tpu_custom_call" | custom-call | flops 2000000000 | bytes 1048576 | tf_op jit(solution)/shard_map/diff_in/pallas_call | solution.py:67
  13.0 1.3 copy-done.15
  14.3 0.0 collective-permute-start.2
  14.3 6.3 %collective-permute-start.3 = (f32[3,512,128]{2,1,0:T(8,128)}, f32[3,512,128]{2,1,0:T(8,128)S(1)}, u32[]{:S(2)}, u32[]{:S(2)}) collective-permute-start(f32[3,512,128]{2,1,0:T(8,128)} %get-tuple-element.44), channel_id=1, source_target_pairs={{1,0},{2,1},{3,2},{4,3},{5,4},{6,5},{7,6},{8,7},{9,8},{10,9},{11,1... | collective-permute-start | bytes 2359304 | tf_op jit(solution)/shard_map/ppermute | solution.py:681
  20.6 0.2 multiply_reduce_fusion
  20.8 0.1 broadcast_in_dim.10
  20.8 0.1 mul.57
  20.9 0.1 broadcast_in_dim.9
  21.0 0.1 reshape.90
  21.1 0.1 copy.18
  21.2 0.1 copy.17
  21.3 0.7 reshape.91.send_rows
  22.0 1.6 mixes.1
  23.6 0.1 convert_reduce_fusion
  23.7 0.2 select_reduce_fusion
  23.9 0.0 copy-start.5
  23.9 1.6 copy-done.5
  25.5 1.3 to_rows.1.m
  26.8 0.0 copy-start.14
  26.8 1.3 copy-done.14
  28.2 23.7 %collective-permute-done.2.du = f32[3,512,128]{2,1,0:T(8,128)S(1)} collective-permute-done((f32[3,512,128]{2,1,0:T(8,128)}, f32[3,512,128]{2,1,0:T(8,128)S(1)}, u32[]{:S(2)}, u32[]{:S(2)}) %collective-permute-start.2) | collective-permute-done | bytes 786464 | tf_op jit(solution)/shard_map/ppermute | solution.py:678
  51.8 0.0 collective-permute-done.3.dn
  51.8 1.0 copy-done.6
  52.8 0.0 collective-permute-done.1.hd
  52.8 0.0 collective-permute-done.hu
  52.8 1.1 copy-done.7
  54.0 10.5 %first_block.1 = (f32[4,512,128]{2,1,0:T(8,128)S(1)}, f32[4,512,128]{2,1,0:T(8,128)}, f32[32,128]{1,0:T(8,128)S(1)}) custom-call(s32[1]{0:T(128)} %bitcast.me, f32[4,512,128]{2,1,0:T(8,128)S(1)} %get-tuple-element.41.top, f32[4,512,128]{2,1,0:T(8,128)} %get-tuple-element.42.bot, f32[4,512,128]{2,1,0:T(8,128)} %collective-permute-done.hu, ...), custom_call_target="tpu_custom_call" | custom-call | flops 7500000256 | bytes 1048576 | tf_op jit(solution)/shard_map/first_block/pallas_call | solution.py:363
  64.5 1.5 collective-permute-start.4
  65.9 2.3 collective-permute-done.4.surf
  68.3 1.4 collective-permute-start.6
  69.7 0.0 collective-permute-start.5
  69.7 1.6 offer.1
  71.3 28.3 %all_to_all.10 = f32[64,8,128]{2,1,0:T(8,128)S(1)} all-to-all(f32[64,8,128]{2,1,0:T(8,128)} %bitcast.29), channel_id=1, replica_groups=mesh['comp'=2,'tile'=64] {'tile'}, dimensions={0} | all-to-all | bytes 524288 | tf_op jit(solution)/shard_map/all_to_all | solution.py:688
  99.6 2.2 copy-done.1
  101.8 6.6 %remap.1.s = f32[32,128]{1,0:T(8,128)S(1)} custom-call(s32[48]{0:T(128)S(1)} %get-tuple-element.58.ids, s32[48]{0:T(128)S(1)} %get-tuple-element.59.pick, s32[48]{0:T(128)S(1)} %get-tuple-element.60.dest, f32[512,128]{1,0:T(8,128)S(1)} %bitcast.22, f32[64,128,128]{2,1,0:T(8,128)S(1)} %bitcast.23, f32[32,128]{1,0:T(8,128)S(1)} %reshape.93.sea), custom_call_target="tpu_custom_call" | custom-call | flops 1500000000 | bytes 1048576 | tf_op jit(solution)/shard_map/remap/pallas_call | solution.py:592
  108.4 3.4 %collective-permute-start.8 = (f32[16,128]{1,0:T(8,128)S(1)}, f32[16,128]{1,0:T(8,128)S(1)}, u32[]{:S(2)}, u32[]{:S(2)}) collective-permute-start(f32[16,128]{1,0:T(8,128)S(1)} %get-tuple-element.83), channel_id=1, source_target_pairs={{1,0},{2,1},{3,2},{4,3},{5,4},{6,5},{7,6},{8,7},{9,8},{10,9},{11,1... | collective-permute-start | bytes 24584 | tf_op jit(solution)/shard_map/ppermute | solution.py:681
  111.8 1.4 collective-permute-done.8.sd
  113.2 6.2 %collective-permute-done.7.su = f32[16,128]{1,0:T(8,128)S(1)} collective-permute-done((f32[16,128]{1,0:T(8,128)S(1)}, f32[16,128]{1,0:T(8,128)S(1)}, u32[]{:S(2)}, u32[]{:S(2)}) %collective-permute-start.7) | collective-permute-done | bytes 8224 | tf_op jit(solution)/shard_map/ppermute | solution.py:678
  119.4 21.1 %middle_block.1 = (f32[8,512,128]{2,1,0:T(8,128)S(1)}, f32[8,512,128]{2,1,0:T(8,128)}, f32[4,512,128]{2,1,0:T(8,128)}, f32[4,512,128]{2,1,0:T(8,128)}, f32[32,12...) custom-call(s32[1]{0:T(128)} %bitcast.me, f32[4,512,128]{2,1,0:T(8,128)S(1)} %get-tuple-element.56.top, ...), custom_call_target="tpu_custom_call" | custom-call | flops 15000000512 | bytes 1048576 | tf_op jit(solution)/shard_map/middle_block/pallas_call | solution.py:453
  140.6 0.0 copy-start.12
  140.6 0.1 collective-permute-start.9
  140.6 6.2 %collective-permute-start.10 = (f32[16,128]{1,0:T(8,128)S(1)}, f32[16,128]{1,0:T(8,128)S(1)}, u32[]{:S(2)}, u32[]{:S(2)}) collective-permute-start(f32[16,128]{1,0:T(8,128)S(1)} %get-tuple-element.71), channel_id=1, source_target_pairs={{1,0},{2,1},{3,2},{4,3},{5,4},{6,5},{7,6},{8,7},{9,8},{10,9},{11,1... | collective-permute-start | bytes 24584 | tf_op jit(solution)/shard_map/ppermute | solution.py:681
  146.9 1.3 collective-permute-done.9.ru
  148.2 0.0 collective-permute-done.10.rd
  148.3 6.3 %collective-permute-start.12 = (f32[4,512,128]{2,1,0:T(8,128)}, f32[4,512,128]{2,1,0:T(8,128)}, u32[]{:S(2)}, u32[]{:S(2)}) collective-permute-start(f32[4,512,128]{2,1,0:T(8,128)} %get-tuple-element.73), channel_id=1, source_target_pairs={{1,0},{2,1},{3,2},{4,3},{5,4},{6,5},{7,6},{8,7},{9,8},{10,9},{11,1... | collective-permute-start | bytes 3145736 | tf_op jit(solution)/shard_map/ppermute | solution.py:681
  154.6 6.1 %remap_back.1 = f32[512,128]{1,0:T(8,128)S(1)} custom-call(s32[1]{0:T(128)} %bitcast.me, s32[48]{0:T(128)S(1)} %get-tuple-element.58.ids, s32[48]{0:T(128)S(1)} %get-tuple-element.59.pick, s32[48]{0:T(128)S(1)} %get-tuple-element.60.dest, f32[32,128]{1,0:T(8,128)S(1)} %get-tuple-element.74.s, f32[16,128]{1,0:T(8,128)S(1)} %collective-permute-done.9.ru, ...), custom_call_target="tpu_custom_call" | custom-call | flops 1500000000 | bytes 1048576 | tf_op jit(solution)/shard_map/remap_back/pallas_call | solution.py:629
  160.7 24.4 %all_to_all.11 = f32[64,8,128]{2,1,0:T(8,128)} all-to-all(f32[64,8,128]{2,1,0:T(8,128)S(1)} %bitcast.21), channel_id=1, replica_groups=mesh['comp'=2,'tile'=64] {'tile'}, dimensions={0} | all-to-all | bytes 524288 | tf_op jit(solution)/shard_map/all_to_all | solution.py:688
  185.1 2.1 collect.1
  187.2 1.4 collective-permute-start.13
  188.6 2.6 %collective-permute-done.13.s = f32[32,128]{1,0:T(8,128)S(1)} collective-permute-done((f32[32,128]{1,0:T(8,128)}, f32[32,128]{1,0:T(8,128)S(1)}, u32[]{:S(2)}, u32[]{:S(2)}) %collective-permute-start.13) | collective-permute-done | bytes 16416 | tf_op jit(solution)/shard_map/ppermute | solution.py:684
  191.2 1.1 copy-done.9
  192.3 12.3 %last_block.1 = (f32[8,512,128]{2,1,0:T(8,128)S(1)}, f32[4,512,128]{2,1,0:T(8,128)S(1)}, f32[4,512,128]{2,1,0:T(8,128)S(1)}) custom-call(s32[1]{0:T(128)} %bitcast.me, f32[8,512,128]{2,1,0:T(8,128)} %get-tuple-element.67.adj, f32[4,512,128]{2,1,0:T(8,128)S(1)} %collective-permute-done.11.ru, f32[4,512,128]{2,1,0:T(8,128)} %collective-permute-done.12.rd, ...), custom_call_target="tpu_custom_call" | custom-call | flops 7500000256 | bytes 1048576 | tf_op jit(solution)/shard_map/last_block/pallas_call | solution.py:523
  204.6 0.1 collective-permute-start.14
  204.7 6.2 %collective-permute-start.15 = (f32[4,512,128]{2,1,0:T(8,128)S(1)}, f32[4,512,128]{2,1,0:T(8,128)S(1)}, u32[]{:S(2)}, u32[]{:S(2)}) collective-permute-start(f32[4,512,128]{2,1,0:T(8,128)S(1)} %get-tuple-element.79), channel_id=1, source_target_pairs={{1,0},{2,1},{3,2},{4,3},{5,4},{6,5},{7,6},{8,7},{9,8},{10,9},{11,1... | collective-permute-start | bytes 3145736 | tf_op jit(solution)/shard_map/ppermute | solution.py:681
  210.9 2.3 to_raw.1
  213.2 17.8 %collective-permute-done.14.up = f32[4,512,128]{2,1,0:T(8,128)S(1)} collective-permute-done((f32[4,512,128]{2,1,0:T(8,128)S(1)}, f32[4,512,128]{2,1,0:T(8,128)S(1)}, u32[]{:S(2)}, u32[]{:S(2)}) %collective-permute-start.14) | collective-permute-done | bytes 1048608 | tf_op jit(solution)/shard_map/ppermute | solution.py:678
  231.0 2.5 %grad_out.1 = f32[1024,512]{1,0:T(8,128)} custom-call(s32[1]{0:T(128)} %bitcast.me, f32[8,512,128]{2,1,0:T(8,128)S(1)} %get-tuple-element.77.x, f32[4,512,128]{2,1,0:T(8,128)S(1)} %collective-permute-done.14.up, f32[4,512,128]{2,1,0:T(8,128)S(1)} %collective-permute-done.15.dn), custom_call_target="tpu_custom_call" | custom-call | flops 2000000000 | bytes 1048576 | tf_op jit(solution)/shard_map/grad_out/pallas_call | solution.py:132
  (46 shorter events, 0.1 us)
Async XLA Ops:
  0.6 20.4 %copy-start = (s32[2,64,64]{2,1,0:T(8,128)S(1)}, s32[2,64,64]{2,1,0:T(8,128)}, u32[]{:S(2)}) copy-start(s32[2,64,64]{2,1,0:T(8,128)} %param.16) | copy-start | bytes 98308
  0.6 1.6 copy-start.3
  2.3 8.1 %copy-start.18 = (s32[8,512]{1,0:T(8,128)S(1)}, s32[8,512]{1,0:T(8,128)}, u32[]{:S(2)}) copy-start(s32[8,512]{1,0:T(8,128)} %param.14) | copy-start | bytes 49156
  2.3 8.1 %copy-start.4 = (f32[1,128,8,512]{3,2,1,0:T(8,128)S(1)}, f32[1,128,8,512]{3,2,1,0:T(8,128)}, u32[]{:S(2)}) copy-start(f32[1,128,8,512]{3,2,1,0:T(8,128)} %param.12) | copy-start | bytes 6291460
  4.6 48.2 %collective-permute-start.1 = (f32[4,512,128]{2,1,0:T(8,128)S(1)}, f32[4,512,128]{2,1,0:T(8,128)}, u32[]{:S(2)}, u32[]{:S(2)}) collective-permute-start(f32[4,512,128]{2,1,0:T(8,128)S(1)} %get-tuple-element.41.top), channel_id=1, source_target_pairs={{1,0},{2,1},{3,2},{4,3},{5,4},{6,5},{7,6},{8,7},{9,8},{10,9},{11,1... | collective-permute-start | bytes 3145736 | tf_op jit(solution)/shard_map/ppermute | solution.py:681
  10.4 42.4 %collective-permute-start = (f32[4,512,128]{2,1,0:T(8,128)}, f32[4,512,128]{2,1,0:T(8,128)}, u32[]{:S(2)}, u32[]{:S(2)}) collective-permute-start(f32[4,512,128]{2,1,0:T(8,128)} %get-tuple-element.42.bot), channel_id=1, source_target_pairs={{0,1},{1,2},{2,3},{3,4},{4,5},{5,6},{6,7},{7,8},{8,9},{9,10},{10,1... | collective-permute-start | bytes 3145736 | tf_op jit(solution)/shard_map/ppermute | solution.py:678
  10.4 10.2 %copy-start.19 = (s32[2,64,8]{1,2,0:T(8,128)S(1)}, s32[2,64,8]{1,2,0:T(8,128)}, u32[]{:S(2)}) copy-start(s32[2,64,8]{1,2,0:T(8,128)} %param.15) | copy-start | bytes 12292
  10.4 10.5 %copy-start.20 = (s32[1,1,8]{2,1,0:T(1,128)S(1)}, s32[1,1,8]{2,1,0:T(1,128)}, u32[]{:S(2)}) copy-start(s32[1,1,8]{2,1,0:T(1,128)} %param.18) | copy-start | bytes 100
  10.4 13.3 %copy-start.21 = (s32[1,1,64]{2,1,0:T(1,128)S(1)}, s32[1,1,64]{2,1,0:T(1,128)}, u32[]{:S(2)}) copy-start(s32[1,1,64]{2,1,0:T(1,128)} %param.17) | copy-start | bytes 772
  13.0 1.3 copy-start.15
  14.3 37.5 %collective-permute-start.2 = (f32[3,512,128]{2,1,0:T(8,128)}, f32[3,512,128]{2,1,0:T(8,128)S(1)}, u32[]{:S(2)}, u32[]{:S(2)}) collective-permute-start(f32[3,512,128]{2,1,0:T(8,128)} %get-tuple-element.43), channel_id=1, source_target_pairs={{0,1},{1,2},{2,3},{3,4},{4,5},{5,6},{6,7},{7,8},{8,9},{9,10},{10,1... | collective-permute-start | bytes 2359304 | tf_op jit(solution)/shard_map/ppermute | solution.py:678
  14.3 37.5 %collective-permute-start.3 = (f32[3,512,128]{2,1,0:T(8,128)}, f32[3,512,128]{2,1,0:T(8,128)S(1)}, u32[]{:S(2)}, u32[]{:S(2)}) collective-permute-start(f32[3,512,128]{2,1,0:T(8,128)} %get-tuple-element.44), channel_id=1, source_target_pairs={{1,0},{2,1},{3,2},{4,3},{5,4},{6,5},{7,6},{8,7},{9,8},{10,9},{11,1... | collective-permute-start | bytes 2359304 | tf_op jit(solution)/shard_map/ppermute | solution.py:681
  23.9 1.6 copy-start.5
  25.5 27.3 %copy-start.11 = (bf16[256,256]{1,0:T(8,128)(2,1)S(1)}, bf16[256,256]{1,0:T(8,128)(2,1)}, u32[]{:S(2)}) copy-start(bf16[256,256]{1,0:T(8,128)(2,1)} %get-tuple-element.52.w2.w2f) | copy-start | bytes 393220
  25.5 27.3 %copy-start.16 = (f32[8,512,128]{2,1,0:T(8,128)S(1)}, f32[8,512,128]{2,1,0:T(8,128)}, u32[]{:S(2)}) copy-start(f32[8,512,128]{2,1,0:T(8,128)} %copy-done.15) | copy-start | bytes 6291460
  26.8 1.3 copy-start.14
  51.8 1.0 copy-start.6
  52.8 1.1 copy-start.7
  64.5 3.8 %collective-permute-start.4 = (f32[32,128]{1,0:T(8,128)S(1)}, f32[32,128]{1,0:T(8,128)S(1)}, u32[]{:S(2)}, u32[]{:S(2)}) collective-permute-start(f32[32,128]{1,0:T(8,128)S(1)} %get-tuple-element.55), channel_id=1, source_target_pairs={{0,64},{64,0},{1,65},{65,1},{2,66},{66,2},{3,67},{67,3},{4,68},{68... | collective-permute-start | bytes 49160 | tf_op jit(solution)/shard_map/ppermute | solution.py:684
  68.3 1.4 copy-start.17
  68.3 51.1 %collective-permute-start.6 = (f32[4,512,128]{2,1,0:T(8,128)S(1)}, f32[4,512,128]{2,1,0:T(8,128)}, u32[]{:S(2)}, u32[]{:S(2)}) collective-permute-start(f32[4,512,128]{2,1,0:T(8,128)S(1)} %get-tuple-element.56.top), channel_id=1, source_target_pairs={{1,0},{2,1},{3,2},{4,3},{5,4},{6,5},{7,6},{8,7},{9,8},{10,9},{11,1... | collective-permute-start | bytes 3145736 | tf_op jit(solution)/shard_map/ppermute | solution.py:681
  69.7 49.7 %collective-permute-start.5 = (f32[4,512,128]{2,1,0:T(8,128)}, f32[4,512,128]{2,1,0:T(8,128)}, u32[]{:S(2)}, u32[]{:S(2)}) collective-permute-start(f32[4,512,128]{2,1,0:T(8,128)} %get-tuple-element.57.bot), channel_id=1, source_target_pairs={{0,1},{1,2},{2,3},{3,4},{4,5},{5,6},{6,7},{7,8},{8,9},{9,10},{10,1... | collective-permute-start | bytes 3145736 | tf_op jit(solution)/shard_map/ppermute | solution.py:678
  99.6 2.2 copy-start.1
  101.8 17.6 %copy-start.8 = (f32[3,512,128]{2,1,0:T(8,128)S(1)}, f32[3,512,128]{2,1,0:T(8,128)}, u32[]{:S(2)}) copy-start(f32[3,512,128]{2,1,0:T(8,128)} %copy-done.6) | copy-start | bytes 2359300
  101.8 17.6 %copy-start.10 = (bf16[256,256]{1,0:T(8,128)(2,1)S(1)}, bf16[256,256]{1,0:T(8,128)(2,1)}, u32[]{:S(2)}) copy-start(bf16[256,256]{1,0:T(8,128)(2,1)} %get-tuple-element.65.w2b) | copy-start | bytes 393220
  108.4 4.7 %collective-permute-start.8 = (f32[16,128]{1,0:T(8,128)S(1)}, f32[16,128]{1,0:T(8,128)S(1)}, u32[]{:S(2)}, u32[]{:S(2)}) collective-permute-start(f32[16,128]{1,0:T(8,128)S(1)} %get-tuple-element.83), channel_id=1, source_target_pairs={{1,0},{2,1},{3,2},{4,3},{5,4},{6,5},{7,6},{8,7},{9,8},{10,9},{11,1... | collective-permute-start | bytes 24584 | tf_op jit(solution)/shard_map/ppermute | solution.py:681
  111.8 42.8 %copy-start.2 = (f32[1,64,128,128]{3,2,1,0:T(8,128)S(1)}, f32[1,64,128,128]{3,2,1,0:T(8,128)}, u32[]{:S(2)}) copy-start(f32[1,64,128,128]{3,2,1,0:T(8,128)} %param.19) | copy-start | bytes 12582916
  111.8 7.6 %collective-permute-start.7 = (f32[16,128]{1,0:T(8,128)S(1)}, f32[16,128]{1,0:T(8,128)S(1)}, u32[]{:S(2)}, u32[]{:S(2)}) collective-permute-start(f32[16,128]{1,0:T(8,128)S(1)} %get-tuple-element.84), channel_id=1, source_target_pairs={{0,1},{1,2},{2,3},{3,4},{4,5},{5,6},{6,7},{7,8},{8,9},{9,10},{10,1... | collective-permute-start | bytes 24584 | tf_op jit(solution)/shard_map/ppermute | solution.py:678
  140.6 20.1 %copy-start.12 = (f32[8,512,128]{2,1,0:T(8,128)}, f32[8,512,128]{2,1,0:T(8,128)S(1)}, u32[]{:S(2)}) copy-start(f32[8,512,128]{2,1,0:T(8,128)S(1)} %get-tuple-element.66.x) | copy-start | bytes 6291460
  140.6 7.7 %collective-permute-start.9 = (f32[16,128]{1,0:T(8,128)S(1)}, f32[16,128]{1,0:T(8,128)S(1)}, u32[]{:S(2)}, u32[]{:S(2)}) collective-permute-start(f32[16,128]{1,0:T(8,128)S(1)} %get-tuple-element.70), channel_id=1, source_target_pairs={{0,1},{1,2},{2,3},{3,4},{4,5},{5,6},{6,7},{7,8},{8,9},{9,10},{10,1... | collective-permute-start | bytes 24584 | tf_op jit(solution)/shard_map/ppermute | solution.py:678
  140.6 7.6 %collective-permute-start.10 = (f32[16,128]{1,0:T(8,128)S(1)}, f32[16,128]{1,0:T(8,128)S(1)}, u32[]{:S(2)}, u32[]{:S(2)}) collective-permute-start(f32[16,128]{1,0:T(8,128)S(1)} %get-tuple-element.71), channel_id=1, source_target_pairs={{1,0},{2,1},{3,2},{4,3},{5,4},{6,5},{7,6},{8,7},{9,8},{10,9},{11,1... | collective-permute-start | bytes 24584 | tf_op jit(solution)/shard_map/ppermute | solution.py:681
  148.3 42.9 %collective-permute-start.11 = (f32[4,512,128]{2,1,0:T(8,128)}, f32[4,512,128]{2,1,0:T(8,128)S(1)}, u32[]{:S(2)}, u32[]{:S(2)}) collective-permute-start(f32[4,512,128]{2,1,0:T(8,128)} %get-tuple-element.72), channel_id=1, source_target_pairs={{0,1},{1,2},{2,3},{3,4},{4,5},{5,6},{6,7},{7,8},{8,9},{9,10},{10,1... | collective-permute-start | bytes 3145736 | tf_op jit(solution)/shard_map/ppermute | solution.py:678
  148.3 42.9 %collective-permute-start.12 = (f32[4,512,128]{2,1,0:T(8,128)}, f32[4,512,128]{2,1,0:T(8,128)}, u32[]{:S(2)}, u32[]{:S(2)}) collective-permute-start(f32[4,512,128]{2,1,0:T(8,128)} %get-tuple-element.73), channel_id=1, source_target_pairs={{1,0},{2,1},{3,2},{4,3},{5,4},{6,5},{7,6},{8,7},{9,8},{10,9},{11,1... | collective-permute-start | bytes 3145736 | tf_op jit(solution)/shard_map/ppermute | solution.py:681
  187.2 3.9 %collective-permute-start.13 = (f32[32,128]{1,0:T(8,128)}, f32[32,128]{1,0:T(8,128)S(1)}, u32[]{:S(2)}, u32[]{:S(2)}) collective-permute-start(f32[32,128]{1,0:T(8,128)} %collect.1), channel_id=1, source_target_pairs={{0,64},{64,0},{1,65},{65,1},{2,66},{66,2},{3,67},{67,3},{4,68},{68... | collective-permute-start | bytes 49160 | tf_op jit(solution)/shard_map/ppermute | solution.py:684
  191.2 1.1 copy-start.9
  192.3 18.6 %copy-start.13 = (f32[8,512,128]{2,1,0:T(8,128)S(1)}, f32[8,512,128]{2,1,0:T(8,128)}, u32[]{:S(2)}) copy-start(f32[8,512,128]{2,1,0:T(8,128)} %copy-done.12) | copy-start | bytes 6291460
  204.6 26.4 %collective-permute-start.14 = (f32[4,512,128]{2,1,0:T(8,128)S(1)}, f32[4,512,128]{2,1,0:T(8,128)S(1)}, u32[]{:S(2)}, u32[]{:S(2)}) collective-permute-start(f32[4,512,128]{2,1,0:T(8,128)S(1)} %get-tuple-element.78), channel_id=1, source_target_pairs={{0,1},{1,2},{2,3},{3,4},{4,5},{5,6},{6,7},{7,8},{8,9},{9,10},{10,1... | collective-permute-start | bytes 3145736 | tf_op jit(solution)/shard_map/ppermute | solution.py:678
  204.7 26.4 %collective-permute-start.15 = (f32[4,512,128]{2,1,0:T(8,128)S(1)}, f32[4,512,128]{2,1,0:T(8,128)S(1)}, u32[]{:S(2)}, u32[]{:S(2)}) collective-permute-start(f32[4,512,128]{2,1,0:T(8,128)S(1)} %get-tuple-element.79), channel_id=1, source_target_pairs={{1,0},{2,1},{3,2},{4,3},{5,4},{6,5},{7,6},{8,7},{9,8},{10,9},{11,1... | collective-permute-start | bytes 3145736 | tf_op jit(solution)/shard_map/ppermute | solution.py:681

commit v2 on v1

--- a/solution.py
+++ b/solution.py
@@ -4,6 +4,7 @@
 from jax.experimental import pallas as pl
 from jax.experimental.pallas import tpu as pltpu
 from jax.sharding import PartitionSpec as P
+
 
 F32 = jnp.float32
 BF = jnp.bfloat16
@@ -24,7 +25,7 @@
 
 
 def params(**kw):
-    return pltpu.CompilerParams(vmem_limit_bytes=44 * 2**20, **kw)
+    return pltpu.CompilerParams(vmem_limit_bytes=60 * 2**20, **kw)
 
 
 def halves(x):
@@ -32,65 +33,110 @@
     return hi, (x - hi.astype(F32)).astype(BF)
 
 
-def start_in_kernel(x, top, bot):
-    for r in range(8):
-        dst = top if r < 4 else bot
-        dst[r % 4] = x[pl.ds(r, 128, stride=8), :].T
+ANY = pl.BlockSpec(memory_space=pltpu.MemorySpace.HBM)
+RAW = pltpu.VMEM((4, 1024, 128), F32)
+ROWS = pltpu.VMEM((8, LON, LEV), F32)
+
+
+def dma_sems(*n):
+    return pltpu.SemaphoreType.DMA(n)
+
+
+def lon_part(ref, j):
+    return ref.at[:, pl.ds(128 * j, 128), :]
+
+
+def start_raw(x, buf, sems):
+    out = [
+        pltpu.make_async_copy(x.at[:, pl.ds(128 * j, 128)], buf.at[j], sems.at[j])
+        for j in range(4)
+    ]
+    for c in out:
+        c.start()
+    return out
+
+
+def turned(buf, j, r):
+    return buf[j, pl.ds(r, 128, stride=8), :].T
+
+
+def start_in_kernel(x, top, bot, buf, out, sems, osems):
+    c = start_raw(x, buf, sems)
+    todo = []
+    for j in range(4):
+        c[j].wait()
+        for r in range(8):
+            out[r, pl.ds(128 * j, 128), :] = turned(buf, j, r)
+        for i, dst in enumerate((top, bot)):
+            src = out.at[pl.ds(4 * i, 4), pl.ds(128 * j, 128), :]
+            todo.append(pltpu.make_async_copy(src, lon_part(dst, j), osems.at[i, j]))
+            todo[-1].start()
+    for d in todo:
+        d.wait()
 
 
 def start_in(x):
-    blk = pl.BlockSpec((4, 128, 128), lambda j: (0, j, 0))
     return pl.pallas_call(
         start_in_kernel,
-        grid=(4,),
         out_shape=(sds(4, LON, LEV), sds(4, LON, LEV)),
-        in_specs=[pl.BlockSpec((1024, 128), lambda j: (0, j))],
-        out_specs=(blk, blk),
+        in_specs=[ANY],
+        out_specs=(ANY, ANY),
+        scratch_shapes=[RAW, ROWS, dma_sems(4), dma_sems(2, 4)],
         compiler_params=params(),
         cost_estimate=cost(4),
         name="start_in",
     )(x)
 
 
-def diff_in_kernel(x, sea, full, top, bot):
-    for r in range(8):
-        y = (x[pl.ds(r, 128, stride=8), :] * sea[r : r + 1, :]).T
-        full[r] = y
-        if r < 3:
-            top[r] = y
-        if r > 4:
-            bot[r - 5] = y
+def diff_in_kernel(x, sea, full, top, bot, buf, out, sems, osems):
+    c = start_raw(x, buf, sems)
+    todo = []
+    for j in range(4):
+        c[j].wait()
+        at = pl.ds(128 * j, 128)
+        for r in range(8):
+            out[r, at, :] = (buf[j, pl.ds(r, 128, stride=8), :] * sea[r : r + 1, at]).T
+        for i, (r0, n, dst) in enumerate(((0, 3, top), (5, 3, bot), (0, 8, full))):
+            src = out.at[pl.ds(r0, n), at, :]
+            todo.append(pltpu.make_async_copy(src, lon_part(dst, j), osems.at[i, j]))
+            todo[-1].start()
+    for d in todo:
+        d.wait()
 
 
 def diff_in(x, sea):
-    blk = pl.BlockSpec((3, 128, 128), lambda j: (0, j, 0))
     return pl.pallas_call(
         diff_in_kernel,
-        grid=(4,),
         out_shape=(sds(8, LON, LEV), sds(3, LON, LEV), sds(3, LON, LEV)),
-        in_specs=[
-            pl.BlockSpec((1024, 128), lambda j: (0, j)),
-            pl.BlockSpec((8, 128), lambda j: (0, j)),
-        ],
-        out_specs=(pl.BlockSpec((8, 128, 128), lambda j: (0, j, 0)), blk, blk),
+        in_specs=[ANY, VM],
+        out_specs=(ANY,) * 3,
+        scratch_shapes=[RAW, ROWS, dma_sems(4), dma_sems(3, 4)],
         compiler_params=params(),
         cost_estimate=cost(4),
         name="diff_in",
     )(x, sea)
 
 
-def to_rows_kernel(x, o):
-    for r in range(8):
-        o[r] = x[pl.ds(r, 128, stride=8), :].T
+def to_rows_kernel(x, o, buf, out, sems, osems):
+    c = start_raw(x, buf, sems)
+    todo = []
+    for j in range(4):
+        c[j].wait()
+        for r in range(8):
+            out[r, pl.ds(128 * j, 128), :] = turned(buf, j, r)
+        todo.append(pltpu.make_async_copy(lon_part(out, j), lon_part(o, j), osems.at[j]))
+        todo[-1].start()
+    for d in todo:
+        d.wait()
 
 
 def to_rows(x):
     return pl.pallas_call(
         to_rows_kernel,
-        grid=(4,),
         out_shape=sds(8, LON, LEV),
-        in_specs=[pl.BlockSpec((1024, 128), lambda j: (0, j))],
-        out_specs=pl.BlockSpec((8, 128, 128), lambda j: (0, j, 0)),
+        in_specs=[ANY],
+        out_specs=ANY,
+        scratch_shapes=[RAW, ROWS, dma_sems(4), dma_sems(4)],
         compiler_params=params(),
         cost_estimate=cost(4),
         name="to_rows",
@@ -115,26 +161,42 @@
     )(x)
 
 
-def grad_out_kernel(me, x, up, dn, o):
-    for r in range(8):
-        add = up[r] if r < 4 else dn[r - 4]
-        o[pl.ds(r, 128, stride=8), :] = (x[r] + add).T
-    for edge, r0 in ((0, 0), (63, 4)):
-
-        @pl.when(me[0] == edge)
-        def _(r0=r0):
-            for r in range(r0, r0 + 4):
-                o[pl.ds(r, 128, stride=8), :] = x[r].T
+def grad_out_kernel(me, x, up, dn, o, base, add, buf, sems, osems):
+    c = []
+    for j in range(4):
+        at = pl.ds(128 * j, 128)
+        for i, (src, dst) in enumerate(
+            (
+                (lon_part(up, j), add.at[pl.ds(0, 4), at, :]),
+                (lon_part(dn, j), add.at[pl.ds(4, 4), at, :]),
+                (lon_part(x, j), lon_part(base, j)),
+            )
+        ):
+            c.append(pltpu.make_async_copy(src, dst, sems.at[i, j]))
+            c[-1].start()
+    keep_up = jnp.where(me[0] > 0, 1.0, 0.0)
+    keep_dn = jnp.where(me[0] < 63, 1.0, 0.0)
+    todo = []
+    for j in range(4):
+        at = pl.ds(128 * j, 128)
+        for d in c[3 * j : 3 * j + 3]:
+            d.wait()
+        for r in range(8):
+            keep = keep_up if r < 4 else keep_dn
+            buf[j, pl.ds(r, 128, stride=8), :] = (base[r, at, :] + keep * add[r, at, :]).T
+        todo.append(pltpu.make_async_copy(buf.at[j], o.at[:, at], osems.at[j]))
+        todo[-1].start()
+    for d in todo:
+        d.wait()
 
 
 def grad_out(me, x, up, dn):
-    blk = pl.BlockSpec((4, 128, 128), lambda j: (0, j, 0))
     return pl.pallas_call(
         grad_out_kernel,
-        grid=(4,),
         out_shape=sds(1024, LON),
-        in_specs=[SM, pl.BlockSpec((8, 128, 128), lambda j: (0, j, 0)), blk, blk],
-        out_specs=pl.BlockSpec((1024, 128), lambda j: (0, j)),
+        in_specs=[SM, ANY, ANY, ANY],
+        out_specs=ANY,
+        scratch_shapes=[ROWS, ROWS, RAW, dma_sems(3, 4), dma_sems(4)],
         compiler_params=params(),
         cost_estimate=cost(4),
         name="grad_out",
@@ -309,14 +371,10 @@
 ]
 U_SCRATCH = pltpu.VMEM((NR, LON, 128), F32)
 COLS = pltpu.VMEM((128, 128), F32)
-ANY = pl.BlockSpec(memory_space=pl.ANY)
-
-
-def dma_sems(n):
-    return pltpu.SemaphoreType.DMA((n,))
-
-
-def first_kernel(me, top, bot, hu, hd, dt, du, dn, w2, o_top, o_bot, o_surf, va, vb, h, d, sems):
+HALF = sds(2, LON, LEV)
+
+
+def first_kernel(me, top, bot, hu, hd, dt, du, dn, w2, o_t0, o_t1, o_b0, o_b1, o_surf, va, vb, h, d, sems):
     c = copies(
         sems,
         [
@@ -354,7 +412,7 @@
     prepare(2, 3)
     prepare(13, 3)
     forward_block(va, vb, h, d, w2, first=True)
-    c = copies(sems, [(tile_rows(va, 5, 4), o_top), (tile_rows(va, 9, 4), o_bot)])
+    c = copies(sems, [(tile_rows(va, 5 + 2 * i, 2), o) for i, o in enumerate((o_t0, o_t1, o_b0, o_b1))])
     o_surf[...] = gather_surface(lambda r, j: va[r + 5, pl.ds(OFF + 128 * j, 128), :], 8)[0:32]
     wait(*c)
 
@@ -362,9 +420,9 @@
 def first_block(*args):
     return pl.pallas_call(
         first_kernel,
-        out_shape=(sds(4, LON, LEV), sds(4, LON, LEV), sds(32, 128)),
+        out_shape=(HALF,) * 4 + (sds(32, 128),),
         in_specs=[SM] + [ANY] * 7 + [VM],
-        out_specs=(ANY, ANY, VM),
+        out_specs=(ANY,) * 4 + (VM,),
         scratch_shapes=BLOCK_SCRATCH + [dma_sems(7)],
         compiler_params=params(),
         cost_estimate=cost(15),
@@ -373,16 +431,20 @@
 
 
 def middle_kernel(
-    me, top, bot, hu, hd, s, su, sd, dt, du, dn, m, w2f, w2b,
-    o_final, o_adj, o_up, o_dn, o_s, o_su, o_sd, va, vb, h, d, u, mm, cols, sems,
+    me, t0, t1, b0, b1, hu0, hu1, hd0, hd1, s, su, sd, dt, du, dn, m, w2f, w2b,
+    o_final, o_adj, o_u0, o_u1, o_d0, o_d1, o_s, o_su, o_sd, va, vb, h, d, u, mm, cols, sems,
 ):
     c = copies(
         sems,
         [
-            (top, tile_rows(va, 5, 4)),
-            (bot, tile_rows(va, 9, 4)),
-            (hu, tile_rows(va, 1, 4)),
-            (hd, tile_rows(va, 13, 4)),
+            (t0, tile_rows(va, 5, 2)),
+            (t1, tile_rows(va, 7, 2)),
+            (b0, tile_rows(va, 9, 2)),
+            (b1, tile_rows(va, 11, 2)),
+            (hu0, tile_rows(va, 1, 2)),
+            (hu1, tile_rows(va, 3, 2)),
+            (hd0, tile_rows(va, 13, 2)),
+            (hd1, tile_rows(va, 15, 2)),
             (dt, d.at[pl.ds(5, 8)]),
             (du, d.at[pl.ds(2, 3)]),
             (dn, d.at[pl.ds(13, 3)]),
@@ -408,16 +470,16 @@
 
         lax.fori_loop(0, 4, cp, 0)
 
-    for i, r0 in ((0, 5), (1, 9)):
-        wait(c[i])
+    for i, r0 in ((0, 5), (2, 9)):
+        wait(c[i], c[i + 1])
         prepare(r0)
-    wait(*c[2:7])
+    wait(*c[4:11])
     clear_ends(me, ((va, 1, 4), (d, 2, 3)), ((va, 13, 4), (d, 13, 3)))
     prepare(1)
     prepare(13)
     forward_block(va, vb, h, d, w2f)
     out = copies(sems, [(tile_rows(va, 5, 8), o_final)])
-    wait(c[7])
+    wait(c[11])
 
     def body(i, carry):
         r = 5 + i
@@ -437,8 +499,10 @@
     out = copies(
         sems,
         [
-            (u.at[pl.ds(1, 4)], o_up),
-            (u.at[pl.ds(13, 4)], o_dn),
+            (u.at[pl.ds(1, 2)], o_u0),
+            (u.at[pl.ds(3, 2)], o_u1),
+            (u.at[pl.ds(13, 2)], o_d0),
+            (u.at[pl.ds(15, 2)], o_d1),
             (u.at[pl.ds(5, 8)], o_adj),
         ],
     )
@@ -453,13 +517,13 @@
     return pl.pallas_call(
         middle_kernel,
         out_shape=(
-            sds(8, LON, LEV), sds(8, LON, LEV), sds(4, LON, LEV), sds(4, LON, LEV),
+            sds(8, LON, LEV), sds(8, LON, LEV), HALF, HALF, HALF, HALF,
             sds(32, 128), sds(16, 128), sds(16, 128),
         ),
-        in_specs=[SM] + [ANY] * 4 + [VM] * 3 + [ANY] * 4 + [VM] * 2,
-        out_specs=(ANY,) * 4 + (VM,) * 3,
+        in_specs=[SM] + [ANY] * 8 + [VM] * 3 + [ANY] * 4 + [VM] * 2,
+        out_specs=(ANY,) * 6 + (VM,) * 3,
         scratch_shapes=BLOCK_SCRATCH
-        + [U_SCRATCH, pltpu.VMEM((8, LON, 128), F32), COLS, dma_sems(8)],
+        + [U_SCRATCH, pltpu.VMEM((8, LON, 128), F32), COLS, dma_sems(12)],
         compiler_params=params(),
         cost_estimate=cost(30),
         name="middle_block",
@@ -467,7 +531,7 @@
 
 
 def last_kernel(
-    me, adj, ru, rd, s, top, bot, dt, du, dn, w2b, o_base, o_up, o_dn,
+    me, adj, ru0, ru1, rd0, rd1, s, top, bot, dt, du, dn, w2b, o_base, o_up, o_dn,
     va, vb, h, d, u, got, base, cols, sems,
 ):
     c = copies(
@@ -475,8 +539,10 @@
         [
             (adj, u.at[pl.ds(5, 8)]),
             (dt, d.at[pl.ds(5, 8)]),
-            (ru, got.at[pl.ds(0, 4)]),
-            (rd, got.at[pl.ds(4, 4)]),
+            (ru0, got.at[pl.ds(0, 2)]),
+            (ru1, got.at[pl.ds(2, 2)]),
+            (rd0, got.at[pl.ds(4, 2)]),
+            (rd1, got.at[pl.ds(6, 2)]),
             (du, d.at[pl.ds(2, 3)]),
             (dn, d.at[pl.ds(13, 3)]),
             (top, base.at[pl.ds(0, 4)]),
@@ -486,7 +552,7 @@
     cols[0:32] = s[...]
     cols[32:128] = jnp.zeros((96, 128), F32)
     cols[...] = cols[...].T
-    wait(*c[0:4])
+    wait(*c[0:6])
     clear_ends(me, ((got, 0, 4),), ((got, 4, 4),))
 
     def cp(i, carry):
@@ -503,7 +569,7 @@
         return carry
 
     lax.fori_loop(0, 8, cp, 0)
-    wait(*c[4:8])
+    wait(*c[6:10])
     clear_ends(me, ((d, 2, 3),), ((d, 13, 3),))
     push_block(vb, va, u, h, d, w2b)
     out = copies(sems, [(u.at[pl.ds(1, 4)], o_up), (u.at[pl.ds(13, 4)], o_dn)])
@@ -523,7 +589,7 @@
     return pl.pallas_call(
         last_kernel,
         out_shape=(sds(8, LON, LEV), sds(4, LON, LEV), sds(4, LON, LEV)),
-        in_specs=[SM] + [ANY] * 3 + [VM] + [ANY] * 5 + [VM],
+        in_specs=[SM] + [ANY] * 5 + [VM] + [ANY] * 5 + [VM],
         out_specs=(ANY,) * 3,
         scratch_shapes=BLOCK_SCRATCH
         + [
@@ -531,7 +597,7 @@
             pltpu.VMEM((8, LON, 128), F32),
             pltpu.VMEM((8, LON, 128), F32),
             COLS,
-            dma_sems(8),
+            dma_sems(10),
         ],
         compiler_params=params(),
         cost_estimate=cost(15),
@@ -679,6 +745,11 @@
 
     def to_prev(x):
         return lax.ppermute(x, "tile", up_pairs)
+
+    def both(last, first):
+        after = to_next(last)
+        before = to_prev(first)
+        return after, before
 
     def swap(x):
         return lax.ppermute(x, "comp", [(0, 1), (1, 0)])
@@ -717,22 +788,27 @@
         )
     )
 
-    v_top, v_bot, surf = first_block(me, s_top, s_bot, s_hu, s_hd, dt, du, dd, w2f)
+    t0, t1, b0, b1, surf = first_block(me, s_top, s_bot, s_hu, s_hd, dt, du, dd, w2f)
     other = swap(surf)
-    v_top, v_bot, other = lax.optimization_barrier((v_top, v_bot, other))
-    v_hu, v_hd = to_next(v_bot), to_prev(v_top)
-    arrived = exchange(offer(me, send_rows, other))
+    hu0, hd0 = both(b0, t0)
+    offered = offer(me, send_rows, other)
+    arrived = exchange(offered)
+    b1s, t1s, arrived = lax.optimization_barrier((b1, t1, arrived))
+    hu1, hd1 = to_next(b1s), to_prev(t1s)
     fix = remap(ids, pick, dest, arrived, weights, sea32)
     f_hu, f_hd = to_next(fix[16:32]), to_prev(fix[0:16])
-    final, adj, a_up, a_dn, a0, a0_up, a0_dn = middle_block(
-        me, v_top, v_bot, v_hu, v_hd, fix, f_hu, f_hd, dt, du, dd, measured, w2f, w2b
+    final, adj, u0, u1, d0, d1, a0, a0_up, a0_dn = middle_block(
+        me, t0, t1, b0, b1, hu0, hu1, hd0, hd1, fix, f_hu, f_hd, dt, du, dd, measured, w2f, w2b
     )
     r0u, r0d = to_next(a0_dn), to_prev(a0_up)
-    a_up, a_dn, r0u, r0d = lax.optimization_barrier((a_up, a_dn, r0u, r0d))
-    ru, rd = to_next(a_dn), to_prev(a_up)
-    back = exchange(remap_back(me, ids, pick, dest, a0, r0u, r0d, weights, sea32))
+    u0, d0, r0u, r0d = lax.optimization_barrier((u0, d0, r0u, r0d))
+    ru0, rd0 = both(d0, u0)
+    offered = remap_back(me, ids, pick, dest, a0, r0u, r0d, weights, sea32)
+    back = exchange(offered)
+    u1, d1, back = lax.optimization_barrier((u1, d1, back))
+    ru1, rd1 = to_next(d1), to_prev(u1)
     back = swap(collect(me, send_rows, back))
-    base, g_up, g_dn = last_block(me, adj, ru, rd, back, s_top, s_bot, dt, du, dd, w2b)
+    base, g_up, g_dn = last_block(me, adj, ru0, ru1, rd0, rd1, back, s_top, s_bot, dt, du, dd, w2b)
     gu, gd = to_next(g_dn), to_prev(g_up)
     final_raw = to_raw(final)
     gradient = grad_out(me, base, gu, gd)
@@ -754,6 +830,7 @@
         P("comp", "tile", None),
         P("comp", "tile", None, None),
     )
+
     return jax.shard_map(
         shards,
         mesh=mesh,

time: 236 us -> 249 us (1.055)
  the two profiles are of different devices: /device:TPU:8 before, /device:TPU:0 now
where the time goes in v2:
time: 249 us; the launch traced here: 248 us
  Pallas kernels  82.7 us (33%)
  starting transfers between devices  80.1 us (32%)
  waiting for transfers between devices  74 us (30%)
  local copies, waits for them, and re-layouts  8.55 us (3%)
    ppermute x9, starting transfers between devices, to_prev(): return lax.ppermute(x, 'tile', up_pairs)  60.7 us
    ppermute x9, waiting for transfers between devices, to_next(): return lax.ppermute(x, 'tile', down_pairs)  55.3 us
    pallas_call x1, Pallas kernels, middle_block(): pl.pallas_call(middle_kernel, out_shape=(sds(8, LON, LEV), sds(8, LON, LE...  24.1 us
    all_to_all x2, starting transfers between devices, exchange(): x = lax.all_to_all(x, 'tile', split_axis=0, concat_axis=0, tiled=True)  14.9 us
    pallas_call x1, Pallas kernels, last_block(): pl.pallas_call(last_kernel, out_shape=(sds(8, LON, LEV), sds(4, LON, LEV)...  14.8 us
    pallas_call x1, Pallas kernels, first_block(): pl.pallas_call(first_kernel, out_shape=(HALF,) * 4 + (sds(32, 128),), in_...  13.4 us
    all_to_all x2, waiting for transfers between devices, exchange(): x = lax.all_to_all(x, 'tile', split_axis=0, concat_axis=0, tiled=True)  8.57 us
    ppermute x2, waiting for transfers between devices, swap(): return lax.ppermute(x, 'comp', [(0, 1), (1, 0)])  7.73 us
  transfers between devices with their start and end apart: 22, of which 10 were waited for; matrix products, arithmetic and copies ran while one was open for 2% of the time, Pallas kernels for 8%

profile of v2, /device:TPU:0, one launch (start us, length us, event | category | flops | bytes accessed | tf_op | source)
XLA Modules:
  0.0 248.2 jit_solution(8610917244108721713)
XLA Ops:
  0.7 2.8 %start_in.1 = (f32[4,512,128]{2,1,0:T(8,128)}, f32[4,512,128]{2,1,0:T(8,128)}) custom-call(f32[1024,512]{1,0:T(8,128)} %bitcast.31), custom_call_target="tpu_custom_call" | custom-call | flops 2000000000 | bytes 1048576 | tf_op jit(solution)/shard_map/start_in/pallas_call | solution.py:79
  3.5 8.6 %collective-permute-start.1 = (f32[4,512,128]{2,1,0:T(8,128)}, f32[4,512,128]{2,1,0:T(8,128)S(1)}, u32[]{:S(2)}, u32[]{:S(2)}) collective-permute-start(f32[4,512,128]{2,1,0:T(8,128)} %get-tuple-element.48.top), channel_id=1, source_target_pairs={{1,0},{2,1},{3,2},{4,3},{5,4},{6,5},{7,6},{8,7},{9,8},{10,9},{11,1... | collective-permute-start | bytes 3145736 | tf_op jit(solution)/shard_map/ppermute | solution.py:747
  12.0 0.6 convert_select_fusion.sea
  12.7 4.0 %diff_in.1 = (f32[8,512,128]{2,1,0:T(8,128)}, f32[3,512,128]{2,1,0:T(8,128)}, f32[3,512,128]{2,1,0:T(8,128)}) custom-call(f32[1024,512]{1,0:T(8,128)} %bitcast.32, f32[8,512]{1,0:T(8,128)} %convert_select_fusion.sea), custom_call_target="tpu_custom_call" | custom-call | flops 2000000000 | bytes 1048576 | tf_op jit(solution)/shard_map/diff_in/pallas_call | solution.py:108
  16.7 0.1 collective-permute-start.2
  16.7 7.5 %collective-permute-start.3 = (f32[3,512,128]{2,1,0:T(8,128)}, f32[3,512,128]{2,1,0:T(8,128)}, u32[]{:S(2)}, u32[]{:S(2)}) collective-permute-start(f32[3,512,128]{2,1,0:T(8,128)} %get-tuple-element.51), channel_id=1, source_target_pairs={{1,0},{2,1},{3,2},{4,3},{5,4},{6,5},{7,6},{8,7},{9,8},{10,9},{11,1... | collective-permute-start | bytes 2359304 | tf_op jit(solution)/shard_map/ppermute | solution.py:747
  24.3 0.6 reshape.93.sea
  24.9 0.2 multiply_reduce_fusion
  25.1 0.1 broadcast_in_dim.10
  25.1 0.1 mul.57
  25.3 0.1 reshape.90
  25.4 0.1 copy.18
  25.5 0.1 copy.17
  25.6 0.6 reshape.91.send_rows
  26.2 1.6 mixes.1
  27.8 0.1 convert_reduce_fusion
  28.0 0.8 select_reduce_fusion
  28.8 2.7 %to_rows.1.m = f32[8,512,128]{2,1,0:T(8,128)} custom-call(f32[1024,512]{1,0:T(8,128)} %bitcast.33), custom_call_target="tpu_custom_call" | custom-call | flops 2000000000 | bytes 1048576 | tf_op jit(solution)/shard_map/to_rows/pallas_call | solution.py:134
  31.5 22.2 %collective-permute-done.2.du = f32[3,512,128]{2,1,0:T(8,128)S(1)} collective-permute-done((f32[3,512,128]{2,1,0:T(8,128)}, f32[3,512,128]{2,1,0:T(8,128)S(1)}, u32[]{:S(2)}, u32[]{:S(2)}) %collective-permute-start.2) | collective-permute-done | bytes 786464 | tf_op jit(solution)/shard_map/ppermute | solution.py:744
  53.7 0.9 copy-done.13
  54.6 0.3 copy-done.9
  54.9 0.4 copy-done.10
  55.3 13.4 %first_block.1 = (f32[2,512,128]{2,1,0:T(8,128)}, f32[2,512,128]{2,1,0:T(8,128)}, f32[2,512,128]{2,1,0:T(8,128)}, f32[2,512,128]{2,1,0:T(8,128)}, f32[32,128]{1,0:T(8,128)}) custom-call(s32[1]{0:T(128)} %bitcast.me, f32[4,512,128]{2,1,0:T(8,128)} %get-tuple-element.48.top, f32[4,512,128]{2,1,0:T(8,128)} %get-tuple-element.49.bot, f32[4,512,128]{2,1,0:T(8,128)} %copy-done.10, ...), custom_call_target="tpu_custom_call" | custom-call | flops 7500000256 | bytes 1048576 | tf_op jit(solution)/shard_map/first_block/pallas_call | solution.py:421
  68.7 1.5 collective-permute-start.5
  70.2 2.5 %collective-permute-done.5.surf = f32[32,128]{1,0:T(8,128)S(1)} collective-permute-done((f32[32,128]{1,0:T(8,128)}, f32[32,128]{1,0:T(8,128)S(1)}, u32[]{:S(2)}, u32[]{:S(2)}) %collective-permute-start.5) | collective-permute-done | bytes 16416 | tf_op jit(solution)/shard_map/ppermute | solution.py:755
  72.7 0.6 copy-done.4
  73.3 1.6 offer.1
  74.9 5.2 %all-to-all-start = ((f32[64,8,128]{2,1,0:T(8,128)}), f32[64,8,128]{2,1,0:T(8,128)S(1)}, u32[]{:S(2)}, u32[]{:S(2)}) async-start(f32[64,8,128]{2,1,0:T(8,128)} %bitcast.22), calls=%async_computation | async-start | bytes 524288 | tf_op jit(solution)/shard_map/all_to_all | solution.py:759
  80.1 7.4 %collective-permute-start.7 = (f32[2,512,128]{2,1,0:T(8,128)}, f32[2,512,128]{2,1,0:T(8,128)S(1)}, u32[]{:S(2)}, u32[]{:S(2)}) collective-permute-start(f32[2,512,128]{2,1,0:T(8,128)} %get-tuple-element.60.t0), channel_id=1, source_target_pairs={{1,0},{2,1},{3,2},{4,3},{5,4},{6,5},{7,6},{8,7},{9,8},{10,9},{11,1... | collective-permute-start | bytes 1572872 | tf_op jit(solution)/shard_map/ppermute | solution.py:747
  87.5 4.1 %all-to-all-done = f32[64,8,128]{2,1,0:T(8,128)S(1)} async-done(((f32[64,8,128]{2,1,0:T(8,128)}), f32[64,8,128]{2,1,0:T(8,128)S(1)}, u32[]{:S(2)}, u32[]{:S(2)}) %all-to-all-start) | async-done | bytes 262176 | tf_op jit(solution)/shard_map/all_to_all | solution.py:759
  91.6 7.4 %collective-permute-start.8 = (f32[2,512,128]{2,1,0:T(8,128)}, f32[2,512,128]{2,1,0:T(8,128)S(1)}, u32[]{:S(2)}, u32[]{:S(2)}) collective-permute-start(f32[2,512,128]{2,1,0:T(8,128)} %get-tuple-element.67.t1), channel_id=1, source_target_pairs={{1,0},{2,1},{3,2},{4,3},{5,4},{6,5},{7,6},{8,7},{9,8},{10,9},{11,1... | collective-permute-start | bytes 1572872 | tf_op jit(solution)/shard_map/ppermute | solution.py:747
  99.1 4.6 %remap.1.s = f32[32,128]{1,0:T(8,128)} custom-call(s32[48]{0:T(128)} %get-tuple-element.68.ids, s32[48]{0:T(128)} %get-tuple-element.69.pick, s32[48]{0:T(128)} %get-tuple-element.70.dest, f32[512,128]{1,0:T(8,128)} %bitcast.23, f32[64,128,128]{2,1,0:T(8,128)} %bitcast.29, f32[32,128]{1,0:T(8,128)} %reshape.93.sea), custom_call_target="tpu_custom_call" | custom-call | flops 1500000000 | bytes 1048576 | tf_op jit(solution)/shard_map/remap/pallas_call | solution.py:658
  103.6 0.7 fusion.4
  104.4 2.3 collective-permute-done.10.sd
  106.7 1.7 collective-permute-start.9
  108.4 7.2 %collective-permute-done.9.su = f32[16,128]{1,0:T(8,128)S(1)} collective-permute-done((f32[16,128]{1,0:T(8,128)S(1)}, f32[16,128]{1,0:T(8,128)S(1)}, u32[]{:S(2)}, u32[]{:S(2)}) %collective-permute-start.9) | collective-permute-done | bytes 8224 | tf_op jit(solution)/shard_map/ppermute | solution.py:744
  115.7 0.5 copy-done.26
  116.2 0.2 copy-done.18
  116.4 0.2 copy-done.19
  116.6 0.2 copy-done.20
  116.8 0.8 copy-done.22
  117.6 24.1 %middle_block.1 = (f32[8,512,128]{2,1,0:T(8,128)}, f32[8,512,128]{2,1,0:T(8,128)}, f32[2,512,128]{2,1,0:T(8,128)}, f32[2,512,128]{2,1,0:T(8,128)}, f32[2,512,128...) custom-call(s32[1]{0:T(128)} %bitcast.me, ...), custom_call_target="tpu_custom_call" | custom-call | flops 15000000512 | bytes 1048576 | tf_op jit(solution)/shard_map/middle_block/pallas_call | solution.py:517
  141.7 0.1 collective-permute-start.11
  141.8 7.5 %collective-permute-start.12 = (f32[16,128]{1,0:T(8,128)}, f32[16,128]{1,0:T(8,128)S(1)}, u32[]{:S(2)}, u32[]{:S(2)}) collective-permute-start(f32[16,128]{1,0:T(8,128)} %get-tuple-element.80), channel_id=1, source_target_pairs={{1,0},{2,1},{3,2},{4,3},{5,4},{6,5},{7,6},{8,7},{9,8},{10,9},{11,1... | collective-permute-start | bytes 24584 | tf_op jit(solution)/shard_map/ppermute | solution.py:747
  149.2 1.5 collective-permute-done.11.ru
  150.8 0.6 copy-done.27
  151.4 3.7 %remap_back.1 = f32[512,128]{1,0:T(8,128)} custom-call(s32[1]{0:T(128)} %bitcast.me, s32[48]{0:T(128)} %get-tuple-element.68.ids, s32[48]{0:T(128)} %get-tuple-element.69.pick, s32[48]{0:T(128)} %get-tuple-element.70.dest, f32[32,128]{1,0:T(8,128)} %get-tuple-element.84.s, f32[16,128]{1,0:T(8,128)} %copy-done.27, f32[16,128]{1,0:T(8,128)} %copy-done.28, ...), custom_call_target="tpu_custom_call" | custom-call | flops 1500000000 | bytes 1048576 | tf_op jit(solution)/shard_map/remap_back/pallas_call | solution.py:695
  155.1 9.7 %all-to-all-start.1 = ((f32[64,8,128]{2,1,0:T(8,128)}), f32[64,8,128]{2,1,0:T(8,128)S(1)}, u32[]{:S(2)}, u32[]{:S(2)}) async-start(f32[64,8,128]{2,1,0:T(8,128)} %bitcast.24), calls=%async_computation.1 | async-start | bytes 524288 | tf_op jit(solution)/shard_map/all_to_all | solution.py:759
  164.8 0.1 collective-permute-start.13
  165.0 7.4 %collective-permute-start.15 = (f32[2,512,128]{2,1,0:T(8,128)S(1)}, f32[2,512,128]{2,1,0:T(8,128)S(1)}, u32[]{:S(2)}, u32[]{:S(2)}) collective-permute-start(f32[2,512,128]{2,1,0:T(8,128)S(1)} %copy-done.16), channel_id=1, source_target_pairs={{1,0},{2,1},{3,2},{4,3},{5,4},{6,5},{7,6},{8,7},{9,8},{10,9},{11,1... | collective-permute-start | bytes 1572872 | tf_op jit(solution)/shard_map/ppermute | solution.py:747
  172.4 4.5 %all-to-all-done.1 = f32[64,8,128]{2,1,0:T(8,128)S(1)} async-done(((f32[64,8,128]{2,1,0:T(8,128)}), f32[64,8,128]{2,1,0:T(8,128)S(1)}, u32[]{:S(2)}, u32[]{:S(2)}) %all-to-all-start.1) | async-done | bytes 262176 | tf_op jit(solution)/shard_map/all_to_all | solution.py:759
  176.9 7.4 %collective-permute-start.16 = (f32[2,512,128]{2,1,0:T(8,128)S(1)}, f32[2,512,128]{2,1,0:T(8,128)}, u32[]{:S(2)}, u32[]{:S(2)}) collective-permute-start(f32[2,512,128]{2,1,0:T(8,128)S(1)} %copy-done.14), channel_id=1, source_target_pairs={{1,0},{2,1},{3,2},{4,3},{5,4},{6,5},{7,6},{8,7},{9,8},{10,9},{11,1... | collective-permute-start | bytes 1572872 | tf_op jit(solution)/shard_map/ppermute | solution.py:747
  184.3 2.2 collect.1
  186.5 0.8 collective-permute-start.17
  187.3 5.2 %collective-permute-done.17.s = f32[32,128]{1,0:T(8,128)S(1)} collective-permute-done((f32[32,128]{1,0:T(8,128)}, f32[32,128]{1,0:T(8,128)S(1)}, u32[]{:S(2)}, u32[]{:S(2)}) %collective-permute-start.17) | collective-permute-done | bytes 16416 | tf_op jit(solution)/shard_map/ppermute | solution.py:755
  192.5 4.8 %collective-permute-done.14.ru1 = f32[2,512,128]{2,1,0:T(8,128)} collective-permute-done((f32[2,512,128]{2,1,0:T(8,128)S(1)}, f32[2,512,128]{2,1,0:T(8,128)}, u32[]{:S(2)}, u32[]{:S(2)}) %collective-permute-start.14) | collective-permute-done | bytes 524320 | tf_op jit(solution)/shard_map/ppermute | solution.py:744
  197.4 14.8 %last_block.1 = (f32[8,512,128]{2,1,0:T(8,128)}, f32[4,512,128]{2,1,0:T(8,128)}, f32[4,512,128]{2,1,0:T(8,128)}) custom-call(s32[1]{0:T(128)} %bitcast.me, f32[8,512,128]{2,1,0:T(8,128)} %get-tuple-element.76.adj, f32[2,512,128]{2,1,0:T(8,128)} %copy-done.21, f32[2,512,128]{2,1,0:T(8,128)} %collective-permute-done.14.ru1, f32[2,512,128]{2,1,0:T(8,128)} %copy-done.23, ...), custom_call_target="tpu_custom_call" | custom-call | flops 7500000256 | bytes 1048576 | tf_op jit(solution)/shard_map/last_block/pallas_call | solution.py:589
  212.2 0.1 collective-permute-start.18
  212.2 7.5 %collective-permute-start.19 = (f32[4,512,128]{2,1,0:T(8,128)}, f32[4,512,128]{2,1,0:T(8,128)S(1)}, u32[]{:S(2)}, u32[]{:S(2)}) collective-permute-start(f32[4,512,128]{2,1,0:T(8,128)} %get-tuple-element.93), channel_id=1, source_target_pairs={{1,0},{2,1},{3,2},{4,3},{5,4},{6,5},{7,6},{8,7},{9,8},{10,9},{11,1... | collective-permute-start | bytes 3145736 | tf_op jit(solution)/shard_map/ppermute | solution.py:747
  219.7 4.1 %to_raw.1 = f32[1024,512]{1,0:T(8,128)} custom-call(f32[8,512,128]{2,1,0:T(8,128)} %get-tuple-element.75.x), custom_call_target="tpu_custom_call" | custom-call | flops 2000000000 | bytes 1048576 | tf_op jit(solution)/shard_map/to_raw/pallas_call | solution.py:152
  223.8 19.6 %collective-permute-done.18.up = f32[4,512,128]{2,1,0:T(8,128)S(1)} collective-permute-done((f32[4,512,128]{2,1,0:T(8,128)}, f32[4,512,128]{2,1,0:T(8,128)S(1)}, u32[]{:S(2)}, u32[]{:S(2)}) %collective-permute-start.18) | collective-permute-done | bytes 1048608 | tf_op jit(solution)/shard_map/ppermute | solution.py:744
  243.4 1.0 copy-done.11
  244.4 0.4 copy-done.12
  244.7 3.3 %grad_out.1 = f32[1024,512]{1,0:T(8,128)} custom-call(s32[1]{0:T(128)} %bitcast.me, f32[8,512,128]{2,1,0:T(8,128)} %get-tuple-element.91.x, f32[4,512,128]{2,1,0:T(8,128)} %copy-done.11, f32[4,512,128]{2,1,0:T(8,128)} %copy-done.12), custom_call_target="tpu_custom_call" | custom-call | flops 2000000000 | bytes 1048576 | tf_op jit(solution)/shard_map/grad_out/pallas_call | solution.py:194
  (70 shorter events, 0.4 us)
Async XLA Ops:
  0.6 24.7 %copy-start = (s32[2,64,64]{2,1,0:T(8,128)S(1)}, s32[2,64,64]{2,1,0:T(8,128)}, u32[]{:S(2)}) copy-start(s32[2,64,64]{2,1,0:T(8,128)} %param.16) | copy-start | bytes 98308
  0.6 11.4 %copy-start.5 = (s32[8,512]{1,0:T(8,128)S(1)}, s32[8,512]{1,0:T(8,128)}, u32[]{:S(2)}) copy-start(s32[8,512]{1,0:T(8,128)} %param.14) | copy-start | bytes 49156
  3.5 50.2 %collective-permute-start.1 = (f32[4,512,128]{2,1,0:T(8,128)}, f32[4,512,128]{2,1,0:T(8,128)S(1)}, u32[]{:S(2)}, u32[]{:S(2)}) collective-permute-start(f32[4,512,128]{2,1,0:T(8,128)} %get-tuple-element.48.top), channel_id=1, source_target_pairs={{1,0},{2,1},{3,2},{4,3},{5,4},{6,5},{7,6},{8,7},{9,8},{10,9},{11,1... | collective-permute-start | bytes 3145736 | tf_op jit(solution)/shard_map/ppermute | solution.py:747
  12.0 41.7 %collective-permute-start = (f32[4,512,128]{2,1,0:T(8,128)}, f32[4,512,128]{2,1,0:T(8,128)S(1)}, u32[]{:S(2)}, u32[]{:S(2)}) collective-permute-start(f32[4,512,128]{2,1,0:T(8,128)} %get-tuple-element.49.bot), channel_id=1, source_target_pairs={{0,1},{1,2},{2,3},{3,4},{4,5},{5,6},{6,7},{7,8},{8,9},{9,10},{10,1... | collective-permute-start | bytes 3145736 | tf_op jit(solution)/shard_map/ppermute | solution.py:744
  12.7 11.6 %copy-start.3 = (f32[8,512]{1,0:T(8,128)S(1)}, f32[8,512]{1,0:T(8,128)}, u32[]{:S(2)}) copy-start(f32[8,512]{1,0:T(8,128)} %convert_select_fusion.sea) | copy-start | bytes 49156
  12.7 12.2 %copy-start.6 = (s32[2,64,8]{1,2,0:T(8,128)S(1)}, s32[2,64,8]{1,2,0:T(8,128)}, u32[]{:S(2)}) copy-start(s32[2,64,8]{1,2,0:T(8,128)} %param.15) | copy-start | bytes 12292
  12.7 12.6 %copy-start.7 = (s32[1,1,8]{2,1,0:T(1,128)S(1)}, s32[1,1,8]{2,1,0:T(1,128)}, u32[]{:S(2)}) copy-start(s32[1,1,8]{2,1,0:T(1,128)} %param.18) | copy-start | bytes 100
  12.7 15.3 %copy-start.8 = (s32[1,1,64]{2,1,0:T(1,128)S(1)}, s32[1,1,64]{2,1,0:T(1,128)}, u32[]{:S(2)}) copy-start(s32[1,1,64]{2,1,0:T(1,128)} %param.17) | copy-start | bytes 772
  16.7 37.0 %collective-permute-start.2 = (f32[3,512,128]{2,1,0:T(8,128)}, f32[3,512,128]{2,1,0:T(8,128)S(1)}, u32[]{:S(2)}, u32[]{:S(2)}) collective-permute-start(f32[3,512,128]{2,1,0:T(8,128)} %get-tuple-element.50), channel_id=1, source_target_pairs={{0,1},{1,2},{2,3},{3,4},{4,5},{5,6},{6,7},{7,8},{8,9},{9,10},{10,1... | collective-permute-start | bytes 2359304 | tf_op jit(solution)/shard_map/ppermute | solution.py:744
  16.7 36.9 %collective-permute-start.3 = (f32[3,512,128]{2,1,0:T(8,128)}, f32[3,512,128]{2,1,0:T(8,128)}, u32[]{:S(2)}, u32[]{:S(2)}) collective-permute-start(f32[3,512,128]{2,1,0:T(8,128)} %get-tuple-element.51), channel_id=1, source_target_pairs={{1,0},{2,1},{3,2},{4,3},{5,4},{6,5},{7,6},{8,7},{9,8},{10,9},{11,1... | collective-permute-start | bytes 2359304 | tf_op jit(solution)/shard_map/ppermute | solution.py:747
  53.7 0.9 copy-start.13
  53.7 1.2 copy-start.9
  53.7 1.6 copy-start.10
  68.7 4.0 %collective-permute-start.5 = (f32[32,128]{1,0:T(8,128)}, f32[32,128]{1,0:T(8,128)S(1)}, u32[]{:S(2)}, u32[]{:S(2)}) collective-permute-start(f32[32,128]{1,0:T(8,128)} %get-tuple-element.65), channel_id=1, source_target_pairs={{0,64},{64,0},{1,65},{65,1},{2,66},{66,2},{3,67},{67,3},{4,68},{68... | collective-permute-start | bytes 49160 | tf_op jit(solution)/shard_map/ppermute | solution.py:755
  72.7 0.6 copy-start.4
  74.9 16.6 %all-to-all-start = ((f32[64,8,128]{2,1,0:T(8,128)}), f32[64,8,128]{2,1,0:T(8,128)S(1)}, u32[]{:S(2)}, u32[]{:S(2)}) async-start(f32[64,8,128]{2,1,0:T(8,128)} %bitcast.22), calls=%async_computation | async-start | bytes 524288 | tf_op jit(solution)/shard_map/all_to_all | solution.py:759
  80.1 35.5 %collective-permute-start.7 = (f32[2,512,128]{2,1,0:T(8,128)}, f32[2,512,128]{2,1,0:T(8,128)S(1)}, u32[]{:S(2)}, u32[]{:S(2)}) collective-permute-start(f32[2,512,128]{2,1,0:T(8,128)} %get-tuple-element.60.t0), channel_id=1, source_target_pairs={{1,0},{2,1},{3,2},{4,3},{5,4},{6,5},{7,6},{8,7},{9,8},{10,9},{11,1... | collective-permute-start | bytes 1572872 | tf_op jit(solution)/shard_map/ppermute | solution.py:747
  87.5 28.1 %collective-permute-start.4 = (f32[2,512,128]{2,1,0:T(8,128)}, f32[2,512,128]{2,1,0:T(8,128)S(1)}, u32[]{:S(2)}, u32[]{:S(2)}) collective-permute-start(f32[2,512,128]{2,1,0:T(8,128)} %get-tuple-element.62.b0), channel_id=1, source_target_pairs={{0,1},{1,2},{2,3},{3,4},{4,5},{5,6},{6,7},{7,8},{8,9},{9,10},{10,1... | collective-permute-start | bytes 1572872 | tf_op jit(solution)/shard_map/ppermute | solution.py:744
  91.6 7.5 %copy-start.2 = (f32[64,8,128]{2,1,0:T(8,128)}, f32[64,8,128]{2,1,0:T(8,128)S(1)}, u32[]{:S(2)}) copy-start(f32[64,8,128]{2,1,0:T(8,128)S(1)} %all-to-all-done) | copy-start | bytes 786436
  91.6 24.0 %collective-permute-start.6 = (f32[2,512,128]{2,1,0:T(8,128)}, f32[2,512,128]{2,1,0:T(8,128)S(1)}, u32[]{:S(2)}, u32[]{:S(2)}) collective-permute-start(f32[2,512,128]{2,1,0:T(8,128)} %get-tuple-element.66.b1), channel_id=1, source_target_pairs={{0,1},{1,2},{2,3},{3,4},{4,5},{5,6},{6,7},{7,8},{8,9},{9,10},{10,1... | collective-permute-start | bytes 1572872 | tf_op jit(solution)/shard_map/ppermute | solution.py:744
  91.6 24.0 %collective-permute-start.8 = (f32[2,512,128]{2,1,0:T(8,128)}, f32[2,512,128]{2,1,0:T(8,128)S(1)}, u32[]{:S(2)}, u32[]{:S(2)}) collective-permute-start(f32[2,512,128]{2,1,0:T(8,128)} %get-tuple-element.67.t1), channel_id=1, source_target_pairs={{1,0},{2,1},{3,2},{4,3},{5,4},{6,5},{7,6},{8,7},{9,8},{10,9},{11,1... | collective-permute-start | bytes 1572872 | tf_op jit(solution)/shard_map/ppermute | solution.py:747
  104.4 2.3 collective-permute-start.10
  106.7 9.0 %copy-start.25 = (f32[16,128]{1,0:T(8,128)}, f32[16,128]{1,0:T(8,128)S(1)}, u32[]{:S(2)}) copy-start(f32[16,128]{1,0:T(8,128)S(1)} %collective-permute-done.10.sd) | copy-start | bytes 24580
  106.7 8.9 %collective-permute-start.9 = (f32[16,128]{1,0:T(8,128)S(1)}, f32[16,128]{1,0:T(8,128)S(1)}, u32[]{:S(2)}, u32[]{:S(2)}) collective-permute-start(f32[16,128]{1,0:T(8,128)S(1)} %get-tuple-element.98), channel_id=1, source_target_pairs={{0,1},{1,2},{2,3},{3,4},{4,5},{5,6},{6,7},{7,8},{8,9},{9,10},{10,1... | collective-permute-start | bytes 24584 | tf_op jit(solution)/shard_map/ppermute | solution.py:744
  115.6 0.6 copy-start.26
  115.6 0.8 copy-start.18
  115.6 1.0 copy-start.19
  115.6 1.2 copy-start.20
  116.8 0.8 copy-start.22
  141.7 9.1 %collective-permute-start.11 = (f32[16,128]{1,0:T(8,128)}, f32[16,128]{1,0:T(8,128)S(1)}, u32[]{:S(2)}, u32[]{:S(2)}) collective-permute-start(f32[16,128]{1,0:T(8,128)} %get-tuple-element.79), channel_id=1, source_target_pairs={{0,1},{1,2},{2,3},{3,4},{4,5},{5,6},{6,7},{7,8},{8,9},{9,10},{10,1... | collective-permute-start | bytes 24584 | tf_op jit(solution)/shard_map/ppermute | solution.py:744
  141.8 9.0 %collective-permute-start.12 = (f32[16,128]{1,0:T(8,128)}, f32[16,128]{1,0:T(8,128)S(1)}, u32[]{:S(2)}, u32[]{:S(2)}) collective-permute-start(f32[16,128]{1,0:T(8,128)} %get-tuple-element.80), channel_id=1, source_target_pairs={{1,0},{2,1},{3,2},{4,3},{5,4},{6,5},{7,6},{8,7},{9,8},{10,9},{11,1... | collective-permute-start | bytes 24584 | tf_op jit(solution)/shard_map/ppermute | solution.py:747
  150.8 0.6 copy-start.27
  150.8 0.6 copy-start.28
  151.4 13.4 %copy-start.17 = (f32[2,512,128]{2,1,0:T(8,128)S(1)}, f32[2,512,128]{2,1,0:T(8,128)}, u32[]{:S(2)}) copy-start(f32[2,512,128]{2,1,0:T(8,128)} %get-tuple-element.81) | copy-start | bytes 1572868
  151.4 13.6 %copy-start.16 = (f32[2,512,128]{2,1,0:T(8,128)S(1)}, f32[2,512,128]{2,1,0:T(8,128)}, u32[]{:S(2)}) copy-start(f32[2,512,128]{2,1,0:T(8,128)} %get-tuple-element.88) | copy-start | bytes 1572868
  151.4 25.5 %copy-start.15 = (f32[2,512,128]{2,1,0:T(8,128)S(1)}, f32[2,512,128]{2,1,0:T(8,128)}, u32[]{:S(2)}) copy-start(f32[2,512,128]{2,1,0:T(8,128)} %get-tuple-element.87) | copy-start | bytes 1572868
  151.4 25.5 %copy-start.14 = (f32[2,512,128]{2,1,0:T(8,128)S(1)}, f32[2,512,128]{2,1,0:T(8,128)}, u32[]{:S(2)}) copy-start(f32[2,512,128]{2,1,0:T(8,128)} %get-tuple-element.89) | copy-start | bytes 1572868
  155.1 21.8 %all-to-all-start.1 = ((f32[64,8,128]{2,1,0:T(8,128)}), f32[64,8,128]{2,1,0:T(8,128)S(1)}, u32[]{:S(2)}, u32[]{:S(2)}) async-start(f32[64,8,128]{2,1,0:T(8,128)} %bitcast.24), calls=%async_computation.1 | async-start | bytes 524288 | tf_op jit(solution)/shard_map/all_to_all | solution.py:759
  164.8 27.7 %collective-permute-start.13 = (f32[2,512,128]{2,1,0:T(8,128)S(1)}, f32[2,512,128]{2,1,0:T(8,128)S(1)}, u32[]{:S(2)}, u32[]{:S(2)}) collective-permute-start(f32[2,512,128]{2,1,0:T(8,128)S(1)} %copy-done.17), channel_id=1, source_target_pairs={{0,1},{1,2},{2,3},{3,4},{4,5},{5,6},{6,7},{7,8},{8,9},{9,10},{10,1... | collective-permute-start | bytes 1572872 | tf_op jit(solution)/shard_map/ppermute | solution.py:744
  165.0 27.6 %collective-permute-start.15 = (f32[2,512,128]{2,1,0:T(8,128)S(1)}, f32[2,512,128]{2,1,0:T(8,128)S(1)}, u32[]{:S(2)}, u32[]{:S(2)}) collective-permute-start(f32[2,512,128]{2,1,0:T(8,128)S(1)} %copy-done.16), channel_id=1, source_target_pairs={{1,0},{2,1},{3,2},{4,3},{5,4},{6,5},{7,6},{8,7},{9,8},{10,9},{11,1... | collective-permute-start | bytes 1572872 | tf_op jit(solution)/shard_map/ppermute | solution.py:747
  176.9 7.5 %copy-start.1 = (f32[64,8,128]{2,1,0:T(8,128)}, f32[64,8,128]{2,1,0:T(8,128)S(1)}, u32[]{:S(2)}) copy-start(f32[64,8,128]{2,1,0:T(8,128)S(1)} %all-to-all-done.1) | copy-start | bytes 786436
  176.9 20.5 %collective-permute-start.14 = (f32[2,512,128]{2,1,0:T(8,128)S(1)}, f32[2,512,128]{2,1,0:T(8,128)}, u32[]{:S(2)}, u32[]{:S(2)}) collective-permute-start(f32[2,512,128]{2,1,0:T(8,128)S(1)} %copy-done.15), channel_id=1, source_target_pairs={{0,1},{1,2},{2,3},{3,4},{4,5},{5,6},{6,7},{7,8},{8,9},{9,10},{10,1... | collective-permute-start | bytes 1572872 | tf_op jit(solution)/shard_map/ppermute | solution.py:744
  176.9 20.5 %collective-permute-start.16 = (f32[2,512,128]{2,1,0:T(8,128)S(1)}, f32[2,512,128]{2,1,0:T(8,128)}, u32[]{:S(2)}, u32[]{:S(2)}) collective-permute-start(f32[2,512,128]{2,1,0:T(8,128)S(1)} %copy-done.14), channel_id=1, source_target_pairs={{1,0},{2,1},{3,2},{4,3},{5,4},{6,5},{7,6},{8,7},{9,8},{10,9},{11,1... | collective-permute-start | bytes 1572872 | tf_op jit(solution)/shard_map/ppermute | solution.py:747
  186.5 6.0 %collective-permute-start.17 = (f32[32,128]{1,0:T(8,128)}, f32[32,128]{1,0:T(8,128)S(1)}, u32[]{:S(2)}, u32[]{:S(2)}) collective-permute-start(f32[32,128]{1,0:T(8,128)} %collect.1), channel_id=1, source_target_pairs={{0,64},{64,0},{1,65},{65,1},{2,66},{66,2},{3,67},{67,3},{4,68},{68... | collective-permute-start | bytes 49160 | tf_op jit(solution)/shard_map/ppermute | solution.py:755
  192.5 4.9 %copy-start.24 = (f32[32,128]{1,0:T(8,128)}, f32[32,128]{1,0:T(8,128)S(1)}, u32[]{:S(2)}) copy-start(f32[32,128]{1,0:T(8,128)S(1)} %collective-permute-done.17.s) | copy-start | bytes 49156
  192.5 4.9 %copy-start.21 = (f32[2,512,128]{2,1,0:T(8,128)}, f32[2,512,128]{2,1,0:T(8,128)S(1)}, u32[]{:S(2)}) copy-start(f32[2,512,128]{2,1,0:T(8,128)S(1)} %collective-permute-done.13.ru0) | copy-start | bytes 1572868
  192.5 4.9 %copy-start.23 = (f32[2,512,128]{2,1,0:T(8,128)}, f32[2,512,128]{2,1,0:T(8,128)S(1)}, u32[]{:S(2)}) copy-start(f32[2,512,128]{2,1,0:T(8,128)S(1)} %collective-permute-done.15.rd0) | copy-start | bytes 1572868
  212.2 31.2 %collective-permute-start.18 = (f32[4,512,128]{2,1,0:T(8,128)}, f32[4,512,128]{2,1,0:T(8,128)S(1)}, u32[]{:S(2)}, u32[]{:S(2)}) collective-permute-start(f32[4,512,128]{2,1,0:T(8,128)} %get-tuple-element.92), channel_id=1, source_target_pairs={{0,1},{1,2},{2,3},{3,4},{4,5},{5,6},{6,7},{7,8},{8,9},{9,10},{10,1... | collective-permute-start | bytes 3145736 | tf_op jit(solution)/shard_map/ppermute | solution.py:744
  212.2 31.1 %collective-permute-start.19 = (f32[4,512,128]{2,1,0:T(8,128)}, f32[4,512,128]{2,1,0:T(8,128)S(1)}, u32[]{:S(2)}, u32[]{:S(2)}) collective-permute-start(f32[4,512,128]{2,1,0:T(8,128)} %get-tuple-element.93), channel_id=1, source_target_pairs={{1,0},{2,1},{3,2},{4,3},{5,4},{6,5},{7,6},{8,7},{9,8},{10,9},{11,1... | collective-permute-start | bytes 3145736 | tf_op jit(solution)/shard_map/ppermute | solution.py:747
  243.4 1.0 copy-start.11
  243.4 1.4 copy-start.12

commit v3 on v2

--- a/solution.py
+++ b/solution.py
@@ -13,6 +13,7 @@
 NR = 18
 VM = pl.BlockSpec(memory_space=pltpu.VMEM)
 SM = pl.BlockSpec(memory_space=pltpu.SMEM)
+BLOCK_MIB = 44
 OFFSETS = tuple(range(-7, 8)) + (32,)
 
 
@@ -24,8 +25,12 @@
     return pl.CostEstimate(flops=int(us * 5e8), bytes_accessed=1 << 20, transcendentals=0)
 
 
-def params(**kw):
-    return pltpu.CompilerParams(vmem_limit_bytes=60 * 2**20, **kw)
+def params(mib=BLOCK_MIB):
+    return pltpu.CompilerParams(vmem_limit_bytes=mib * 2**20)
+
+
+def parity(me):
+    return lax.rem(me[0], 2)
 
 
 def halves(x):
@@ -60,35 +65,37 @@
     return buf[j, pl.ds(r, 128, stride=8), :].T
 
 
-def start_in_kernel(x, top, bot, buf, out, sems, osems):
+def start_in_kernel(me, x, outer, inner, buf, out, sems, osems):
+    odd = parity(me)
     c = start_raw(x, buf, sems)
     todo = []
     for j in range(4):
         c[j].wait()
         for r in range(8):
             out[r, pl.ds(128 * j, 128), :] = turned(buf, j, r)
-        for i, dst in enumerate((top, bot)):
-            src = out.at[pl.ds(4 * i, 4), pl.ds(128 * j, 128), :]
+        for i, (r0, dst) in enumerate(((4 * odd, outer), (4 - 4 * odd, inner))):
+            src = out.at[pl.ds(r0, 4), pl.ds(128 * j, 128), :]
             todo.append(pltpu.make_async_copy(src, lon_part(dst, j), osems.at[i, j]))
             todo[-1].start()
     for d in todo:
         d.wait()
 
 
-def start_in(x):
+def start_in(me, x):
     return pl.pallas_call(
         start_in_kernel,
         out_shape=(sds(4, LON, LEV), sds(4, LON, LEV)),
-        in_specs=[ANY],
+        in_specs=[SM, ANY],
         out_specs=(ANY, ANY),
         scratch_shapes=[RAW, ROWS, dma_sems(4), dma_sems(2, 4)],
         compiler_params=params(),
         cost_estimate=cost(4),
         name="start_in",
-    )(x)
-
-
-def diff_in_kernel(x, sea, full, top, bot, buf, out, sems, osems):
+    )(me, x)
+
+
+def diff_in_kernel(me, x, sea, outer, inner, full, buf, out, sems, osems):
+    odd = parity(me)
     c = start_raw(x, buf, sems)
     todo = []
     for j in range(4):
@@ -96,7 +103,7 @@
         at = pl.ds(128 * j, 128)
         for r in range(8):
             out[r, at, :] = (buf[j, pl.ds(r, 128, stride=8), :] * sea[r : r + 1, at]).T
-        for i, (r0, n, dst) in enumerate(((0, 3, top), (5, 3, bot), (0, 8, full))):
+        for i, (r0, n, dst) in enumerate(((5 * odd, 3, outer), (5 - 5 * odd, 3, inner), (0, 8, full))):
             src = out.at[pl.ds(r0, n), at, :]
             todo.append(pltpu.make_async_copy(src, lon_part(dst, j), osems.at[i, j]))
             todo[-1].start()
@@ -104,17 +111,17 @@
         d.wait()
 
 
-def diff_in(x, sea):
+def diff_in(me, x, sea):
     return pl.pallas_call(
         diff_in_kernel,
-        out_shape=(sds(8, LON, LEV), sds(3, LON, LEV), sds(3, LON, LEV)),
-        in_specs=[ANY, VM],
+        out_shape=(sds(3, LON, LEV), sds(3, LON, LEV), sds(8, LON, LEV)),
+        in_specs=[SM, ANY, VM],
         out_specs=(ANY,) * 3,
         scratch_shapes=[RAW, ROWS, dma_sems(4), dma_sems(3, 4)],
         compiler_params=params(),
         cost_estimate=cost(4),
         name="diff_in",
-    )(x, sea)
+    )(me, x, sea)
 
 
 def to_rows_kernel(x, o, buf, out, sems, osems):
@@ -161,14 +168,15 @@
     )(x)
 
 
-def grad_out_kernel(me, x, up, dn, o, base, add, buf, sems, osems):
+def grad_out_kernel(me, x, outer, inner, o, base, add, buf, sems, osems):
+    odd = parity(me)
     c = []
     for j in range(4):
         at = pl.ds(128 * j, 128)
         for i, (src, dst) in enumerate(
             (
-                (lon_part(up, j), add.at[pl.ds(0, 4), at, :]),
-                (lon_part(dn, j), add.at[pl.ds(4, 4), at, :]),
+                (lon_part(outer, j), add.at[pl.ds(4 * odd, 4), at, :]),
+                (lon_part(inner, j), add.at[pl.ds(4 - 4 * odd, 4), at, :]),
                 (lon_part(x, j), lon_part(base, j)),
             )
         ):
@@ -190,7 +198,7 @@
         d.wait()
 
 
-def grad_out(me, x, up, dn):
+def grad_out(me, x, outer, inner):
     return pl.pallas_call(
         grad_out_kernel,
         out_shape=sds(1024, LON),
@@ -200,7 +208,7 @@
         compiler_params=params(),
         cost_estimate=cost(4),
         name="grad_out",
-    )(me, x, up, dn)
+    )(me, x, outer, inner)
 
 
 def mix_kernel(w, fwd, bwd):
@@ -332,6 +340,10 @@
         c.wait()
 
 
+def plain_rows(v, r0, n):
+    return v.at[pl.ds(r0, n)]
+
+
 def tile_rows(v, r0, n):
     return v.at[pl.ds(r0, n), pl.ds(OFF, LON), :]
 
@@ -371,20 +383,33 @@
 ]
 U_SCRATCH = pltpu.VMEM((NR, LON, 128), F32)
 COLS = pltpu.VMEM((128, 128), F32)
-HALF = sds(2, LON, LEV)
-
-
-def first_kernel(me, top, bot, hu, hd, dt, du, dn, w2, o_t0, o_t1, o_b0, o_b1, o_surf, va, vb, h, d, sems):
+PARTS = (sds(3, LON, LEV), sds(1, LON, LEV), sds(4, LON, LEV))
+
+
+def near_far(up, dn, odd):
+    return up + (dn - up) * odd, dn + (up - dn) * odd
+
+
+def edge_refs(v, up, dn, odd, cut):
+    outer, inner = near_far(up, dn, odd)
+    return cut(v, outer, 3), cut(v, outer + 3, 1), cut(v, inner, 4)
+
+
+def first_kernel(me, so, si, ho, hi, dt, do, di, w2, o0, o1, o2, o_surf, va, vb, h, d, sems):
+    odd = parity(me)
+    own_o, own_i = near_far(5, 9, odd)
+    far_o, far_i = near_far(1, 13, odd)
+    d_o, d_i = near_far(2, 13, odd)
     c = copies(
         sems,
         [
             (dt, d.at[pl.ds(5, 8)]),
-            (top, tile_rows(va, 5, 4)),
-            (bot, tile_rows(va, 9, 4)),
-            (du, d.at[pl.ds(2, 3)]),
-            (hu, tile_rows(va, 1, 4)),
-            (dn, d.at[pl.ds(13, 3)]),
-            (hd, tile_rows(va, 13, 4)),
+            (so, tile_rows(va, own_o, 4)),
+            (si, tile_rows(va, own_i, 4)),
+            (do, d.at[pl.ds(d_o, 3)]),
+            (ho, tile_rows(va, far_o, 4)),
+            (di, d.at[pl.ds(d_i, 3)]),
+            (hi, tile_rows(va, far_i, 4)),
         ],
     )
 
@@ -404,15 +429,15 @@
         lax.fori_loop(0, n, cp, 0)
 
     wait(c[0], c[1])
-    prepare(5, 4)
+    prepare(own_o, 4)
     wait(c[2])
-    prepare(9, 4)
+    prepare(own_i, 4)
     wait(*c[3:])
     clear_ends(me, ((va, 1, 4), (d, 2, 3)), ((va, 13, 4), (d, 13, 3)))
     prepare(2, 3)
     prepare(13, 3)
     forward_block(va, vb, h, d, w2, first=True)
-    c = copies(sems, [(tile_rows(va, 5 + 2 * i, 2), o) for i, o in enumerate((o_t0, o_t1, o_b0, o_b1))])
+    c = copies(sems, list(zip(edge_refs(va, 5, 9, odd, tile_rows), (o0, o1, o2))))
     o_surf[...] = gather_surface(lambda r, j: va[r + 5, pl.ds(OFF + 128 * j, 128), :], 8)[0:32]
     wait(*c)
 
@@ -420,9 +445,9 @@
 def first_block(*args):
     return pl.pallas_call(
         first_kernel,
-        out_shape=(HALF,) * 4 + (sds(32, 128),),
+        out_shape=PARTS + (sds(32, 128),),
         in_specs=[SM] + [ANY] * 7 + [VM],
-        out_specs=(ANY,) * 4 + (VM,),
+        out_specs=(ANY,) * 3 + (VM,),
         scratch_shapes=BLOCK_SCRATCH + [dma_sems(7)],
         compiler_params=params(),
         cost_estimate=cost(15),
@@ -431,29 +456,32 @@
 
 
 def middle_kernel(
-    me, t0, t1, b0, b1, hu0, hu1, hd0, hd1, s, su, sd, dt, du, dn, m, w2f, w2b,
-    o_final, o_adj, o_u0, o_u1, o_d0, o_d1, o_s, o_su, o_sd, va, vb, h, d, u, mm, cols, sems,
+    me, v0, v1, v2, h0, h1, h2, s, so, si, dt, do, di, m, w2f, w2b,
+    o_final, o_adj, o0, o1, o2, o_s, o_so, o_si, va, vb, h, d, u, mm, cols, sems,
 ):
+    odd = parity(me)
+    own = edge_refs(va, 5, 9, odd, tile_rows)
+    far = edge_refs(va, 1, 13, odd, tile_rows)
+    d_o, d_i = near_far(2, 13, odd)
     c = copies(
         sems,
         [
-            (t0, tile_rows(va, 5, 2)),
-            (t1, tile_rows(va, 7, 2)),
-            (b0, tile_rows(va, 9, 2)),
-            (b1, tile_rows(va, 11, 2)),
-            (hu0, tile_rows(va, 1, 2)),
-            (hu1, tile_rows(va, 3, 2)),
-            (hd0, tile_rows(va, 13, 2)),
-            (hd1, tile_rows(va, 15, 2)),
+            (v0, own[0]),
+            (v1, own[1]),
+            (v2, own[2]),
+            (h0, far[0]),
+            (h1, far[1]),
+            (h2, far[2]),
             (dt, d.at[pl.ds(5, 8)]),
-            (du, d.at[pl.ds(2, 3)]),
-            (dn, d.at[pl.ds(13, 3)]),
+            (do, d.at[pl.ds(d_o, 3)]),
+            (di, d.at[pl.ds(d_i, 3)]),
             (m, mm),
         ],
     )
-    cols[0:16] = su[...]
+    c_o, c_i = near_far(0, 48, odd)
+    cols[pl.ds(pl.multiple_of(c_o, 16), 16)] = so[...]
+    cols[pl.ds(pl.multiple_of(c_i, 16), 16)] = si[...]
     cols[16:48] = s[...]
-    cols[48:64] = sd[...]
     cols[64:128] = jnp.zeros((64, 128), F32)
     clear_ends(me, ((cols, 0, 16),), ((cols, 48, 16),))
     cols[...] = cols[...].T
@@ -470,16 +498,16 @@
 
         lax.fori_loop(0, 4, cp, 0)
 
-    for i, r0 in ((0, 5), (2, 9)):
-        wait(c[i], c[i + 1])
-        prepare(r0)
-    wait(*c[4:11])
+    wait(*c[0:3])
+    prepare(5)
+    prepare(9)
+    wait(*c[3:9])
     clear_ends(me, ((va, 1, 4), (d, 2, 3)), ((va, 13, 4), (d, 13, 3)))
     prepare(1)
     prepare(13)
     forward_block(va, vb, h, d, w2f)
     out = copies(sems, [(tile_rows(va, 5, 8), o_final)])
-    wait(c[11])
+    wait(c[9])
 
     def body(i, carry):
         r = 5 + i
@@ -498,18 +526,13 @@
     push_block(vb, va, u, h, d, w2b)
     out = copies(
         sems,
-        [
-            (u.at[pl.ds(1, 2)], o_u0),
-            (u.at[pl.ds(3, 2)], o_u1),
-            (u.at[pl.ds(13, 2)], o_d0),
-            (u.at[pl.ds(15, 2)], o_d1),
-            (u.at[pl.ds(5, 8)], o_adj),
-        ],
+        list(zip(edge_refs(u, 1, 13, odd, plain_rows), (o0, o1, o2)))
+        + [(u.at[pl.ds(5, 8)], o_adj)],
     )
-    g = gather_surface(lambda r, j: u[r + 1, pl.ds(128 * j, 128), :], 16)
-    o_su[...] = g[0:16]
-    o_s[...] = g[16:48]
-    o_sd[...] = g[48:64]
+    cols[...] = gather_surface(lambda r, j: u[r + 1, pl.ds(128 * j, 128), :], 16)
+    o_so[...] = cols[pl.ds(pl.multiple_of(c_o, 16), 16)]
+    o_s[...] = cols[16:48]
+    o_si[...] = cols[pl.ds(pl.multiple_of(c_i, 16), 16)]
     wait(*out)
 
 
@@ -517,11 +540,11 @@
     return pl.pallas_call(
         middle_kernel,
         out_shape=(
-            sds(8, LON, LEV), sds(8, LON, LEV), HALF, HALF, HALF, HALF,
+            sds(8, LON, LEV), sds(8, LON, LEV), *PARTS,
             sds(32, 128), sds(16, 128), sds(16, 128),
         ),
-        in_specs=[SM] + [ANY] * 8 + [VM] * 3 + [ANY] * 4 + [VM] * 2,
-        out_specs=(ANY,) * 6 + (VM,) * 3,
+        in_specs=[SM] + [ANY] * 6 + [VM] * 3 + [ANY] * 4 + [VM] * 2,
+        out_specs=(ANY,) * 5 + (VM,) * 3,
         scratch_shapes=BLOCK_SCRATCH
         + [U_SCRATCH, pltpu.VMEM((8, LON, 128), F32), COLS, dma_sems(12)],
         compiler_params=params(),
@@ -531,28 +554,31 @@
 
 
 def last_kernel(
-    me, adj, ru0, ru1, rd0, rd1, s, top, bot, dt, du, dn, w2b, o_base, o_up, o_dn,
+    me, adj, r0, r1, r2, s, so, si, dt, do, di, w2b, o_base, o_outer, o_inner,
     va, vb, h, d, u, got, base, cols, sems,
 ):
+    odd = parity(me)
+    e_o, e_i = near_far(0, 4, odd)
+    d_o, d_i = near_far(2, 13, odd)
+    parts = edge_refs(got, 0, 4, odd, plain_rows)
     c = copies(
         sems,
         [
             (adj, u.at[pl.ds(5, 8)]),
             (dt, d.at[pl.ds(5, 8)]),
-            (ru0, got.at[pl.ds(0, 2)]),
-            (ru1, got.at[pl.ds(2, 2)]),
-            (rd0, got.at[pl.ds(4, 2)]),
-            (rd1, got.at[pl.ds(6, 2)]),
-            (du, d.at[pl.ds(2, 3)]),
-            (dn, d.at[pl.ds(13, 3)]),
-            (top, base.at[pl.ds(0, 4)]),
-            (bot, base.at[pl.ds(4, 4)]),
+            (r0, parts[0]),
+            (r1, parts[1]),
+            (r2, parts[2]),
+            (do, d.at[pl.ds(d_o, 3)]),
+            (di, d.at[pl.ds(d_i, 3)]),
+            (so, base.at[pl.ds(e_o, 4)]),
+            (si, base.at[pl.ds(e_i, 4)]),
         ],
     )
     cols[0:32] = s[...]
     cols[32:128] = jnp.zeros((96, 128), F32)
     cols[...] = cols[...].T
-    wait(*c[0:6])
+    wait(*c[0:5])
     clear_ends(me, ((got, 0, 4),), ((got, 4, 4),))
 
     def cp(i, carry):
@@ -569,10 +595,11 @@
         return carry
 
     lax.fori_loop(0, 8, cp, 0)
-    wait(*c[6:10])
+    wait(*c[5:9])
     clear_ends(me, ((d, 2, 3),), ((d, 13, 3),))
     push_block(vb, va, u, h, d, w2b)
-    out = copies(sems, [(u.at[pl.ds(1, 4)], o_up), (u.at[pl.ds(13, 4)], o_dn)])
+    out_o, out_i = near_far(1, 13, odd)
+    out = copies(sems, [(u.at[pl.ds(out_o, 4)], o_outer), (u.at[pl.ds(out_i, 4)], o_inner)])
 
     def add(i, carry):
         base[i] = base[i] + u[5 + i]
@@ -589,7 +616,7 @@
     return pl.pallas_call(
         last_kernel,
         out_shape=(sds(8, LON, LEV), sds(4, LON, LEV), sds(4, LON, LEV)),
-        in_specs=[SM] + [ANY] * 5 + [VM] + [ANY] * 5 + [VM],
+        in_specs=[SM] + [ANY] * 4 + [VM] + [ANY] * 5 + [VM],
         out_specs=(ANY,) * 3,
         scratch_shapes=BLOCK_SCRATCH
         + [
@@ -623,54 +650,41 @@
     )(me, send_rows, surf)
 
 
-def fetch_blocks(ids, w, buf, sems):
-    for k in range(LIVE):
-        pltpu.make_async_copy(w.at[ids[k]], buf.at[k], sems.at[k // 12]).start()
-
-
-def fetched(w, buf, sems, part):
-    pltpu.make_async_copy(w.at[pl.ds(0, 12)], buf.at[pl.ds(12 * part, 12)], sems.at[part]).wait()
-
-
 LIVE = 48
-WEIGHTS = [pltpu.VMEM((LIVE, 128, 128), F32), pltpu.SemaphoreType.DMA((4,))]
-
-
-def remap_kernel(ids, pick, dest, arrived, w, sea, o, buf, sems):
-    fetch_blocks(ids, w, buf, sems)
-    acc = jnp.zeros((128, 128), F32)
-    for part in range(4):
-        fetched(w, buf, sems, part)
-
-        def step(i, acc, part=part):
-            for q in range(4):
-                k = 12 * part + 4 * i + q
-                x = arrived[pl.ds(pick[k], 1), :]
-                red = jnp.sum(buf[k] * x, axis=1, keepdims=True)
-                acc = acc + jnp.where(lanes() == dest[k], red, 0.0)
-            return acc
-
-        acc = lax.fori_loop(0, 3, step, acc)
+
+
+def remap_kernel(me, ids, pick, dest, arrived, w, sea, o, o_outer, o_inner):
+    def step(i, acc):
+        for q in range(4):
+            k = 4 * i + q
+            x = arrived[pl.ds(pick[k], 1), :]
+            red = jnp.sum(w[ids[k]] * x, axis=1, keepdims=True)
+            acc = acc + jnp.where(lanes() == dest[k], red, 0.0)
+        return acc
+
+    acc = lax.fori_loop(0, LIVE // 4, step, jnp.zeros((128, 128), F32))
     o[...] = acc.T[0:32] * sea[...]
-
-
-def remap(ids, pick, dest, arrived, w, sea):
+    e_o, e_i = near_far(0, 16, parity(me))
+    o_outer[...] = o[pl.ds(pl.multiple_of(e_o, 16), 16)]
+    o_inner[...] = o[pl.ds(pl.multiple_of(e_i, 16), 16)]
+
+
+def remap(me, ids, pick, dest, arrived, w, sea):
     return pl.pallas_call(
         remap_kernel,
-        out_shape=sds(32, 128),
-        in_specs=[SM, SM, SM, VM, ANY, VM],
-        out_specs=VM,
-        scratch_shapes=WEIGHTS,
-        compiler_params=params(),
+        out_shape=(sds(32, 128), sds(16, 128), sds(16, 128)),
+        in_specs=[SM, SM, SM, SM, VM, VM, VM],
+        out_specs=(VM,) * 3,
+        compiler_params=params(16),
         cost_estimate=cost(3),
         name="remap",
-    )(ids, pick, dest, arrived, w, sea)
-
-
-def remap_back_kernel(me, ids, pick, dest, s, ru, rd, w, sea, o, cols, wide, buf, sems):
-    fetch_blocks(ids, w, buf, sems)
-    cols[0:16] = ru[...]
-    cols[16:32] = rd[...]
+    )(me, ids, pick, dest, arrived, w, sea)
+
+
+def remap_back_kernel(me, ids, pick, dest, s, so, si, w, sea, o, cols, wide):
+    e_o, e_i = near_far(0, 16, parity(me))
+    cols[pl.ds(pl.multiple_of(e_o, 16), 16)] = so[...]
+    cols[pl.ds(pl.multiple_of(e_i, 16), 16)] = si[...]
     clear_ends(me, ((cols, 0, 16),), ((cols, 16, 16),))
     cols[0:32] = (cols[0:32] + s[...]) * sea[...]
     cols[32:128] = jnp.zeros((96, 128), F32)
@@ -678,30 +692,28 @@
     for p in range(32):
         wide[p] = jnp.broadcast_to(cols[:, p : p + 1], (128, 128))
     o[...] = jnp.zeros((512, 128), F32)
-    for part in range(4):
-        fetched(w, buf, sems, part)
-
-        def step(i, carry, part=part):
-            for q in range(4):
-                k = 12 * part + 4 * i + q
-                red = jnp.sum(buf[k] * wide[dest[k]], axis=0, keepdims=True)
-                o[pl.ds(pick[k], 1), :] = red
-            return carry
-
-        lax.fori_loop(0, 3, step, 0)
-
-
-def remap_back(me, ids, pick, dest, s, ru, rd, w, sea):
+
+    def step(i, carry):
+        for q in range(4):
+            k = 4 * i + q
+            red = jnp.sum(w[ids[k]] * wide[dest[k]], axis=0, keepdims=True)
+            o[pl.ds(pick[k], 1), :] = red
+        return carry
+
+    lax.fori_loop(0, LIVE // 4, step, 0)
+
+
+def remap_back(me, ids, pick, dest, s, so, si, w, sea):
     return pl.pallas_call(
         remap_back_kernel,
         out_shape=sds(512, 128),
-        in_specs=[SM, SM, SM, SM, VM, VM, VM, ANY, VM],
+        in_specs=[SM, SM, SM, SM, VM, VM, VM, VM, VM],
         out_specs=VM,
-        scratch_shapes=[COLS, pltpu.VMEM((32, 128, 128), F32)] + WEIGHTS,
-        compiler_params=params(),
+        scratch_shapes=[COLS, pltpu.VMEM((32, 128, 128), F32)],
+        compiler_params=params(16),
         cost_estimate=cost(3),
         name="remap_back",
-    )(me, ids, pick, dest, s, ru, rd, w, sea)
+    )(me, ids, pick, dest, s, so, si, w, sea)
 
 
 def collect_kernel(me, send_rows, got, o):
@@ -737,19 +749,14 @@
 ):
     component = lax.axis_index("comp")
     own_tile = lax.axis_index("tile")
-    down_pairs = [(i, (i + 1) % 64) for i in range(64)]
-    up_pairs = [((i + 1) % 64, i) for i in range(64)]
-
-    def to_next(x):
-        return lax.ppermute(x, "tile", down_pairs)
-
-    def to_prev(x):
-        return lax.ppermute(x, "tile", up_pairs)
-
-    def both(last, first):
-        after = to_next(last)
-        before = to_prev(first)
-        return after, before
+    across = [(i, (i + 1 if i % 2 else i - 1) % 64) for i in range(64)]
+    on_chip = [(i, i ^ 1) for i in range(64)]
+
+    def far(x):
+        return lax.ppermute(x, "tile", across)
+
+    def near(x):
+        return lax.ppermute(x, "tile", on_chip)
 
     def swap(x):
         return lax.ppermute(x, "comp", [(0, 1), (1, 0)])
@@ -759,13 +766,13 @@
         x = lax.all_to_all(x, "tile", split_axis=0, concat_axis=0, tiled=True)
         return x.reshape(512, 128)
 
-    start = starting_perturbation.reshape(1024, LON)
-    s_top, s_bot = start_in(start)
-    s_hu, s_hd = to_next(s_bot), to_prev(s_top)
+    me = own_tile.reshape(1)
+    so, si = start_in(me, starting_perturbation.reshape(1024, LON))
+    ho, hi = far(so), near(si)
     sea = jnp.where(component == 1, ocean_mask.astype(F32), 1.0)
     sea32 = sea.reshape(32, 128)
-    dt, d_top, d_bot = diff_in(diffusion.reshape(1024, LON), sea)
-    du, dd = to_next(d_bot), to_prev(d_top)
+    d_o, d_i, dt = diff_in(me, diffusion.reshape(1024, LON), sea)
+    do, di = far(d_o), near(d_i)
     w2f, w2b = mixes(vert_mix[0])
 
     slots = jnp.arange(64, dtype=jnp.int32)
@@ -779,39 +786,38 @@
     hits = (pair_tile[component] == own_tile).astype(jnp.int32)
     sources = pair_patch[component].reshape(64, 8, 8)
     send_rows = jnp.sum(hits[:, :, None] * sources, axis=1).reshape(512)
-    me = own_tile.reshape(1)
     weights = remap_weight[0]
     measured = to_rows(measured_discrepancy.reshape(1024, LON))
-    s_hu, s_hd, du, dd, w2f, w2b, ids, pick, dest, send_rows, measured, sea32 = (
+    ho, hi, do, di, w2f, w2b, ids, pick, dest, send_rows, measured, sea32 = (
         lax.optimization_barrier(
-            (s_hu, s_hd, du, dd, w2f, w2b, ids, pick, dest, send_rows, measured, sea32)
+            (ho, hi, do, di, w2f, w2b, ids, pick, dest, send_rows, measured, sea32)
         )
     )
 
-    t0, t1, b0, b1, surf = first_block(me, s_top, s_bot, s_hu, s_hd, dt, du, dd, w2f)
+    v0, v1, v2, surf = first_block(me, so, si, ho, hi, dt, do, di, w2f)
     other = swap(surf)
-    hu0, hd0 = both(b0, t0)
+    h0, h2 = far(v0), near(v2)
     offered = offer(me, send_rows, other)
     arrived = exchange(offered)
-    b1s, t1s, arrived = lax.optimization_barrier((b1, t1, arrived))
-    hu1, hd1 = to_next(b1s), to_prev(t1s)
-    fix = remap(ids, pick, dest, arrived, weights, sea32)
-    f_hu, f_hd = to_next(fix[16:32]), to_prev(fix[0:16])
-    final, adj, u0, u1, d0, d1, a0, a0_up, a0_dn = middle_block(
-        me, t0, t1, b0, b1, hu0, hu1, hd0, hd1, fix, f_hu, f_hd, dt, du, dd, measured, w2f, w2b
+    v1s, arrived = lax.optimization_barrier((v1, arrived))
+    h1 = far(v1s)
+    fix, fix_o, fix_i = remap(me, ids, pick, dest, arrived, weights, sea32)
+    fo, fi = far(fix_o), near(fix_i)
+    final, adj, a0, a1, a2, s0, s0_o, s0_i = middle_block(
+        me, v0, v1, v2, h0, h1, h2, fix, fo, fi, dt, do, di, measured, w2f, w2b
     )
-    r0u, r0d = to_next(a0_dn), to_prev(a0_up)
-    u0, d0, r0u, r0d = lax.optimization_barrier((u0, d0, r0u, r0d))
-    ru0, rd0 = both(d0, u0)
-    offered = remap_back(me, ids, pick, dest, a0, r0u, r0d, weights, sea32)
+    ro, ri = far(s0_o), near(s0_i)
+    a0, a2, ro, ri = lax.optimization_barrier((a0, a2, ro, ri))
+    r0, r2 = far(a0), near(a2)
+    offered = remap_back(me, ids, pick, dest, s0, ro, ri, weights, sea32)
     back = exchange(offered)
-    u1, d1, back = lax.optimization_barrier((u1, d1, back))
-    ru1, rd1 = to_next(d1), to_prev(u1)
+    a1, back = lax.optimization_barrier((a1, back))
+    r1 = far(a1)
     back = swap(collect(me, send_rows, back))
-    base, g_up, g_dn = last_block(me, adj, ru0, ru1, rd0, rd1, back, s_top, s_bot, dt, du, dd, w2b)
-    gu, gd = to_next(g_dn), to_prev(g_up)
+    base, g_o, g_i = last_block(me, adj, r0, r1, r2, back, so, si, dt, do, di, w2b)
+    go, gi = far(g_o), near(g_i)
     final_raw = to_raw(final)
-    gradient = grad_out(me, base, gu, gd)
+    gradient = grad_out(me, base, go, gi)
     shape = starting_perturbation.shape
     return final_raw.reshape(shape), gradient.reshape(shape)
 

time: 249 us -> 233 us (0.936)
  the two profiles are of different devices: /device:TPU:0 before, /device:TPU:8 now
where the time goes in v3:
time: 233 us; the launch traced here: 230 us
  waiting for transfers between devices  79.5 us (34%)
  Pallas kernels  63.4 us (27%)
  blocking collectives  43.7 us (19%)
  starting transfers between devices  28.6 us (12%)
  local copies, waits for them, and re-layouts  13 us (6%)
    ppermute x9, waiting for transfers between devices, far(): return lax.ppermute(x, 'tile', across)  58.6 us
    all_to_all x2, blocking collectives, exchange(): x = lax.all_to_all(x, 'tile', split_axis=0, concat_axis=0, tiled=True)  43.7 us
    ppermute x9, starting transfers between devices, far(): return lax.ppermute(x, 'tile', across)  28 us
    pallas_call x1, Pallas kernels, middle_block(): pl.pallas_call(middle_kernel, out_shape=(sds(8, LON, LEV), sds(8, LON, LE...  21.2 us
    ppermute x2, waiting for transfers between devices, swap(): return lax.ppermute(x, 'comp', [(0, 1), (1, 0)])  20.9 us
    pallas_call x1, Pallas kernels, last_block(): pl.pallas_call(last_kernel, out_shape=(sds(8, LON, LEV), sds(4, LON, LEV)...  12.2 us
    unnamed x47, local copies, waits for them, and re-layouts  11.9 us
    pallas_call x1, Pallas kernels, first_block(): pl.pallas_call(first_kernel, out_shape=PARTS + (sds(32, 128),), in_specs=...  10.5 us
  transfers between devices with their start and end apart: 18, of which 7 were waited for; matrix products, arithmetic and copies ran while one was open for 1% of the time, Pallas kernels for 7%

profile of v3, /device:TPU:8, one launch (start us, length us, event | category | flops | bytes accessed | tf_op | source)
XLA Modules:
  0.0 229.8 jit_solution(12884814534354714120)
XLA Ops:
  0.6 0.0 copy-start
  0.7 1.6 copy-done.3
  2.3 2.0 start_in.1
  4.3 5.9 %collective-permute-start = (f32[4,512,128]{2,1,0:T(8,128)S(1)}, f32[4,512,128]{2,1,0:T(8,128)}, u32[]{:S(2)}, u32[]{:S(2)}) collective-permute-start(f32[4,512,128]{2,1,0:T(8,128)S(1)} %get-tuple-element.47.so), channel_id=1, source_target_pairs={{0,63},{1,2},{2,1},{3,4},{4,3},{5,6},{6,5},{7,8},{8,7},{9,10},{10,... | collective-permute-start | bytes 3145736 | tf_op jit(solution)/shard_map/ppermute | solution.py:756
  10.2 0.0 copy-start.20
  10.2 0.0 copy-start.21
  10.2 0.0 copy-start.22
  10.2 2.1 diff_in.1
  12.3 0.0 copy-start.16
  12.4 1.3 copy-done.16
  13.7 0.8 collective-permute-start.2
  14.4 0.0 collective-permute-start.3
  14.4 0.2 multiply_reduce_fusion
  14.6 0.1 broadcast_in_dim.10
  14.7 0.1 mul.57
  14.8 0.1 broadcast_in_dim.9
  14.9 0.1 reshape.90
  15.0 0.1 copy.18
  15.1 0.1 copy.17
  15.2 0.7 reshape.91.send_rows
  15.8 1.6 mixes.1
  17.4 0.1 convert_reduce_fusion
  17.5 0.2 select_reduce_fusion
  17.8 0.0 copy-start.5
  17.8 1.6 copy-done.5
  19.4 1.3 to_rows.1.m
  20.7 0.0 copy-start.15
  20.7 1.3 copy-done.15
  22.0 28.7 %collective-permute-done.2.do = f32[3,512,128]{2,1,0:T(8,128)S(1)} collective-permute-done((f32[3,512,128]{2,1,0:T(8,128)}, f32[3,512,128]{2,1,0:T(8,128)S(1)}, u32[]{:S(2)}, u32[]{:S(2)}) %collective-permute-start.2) | collective-permute-done | bytes 786464 | tf_op jit(solution)/shard_map/ppermute | solution.py:756
  50.7 0.0 collective-permute-done.3.di
  50.7 0.9 copy-done.6
  51.6 0.0 collective-permute-done.ho
  51.7 1.1 copy-done.7
  52.8 10.5 %first_block.1 = (f32[3,512,128]{2,1,0:T(8,128)}, f32[1,512,128]{2,1,0:T(8,128)S(1)}, f32[4,512,128]{2,1,0:T(8,128)S(1)}, f32[32,128]{1,0:T(8,128)S(1)}) custom-call(s32[1]{0:T(128)} %bitcast.me, f32[4,512,128]{2,1,0:T(8,128)S(1)} %get-tuple-element.47.so, f32[4,512,128]{2,1,0:T(8,128)} %get-tuple-element.48.si, f32[4,512,128]{2,1,0:T(8,128)} %collective-permute-done.ho, ...), custom_call_target="tpu_custom_call" | custom-call | flops 7500000256 | bytes 1048576 | tf_op jit(solution)/shard_map/first_block/pallas_call | solution.py:446
  63.3 0.1 collective-permute-start.7
  63.4 3.8 %collective-permute-start.4 = (f32[3,512,128]{2,1,0:T(8,128)}, f32[3,512,128]{2,1,0:T(8,128)}, u32[]{:S(2)}, u32[]{:S(2)}) collective-permute-start(f32[3,512,128]{2,1,0:T(8,128)} %get-tuple-element.59.v0), channel_id=1, source_target_pairs={{0,63},{1,2},{2,1},{3,4},{4,3},{5,6},{6,5},{7,8},{8,7},{9,10},{10,... | collective-permute-start | bytes 2359304 | tf_op jit(solution)/shard_map/ppermute | solution.py:756
  67.2 0.5 collective-permute-start.5
  67.7 16.0 %collective-permute-done.5.surf = f32[32,128]{1,0:T(8,128)S(1)} collective-permute-done((f32[32,128]{1,0:T(8,128)S(1)}, f32[32,128]{1,0:T(8,128)S(1)}, u32[]{:S(2)}, u32[]{:S(2)}) %collective-permute-start.5) | collective-permute-done | bytes 16416 | tf_op jit(solution)/shard_map/ppermute | solution.py:762
  83.7 0.6 copy-done.18
  84.3 1.6 offer.1
  85.8 19.8 %all_to_all.10 = f32[64,8,128]{2,1,0:T(8,128)S(1)} all-to-all(f32[64,8,128]{2,1,0:T(8,128)} %bitcast.29), channel_id=1, replica_groups=mesh['comp'=2,'tile'=64] {'tile'}, dimensions={0} | all-to-all | bytes 524288 | tf_op jit(solution)/shard_map/all_to_all | solution.py:766
  105.7 1.7 collective-permute-start.6
  107.4 2.2 copy-done.1
  109.6 2.3 %remap.1 = (f32[32,128]{1,0:T(8,128)S(1)}, f32[16,128]{1,0:T(8,128)S(1)}, f32[16,128]{1,0:T(8,128)S(1)}) custom-call(s32[1]{0:T(128)} %bitcast.me, s32[48]{0:T(128)S(1)} %get-tuple-element.65.ids, s32[48]{0:T(128)S(1)} %get-tuple-element.66.pick, s32[48]{0:T(128)S(1)} %get-tuple-element.67.dest, f32[512,128]{1,0:T(8,128)S(1)} %bitcast.21, ...), custom_call_target="tpu_custom_call" | custom-call | flops 1500000000 | bytes 1048576 | tf_op jit(solution)/shard_map/remap/pallas_call | solution.py:673
  111.9 4.6 %collective-permute-start.8 = (f32[16,128]{1,0:T(8,128)S(1)}, f32[16,128]{1,0:T(8,128)S(1)}, u32[]{:S(2)}, u32[]{:S(2)}) collective-permute-start(f32[16,128]{1,0:T(8,128)S(1)} %get-tuple-element.71), channel_id=1, source_target_pairs={{0,63},{1,2},{2,1},{3,4},{4,3},{5,6},{6,5},{7,8},{8,7},{9,10},{10,... | collective-permute-start | bytes 24584 | tf_op jit(solution)/shard_map/ppermute | solution.py:756
  116.5 0.0 collective-permute-start.9
  116.5 3.1 %collective-permute-done.8.so = f32[16,128]{1,0:T(8,128)S(1)} collective-permute-done((f32[16,128]{1,0:T(8,128)S(1)}, f32[16,128]{1,0:T(8,128)S(1)}, u32[]{:S(2)}, u32[]{:S(2)}) %collective-permute-start.8) | collective-permute-done | bytes 8224 | tf_op jit(solution)/shard_map/ppermute | solution.py:756
  119.6 0.0 copy-start.2
  119.7 21.2 %middle_block.1 = (f32[8,512,128]{2,1,0:T(8,128)S(1)}, f32[8,512,128]{2,1,0:T(8,128)}, f32[3,512,128]{2,1,0:T(8,128)}, f32[1,512,128]{2,1,0:T(8,128)}, f32[4,512...) custom-call(s32[1]{0:T(128)} %bitcast.me, ...), custom_call_target="tpu_custom_call" | custom-call | flops 15000000512 | bytes 1048576 | tf_op jit(solution)/shard_map/middle_block/pallas_call | solution.py:540
  140.8 0.0 copy-start.13
  140.9 4.6 %collective-permute-start.10 = (f32[16,128]{1,0:T(8,128)S(1)}, f32[16,128]{1,0:T(8,128)S(1)}, u32[]{:S(2)}, u32[]{:S(2)}) collective-permute-start(f32[16,128]{1,0:T(8,128)S(1)} %get-tuple-element.79), channel_id=1, source_target_pairs={{0,63},{1,2},{2,1},{3,4},{4,3},{5,6},{6,5},{7,8},{8,7},{9,10},{10,... | collective-permute-start | bytes 24584 | tf_op jit(solution)/shard_map/ppermute | solution.py:756
  145.4 3.1 %collective-permute-done.10.so = f32[16,128]{1,0:T(8,128)S(1)} collective-permute-done((f32[16,128]{1,0:T(8,128)S(1)}, f32[16,128]{1,0:T(8,128)S(1)}, u32[]{:S(2)}, u32[]{:S(2)}) %collective-permute-start.10) | collective-permute-done | bytes 8224 | tf_op jit(solution)/shard_map/ppermute | solution.py:756
  148.5 4.5 %collective-permute-start.12 = (f32[3,512,128]{2,1,0:T(8,128)}, f32[3,512,128]{2,1,0:T(8,128)}, u32[]{:S(2)}, u32[]{:S(2)}) collective-permute-start(f32[3,512,128]{2,1,0:T(8,128)} %get-tuple-element.81), channel_id=1, source_target_pairs={{0,63},{1,2},{2,1},{3,4},{4,3},{5,6},{6,5},{7,8},{8,7},{9,10},{10,... | collective-permute-start | bytes 2359304 | tf_op jit(solution)/shard_map/ppermute | solution.py:756
  153.0 2.0 remap_back.1
  155.0 23.8 %all_to_all.11 = f32[64,8,128]{2,1,0:T(8,128)} all-to-all(f32[64,8,128]{2,1,0:T(8,128)S(1)} %bitcast.22), channel_id=1, replica_groups=mesh['comp'=2,'tile'=64] {'tile'}, dimensions={0} | all-to-all | bytes 524288 | tf_op jit(solution)/shard_map/all_to_all | solution.py:766
  178.9 2.2 collect.1
  181.1 4.9 %collective-permute-done.15.s = f32[32,128]{1,0:T(8,128)S(1)} collective-permute-done((f32[32,128]{1,0:T(8,128)}, f32[32,128]{1,0:T(8,128)S(1)}, u32[]{:S(2)}, u32[]{:S(2)}) %collective-permute-start.15) | collective-permute-done | bytes 16416 | tf_op jit(solution)/shard_map/ppermute | solution.py:762
  186.0 3.7 %collective-permute-done.13.r1 = f32[1,512,128]{2,1,0:T(8,128)S(1)} collective-permute-done((f32[1,512,128]{2,1,0:T(8,128)}, f32[1,512,128]{2,1,0:T(8,128)S(1)}, u32[]{:S(2)}, u32[]{:S(2)}) %collective-permute-start.13) | collective-permute-done | bytes 262176 | tf_op jit(solution)/shard_map/ppermute | solution.py:756
  189.7 1.1 copy-done.9
  190.8 12.2 %last_block.1 = (f32[8,512,128]{2,1,0:T(8,128)S(1)}, f32[4,512,128]{2,1,0:T(8,128)S(1)}, f32[4,512,128]{2,1,0:T(8,128)S(1)}) custom-call(s32[1]{0:T(128)} %bitcast.me, f32[8,512,128]{2,1,0:T(8,128)} %get-tuple-element.76.adj, f32[3,512,128]{2,1,0:T(8,128)} %collective-permute-done.12.r0, f32[1,512,128]{2,1,0:T(8,128)S(1)} %collective-permute-done.13.r1, ...), custom_call_target="tpu_custom_call" | custom-call | flops 7500000256 | bytes 1048576 | tf_op jit(solution)/shard_map/last_block/pallas_call | solution.py:616
  203.1 2.1 collective-permute-start.16
  205.2 2.3 %to_raw.1 = f32[1024,512]{1,0:T(8,128)} custom-call(f32[8,512,128]{2,1,0:T(8,128)S(1)} %copy-done.14), custom_call_target="tpu_custom_call" | custom-call | flops 2000000000 | bytes 1048576 | tf_op jit(solution)/shard_map/to_raw/pallas_call | solution.py:159
  207.5 20.0 %collective-permute-done.16.outer = f32[4,512,128]{2,1,0:T(8,128)S(1)} collective-permute-done((f32[4,512,128]{2,1,0:T(8,128)S(1)}, f32[4,512,128]{2,1,0:T(8,128)S(1)}, u32[]{:S(2)}, u32[]{:S(2)}) %collective-permute-start.16) | collective-permute-done | bytes 1048608 | tf_op jit(solution)/shard_map/ppermute | solution.py:756
  227.6 2.1 grad_out.1
  (51 shorter events, 0.1 us)
Async XLA Ops:
  0.6 14.3 %copy-start = (s32[2,64,64]{2,1,0:T(8,128)S(1)}, s32[2,64,64]{2,1,0:T(8,128)}, u32[]{:S(2)}) copy-start(s32[2,64,64]{2,1,0:T(8,128)} %param.16) | copy-start | bytes 98308
  0.7 1.6 copy-start.3
  2.3 7.9 %copy-start.19 = (s32[8,512]{1,0:T(8,128)S(1)}, s32[8,512]{1,0:T(8,128)}, u32[]{:S(2)}) copy-start(s32[8,512]{1,0:T(8,128)} %param.14) | copy-start | bytes 49156
  2.3 7.9 %copy-start.4 = (f32[1,128,8,512]{3,2,1,0:T(8,128)S(1)}, f32[1,128,8,512]{3,2,1,0:T(8,128)}, u32[]{:S(2)}) copy-start(f32[1,128,8,512]{3,2,1,0:T(8,128)} %param.12) | copy-start | bytes 6291460
  4.3 47.4 %collective-permute-start = (f32[4,512,128]{2,1,0:T(8,128)S(1)}, f32[4,512,128]{2,1,0:T(8,128)}, u32[]{:S(2)}, u32[]{:S(2)}) collective-permute-start(f32[4,512,128]{2,1,0:T(8,128)S(1)} %get-tuple-element.47.so), channel_id=1, source_target_pairs={{0,63},{1,2},{2,1},{3,4},{4,3},{5,6},{6,5},{7,8},{8,7},{9,10},{10,... | collective-permute-start | bytes 3145736 | tf_op jit(solution)/shard_map/ppermute | solution.py:756
  10.2 41.5 %collective-permute-start.1 = (f32[4,512,128]{2,1,0:T(8,128)}, f32[4,512,128]{2,1,0:T(8,128)}, u32[]{:S(2)}, u32[]{:S(2)}) collective-permute-start(f32[4,512,128]{2,1,0:T(8,128)} %get-tuple-element.48.si), channel_id=1, source_target_pairs={{0,1},{1,0},{2,3},{3,2},{4,5},{5,4},{6,7},{7,6},{8,9},{9,8},{10,11... | collective-permute-start | bytes 3145736 | tf_op jit(solution)/shard_map/ppermute | solution.py:759
  10.2 4.3 %copy-start.20 = (s32[2,64,8]{1,2,0:T(8,128)S(1)}, s32[2,64,8]{1,2,0:T(8,128)}, u32[]{:S(2)}) copy-start(s32[2,64,8]{1,2,0:T(8,128)} %param.15) | copy-start | bytes 12292
  10.2 4.6 %copy-start.21 = (s32[1,1,8]{2,1,0:T(1,128)S(1)}, s32[1,1,8]{2,1,0:T(1,128)}, u32[]{:S(2)}) copy-start(s32[1,1,8]{2,1,0:T(1,128)} %param.18) | copy-start | bytes 100
  10.2 7.3 %copy-start.22 = (s32[1,1,64]{2,1,0:T(1,128)S(1)}, s32[1,1,64]{2,1,0:T(1,128)}, u32[]{:S(2)}) copy-start(s32[1,1,64]{2,1,0:T(1,128)} %param.17) | copy-start | bytes 772
  12.3 1.3 copy-start.16
  13.7 37.1 %collective-permute-start.2 = (f32[3,512,128]{2,1,0:T(8,128)}, f32[3,512,128]{2,1,0:T(8,128)S(1)}, u32[]{:S(2)}, u32[]{:S(2)}) collective-permute-start(f32[3,512,128]{2,1,0:T(8,128)} %get-tuple-element.49), channel_id=1, source_target_pairs={{0,63},{1,2},{2,1},{3,4},{4,3},{5,6},{6,5},{7,8},{8,7},{9,10},{10,... | collective-permute-start | bytes 2359304 | tf_op jit(solution)/shard_map/ppermute | solution.py:756
  14.4 36.3 %collective-permute-start.3 = (f32[3,512,128]{2,1,0:T(8,128)}, f32[3,512,128]{2,1,0:T(8,128)S(1)}, u32[]{:S(2)}, u32[]{:S(2)}) collective-permute-start(f32[3,512,128]{2,1,0:T(8,128)} %get-tuple-element.50), channel_id=1, source_target_pairs={{0,1},{1,0},{2,3},{3,2},{4,5},{5,4},{6,7},{7,6},{8,9},{9,8},{10,11... | collective-permute-start | bytes 2359304 | tf_op jit(solution)/shard_map/ppermute | solution.py:759
  17.8 1.6 copy-start.5
  19.4 32.3 %copy-start.11 = (bf16[256,256]{1,0:T(8,128)(2,1)S(1)}, bf16[256,256]{1,0:T(8,128)(2,1)}, u32[]{:S(2)}) copy-start(bf16[256,256]{1,0:T(8,128)(2,1)} %get-tuple-element.58.w2.w2f) | copy-start | bytes 393220
  19.4 32.3 %copy-start.17 = (f32[8,512,128]{2,1,0:T(8,128)S(1)}, f32[8,512,128]{2,1,0:T(8,128)}, u32[]{:S(2)}) copy-start(f32[8,512,128]{2,1,0:T(8,128)} %copy-done.16) | copy-start | bytes 6291460
  20.7 1.3 copy-start.15
  50.7 0.9 copy-start.6
  51.6 1.1 copy-start.7
  63.3 56.3 %collective-permute-start.7 = (f32[4,512,128]{2,1,0:T(8,128)S(1)}, f32[4,512,128]{2,1,0:T(8,128)}, u32[]{:S(2)}, u32[]{:S(2)}) collective-permute-start(f32[4,512,128]{2,1,0:T(8,128)S(1)} %get-tuple-element.61.v2), channel_id=1, source_target_pairs={{0,1},{1,0},{2,3},{3,2},{4,5},{5,4},{6,7},{7,6},{8,9},{9,8},{10,11... | collective-permute-start | bytes 3145736 | tf_op jit(solution)/shard_map/ppermute | solution.py:759
  63.4 56.2 %collective-permute-start.4 = (f32[3,512,128]{2,1,0:T(8,128)}, f32[3,512,128]{2,1,0:T(8,128)}, u32[]{:S(2)}, u32[]{:S(2)}) collective-permute-start(f32[3,512,128]{2,1,0:T(8,128)} %get-tuple-element.59.v0), channel_id=1, source_target_pairs={{0,63},{1,2},{2,1},{3,4},{4,3},{5,6},{6,5},{7,8},{8,7},{9,10},{10,... | collective-permute-start | bytes 2359304 | tf_op jit(solution)/shard_map/ppermute | solution.py:756
  67.2 16.5 %collective-permute-start.5 = (f32[32,128]{1,0:T(8,128)S(1)}, f32[32,128]{1,0:T(8,128)S(1)}, u32[]{:S(2)}, u32[]{:S(2)}) collective-permute-start(f32[32,128]{1,0:T(8,128)S(1)} %get-tuple-element.63), channel_id=1, source_target_pairs={{0,64},{64,0},{1,65},{65,1},{2,66},{66,2},{3,67},{67,3},{4,68},{68... | collective-permute-start | bytes 49160 | tf_op jit(solution)/shard_map/ppermute | solution.py:762
  83.7 0.6 copy-start.18
  105.7 13.9 %collective-permute-start.6 = (f32[1,512,128]{2,1,0:T(8,128)S(1)}, f32[1,512,128]{2,1,0:T(8,128)S(1)}, u32[]{:S(2)}, u32[]{:S(2)}) collective-permute-start(f32[1,512,128]{2,1,0:T(8,128)S(1)} %get-tuple-element.64.v1), channel_id=1, source_target_pairs={{0,63},{1,2},{2,1},{3,4},{4,3},{5,6},{6,5},{7,8},{8,7},{9,10},{10,... | collective-permute-start | bytes 786440 | tf_op jit(solution)/shard_map/ppermute | solution.py:756
  107.4 2.2 copy-start.1
  109.6 10.0 %copy-start.8 = (f32[3,512,128]{2,1,0:T(8,128)S(1)}, f32[3,512,128]{2,1,0:T(8,128)}, u32[]{:S(2)}) copy-start(f32[3,512,128]{2,1,0:T(8,128)} %copy-done.6) | copy-start | bytes 2359300
  109.6 10.0 %copy-start.10 = (bf16[256,256]{1,0:T(8,128)(2,1)S(1)}, bf16[256,256]{1,0:T(8,128)(2,1)}, u32[]{:S(2)}) copy-start(bf16[256,256]{1,0:T(8,128)(2,1)} %get-tuple-element.74.w2b) | copy-start | bytes 393220
  109.6 10.1 %copy-start.12 = (bf16[256,256]{1,0:T(8,128)(2,1)S(1)}, bf16[256,256]{1,0:T(8,128)(2,1)}, u32[]{:S(2)}) copy-start(bf16[256,256]{1,0:T(8,128)(2,1)} %get-tuple-element.58.w2.w2f) | copy-start | bytes 393220
  111.9 7.7 %collective-permute-start.8 = (f32[16,128]{1,0:T(8,128)S(1)}, f32[16,128]{1,0:T(8,128)S(1)}, u32[]{:S(2)}, u32[]{:S(2)}) collective-permute-start(f32[16,128]{1,0:T(8,128)S(1)} %get-tuple-element.71), channel_id=1, source_target_pairs={{0,63},{1,2},{2,1},{3,4},{4,3},{5,6},{6,5},{7,8},{8,7},{9,10},{10,... | collective-permute-start | bytes 24584 | tf_op jit(solution)/shard_map/ppermute | solution.py:756
  116.5 3.1 %collective-permute-start.9 = (f32[16,128]{1,0:T(8,128)S(1)}, f32[16,128]{1,0:T(8,128)S(1)}, u32[]{:S(2)}, u32[]{:S(2)}) collective-permute-start(f32[16,128]{1,0:T(8,128)S(1)} %get-tuple-element.72), channel_id=1, source_target_pairs={{0,1},{1,0},{2,3},{3,2},{4,5},{5,4},{6,7},{7,6},{8,9},{9,8},{10,11... | collective-permute-start | bytes 24584 | tf_op jit(solution)/shard_map/ppermute | solution.py:759
  119.6 33.4 %copy-start.2 = (f32[1,64,128,128]{3,2,1,0:T(8,128)S(1)}, f32[1,64,128,128]{3,2,1,0:T(8,128)}, u32[]{:S(2)}) copy-start(f32[1,64,128,128]{3,2,1,0:T(8,128)} %param.19) | copy-start | bytes 12582916
  140.8 14.2 %copy-start.13 = (f32[8,512,128]{2,1,0:T(8,128)}, f32[8,512,128]{2,1,0:T(8,128)S(1)}, u32[]{:S(2)}) copy-start(f32[8,512,128]{2,1,0:T(8,128)S(1)} %get-tuple-element.75.x) | copy-start | bytes 6291460
  140.9 7.7 %collective-permute-start.10 = (f32[16,128]{1,0:T(8,128)S(1)}, f32[16,128]{1,0:T(8,128)S(1)}, u32[]{:S(2)}, u32[]{:S(2)}) collective-permute-start(f32[16,128]{1,0:T(8,128)S(1)} %get-tuple-element.79), channel_id=1, source_target_pairs={{0,63},{1,2},{2,1},{3,4},{4,3},{5,6},{6,5},{7,8},{8,7},{9,10},{10,... | collective-permute-start | bytes 24584 | tf_op jit(solution)/shard_map/ppermute | solution.py:756
  145.4 3.1 %collective-permute-start.11 = (f32[16,128]{1,0:T(8,128)S(1)}, f32[16,128]{1,0:T(8,128)S(1)}, u32[]{:S(2)}, u32[]{:S(2)}) collective-permute-start(f32[16,128]{1,0:T(8,128)S(1)} %get-tuple-element.80), channel_id=1, source_target_pairs={{0,1},{1,0},{2,3},{3,2},{4,5},{5,4},{6,7},{7,6},{8,9},{9,8},{10,11... | collective-permute-start | bytes 24584 | tf_op jit(solution)/shard_map/ppermute | solution.py:759
  148.5 41.2 %collective-permute-start.14 = (f32[4,512,128]{2,1,0:T(8,128)}, f32[4,512,128]{2,1,0:T(8,128)S(1)}, u32[]{:S(2)}, u32[]{:S(2)}) collective-permute-start(f32[4,512,128]{2,1,0:T(8,128)} %get-tuple-element.87), channel_id=1, source_target_pairs={{0,1},{1,0},{2,3},{3,2},{4,5},{5,4},{6,7},{7,6},{8,9},{9,8},{10,11... | collective-permute-start | bytes 3145736 | tf_op jit(solution)/shard_map/ppermute | solution.py:759
  148.5 41.2 %collective-permute-start.12 = (f32[3,512,128]{2,1,0:T(8,128)}, f32[3,512,128]{2,1,0:T(8,128)}, u32[]{:S(2)}, u32[]{:S(2)}) collective-permute-start(f32[3,512,128]{2,1,0:T(8,128)} %get-tuple-element.81), channel_id=1, source_target_pairs={{0,63},{1,2},{2,1},{3,4},{4,3},{5,6},{6,5},{7,8},{8,7},{9,10},{10,... | collective-permute-start | bytes 2359304 | tf_op jit(solution)/shard_map/ppermute | solution.py:756
  178.9 10.8 %collective-permute-start.13 = (f32[1,512,128]{2,1,0:T(8,128)}, f32[1,512,128]{2,1,0:T(8,128)S(1)}, u32[]{:S(2)}, u32[]{:S(2)}) collective-permute-start(f32[1,512,128]{2,1,0:T(8,128)} %get-tuple-element.86), channel_id=1, source_target_pairs={{0,63},{1,2},{2,1},{3,4},{4,3},{5,6},{6,5},{7,8},{8,7},{9,10},{10,... | collective-permute-start | bytes 786440 | tf_op jit(solution)/shard_map/ppermute | solution.py:756
  181.1 4.9 %collective-permute-start.15 = (f32[32,128]{1,0:T(8,128)}, f32[32,128]{1,0:T(8,128)S(1)}, u32[]{:S(2)}, u32[]{:S(2)}) collective-permute-start(f32[32,128]{1,0:T(8,128)} %collect.1), channel_id=1, source_target_pairs={{0,64},{64,0},{1,65},{65,1},{2,66},{66,2},{3,67},{67,3},{4,68},{68... | collective-permute-start | bytes 49160 | tf_op jit(solution)/shard_map/ppermute | solution.py:762
  189.7 1.1 copy-start.9
  190.8 14.4 %copy-start.14 = (f32[8,512,128]{2,1,0:T(8,128)S(1)}, f32[8,512,128]{2,1,0:T(8,128)}, u32[]{:S(2)}) copy-start(f32[8,512,128]{2,1,0:T(8,128)} %copy-done.13) | copy-start | bytes 6291460
  203.1 24.5 %collective-permute-start.16 = (f32[4,512,128]{2,1,0:T(8,128)S(1)}, f32[4,512,128]{2,1,0:T(8,128)S(1)}, u32[]{:S(2)}, u32[]{:S(2)}) collective-permute-start(f32[4,512,128]{2,1,0:T(8,128)S(1)} %get-tuple-element.90), channel_id=1, source_target_pairs={{0,63},{1,2},{2,1},{3,4},{4,3},{5,6},{6,5},{7,8},{8,7},{9,10},{10,... | collective-permute-start | bytes 3145736 | tf_op jit(solution)/shard_map/ppermute | solution.py:756
  205.2 22.4 %collective-permute-start.17 = (f32[4,512,128]{2,1,0:T(8,128)S(1)}, f32[4,512,128]{2,1,0:T(8,128)S(1)}, u32[]{:S(2)}, u32[]{:S(2)}) collective-permute-start(f32[4,512,128]{2,1,0:T(8,128)S(1)} %get-tuple-element.91), channel_id=1, source_target_pairs={{0,1},{1,0},{2,3},{3,2},{4,5},{5,4},{6,7},{7,6},{8,9},{9,8},{10,11... | collective-permute-start | bytes 3145736 | tf_op jit(solution)/shard_map/ppermute | solution.py:759

commit v4 on v3

--- a/solution.py
+++ b/solution.py
@@ -65,7 +65,7 @@
     return buf[j, pl.ds(r, 128, stride=8), :].T
 
 
-def start_in_kernel(me, x, outer, inner, buf, out, sems, osems):
+def start_in_kernel(me, x, outer, inner, full, buf, out, sems, osems):
     odd = parity(me)
     c = start_raw(x, buf, sems)
     todo = []
@@ -73,8 +73,8 @@
         c[j].wait()
         for r in range(8):
             out[r, pl.ds(128 * j, 128), :] = turned(buf, j, r)
-        for i, (r0, dst) in enumerate(((4 * odd, outer), (4 - 4 * odd, inner))):
-            src = out.at[pl.ds(r0, 4), pl.ds(128 * j, 128), :]
+        for i, (r0, n, dst) in enumerate(((7 * odd, 1, outer), (7 - 7 * odd, 1, inner), (0, 8, full))):
+            src = out.at[pl.ds(r0, n), pl.ds(128 * j, 128), :]
             todo.append(pltpu.make_async_copy(src, lon_part(dst, j), osems.at[i, j]))
             todo[-1].start()
     for d in todo:
@@ -84,17 +84,17 @@
 def start_in(me, x):
     return pl.pallas_call(
         start_in_kernel,
-        out_shape=(sds(4, LON, LEV), sds(4, LON, LEV)),
+        out_shape=(sds(1, LON, LEV), sds(1, LON, LEV), sds(8, LON, LEV)),
         in_specs=[SM, ANY],
-        out_specs=(ANY, ANY),
-        scratch_shapes=[RAW, ROWS, dma_sems(4), dma_sems(2, 4)],
-        compiler_params=params(),
+        out_specs=(ANY,) * 3,
+        scratch_shapes=[RAW, ROWS, dma_sems(4), dma_sems(3, 4)],
+        compiler_params=params(60),
         cost_estimate=cost(4),
         name="start_in",
     )(me, x)
 
 
-def diff_in_kernel(me, x, sea, outer, inner, full, buf, out, sems, osems):
+def diff_in_kernel(me, x, sea, outer, third, inner, full, buf, out, sems, osems):
     odd = parity(me)
     c = start_raw(x, buf, sems)
     todo = []
@@ -103,7 +103,7 @@
         at = pl.ds(128 * j, 128)
         for r in range(8):
             out[r, at, :] = (buf[j, pl.ds(r, 128, stride=8), :] * sea[r : r + 1, at]).T
-        for i, (r0, n, dst) in enumerate(((5 * odd, 3, outer), (5 - 5 * odd, 3, inner), (0, 8, full))):
+        for i, (r0, n, dst) in enumerate(((6 * odd, 2, outer), (2 + 3 * odd, 1, third), (5 - 5 * odd, 3, inner), (0, 8, full))):
             src = out.at[pl.ds(r0, n), at, :]
             todo.append(pltpu.make_async_copy(src, lon_part(dst, j), osems.at[i, j]))
             todo[-1].start()
@@ -114,11 +114,11 @@
 def diff_in(me, x, sea):
     return pl.pallas_call(
         diff_in_kernel,
-        out_shape=(sds(3, LON, LEV), sds(3, LON, LEV), sds(8, LON, LEV)),
+        out_shape=(sds(2, LON, LEV), sds(1, LON, LEV), sds(3, LON, LEV), sds(8, LON, LEV)),
         in_specs=[SM, ANY, VM],
-        out_specs=(ANY,) * 3,
-        scratch_shapes=[RAW, ROWS, dma_sems(4), dma_sems(3, 4)],
-        compiler_params=params(),
+        out_specs=(ANY,) * 4,
+        scratch_shapes=[RAW, ROWS, dma_sems(4), dma_sems(4, 4)],
+        compiler_params=params(60),
         cost_estimate=cost(4),
         name="diff_in",
     )(me, x, sea)
@@ -395,50 +395,93 @@
     return cut(v, outer, 3), cut(v, outer + 3, 1), cut(v, inner, 4)
 
 
-def first_kernel(me, so, si, ho, hi, dt, do, di, w2, o0, o1, o2, o_surf, va, vb, h, d, sems):
+def diffusion_copies(d, odd, dt, do, dx, di):
+    return [
+        (dt, d.at[pl.ds(5, 8)]),
+        (do, d.at[pl.ds(3 + 10 * odd, 2)]),
+        (di, d.at[pl.ds(13 - 11 * odd, 3)]),
+    ] + ([] if dx is None else [(dx, d.at[pl.ds(2 + 13 * odd, 1)])])
+
+
+def prepare_rows(va, h, r0, n, d=None):
+    def cp(i, carry):
+        r = r0 + i
+        for j in range(4):
+            x = va[r, pl.ds(OFF + 128 * j, 128), :]
+            if j == 0:
+                va[r, pl.ds(OFF + LON, 1), :] = x[0:1]
+            if j == 3:
+                va[r, pl.ds(OFF - 1, 1), :] = x[127:128]
+            if d is not None:
+                x = jnp.where(d[r, pl.ds(128 * j, 128), :] > 0.0, x, 0.0)
+            put_halves(h, r, j, x)
+        return carry
+
+    lax.fori_loop(0, n, cp, 0)
+
+
+def first_step_kernel(me, own, eo, ei, dt, w2, o_outer, o_inner, o_own, va, vb, h, d, sems):
     odd = parity(me)
-    own_o, own_i = near_far(5, 9, odd)
-    far_o, far_i = near_far(1, 13, odd)
-    d_o, d_i = near_far(2, 13, odd)
     c = copies(
         sems,
         [
             (dt, d.at[pl.ds(5, 8)]),
-            (so, tile_rows(va, own_o, 4)),
-            (si, tile_rows(va, own_i, 4)),
-            (do, d.at[pl.ds(d_o, 3)]),
-            (ho, tile_rows(va, far_o, 4)),
-            (di, d.at[pl.ds(d_i, 3)]),
-            (hi, tile_rows(va, far_i, 4)),
+            (own, tile_rows(va, 5, 8)),
+            (eo, tile_rows(va, 4 + 9 * odd, 1)),
+            (ei, tile_rows(va, 13 - 9 * odd, 1)),
         ],
     )
-
-    def prepare(r0, n):
-        def cp(i, carry):
-            r = r0 + i
-            for j in range(4):
-                x = va[r, pl.ds(OFF + 128 * j, 128), :]
-                if j == 0:
-                    va[r, pl.ds(OFF + LON, 1), :] = x[0:1]
-                if j == 3:
-                    va[r, pl.ds(OFF - 1, 1), :] = x[127:128]
-                keep = d[r, pl.ds(128 * j, 128), :] > 0.0
-                put_halves(h, r, j, jnp.where(keep, x, 0.0))
-            return carry
-
-        lax.fori_loop(0, n, cp, 0)
-
-    wait(c[0], c[1])
-    prepare(own_o, 4)
-    wait(c[2])
-    prepare(own_i, 4)
-    wait(*c[3:])
-    clear_ends(me, ((va, 1, 4), (d, 2, 3)), ((va, 13, 4), (d, 13, 3)))
-    prepare(2, 3)
-    prepare(13, 3)
-    forward_block(va, vb, h, d, w2, first=True)
-    c = copies(sems, list(zip(edge_refs(va, 5, 9, odd, tile_rows), (o0, o1, o2))))
-    o_surf[...] = gather_surface(lambda r, j: va[r + 5, pl.ds(OFF + 128 * j, 128), :], 8)[0:32]
+    wait(*c[0:2])
+    prepare_rows(va, h, 5, 8, d)
+    wait(*c[2:4])
+    clear_ends(me, ((va, 4, 1),), ((va, 13, 1),))
+    forward_step(va, vb, h, d, w2, 4, first=True, last=True)
+    c = copies(
+        sems,
+        [
+            (tile_rows(vb, 5 + 5 * odd, 3), o_outer),
+            (tile_rows(vb, 10 - 5 * odd, 3), o_inner),
+            (tile_rows(vb, 5, 8), o_own),
+        ],
+    )
+    wait(*c)
+
+
+def first_step(*args):
+    return pl.pallas_call(
+        first_step_kernel,
+        out_shape=(sds(3, LON, LEV), sds(3, LON, LEV), sds(8, LON, LEV)),
+        in_specs=[SM] + [ANY] * 4 + [VM],
+        out_specs=(ANY,) * 3,
+        scratch_shapes=BLOCK_SCRATCH + [dma_sems(4)],
+        compiler_params=params(60),
+        cost_estimate=cost(4),
+        name="first_step",
+    )(*args)
+
+
+def first_kernel(me, own, ho, hi, dt, do, di, w2, o0, o1, o2, o_surf, va, vb, h, d, sems):
+    odd = parity(me)
+    c = copies(
+        sems,
+        [
+            (own, tile_rows(va, 5, 8)),
+            (ho, tile_rows(va, 2 + 11 * odd, 3)),
+            (hi, tile_rows(va, 13 - 11 * odd, 3)),
+        ]
+        + diffusion_copies(d, odd, dt, do, None, di),
+    )
+    wait(c[0])
+    prepare_rows(va, h, 5, 8)
+    wait(*c[1:])
+    clear_ends(me, ((va, 2, 3), (d, 2, 3)), ((va, 13, 3), (d, 13, 3)))
+    prepare_rows(va, h, 3, 2)
+    prepare_rows(va, h, 13, 2)
+    forward_step(va, vb, h, d, w2, 2)
+    forward_step(vb, va, h, d, w2, 3)
+    forward_step(va, vb, h, d, w2, 4, last=True)
+    c = copies(sems, list(zip(edge_refs(vb, 5, 9, odd, tile_rows), (o0, o1, o2))))
+    o_surf[...] = gather_surface(lambda r, j: vb[r + 5, pl.ds(OFF + 128 * j, 128), :], 8)[0:32]
     wait(*c)
 
 
@@ -446,23 +489,22 @@
     return pl.pallas_call(
         first_kernel,
         out_shape=PARTS + (sds(32, 128),),
-        in_specs=[SM] + [ANY] * 7 + [VM],
+        in_specs=[SM] + [ANY] * 6 + [VM],
         out_specs=(ANY,) * 3 + (VM,),
-        scratch_shapes=BLOCK_SCRATCH + [dma_sems(7)],
+        scratch_shapes=BLOCK_SCRATCH + [dma_sems(6)],
         compiler_params=params(),
-        cost_estimate=cost(15),
+        cost_estimate=cost(10),
         name="first_block",
     )(*args)
 
 
 def middle_kernel(
-    me, v0, v1, v2, h0, h1, h2, s, so, si, dt, do, di, m, w2f, w2b,
+    me, v0, v1, v2, h0, h1, h2, s, so, si, dt, do, dx, di, m, w2f, w2b,
     o_final, o_adj, o0, o1, o2, o_s, o_so, o_si, va, vb, h, d, u, mm, cols, sems,
 ):
     odd = parity(me)
     own = edge_refs(va, 5, 9, odd, tile_rows)
     far = edge_refs(va, 1, 13, odd, tile_rows)
-    d_o, d_i = near_far(2, 13, odd)
     c = copies(
         sems,
         [
@@ -472,11 +514,9 @@
             (h0, far[0]),
             (h1, far[1]),
             (h2, far[2]),
-            (dt, d.at[pl.ds(5, 8)]),
-            (do, d.at[pl.ds(d_o, 3)]),
-            (di, d.at[pl.ds(d_i, 3)]),
-            (m, mm),
-        ],
+        ]
+        + diffusion_copies(d, odd, dt, do, dx, di)
+        + [(m, mm)],
     )
     c_o, c_i = near_far(0, 48, odd)
     cols[pl.ds(pl.multiple_of(c_o, 16), 16)] = so[...]
@@ -501,13 +541,13 @@
     wait(*c[0:3])
     prepare(5)
     prepare(9)
-    wait(*c[3:9])
+    wait(*c[3:10])
     clear_ends(me, ((va, 1, 4), (d, 2, 3)), ((va, 13, 4), (d, 13, 3)))
     prepare(1)
     prepare(13)
     forward_block(va, vb, h, d, w2f)
     out = copies(sems, [(tile_rows(va, 5, 8), o_final)])
-    wait(c[9])
+    wait(c[10])
 
     def body(i, carry):
         r = 5 + i
@@ -543,7 +583,7 @@
             sds(8, LON, LEV), sds(8, LON, LEV), *PARTS,
             sds(32, 128), sds(16, 128), sds(16, 128),
         ),
-        in_specs=[SM] + [ANY] * 6 + [VM] * 3 + [ANY] * 4 + [VM] * 2,
+        in_specs=[SM] + [ANY] * 6 + [VM] * 3 + [ANY] * 5 + [VM] * 2,
         out_specs=(ANY,) * 5 + (VM,) * 3,
         scratch_shapes=BLOCK_SCRATCH
         + [U_SCRATCH, pltpu.VMEM((8, LON, 128), F32), COLS, dma_sems(12)],
@@ -554,26 +594,21 @@
 
 
 def last_kernel(
-    me, adj, r0, r1, r2, s, so, si, dt, do, di, w2b, o_base, o_outer, o_inner,
+    me, adj, r0, r1, r2, s, own, dt, do, dx, di, w2b, o_base, o_outer, o_inner,
     va, vb, h, d, u, got, base, cols, sems,
 ):
     odd = parity(me)
-    e_o, e_i = near_far(0, 4, odd)
-    d_o, d_i = near_far(2, 13, odd)
     parts = edge_refs(got, 0, 4, odd, plain_rows)
     c = copies(
         sems,
         [
             (adj, u.at[pl.ds(5, 8)]),
-            (dt, d.at[pl.ds(5, 8)]),
             (r0, parts[0]),
             (r1, parts[1]),
             (r2, parts[2]),
-            (do, d.at[pl.ds(d_o, 3)]),
-            (di, d.at[pl.ds(d_i, 3)]),
-            (so, base.at[pl.ds(e_o, 4)]),
-            (si, base.at[pl.ds(e_i, 4)]),
-        ],
+        ]
+        + diffusion_copies(d, odd, dt, do, dx, di)
+        + [(own, base)],
     )
     cols[0:32] = s[...]
     cols[32:128] = jnp.zeros((96, 128), F32)
@@ -749,7 +784,7 @@
 ):
     component = lax.axis_index("comp")
     own_tile = lax.axis_index("tile")
-    across = [(i, (i + 1 if i % 2 else i - 1) % 64) for i in range(64)]
+    across = [(i, min(max(i + 1 if i % 2 else i - 1, 0), 63)) for i in range(64)]
     on_chip = [(i, i ^ 1) for i in range(64)]
 
     def far(x):
@@ -767,13 +802,16 @@
         return x.reshape(512, 128)
 
     me = own_tile.reshape(1)
-    so, si = start_in(me, starting_perturbation.reshape(1024, LON))
-    ho, hi = far(so), near(si)
+    e_o, e_i, start = start_in(me, starting_perturbation.reshape(1024, LON))
+    eo, ei = far(e_o), near(e_i)
     sea = jnp.where(component == 1, ocean_mask.astype(F32), 1.0)
     sea32 = sea.reshape(32, 128)
-    d_o, d_i, dt = diff_in(me, diffusion.reshape(1024, LON), sea)
+    d_o, d_x, d_i, dt = diff_in(me, diffusion.reshape(1024, LON), sea)
     do, di = far(d_o), near(d_i)
     w2f, w2b = mixes(vert_mix[0])
+    s_o, s_i, one = first_step(me, start, eo, ei, dt, w2f)
+    ho, hi = far(s_o), near(s_i)
+    dx = far(d_x)
 
     slots = jnp.arange(64, dtype=jnp.int32)
     live = slots % 8 < jnp.repeat(pair_blocks[0, 0], 8)
@@ -788,13 +826,13 @@
     send_rows = jnp.sum(hits[:, :, None] * sources, axis=1).reshape(512)
     weights = remap_weight[0]
     measured = to_rows(measured_discrepancy.reshape(1024, LON))
-    ho, hi, do, di, w2f, w2b, ids, pick, dest, send_rows, measured, sea32 = (
+    ho, hi, do, di, w2b, ids, pick, dest, send_rows, measured, sea32 = (
         lax.optimization_barrier(
-            (ho, hi, do, di, w2f, w2b, ids, pick, dest, send_rows, measured, sea32)
+            (ho, hi, do, di, w2b, ids, pick, dest, send_rows, measured, sea32)
         )
     )
 
-    v0, v1, v2, surf = first_block(me, so, si, ho, hi, dt, do, di, w2f)
+    v0, v1, v2, surf = first_block(me, one, ho, hi, dt, do, di, w2f)
     other = swap(surf)
     h0, h2 = far(v0), near(v2)
     offered = offer(me, send_rows, other)
@@ -804,7 +842,7 @@
     fix, fix_o, fix_i = remap(me, ids, pick, dest, arrived, weights, sea32)
     fo, fi = far(fix_o), near(fix_i)
     final, adj, a0, a1, a2, s0, s0_o, s0_i = middle_block(
-        me, v0, v1, v2, h0, h1, h2, fix, fo, fi, dt, do, di, measured, w2f, w2b
+        me, v0, v1, v2, h0, h1, h2, fix, fo, fi, dt, do, dx, di, measured, w2f, w2b
     )
     ro, ri = far(s0_o), near(s0_i)
     a0, a2, ro, ri = lax.optimization_barrier((a0, a2, ro, ri))
@@ -814,7 +852,7 @@
     a1, back = lax.optimization_barrier((a1, back))
     r1 = far(a1)
     back = swap(collect(me, send_rows, back))
-    base, g_o, g_i = last_block(me, adj, r0, r1, r2, back, so, si, dt, do, di, w2b)
+    base, g_o, g_i = last_block(me, adj, r0, r1, r2, back, start, dt, do, dx, di, w2b)
     go, gi = far(g_o), near(g_i)
     final_raw = to_raw(final)
     gradient = grad_out(me, base, go, gi)

time: 233 us -> 245 us (1.052)
  starting transfers between devices: 28.6 us -> 68 us
  blocking collectives: 43.7 us -> 19.3 us
  waiting for transfers between devices: 79.5 us -> 72 us
  Pallas kernels: 63.4 us -> 69.5 us
    ppermute x9 -> x11, starting transfers between devices: 28 us -> 58 us  [far(): return lax.ppermute(x, 'tile', across)]
    all_to_all x2 -> x1, blocking collectives: 43.7 us -> 19.3 us  [exchange(): x = lax.all_to_all(x, 'tile', split_axis=0, concat_axis=0, tiled=True)]
    ppermute x9 -> x11, waiting for transfers between devices: 58.6 us -> 48 us  [far(): return lax.ppermute(x, 'tile', across)]
    pallas_call x2 -> x3, Pallas kernels: 4.09 us -> 13.5 us  [the longest x1 6.62 us: first_step(): pl.pallas_call(first_step_kernel, out_shape=(sds(3, LON, LEV), sds(3, LON...]
    all_to_all x0 -> x1, starting transfers between devices: none -> 8.74 us  [exchange(): x = lax.all_to_all(x, 'tile', split_axis=0, concat_axis=0, tiled=True)]
    all_to_all x0 -> x1, waiting for transfers between devices: none -> 3.68 us  [exchange(): x = lax.all_to_all(x, 'tile', split_axis=0, concat_axis=0, tiled=True)]
    pallas_call x1, Pallas kernels: 10.5 us -> 7.47 us  [first_block(): pl.pallas_call(first_kernel, out_shape=PARTS + (sds(32, 128),), in_specs=...]
    unnamed x47 -> x65, local copies, waits for them, and re-layouts: 11.9 us -> 11.2 us
  transfers between devices with their start and end apart: 18 -> 22, of which waited for: 7 -> 8; matrix products, arithmetic and copies ran while one was open for 1% -> 1% of each run, Pallas kernels for 7% -> 10%
where the time goes in v4:
time: 245 us; the launch traced here: 244 us
  waiting for transfers between devices  72 us (29%)
  Pallas kernels  69.5 us (28%)
  starting transfers between devices  68 us (28%)
  blocking collectives  19.3 us (8%)
  local copies, waits for them, and re-layouts  12.3 us (5%)
    ppermute x11, starting transfers between devices, far(): return lax.ppermute(x, 'tile', across)  58 us
    ppermute x11, waiting for transfers between devices, far(): return lax.ppermute(x, 'tile', across)  48 us
    pallas_call x1, Pallas kernels, middle_block(): pl.pallas_call(middle_kernel, out_shape=(sds(8, LON, LEV), sds(8, LON, LE...  21.3 us
    ppermute x2, waiting for transfers between devices, swap(): return lax.ppermute(x, 'comp', [(0, 1), (1, 0)])  20.2 us
    all_to_all x1, blocking collectives, exchange(): x = lax.all_to_all(x, 'tile', split_axis=0, concat_axis=0, tiled=True)  19.3 us
    pallas_call x1, Pallas kernels, last_block(): pl.pallas_call(last_kernel, out_shape=(sds(8, LON, LEV), sds(4, LON, LEV)...  11.7 us
    unnamed x65, local copies, waits for them, and re-layouts  11.2 us
    all_to_all x1, starting transfers between devices, exchange(): x = lax.all_to_all(x, 'tile', split_axis=0, concat_axis=0, tiled=True)  8.74 us
  transfers between devices with their start and end apart: 22, of which 8 were waited for; matrix products, arithmetic and copies ran while one was open for 1% of the time, Pallas kernels for 10%

profile of v4, /device:TPU:8, one launch (start us, length us, event | category | flops | bytes accessed | tf_op | source)
XLA Modules:
  0.0 243.5 jit_solution(7464615786474060895)
XLA Ops:
  0.7 2.9 %start_in.1 = (f32[1,512,128]{2,1,0:T(8,128)}, f32[1,512,128]{2,1,0:T(8,128)}, f32[8,512,128]{2,1,0:T(8,128)}) custom-call(s32[1]{0:T(128)} %bitcast.me, f32[1024,512]{1,0:T(8,128)} %bitcast.32), custom_call_target="tpu_custom_call" | custom-call | flops 2000000000 | bytes 1048576 | tf_op jit(solution)/shard_map/start_in/pallas_call | solution.py:85
  3.6 7.7 %collective-permute-start = (f32[1,512,128]{2,1,0:T(8,128)}, f32[1,512,128]{2,1,0:T(8,128)S(1)}, u32[]{:S(2)}, u32[]{:S(2)}) collective-permute-start(f32[1,512,128]{2,1,0:T(8,128)} %get-tuple-element.52), channel_id=1, source_target_pairs={{0,0},{1,2},{2,1},{3,4},{4,3},{5,6},{6,5},{7,8},{8,7},{9,10},{10,9... | collective-permute-start | bytes 786440 | tf_op jit(solution)/shard_map/ppermute | solution.py:791
  11.3 0.1 collective-permute-start.1
  11.4 0.6 convert_select_fusion.sea
  12.0 4.0 %diff_in.1 = (f32[2,512,128]{2,1,0:T(8,128)}, f32[1,512,128]{2,1,0:T(8,128)}, f32[3,512,128]{2,1,0:T(8,128)}, f32[8,512,128]{2,1,0:T(8,128)}) custom-call(s32[1]{0:T(128)} %bitcast.me, f32[1024,512]{1,0:T(8,128)} %bitcast.33, f32[8,512]{1,0:T(8,128)} %convert_select_fusion.sea), custom_call_target="tpu_custom_call" | custom-call | flops 2000000000 | bytes 1048576 | tf_op jit(solution)/shard_map/diff_in/pallas_call | solution.py:115
  16.1 2.6 %collective-permute-start.4 = (f32[2,512,128]{2,1,0:T(8,128)}, f32[2,512,128]{2,1,0:T(8,128)}, u32[]{:S(2)}, u32[]{:S(2)}) collective-permute-start(f32[2,512,128]{2,1,0:T(8,128)} %get-tuple-element.59), channel_id=1, source_target_pairs={{0,0},{1,2},{2,1},{3,4},{4,3},{5,6},{6,5},{7,8},{8,7},{9,10},{10,9... | collective-permute-start | bytes 1572872 | tf_op jit(solution)/shard_map/ppermute | solution.py:791
  18.6 0.1 collective-permute-start.5
  18.8 0.2 multiply_reduce_fusion
  19.0 0.1 broadcast_in_dim.10
  19.1 0.1 mul.57
  19.1 0.1 broadcast_in_dim.9
  19.2 0.1 reshape.90
  19.3 0.1 copy.18
  19.4 0.1 copy.17
  19.5 0.7 reshape.91.send_rows
  20.2 1.6 mixes.1
  21.8 0.7 copy-done.31
  22.5 0.0 copy-done.30
  22.6 6.6 %first_step.1 = (f32[3,512,128]{2,1,0:T(8,128)}, f32[3,512,128]{2,1,0:T(8,128)}, f32[8,512,128]{2,1,0:T(8,128)}) custom-call(s32[1]{0:T(128)} %bitcast.me, f32[8,512,128]{2,1,0:T(8,128)} %get-tuple-element.51.own, f32[1,512,128]{2,1,0:T(8,128)} %copy-done.30, f32[1,512,128]{2,1,0:T(8,128)} %copy-done.31, f32[8,512,128]{2,1,0:T(8,128)} %get-tuple-element.54.dt, ...), custom_call_target="tpu_custom_call" | custom-call | flops 2000000000 | bytes 1048576 | tf_op jit(solution)/shard_map/first_step/pallas_call | solution.py:451
  29.2 7.5 %collective-permute-start.2 = (f32[3,512,128]{2,1,0:T(8,128)}, f32[3,512,128]{2,1,0:T(8,128)S(1)}, u32[]{:S(2)}, u32[]{:S(2)}) collective-permute-start(f32[3,512,128]{2,1,0:T(8,128)} %get-tuple-element.57), channel_id=1, source_target_pairs={{0,0},{1,2},{2,1},{3,4},{4,3},{5,6},{6,5},{7,8},{8,7},{9,10},{10,9... | collective-permute-start | bytes 2359304 | tf_op jit(solution)/shard_map/ppermute | solution.py:791
  36.7 0.1 collective-permute-start.3
  36.8 0.1 convert_reduce_fusion
  37.0 0.2 select_reduce_fusion
  37.2 1.3 to_rows.1.m
  38.5 1.3 copy-done.20
  39.9 15.7 %collective-permute-done.2.ho = f32[3,512,128]{2,1,0:T(8,128)S(1)} collective-permute-done((f32[3,512,128]{2,1,0:T(8,128)}, f32[3,512,128]{2,1,0:T(8,128)S(1)}, u32[]{:S(2)}, u32[]{:S(2)}) %collective-permute-start.2) | collective-permute-done | bytes 786464 | tf_op jit(solution)/shard_map/ppermute | solution.py:791
  55.7 7.5 %first_block.1 = (f32[3,512,128]{2,1,0:T(8,128)}, f32[1,512,128]{2,1,0:T(8,128)S(1)}, f32[4,512,128]{2,1,0:T(8,128)S(1)}, f32[32,128]{1,0:T(8,128)S(1)}) custom-call(s32[1]{0:T(128)} %bitcast.me, f32[8,512,128]{2,1,0:T(8,128)S(1)} %copy-done.19, f32[3,512,128]{2,1,0:T(8,128)S(1)} %collective-permute-done.2.ho, f32[3,512,128]{2,1,0:T(8,128)S(1)} %collective-permute-done.3.hi, ...), custom_call_target="tpu_custom_call" | custom-call | flops 5000000000 | bytes 1048576 | tf_op jit(solution)/shard_map/first_block/pallas_call | solution.py:489
  63.2 0.1 collective-permute-start.9
  63.2 4.3 %collective-permute-start.6 = (f32[3,512,128]{2,1,0:T(8,128)}, f32[3,512,128]{2,1,0:T(8,128)S(1)}, u32[]{:S(2)}, u32[]{:S(2)}) collective-permute-start(f32[3,512,128]{2,1,0:T(8,128)} %get-tuple-element.66.v0), channel_id=1, source_target_pairs={{0,0},{1,2},{2,1},{3,4},{4,3},{5,6},{6,5},{7,8},{8,7},{9,10},{10,9... | collective-permute-start | bytes 2359304 | tf_op jit(solution)/shard_map/ppermute | solution.py:791
  67.5 0.7 collective-permute-start.7
  68.2 16.3 %collective-permute-done.7.surf = f32[32,128]{1,0:T(8,128)S(1)} collective-permute-done((f32[32,128]{1,0:T(8,128)S(1)}, f32[32,128]{1,0:T(8,128)S(1)}, u32[]{:S(2)}, u32[]{:S(2)}) %collective-permute-start.7) | collective-permute-done | bytes 16416 | tf_op jit(solution)/shard_map/ppermute | solution.py:797
  84.5 0.6 copy-done.25
  85.1 1.6 offer.1
  86.7 8.7 %all-to-all-start = ((f32[64,8,128]{2,1,0:T(8,128)}), f32[64,8,128]{2,1,0:T(8,128)S(1)}, u32[]{:S(2)}, u32[]{:S(2)}) async-start(f32[64,8,128]{2,1,0:T(8,128)} %bitcast.26), calls=%async_computation | async-start | bytes 524288 | tf_op jit(solution)/shard_map/all_to_all | solution.py:801
  95.4 6.7 %collective-permute-start.12 = (f32[1,512,128]{2,1,0:T(8,128)}, f32[1,512,128]{2,1,0:T(8,128)S(1)}, u32[]{:S(2)}, u32[]{:S(2)}) collective-permute-start(f32[1,512,128]{2,1,0:T(8,128)} %get-tuple-element.80), channel_id=1, source_target_pairs={{0,0},{1,2},{2,1},{3,4},{4,3},{5,6},{6,5},{7,8},{8,7},{9,10},{10,9... | collective-permute-start | bytes 786440 | tf_op jit(solution)/shard_map/ppermute | solution.py:791
  102.1 3.7 %all-to-all-done = f32[64,8,128]{2,1,0:T(8,128)S(1)} async-done(((f32[64,8,128]{2,1,0:T(8,128)}), f32[64,8,128]{2,1,0:T(8,128)S(1)}, u32[]{:S(2)}, u32[]{:S(2)}) %all-to-all-start) | async-done | bytes 262176 | tf_op jit(solution)/shard_map/all_to_all | solution.py:801
  105.8 3.6 %collective-permute-start.8 = (f32[1,512,128]{2,1,0:T(8,128)}, f32[1,512,128]{2,1,0:T(8,128)S(1)}, u32[]{:S(2)}, u32[]{:S(2)}) collective-permute-start(f32[1,512,128]{2,1,0:T(8,128)} %copy-done.12), channel_id=1, source_target_pairs={{0,0},{1,2},{2,1},{3,4},{4,3},{5,6},{6,5},{7,8},{8,7},{9,10},{10,9... | collective-permute-start | bytes 786440 | tf_op jit(solution)/shard_map/ppermute | solution.py:791
  109.4 2.2 copy-done.1
  111.6 2.3 remap.1
  114.0 6.5 %collective-permute-start.10 = (f32[16,128]{1,0:T(8,128)S(1)}, f32[16,128]{1,0:T(8,128)S(1)}, u32[]{:S(2)}, u32[]{:S(2)}) collective-permute-start(f32[16,128]{1,0:T(8,128)S(1)} %get-tuple-element.78), channel_id=1, source_target_pairs={{0,0},{1,2},{2,1},{3,4},{4,3},{5,6},{6,5},{7,8},{8,7},{9,10},{10,9... | collective-permute-start | bytes 24584 | tf_op jit(solution)/shard_map/ppermute | solution.py:791
  120.5 0.7 copy-done.9
  121.1 2.3 collective-permute-done.10.so
  123.5 0.9 copy-done.7
  124.4 1.1 copy-done.8
  125.5 0.9 copy-done.10
  126.5 21.3 %middle_block.1 = (f32[8,512,128]{2,1,0:T(8,128)S(1)}, f32[8,512,128]{2,1,0:T(8,128)}, f32[3,512,128]{2,1,0:T(8,128)}, f32[1,512,128]{2,1,0:T(8,128)}, f32[4,512...) custom-call(s32[1]{0:T(128)} %bitcast.me, ...), custom_call_target="tpu_custom_call" | custom-call | flops 15000000512 | bytes 1048576 | tf_op jit(solution)/shard_map/middle_block/pallas_call | solution.py:580
  147.8 6.4 %collective-permute-start.13 = (f32[16,128]{1,0:T(8,128)S(1)}, f32[16,128]{1,0:T(8,128)S(1)}, u32[]{:S(2)}, u32[]{:S(2)}) collective-permute-start(f32[16,128]{1,0:T(8,128)S(1)} %get-tuple-element.87), channel_id=1, source_target_pairs={{0,0},{1,2},{2,1},{3,4},{4,3},{5,6},{6,5},{7,8},{8,7},{9,10},{10,9... | collective-permute-start | bytes 24584 | tf_op jit(solution)/shard_map/ppermute | solution.py:791
  154.2 0.1 collective-permute-start.14
  154.3 2.9 %collective-permute-done.13.so = f32[16,128]{1,0:T(8,128)S(1)} collective-permute-done((f32[16,128]{1,0:T(8,128)S(1)}, f32[16,128]{1,0:T(8,128)S(1)}, u32[]{:S(2)}, u32[]{:S(2)}) %collective-permute-start.13) | collective-permute-done | bytes 8224 | tf_op jit(solution)/shard_map/ppermute | solution.py:791
  157.3 6.4 %collective-permute-start.15 = (f32[3,512,128]{2,1,0:T(8,128)}, f32[3,512,128]{2,1,0:T(8,128)}, u32[]{:S(2)}, u32[]{:S(2)}) collective-permute-start(f32[3,512,128]{2,1,0:T(8,128)} %get-tuple-element.89), channel_id=1, source_target_pairs={{0,0},{1,2},{2,1},{3,4},{4,3},{5,6},{6,5},{7,8},{8,7},{9,10},{10,9... | collective-permute-start | bytes 2359304 | tf_op jit(solution)/shard_map/ppermute | solution.py:791
  163.7 2.0 remap_back.1
  165.7 19.3 %all_to_all.10 = f32[64,8,128]{2,1,0:T(8,128)} all-to-all(f32[64,8,128]{2,1,0:T(8,128)S(1)} %bitcast.22), channel_id=1, replica_groups=mesh['comp'=2,'tile'=64] {'tile'}, dimensions={0} | all-to-all | bytes 524288 | tf_op jit(solution)/shard_map/all_to_all | solution.py:801
  185.0 3.8 %collective-permute-start.16 = (f32[1,512,128]{2,1,0:T(8,128)}, f32[1,512,128]{2,1,0:T(8,128)S(1)}, u32[]{:S(2)}, u32[]{:S(2)}) collective-permute-start(f32[1,512,128]{2,1,0:T(8,128)} %get-tuple-element.94), channel_id=1, source_target_pairs={{0,0},{1,2},{2,1},{3,4},{4,3},{5,6},{6,5},{7,8},{8,7},{9,10},{10,9... | collective-permute-start | bytes 786440 | tf_op jit(solution)/shard_map/ppermute | solution.py:791
  188.8 2.2 collect.1
  191.1 3.9 %collective-permute-done.18.s = f32[32,128]{1,0:T(8,128)S(1)} collective-permute-done((f32[32,128]{1,0:T(8,128)}, f32[32,128]{1,0:T(8,128)S(1)}, u32[]{:S(2)}, u32[]{:S(2)}) %collective-permute-start.18) | collective-permute-done | bytes 16416 | tf_op jit(solution)/shard_map/ppermute | solution.py:797
  195.0 4.2 %collective-permute-done.16.r1 = f32[1,512,128]{2,1,0:T(8,128)S(1)} collective-permute-done((f32[1,512,128]{2,1,0:T(8,128)}, f32[1,512,128]{2,1,0:T(8,128)S(1)}, u32[]{:S(2)}, u32[]{:S(2)}) %collective-permute-start.16) | collective-permute-done | bytes 262176 | tf_op jit(solution)/shard_map/ppermute | solution.py:791
  199.3 0.9 copy-done.15
  200.2 1.6 copy-done.23
  201.8 11.7 %last_block.1 = (f32[8,512,128]{2,1,0:T(8,128)S(1)}, f32[4,512,128]{2,1,0:T(8,128)S(1)}, f32[4,512,128]{2,1,0:T(8,128)S(1)}) custom-call(s32[1]{0:T(128)} %bitcast.me, f32[8,512,128]{2,1,0:T(8,128)S(1)} %copy-done.23, f32[3,512,128]{2,1,0:T(8,128)} %collective-permute-done.15.r0, f32[1,512,128]{2,1,0:T(8,128)S(1)} %collective-permute-done.16.r1, ...), custom_call_target="tpu_custom_call" | custom-call | flops 7500000256 | bytes 1048576 | tf_op jit(solution)/shard_map/last_block/pallas_call | solution.py:651
  213.5 2.6 %collective-permute-start.19 = (f32[4,512,128]{2,1,0:T(8,128)S(1)}, f32[4,512,128]{2,1,0:T(8,128)S(1)}, u32[]{:S(2)}, u32[]{:S(2)}) collective-permute-start(f32[4,512,128]{2,1,0:T(8,128)S(1)} %get-tuple-element.98), channel_id=1, source_target_pairs={{0,0},{1,2},{2,1},{3,4},{4,3},{5,6},{6,5},{7,8},{8,7},{9,10},{10,9... | collective-permute-start | bytes 3145736 | tf_op jit(solution)/shard_map/ppermute | solution.py:791
  216.0 0.1 collective-permute-start.20
  216.1 2.3 to_raw.1
  218.5 22.8 %collective-permute-done.19.outer = f32[4,512,128]{2,1,0:T(8,128)S(1)} collective-permute-done((f32[4,512,128]{2,1,0:T(8,128)S(1)}, f32[4,512,128]{2,1,0:T(8,128)S(1)}, u32[]{:S(2)}, u32[]{:S(2)}) %collective-permute-start.19) | collective-permute-done | bytes 1048608 | tf_op jit(solution)/shard_map/ppermute | solution.py:791
  241.3 2.1 grad_out.1
  (77 shorter events, 0.2 us)
Async XLA Ops:
  0.6 18.1 %copy-start = (s32[2,64,64]{2,1,0:T(8,128)S(1)}, s32[2,64,64]{2,1,0:T(8,128)}, u32[]{:S(2)}) copy-start(s32[2,64,64]{2,1,0:T(8,128)} %param.16) | copy-start | bytes 98308
  0.7 10.8 %copy-start.26 = (s32[8,512]{1,0:T(8,128)S(1)}, s32[8,512]{1,0:T(8,128)}, u32[]{:S(2)}) copy-start(s32[8,512]{1,0:T(8,128)} %param.14) | copy-start | bytes 49156
  3.6 18.2 %collective-permute-start = (f32[1,512,128]{2,1,0:T(8,128)}, f32[1,512,128]{2,1,0:T(8,128)S(1)}, u32[]{:S(2)}, u32[]{:S(2)}) collective-permute-start(f32[1,512,128]{2,1,0:T(8,128)} %get-tuple-element.52), channel_id=1, source_target_pairs={{0,0},{1,2},{2,1},{3,4},{4,3},{5,6},{6,5},{7,8},{8,7},{9,10},{10,9... | collective-permute-start | bytes 786440 | tf_op jit(solution)/shard_map/ppermute | solution.py:791
  11.3 10.5 %collective-permute-start.1 = (f32[1,512,128]{2,1,0:T(8,128)}, f32[1,512,128]{2,1,0:T(8,128)S(1)}, u32[]{:S(2)}, u32[]{:S(2)}) collective-permute-start(f32[1,512,128]{2,1,0:T(8,128)} %get-tuple-element.53), channel_id=1, source_target_pairs={{0,1},{1,0},{2,3},{3,2},{4,5},{5,4},{6,7},{7,6},{8,9},{9,8},{10,11... | collective-permute-start | bytes 786440 | tf_op jit(solution)/shard_map/ppermute | solution.py:794
  12.0 6.7 %copy-start.24 = (f32[8,512]{1,0:T(8,128)S(1)}, f32[8,512]{1,0:T(8,128)}, u32[]{:S(2)}) copy-start(f32[8,512]{1,0:T(8,128)} %convert_select_fusion.sea) | copy-start | bytes 49156
  12.0 6.8 %copy-start.27 = (s32[2,64,8]{1,2,0:T(8,128)S(1)}, s32[2,64,8]{1,2,0:T(8,128)}, u32[]{:S(2)}) copy-start(s32[2,64,8]{1,2,0:T(8,128)} %param.15) | copy-start | bytes 12292
  12.0 7.1 %copy-start.28 = (s32[1,1,8]{2,1,0:T(1,128)S(1)}, s32[1,1,8]{2,1,0:T(1,128)}, u32[]{:S(2)}) copy-start(s32[1,1,8]{2,1,0:T(1,128)} %param.18) | copy-start | bytes 100
  16.1 23.8 %collective-permute-start.4 = (f32[2,512,128]{2,1,0:T(8,128)}, f32[2,512,128]{2,1,0:T(8,128)}, u32[]{:S(2)}, u32[]{:S(2)}) collective-permute-start(f32[2,512,128]{2,1,0:T(8,128)} %get-tuple-element.59), channel_id=1, source_target_pairs={{0,0},{1,2},{2,1},{3,4},{4,3},{5,6},{6,5},{7,8},{8,7},{9,10},{10,9... | collective-permute-start | bytes 1572872 | tf_op jit(solution)/shard_map/ppermute | solution.py:791
  18.6 21.2 %collective-permute-start.5 = (f32[3,512,128]{2,1,0:T(8,128)}, f32[3,512,128]{2,1,0:T(8,128)S(1)}, u32[]{:S(2)}, u32[]{:S(2)}) collective-permute-start(f32[3,512,128]{2,1,0:T(8,128)} %get-tuple-element.60), channel_id=1, source_target_pairs={{0,1},{1,0},{2,3},{3,2},{4,5},{5,4},{6,7},{7,6},{8,9},{9,8},{10,11... | collective-permute-start | bytes 2359304 | tf_op jit(solution)/shard_map/ppermute | solution.py:794
  21.8 0.8 copy-start.30
  21.8 0.7 copy-start.31
  22.6 14.4 %copy-start.29 = (s32[1,1,64]{2,1,0:T(1,128)S(1)}, s32[1,1,64]{2,1,0:T(1,128)}, u32[]{:S(2)}) copy-start(s32[1,1,64]{2,1,0:T(1,128)} %param.17) | copy-start | bytes 772
  22.6 14.6 %copy-start.3 = (f32[1,128,8,512]{3,2,1,0:T(8,128)S(1)}, f32[1,128,8,512]{3,2,1,0:T(8,128)}, u32[]{:S(2)}) copy-start(f32[1,128,8,512]{3,2,1,0:T(8,128)} %param.11) | copy-start | bytes 6291460
  29.2 26.4 %collective-permute-start.2 = (f32[3,512,128]{2,1,0:T(8,128)}, f32[3,512,128]{2,1,0:T(8,128)S(1)}, u32[]{:S(2)}, u32[]{:S(2)}) collective-permute-start(f32[3,512,128]{2,1,0:T(8,128)} %get-tuple-element.57), channel_id=1, source_target_pairs={{0,0},{1,2},{2,1},{3,4},{4,3},{5,6},{6,5},{7,8},{8,7},{9,10},{10,9... | collective-permute-start | bytes 2359304 | tf_op jit(solution)/shard_map/ppermute | solution.py:791
  36.7 18.9 %collective-permute-start.3 = (f32[3,512,128]{2,1,0:T(8,128)}, f32[3,512,128]{2,1,0:T(8,128)S(1)}, u32[]{:S(2)}, u32[]{:S(2)}) collective-permute-start(f32[3,512,128]{2,1,0:T(8,128)} %get-tuple-element.58), channel_id=1, source_target_pairs={{0,1},{1,0},{2,3},{3,2},{4,5},{5,4},{6,7},{7,6},{8,9},{9,8},{10,11... | collective-permute-start | bytes 2359304 | tf_op jit(solution)/shard_map/ppermute | solution.py:794
  37.2 18.5 %copy-start.16 = (bf16[256,256]{1,0:T(8,128)(2,1)S(1)}, bf16[256,256]{1,0:T(8,128)(2,1)}, u32[]{:S(2)}) copy-start(bf16[256,256]{1,0:T(8,128)(2,1)} %get-tuple-element.55.w2.w2f) | copy-start | bytes 393220
  37.2 18.5 %copy-start.18 = (f32[8,512,128]{2,1,0:T(8,128)S(1)}, f32[8,512,128]{2,1,0:T(8,128)}, u32[]{:S(2)}) copy-start(f32[8,512,128]{2,1,0:T(8,128)} %get-tuple-element.54.dt) | copy-start | bytes 6291460
  37.2 18.4 %copy-start.19 = (f32[8,512,128]{2,1,0:T(8,128)S(1)}, f32[8,512,128]{2,1,0:T(8,128)}, u32[]{:S(2)}) copy-start(f32[8,512,128]{2,1,0:T(8,128)} %get-tuple-element.56.own) | copy-start | bytes 6291460
  38.5 1.3 copy-start.20
  39.9 23.2 %copy-start.4 = (f32[3,512,128]{2,1,0:T(8,128)}, f32[3,512,128]{2,1,0:T(8,128)S(1)}, u32[]{:S(2)}) copy-start(f32[3,512,128]{2,1,0:T(8,128)S(1)} %collective-permute-done.5.di) | copy-start | bytes 2359300
  63.1 23.5 %copy-start.12 = (f32[1,512,128]{2,1,0:T(8,128)}, f32[1,512,128]{2,1,0:T(8,128)S(1)}, u32[]{:S(2)}) copy-start(f32[1,512,128]{2,1,0:T(8,128)S(1)} %get-tuple-element.71.v1) | copy-start | bytes 786436
  63.2 61.2 %collective-permute-start.9 = (f32[4,512,128]{2,1,0:T(8,128)S(1)}, f32[4,512,128]{2,1,0:T(8,128)S(1)}, u32[]{:S(2)}, u32[]{:S(2)}) collective-permute-start(f32[4,512,128]{2,1,0:T(8,128)S(1)} %get-tuple-element.68.v2), channel_id=1, source_target_pairs={{0,1},{1,0},{2,3},{3,2},{4,5},{5,4},{6,7},{7,6},{8,9},{9,8},{10,11... | collective-permute-start | bytes 3145736 | tf_op jit(solution)/shard_map/ppermute | solution.py:794
  63.2 60.2 %collective-permute-start.6 = (f32[3,512,128]{2,1,0:T(8,128)}, f32[3,512,128]{2,1,0:T(8,128)S(1)}, u32[]{:S(2)}, u32[]{:S(2)}) collective-permute-start(f32[3,512,128]{2,1,0:T(8,128)} %get-tuple-element.66.v0), channel_id=1, source_target_pairs={{0,0},{1,2},{2,1},{3,4},{4,3},{5,6},{6,5},{7,8},{8,7},{9,10},{10,9... | collective-permute-start | bytes 2359304 | tf_op jit(solution)/shard_map/ppermute | solution.py:791
  67.5 17.0 %collective-permute-start.7 = (f32[32,128]{1,0:T(8,128)S(1)}, f32[32,128]{1,0:T(8,128)S(1)}, u32[]{:S(2)}, u32[]{:S(2)}) collective-permute-start(f32[32,128]{1,0:T(8,128)S(1)} %get-tuple-element.70), channel_id=1, source_target_pairs={{0,64},{64,0},{1,65},{65,1},{2,66},{66,2},{3,67},{67,3},{4,68},{68... | collective-permute-start | bytes 49160 | tf_op jit(solution)/shard_map/ppermute | solution.py:797
  84.5 0.6 copy-start.25
  86.7 19.1 %all-to-all-start = ((f32[64,8,128]{2,1,0:T(8,128)}), f32[64,8,128]{2,1,0:T(8,128)S(1)}, u32[]{:S(2)}, u32[]{:S(2)}) async-start(f32[64,8,128]{2,1,0:T(8,128)} %bitcast.26), calls=%async_computation | async-start | bytes 524288 | tf_op jit(solution)/shard_map/all_to_all | solution.py:801
  95.4 25.0 %collective-permute-start.12 = (f32[1,512,128]{2,1,0:T(8,128)}, f32[1,512,128]{2,1,0:T(8,128)S(1)}, u32[]{:S(2)}, u32[]{:S(2)}) collective-permute-start(f32[1,512,128]{2,1,0:T(8,128)} %get-tuple-element.80), channel_id=1, source_target_pairs={{0,0},{1,2},{2,1},{3,4},{4,3},{5,6},{6,5},{7,8},{8,7},{9,10},{10,9... | collective-permute-start | bytes 786440 | tf_op jit(solution)/shard_map/ppermute | solution.py:791
  105.8 17.7 %collective-permute-start.8 = (f32[1,512,128]{2,1,0:T(8,128)}, f32[1,512,128]{2,1,0:T(8,128)S(1)}, u32[]{:S(2)}, u32[]{:S(2)}) collective-permute-start(f32[1,512,128]{2,1,0:T(8,128)} %copy-done.12), channel_id=1, source_target_pairs={{0,0},{1,2},{2,1},{3,4},{4,3},{5,6},{6,5},{7,8},{8,7},{9,10},{10,9... | collective-permute-start | bytes 786440 | tf_op jit(solution)/shard_map/ppermute | solution.py:791
  109.4 2.2 copy-start.1
  111.6 12.7 %copy-start.5 = (f32[3,512,128]{2,1,0:T(8,128)S(1)}, f32[3,512,128]{2,1,0:T(8,128)}, u32[]{:S(2)}) copy-start(f32[3,512,128]{2,1,0:T(8,128)} %copy-done.4) | copy-start | bytes 2359300
  111.6 12.7 %copy-start.13 = (f32[1,512,128]{2,1,0:T(8,128)S(1)}, f32[1,512,128]{2,1,0:T(8,128)}, u32[]{:S(2)}) copy-start(f32[1,512,128]{2,1,0:T(8,128)} %copy-done.12) | copy-start | bytes 786436
  111.6 12.7 %copy-start.14 = (bf16[256,256]{1,0:T(8,128)(2,1)S(1)}, bf16[256,256]{1,0:T(8,128)(2,1)}, u32[]{:S(2)}) copy-start(bf16[256,256]{1,0:T(8,128)(2,1)} %get-tuple-element.82.w2b) | copy-start | bytes 393220
  111.6 12.8 %copy-start.17 = (bf16[256,256]{1,0:T(8,128)(2,1)S(1)}, bf16[256,256]{1,0:T(8,128)(2,1)}, u32[]{:S(2)}) copy-start(bf16[256,256]{1,0:T(8,128)(2,1)} %get-tuple-element.55.w2.w2f) | copy-start | bytes 393220
  114.0 9.5 %collective-permute-start.10 = (f32[16,128]{1,0:T(8,128)S(1)}, f32[16,128]{1,0:T(8,128)S(1)}, u32[]{:S(2)}, u32[]{:S(2)}) collective-permute-start(f32[16,128]{1,0:T(8,128)S(1)} %get-tuple-element.78), channel_id=1, source_target_pairs={{0,0},{1,2},{2,1},{3,4},{4,3},{5,6},{6,5},{7,8},{8,7},{9,10},{10,9... | collective-permute-start | bytes 24584 | tf_op jit(solution)/shard_map/ppermute | solution.py:791
  120.4 0.7 copy-start.9
  121.1 2.3 collective-permute-start.11
  123.5 0.9 copy-start.7
  124.4 1.1 copy-start.8
  125.5 0.9 copy-start.10
  126.5 37.2 %copy-start.2 = (f32[1,64,128,128]{3,2,1,0:T(8,128)S(1)}, f32[1,64,128,128]{3,2,1,0:T(8,128)}, u32[]{:S(2)}) copy-start(f32[1,64,128,128]{3,2,1,0:T(8,128)} %param.19) | copy-start | bytes 12582916
  147.8 17.9 %copy-start.21 = (f32[8,512,128]{2,1,0:T(8,128)}, f32[8,512,128]{2,1,0:T(8,128)S(1)}, u32[]{:S(2)}) copy-start(f32[8,512,128]{2,1,0:T(8,128)S(1)} %get-tuple-element.83.x) | copy-start | bytes 6291460
  147.8 9.5 %collective-permute-start.13 = (f32[16,128]{1,0:T(8,128)S(1)}, f32[16,128]{1,0:T(8,128)S(1)}, u32[]{:S(2)}, u32[]{:S(2)}) collective-permute-start(f32[16,128]{1,0:T(8,128)S(1)} %get-tuple-element.87), channel_id=1, source_target_pairs={{0,0},{1,2},{2,1},{3,4},{4,3},{5,6},{6,5},{7,8},{8,7},{9,10},{10,9... | collective-permute-start | bytes 24584 | tf_op jit(solution)/shard_map/ppermute | solution.py:791
  154.2 3.0 %collective-permute-start.14 = (f32[16,128]{1,0:T(8,128)S(1)}, f32[16,128]{1,0:T(8,128)S(1)}, u32[]{:S(2)}, u32[]{:S(2)}) collective-permute-start(f32[16,128]{1,0:T(8,128)S(1)} %get-tuple-element.88), channel_id=1, source_target_pairs={{0,1},{1,0},{2,3},{3,2},{4,5},{5,4},{6,7},{7,6},{8,9},{9,8},{10,11... | collective-permute-start | bytes 24584 | tf_op jit(solution)/shard_map/ppermute | solution.py:794
  157.3 42.0 %collective-permute-start.17 = (f32[4,512,128]{2,1,0:T(8,128)S(1)}, f32[4,512,128]{2,1,0:T(8,128)S(1)}, u32[]{:S(2)}, u32[]{:S(2)}) collective-permute-start(f32[4,512,128]{2,1,0:T(8,128)S(1)} %get-tuple-element.95), channel_id=1, source_target_pairs={{0,1},{1,0},{2,3},{3,2},{4,5},{5,4},{6,7},{7,6},{8,9},{9,8},{10,11... | collective-permute-start | bytes 3145736 | tf_op jit(solution)/shard_map/ppermute | solution.py:794
  157.3 42.0 %collective-permute-start.15 = (f32[3,512,128]{2,1,0:T(8,128)}, f32[3,512,128]{2,1,0:T(8,128)}, u32[]{:S(2)}, u32[]{:S(2)}) collective-permute-start(f32[3,512,128]{2,1,0:T(8,128)} %get-tuple-element.89), channel_id=1, source_target_pairs={{0,0},{1,2},{2,1},{3,4},{4,3},{5,6},{6,5},{7,8},{8,7},{9,10},{10,9... | collective-permute-start | bytes 2359304 | tf_op jit(solution)/shard_map/ppermute | solution.py:791
  163.7 35.5 %copy-start.6 = (f32[3,512,128]{2,1,0:T(8,128)S(1)}, f32[3,512,128]{2,1,0:T(8,128)}, u32[]{:S(2)}) copy-start(f32[3,512,128]{2,1,0:T(8,128)} %copy-done.4) | copy-start | bytes 2359300
  163.7 35.5 %copy-start.11 = (f32[1,512,128]{2,1,0:T(8,128)S(1)}, f32[1,512,128]{2,1,0:T(8,128)}, u32[]{:S(2)}) copy-start(f32[1,512,128]{2,1,0:T(8,128)} %copy-done.9) | copy-start | bytes 786436
  185.0 14.2 %collective-permute-start.16 = (f32[1,512,128]{2,1,0:T(8,128)}, f32[1,512,128]{2,1,0:T(8,128)S(1)}, u32[]{:S(2)}, u32[]{:S(2)}) collective-permute-start(f32[1,512,128]{2,1,0:T(8,128)} %get-tuple-element.94), channel_id=1, source_target_pairs={{0,0},{1,2},{2,1},{3,4},{4,3},{5,6},{6,5},{7,8},{8,7},{9,10},{10,9... | collective-permute-start | bytes 786440 | tf_op jit(solution)/shard_map/ppermute | solution.py:791
  191.0 3.9 %collective-permute-start.18 = (f32[32,128]{1,0:T(8,128)}, f32[32,128]{1,0:T(8,128)S(1)}, u32[]{:S(2)}, u32[]{:S(2)}) collective-permute-start(f32[32,128]{1,0:T(8,128)} %collect.1), channel_id=1, source_target_pairs={{0,64},{64,0},{1,65},{65,1},{2,66},{66,2},{3,67},{67,3},{4,68},{68... | collective-permute-start | bytes 49160 | tf_op jit(solution)/shard_map/ppermute | solution.py:797
  199.3 0.9 copy-start.15
  200.2 1.6 copy-start.23
  201.8 14.4 %copy-start.22 = (f32[8,512,128]{2,1,0:T(8,128)S(1)}, f32[8,512,128]{2,1,0:T(8,128)}, u32[]{:S(2)}) copy-start(f32[8,512,128]{2,1,0:T(8,128)} %copy-done.21) | copy-start | bytes 6291460
  213.5 27.8 %collective-permute-start.19 = (f32[4,512,128]{2,1,0:T(8,128)S(1)}, f32[4,512,128]{2,1,0:T(8,128)S(1)}, u32[]{:S(2)}, u32[]{:S(2)}) collective-permute-start(f32[4,512,128]{2,1,0:T(8,128)S(1)} %get-tuple-element.98), channel_id=1, source_target_pairs={{0,0},{1,2},{2,1},{3,4},{4,3},{5,6},{6,5},{7,8},{8,7},{9,10},{10,9... | collective-permute-start | bytes 3145736 | tf_op jit(solution)/shard_map/ppermute | solution.py:791
  216.0 25.2 %collective-permute-start.20 = (f32[4,512,128]{2,1,0:T(8,128)S(1)}, f32[4,512,128]{2,1,0:T(8,128)S(1)}, u32[]{:S(2)}, u32[]{:S(2)}) collective-permute-start(f32[4,512,128]{2,1,0:T(8,128)S(1)} %get-tuple-element.99), channel_id=1, source_target_pairs={{0,1},{1,0},{2,3},{3,2},{4,5},{5,4},{6,7},{7,6},{8,9},{9,8},{10,11... | collective-permute-start | bytes 3145736 | tf_op jit(solution)/shard_map/ppermute | solution.py:794

commit v5 on v4

--- a/solution.py
+++ b/solution.py
@@ -94,7 +94,7 @@
     )(me, x)
 
 
-def diff_in_kernel(me, x, sea, outer, third, inner, full, buf, out, sems, osems):
+def diff_in_kernel(me, x, mask, outer, third, inner, full, buf, out, sems, osems):
     odd = parity(me)
     c = start_raw(x, buf, sems)
     todo = []
@@ -102,7 +102,8 @@
         c[j].wait()
         at = pl.ds(128 * j, 128)
         for r in range(8):
-            out[r, at, :] = (buf[j, pl.ds(r, 128, stride=8), :] * sea[r : r + 1, at]).T
+            sea = jnp.where(me[1] == 1, mask[r : r + 1, at].astype(F32), 1.0)
+            out[r, at, :] = (buf[j, pl.ds(r, 128, stride=8), :] * sea).T
         for i, (r0, n, dst) in enumerate(((6 * odd, 2, outer), (2 + 3 * odd, 1, third), (5 - 5 * odd, 3, inner), (0, 8, full))):
             src = out.at[pl.ds(r0, n), at, :]
             todo.append(pltpu.make_async_copy(src, lon_part(dst, j), osems.at[i, j]))
@@ -111,7 +112,7 @@
         d.wait()
 
 
-def diff_in(me, x, sea):
+def diff_in(me, x, mask):
     return pl.pallas_call(
         diff_in_kernel,
         out_shape=(sds(2, LON, LEV), sds(1, LON, LEV), sds(3, LON, LEV), sds(8, LON, LEV)),
@@ -121,7 +122,7 @@
         compiler_params=params(60),
         cost_estimate=cost(4),
         name="diff_in",
-    )(me, x, sea)
+    )(me, x, mask)
 
 
 def to_rows_kernel(x, o, buf, out, sems, osems):
@@ -220,16 +221,6 @@
         dst[128:256, 128:256] = jnp.zeros((128, 128), BF)
 
 
-def mixes(w):
-    return pl.pallas_call(
-        mix_kernel,
-        out_shape=(sds(256, 256, dtype=BF), sds(256, 256, dtype=BF)),
-        in_specs=[VM],
-        out_specs=(VM, VM),
-        name="mixes",
-    )(w)
-
-
 def put(v, r, j, new):
     v[r, pl.ds(OFF + 128 * j, 128), :] = new
     if j == 0:
@@ -420,7 +411,9 @@
     lax.fori_loop(0, n, cp, 0)
 
 
-def first_step_kernel(me, own, eo, ei, dt, w2, o_outer, o_inner, o_own, va, vb, h, d, sems):
+def first_step_kernel(
+    me, own, eo, ei, dt, w, o_outer, o_inner, o_mid, w2, w2b, va, vb, h, d, sems
+):
     odd = parity(me)
     c = copies(
         sems,
@@ -431,6 +424,7 @@
             (ei, tile_rows(va, 13 - 9 * odd, 1)),
         ],
     )
+    mix_kernel(w, w2, w2b)
     wait(*c[0:2])
     prepare_rows(va, h, 5, 8, d)
     wait(*c[2:4])
@@ -441,7 +435,7 @@
         [
             (tile_rows(vb, 5 + 5 * odd, 3), o_outer),
             (tile_rows(vb, 10 - 5 * odd, 3), o_inner),
-            (tile_rows(vb, 5, 8), o_own),
+            (tile_rows(vb, 8, 2), o_mid),
         ],
     )
     wait(*c)
@@ -450,9 +444,12 @@
 def first_step(*args):
     return pl.pallas_call(
         first_step_kernel,
-        out_shape=(sds(3, LON, LEV), sds(3, LON, LEV), sds(8, LON, LEV)),
+        out_shape=(
+            sds(3, LON, LEV), sds(3, LON, LEV), sds(2, LON, LEV),
+            sds(256, 256, dtype=BF), sds(256, 256, dtype=BF),
+        ),
         in_specs=[SM] + [ANY] * 4 + [VM],
-        out_specs=(ANY,) * 3,
+        out_specs=(ANY,) * 3 + (VM,) * 2,
         scratch_shapes=BLOCK_SCRATCH + [dma_sems(4)],
         compiler_params=params(60),
         cost_estimate=cost(4),
@@ -460,20 +457,22 @@
     )(*args)
 
 
-def first_kernel(me, own, ho, hi, dt, do, di, w2, o0, o1, o2, o_surf, va, vb, h, d, sems):
+def first_kernel(me, so, si, mid, ho, hi, dt, do, di, w2, o0, o1, o2, o_surf, va, vb, h, d, sems):
     odd = parity(me)
     c = copies(
         sems,
         [
-            (own, tile_rows(va, 5, 8)),
+            (so, tile_rows(va, 5 + 5 * odd, 3)),
+            (si, tile_rows(va, 10 - 5 * odd, 3)),
+            (mid, tile_rows(va, 8, 2)),
             (ho, tile_rows(va, 2 + 11 * odd, 3)),
             (hi, tile_rows(va, 13 - 11 * odd, 3)),
         ]
         + diffusion_copies(d, odd, dt, do, None, di),
     )
-    wait(c[0])
+    wait(*c[0:3])
     prepare_rows(va, h, 5, 8)
-    wait(*c[1:])
+    wait(*c[3:])
     clear_ends(me, ((va, 2, 3), (d, 2, 3)), ((va, 13, 3), (d, 13, 3)))
     prepare_rows(va, h, 3, 2)
     prepare_rows(va, h, 13, 2)
@@ -489,9 +488,9 @@
     return pl.pallas_call(
         first_kernel,
         out_shape=PARTS + (sds(32, 128),),
-        in_specs=[SM] + [ANY] * 6 + [VM],
+        in_specs=[SM] + [ANY] * 8 + [VM],
         out_specs=(ANY,) * 3 + (VM,),
-        scratch_shapes=BLOCK_SCRATCH + [dma_sems(6)],
+        scratch_shapes=BLOCK_SCRATCH + [dma_sems(8)],
         compiler_params=params(),
         cost_estimate=cost(10),
         name="first_block",
@@ -784,7 +783,7 @@
 ):
     component = lax.axis_index("comp")
     own_tile = lax.axis_index("tile")
-    across = [(i, min(max(i + 1 if i % 2 else i - 1, 0), 63)) for i in range(64)]
+    across = [(i, (i + 1 if i % 2 else i - 1) % 64) for i in range(64)]
     on_chip = [(i, i ^ 1) for i in range(64)]
 
     def far(x):
@@ -801,18 +800,20 @@
         x = lax.all_to_all(x, "tile", split_axis=0, concat_axis=0, tiled=True)
         return x.reshape(512, 128)
 
-    me = own_tile.reshape(1)
+    me = jnp.stack([own_tile, component]).astype(jnp.int32)
     e_o, e_i, start = start_in(me, starting_perturbation.reshape(1024, LON))
     eo, ei = far(e_o), near(e_i)
+    d_o, d_x, d_i, dt = diff_in(me, diffusion.reshape(1024, LON), ocean_mask)
+    do, di = far(d_o), near(d_i)
+    s_o, s_i, mid, w2f, w2b = first_step(me, start, eo, ei, dt, vert_mix[0])
+    ho, hi = far(s_o), near(s_i)
+    dx = far(d_x)
+    pair_tile, pair_patch, dest_patch, pair_blocks, ocean_mask, do = lax.optimization_barrier(
+        (pair_tile, pair_patch, dest_patch, pair_blocks, ocean_mask, do)
+    )
+
     sea = jnp.where(component == 1, ocean_mask.astype(F32), 1.0)
     sea32 = sea.reshape(32, 128)
-    d_o, d_x, d_i, dt = diff_in(me, diffusion.reshape(1024, LON), sea)
-    do, di = far(d_o), near(d_i)
-    w2f, w2b = mixes(vert_mix[0])
-    s_o, s_i, one = first_step(me, start, eo, ei, dt, w2f)
-    ho, hi = far(s_o), near(s_i)
-    dx = far(d_x)
-
     slots = jnp.arange(64, dtype=jnp.int32)
     live = slots % 8 < jnp.repeat(pair_blocks[0, 0], 8)
     place = jnp.sum((slots[None, :] < slots[:, None]) & live[None, :], axis=1)
@@ -832,7 +833,7 @@
         )
     )
 
-    v0, v1, v2, surf = first_block(me, one, ho, hi, dt, do, di, w2f)
+    v0, v1, v2, surf = first_block(me, s_o, s_i, mid, ho, hi, dt, do, di, w2f)
     other = swap(surf)
     h0, h2 = far(v0), near(v2)
     offered = offer(me, send_rows, other)

time: 245 us -> 253 us (1.033)
  starting transfers between devices: 68 us -> 45.1 us
  waiting for transfers between devices: 72 us -> 84 us
  local copies, waits for them, and re-layouts: 12.3 us -> 23.9 us
  blocking collectives: 19.3 us -> 23.9 us
    ppermute x11, starting transfers between devices: 58 us -> 35.2 us  [far(): return lax.ppermute(x, 'tile', across)]
    unnamed x65 -> x82, local copies, waits for them, and re-layouts: 11.2 us -> 22.8 us
    ppermute x11, waiting for transfers between devices: 48 us -> 55.7 us  [far(): return lax.ppermute(x, 'tile', across)]
    all_to_all x1, blocking collectives: 19.3 us -> 23.9 us  [exchange(): x = lax.all_to_all(x, 'tile', split_axis=0, concat_axis=0, tiled=True)]
  transfers between devices with their start and end apart: 22 -> 22, of which waited for: 8 -> 9; matrix products, arithmetic and copies ran while one was open for 1% -> 1% of each run, Pallas kernels for 10% -> 9%
where the time goes in v5:
time: 253 us; the launch traced here: 250 us
  waiting for transfers between devices  84 us (33%)
  Pallas kernels  70.3 us (28%)
  starting transfers between devices  45.1 us (18%)
  local copies, waits for them, and re-layouts  23.9 us (9%)
  blocking collectives  23.9 us (9%)
    ppermute x11, waiting for transfers between devices, far(): return lax.ppermute(x, 'tile', across)  55.7 us
    ppermute x11, starting transfers between devices, far(): return lax.ppermute(x, 'tile', across)  35.2 us
    all_to_all x1, blocking collectives, exchange(): x = lax.all_to_all(x, 'tile', split_axis=0, concat_axis=0, tiled=True)  23.9 us
    unnamed x82, local copies, waits for them, and re-layouts  22.8 us
    ppermute x2, waiting for transfers between devices, swap(): return lax.ppermute(x, 'comp', [(0, 1), (1, 0)])  22.4 us
    pallas_call x1, Pallas kernels, middle_block(): pl.pallas_call(middle_kernel, out_shape=(sds(8, LON, LEV), sds(8, LON, LE...  21.8 us
    pallas_call x1, Pallas kernels, last_block(): pl.pallas_call(last_kernel, out_shape=(sds(8, LON, LEV), sds(4, LON, LEV)...  12.2 us
    all_to_all x1, starting transfers between devices, exchange(): x = lax.all_to_all(x, 'tile', split_axis=0, concat_axis=0, tiled=True)  8.27 us
  transfers between devices with their start and end apart: 22, of which 9 were waited for; matrix products, arithmetic and copies ran while one was open for 1% of the time, Pallas kernels for 9%

profile of v5, /device:TPU:8, one launch (start us, length us, event | category | flops | bytes accessed | tf_op | source)
XLA Modules:
  0.0 249.5 jit_solution(16250112916642678574)
XLA Ops:
  0.6 0.6 pad_add_fusion.me
  1.3 4.0 %diff_in.1 = (f32[2,512,128]{2,1,0:T(8,128)}, f32[1,512,128]{2,1,0:T(8,128)}, f32[3,512,128]{2,1,0:T(8,128)}, f32[8,512,128]{2,1,0:T(8,128)}) custom-call(s32[2]{0:T(128)} %pad_add_fusion.me, f32[1024,512]{1,0:T(8,128)} %bitcast.32, s32[8,512]{1,0:T(8,128)} %mask.1), custom_call_target="tpu_custom_call" | custom-call | flops 2000000000 | bytes 1048576 | tf_op jit(solution)/shard_map/diff_in/pallas_call | solution.py:116
  5.3 5.9 %collective-permute-start.4 = (f32[2,512,128]{2,1,0:T(8,128)}, f32[2,512,128]{2,1,0:T(8,128)S(1)}, u32[]{:S(2)}, u32[]{:S(2)}) collective-permute-start(f32[2,512,128]{2,1,0:T(8,128)} %get-tuple-element.64), channel_id=1, source_target_pairs={{0,63},{1,2},{2,1},{3,4},{4,3},{5,6},{6,5},{7,8},{8,7},{9,10},{10,... | collective-permute-start | bytes 1572872 | tf_op jit(solution)/shard_map/ppermute | solution.py:790
  11.2 3.7 %start_in.1 = (f32[1,512,128]{2,1,0:T(8,128)}, f32[1,512,128]{2,1,0:T(8,128)}, f32[8,512,128]{2,1,0:T(8,128)}) custom-call(s32[2]{0:T(128)} %pad_add_fusion.me, f32[1024,512]{1,0:T(8,128)} %bitcast.33), custom_call_target="tpu_custom_call" | custom-call | flops 2000000000 | bytes 1048576 | tf_op jit(solution)/shard_map/start_in/pallas_call | solution.py:85
  14.8 0.5 collective-permute-start
  15.3 0.5 collective-permute-start.5
  15.9 1.3 to_rows.1.m
  17.2 1.3 copy-done.26
  18.5 11.1 %collective-permute-done.eo = f32[1,512,128]{2,1,0:T(8,128)} collective-permute-done((f32[1,512,128]{2,1,0:T(8,128)}, f32[1,512,128]{2,1,0:T(8,128)}, u32[]{:S(2)}, u32[]{:S(2)}) %collective-permute-start) | collective-permute-done | bytes 262176 | tf_op jit(solution)/shard_map/ppermute | solution.py:790
  29.6 6.7 %first_step.1 = (f32[3,512,128]{2,1,0:T(8,128)}, f32[3,512,128]{2,1,0:T(8,128)}, f32[2,512,128]{2,1,0:T(8,128)}, bf16[256,256]{1,0:T(8,128)(2,1)}, bf16[256,256]{1,0:T(8,128)(2,1)}) custom-call(s32[2]{0:T(128)} %pad_add_fusion.me, f32[8,512,128]{2,1,0:T(8,128)} %get-tuple-element.57.own, f32[1,512,128]{2,1,0:T(8,128)} %collective-permute-done.eo, ...), custom_call_target="tpu_custom_call" | custom-call | flops 2000000000 | bytes 1048576 | tf_op jit(solution)/shard_map/first_step/pallas_call | solution.py:445
  36.3 3.0 %collective-permute-start.2 = (f32[3,512,128]{2,1,0:T(8,128)}, f32[3,512,128]{2,1,0:T(8,128)S(1)}, u32[]{:S(2)}, u32[]{:S(2)}) collective-permute-start(f32[3,512,128]{2,1,0:T(8,128)} %get-tuple-element.61.so), channel_id=1, source_target_pairs={{0,63},{1,2},{2,1},{3,4},{4,3},{5,6},{6,5},{7,8},{8,7},{9,10},{10,... | collective-permute-start | bytes 2359304 | tf_op jit(solution)/shard_map/ppermute | solution.py:790
  39.3 0.2 multiply_reduce_fusion
  40.0 0.1 copy.17
  40.1 0.7 reshape.87.send_rows
  40.8 0.1 convert_reduce_fusion
  40.9 0.2 select_reduce_fusion
  41.1 17.6 %collective-permute-done.2.ho = f32[3,512,128]{2,1,0:T(8,128)S(1)} collective-permute-done((f32[3,512,128]{2,1,0:T(8,128)}, f32[3,512,128]{2,1,0:T(8,128)S(1)}, u32[]{:S(2)}, u32[]{:S(2)}) %collective-permute-start.2) | collective-permute-done | bytes 786464 | tf_op jit(solution)/shard_map/ppermute | solution.py:790
  58.7 0.9 copy-done.13
  59.6 0.9 copy-done.15
  60.5 1.1 copy-done.11
  61.6 1.1 copy-done.12
  62.8 1.1 copy-done.14
  63.9 1.1 copy-done.16
  65.0 1.6 copy-done.25
  66.6 1.0 copy-done.29
  67.7 0.9 copy-done.32
  68.6 7.6 %first_block.1 = (f32[3,512,128]{2,1,0:T(8,128)}, f32[1,512,128]{2,1,0:T(8,128)S(1)}, f32[4,512,128]{2,1,0:T(8,128)S(1)}, f32[32,128]{1,0:T(8,128)S(1)}) custom-call(s32[2]{0:T(128)S(1)} %copy-done, f32[3,512,128]{2,1,0:T(8,128)S(1)} %copy-done.11, f32[3,512,128]{2,1,0:T(8,128)S(1)} %copy-done.12, f32[2,512,128]{2,1,0:T(8,128)S(1)} %copy-done.29, ...), custom_call_target="tpu_custom_call" | custom-call | flops 5000000000 | bytes 1048576 | tf_op jit(solution)/shard_map/first_block/pallas_call | solution.py:488
  76.2 0.8 copy-done.17
  77.0 0.7 copy-done.23
  77.7 2.3 collective-permute-start.6
  80.0 0.6 collective-permute-start.7
  80.6 17.4 %collective-permute-done.7.surf = f32[32,128]{1,0:T(8,128)S(1)} collective-permute-done((f32[32,128]{1,0:T(8,128)S(1)}, f32[32,128]{1,0:T(8,128)S(1)}, u32[]{:S(2)}, u32[]{:S(2)}) %collective-permute-start.7) | collective-permute-done | bytes 16416 | tf_op jit(solution)/shard_map/ppermute | solution.py:796
  98.0 0.6 copy-done.36
  98.6 1.6 offer.1
  100.1 8.3 %all-to-all-start = ((f32[64,8,128]{2,1,0:T(8,128)}), f32[64,8,128]{2,1,0:T(8,128)S(1)}, u32[]{:S(2)}, u32[]{:S(2)}) async-start(f32[64,8,128]{2,1,0:T(8,128)} %bitcast.27), calls=%async_computation | async-start | bytes 524288 | tf_op jit(solution)/shard_map/all_to_all | solution.py:800
  108.4 4.9 %collective-permute-start.12 = (f32[1,512,128]{2,1,0:T(8,128)}, f32[1,512,128]{2,1,0:T(8,128)S(1)}, u32[]{:S(2)}, u32[]{:S(2)}) collective-permute-start(f32[1,512,128]{2,1,0:T(8,128)} %get-tuple-element.92), channel_id=1, source_target_pairs={{0,63},{1,2},{2,1},{3,4},{4,3},{5,6},{6,5},{7,8},{8,7},{9,10},{10,... | collective-permute-start | bytes 786440 | tf_op jit(solution)/shard_map/ppermute | solution.py:790
  113.3 5.9 %all-to-all-done = f32[64,8,128]{2,1,0:T(8,128)S(1)} async-done(((f32[64,8,128]{2,1,0:T(8,128)}), f32[64,8,128]{2,1,0:T(8,128)S(1)}, u32[]{:S(2)}, u32[]{:S(2)}) %all-to-all-start) | async-done | bytes 262176 | tf_op jit(solution)/shard_map/all_to_all | solution.py:800
  119.2 1.3 collective-permute-start.8
  120.5 2.2 copy-done.3
  122.7 2.4 remap.1
  125.1 5.0 %collective-permute-start.10 = (f32[16,128]{1,0:T(8,128)S(1)}, f32[16,128]{1,0:T(8,128)S(1)}, u32[]{:S(2)}, u32[]{:S(2)}) collective-permute-start(f32[16,128]{1,0:T(8,128)S(1)} %get-tuple-element.90), channel_id=1, source_target_pairs={{0,63},{1,2},{2,1},{3,4},{4,3},{5,6},{6,5},{7,8},{8,7},{9,10},{10,... | collective-permute-start | bytes 24584 | tf_op jit(solution)/shard_map/ppermute | solution.py:790
  130.1 0.7 copy-done.20
  130.8 1.9 collective-permute-done.10.so
  132.8 0.9 copy-done.9
  133.7 1.1 copy-done.10
  134.8 0.9 copy-done.21
  135.8 21.8 %middle_block.1 = (f32[8,512,128]{2,1,0:T(8,128)S(1)}, f32[8,512,128]{2,1,0:T(8,128)}, f32[3,512,128]{2,1,0:T(8,128)}, f32[1,512,128]{2,1,0:T(8,128)}, f32[4,512...) custom-call(s32[2]{0:T(128)S(1)} %copy-done.1, ...), custom_call_target="tpu_custom_call" | custom-call | flops 15000000512 | bytes 1048576 | tf_op jit(solution)/shard_map/middle_block/pallas_call | solution.py:579
  157.6 5.0 %collective-permute-start.13 = (f32[16,128]{1,0:T(8,128)S(1)}, f32[16,128]{1,0:T(8,128)S(1)}, u32[]{:S(2)}, u32[]{:S(2)}) collective-permute-start(f32[16,128]{1,0:T(8,128)S(1)} %get-tuple-element.99), channel_id=1, source_target_pairs={{0,63},{1,2},{2,1},{3,4},{4,3},{5,6},{6,5},{7,8},{8,7},{9,10},{10,... | collective-permute-start | bytes 24584 | tf_op jit(solution)/shard_map/ppermute | solution.py:790
  162.6 2.6 %collective-permute-done.13.so = f32[16,128]{1,0:T(8,128)S(1)} collective-permute-done((f32[16,128]{1,0:T(8,128)S(1)}, f32[16,128]{1,0:T(8,128)S(1)}, u32[]{:S(2)}, u32[]{:S(2)}) %collective-permute-start.13) | collective-permute-done | bytes 8224 | tf_op jit(solution)/shard_map/ppermute | solution.py:790
  165.2 5.0 %collective-permute-start.15 = (f32[3,512,128]{2,1,0:T(8,128)}, f32[3,512,128]{2,1,0:T(8,128)}, u32[]{:S(2)}, u32[]{:S(2)}) collective-permute-start(f32[3,512,128]{2,1,0:T(8,128)} %get-tuple-element.101), channel_id=1, source_target_pairs={{0,63},{1,2},{2,1},{3,4},{4,3},{5,6},{6,5},{7,8},{8,7},{9,10},{10,... | collective-permute-start | bytes 2359304 | tf_op jit(solution)/shard_map/ppermute | solution.py:790
  170.2 2.0 remap_back.1
  172.2 23.9 %all_to_all.10 = f32[64,8,128]{2,1,0:T(8,128)} all-to-all(f32[64,8,128]{2,1,0:T(8,128)S(1)} %bitcast.23), channel_id=1, replica_groups=mesh['comp'=2,'tile'=64] {'tile'}, dimensions={0} | all-to-all | bytes 524288 | tf_op jit(solution)/shard_map/all_to_all | solution.py:800
  196.1 2.3 collect.1
  198.3 0.5 collective-permute-start.18
  198.8 5.0 %collective-permute-done.18.s = f32[32,128]{1,0:T(8,128)S(1)} collective-permute-done((f32[32,128]{1,0:T(8,128)}, f32[32,128]{1,0:T(8,128)S(1)}, u32[]{:S(2)}, u32[]{:S(2)}) %collective-permute-start.18) | collective-permute-done | bytes 16416 | tf_op jit(solution)/shard_map/ppermute | solution.py:796
  203.7 3.0 %collective-permute-done.16.r1 = f32[1,512,128]{2,1,0:T(8,128)S(1)} collective-permute-done((f32[1,512,128]{2,1,0:T(8,128)}, f32[1,512,128]{2,1,0:T(8,128)S(1)}, u32[]{:S(2)}, u32[]{:S(2)}) %collective-permute-start.16) | collective-permute-done | bytes 262176 | tf_op jit(solution)/shard_map/ppermute | solution.py:790
  206.8 1.0 copy-done.19
  207.8 0.9 copy-done.31
  208.7 1.6 copy-done.34
  210.3 12.2 %last_block.1 = (f32[8,512,128]{2,1,0:T(8,128)S(1)}, f32[4,512,128]{2,1,0:T(8,128)S(1)}, f32[4,512,128]{2,1,0:T(8,128)S(1)}) custom-call(s32[2]{0:T(128)S(1)} %copy-done.2, f32[8,512,128]{2,1,0:T(8,128)S(1)} %copy-done.34, f32[3,512,128]{2,1,0:T(8,128)} %collective-permute-done.15.r0, f32[1,512,128]{2,1,0:T(8,128)S(1)} %collective-permute-done.16.r1, ...), custom_call_target="tpu_custom_call" | custom-call | flops 7500000256 | bytes 1048576 | tf_op jit(solution)/shard_map/last_block/pallas_call | solution.py:650
  222.5 2.3 collective-permute-start.19
  224.9 2.3 to_raw.1
  227.2 19.5 %collective-permute-done.19.outer = f32[4,512,128]{2,1,0:T(8,128)S(1)} collective-permute-done((f32[4,512,128]{2,1,0:T(8,128)S(1)}, f32[4,512,128]{2,1,0:T(8,128)S(1)}, u32[]{:S(2)}, u32[]{:S(2)}) %collective-permute-start.19) | collective-permute-done | bytes 1048608 | tf_op jit(solution)/shard_map/ppermute | solution.py:790
  246.7 2.6 %grad_out.1 = f32[1024,512]{1,0:T(8,128)} custom-call(s32[2]{0:T(128)S(1)} %copy-done.2, f32[8,512,128]{2,1,0:T(8,128)S(1)} %get-tuple-element.109.x, f32[4,512,128]{2,1,0:T(8,128)S(1)} %collective-permute-done.19.outer, f32[4,512,128]{2,1,0:T(8,128)S(1)} %collective-permute-done.20.inner), custom_call_target="tpu_custom_call" | custom-call | flops 2000000000 | bytes 1048576 | tf_op jit(solution)/shard_map/grad_out/pallas_call | solution.py:203
  (94 shorter events, 0.6 us)
Async XLA Ops:
  5.3 34.1 %collective-permute-start.4 = (f32[2,512,128]{2,1,0:T(8,128)}, f32[2,512,128]{2,1,0:T(8,128)S(1)}, u32[]{:S(2)}, u32[]{:S(2)}) collective-permute-start(f32[2,512,128]{2,1,0:T(8,128)} %get-tuple-element.64), channel_id=1, source_target_pairs={{0,63},{1,2},{2,1},{3,4},{4,3},{5,6},{6,5},{7,8},{8,7},{9,10},{10,... | collective-permute-start | bytes 1572872 | tf_op jit(solution)/shard_map/ppermute | solution.py:790
  11.2 4.7 %copy-start.5 = (f32[1,128,8,512]{3,2,1,0:T(8,128)S(1)}, f32[1,128,8,512]{3,2,1,0:T(8,128)}, u32[]{:S(2)}) copy-start(f32[1,128,8,512]{3,2,1,0:T(8,128)} %param.11) | copy-start | bytes 6291460
  14.8 14.8 %collective-permute-start = (f32[1,512,128]{2,1,0:T(8,128)}, f32[1,512,128]{2,1,0:T(8,128)}, u32[]{:S(2)}, u32[]{:S(2)}) collective-permute-start(f32[1,512,128]{2,1,0:T(8,128)} %get-tuple-element.58), channel_id=1, source_target_pairs={{0,63},{1,2},{2,1},{3,4},{4,3},{5,6},{6,5},{7,8},{8,7},{9,10},{10,... | collective-permute-start | bytes 786440 | tf_op jit(solution)/shard_map/ppermute | solution.py:790
  15.3 14.2 %collective-permute-start.1 = (f32[1,512,128]{2,1,0:T(8,128)}, f32[1,512,128]{2,1,0:T(8,128)}, u32[]{:S(2)}, u32[]{:S(2)}) collective-permute-start(f32[1,512,128]{2,1,0:T(8,128)} %get-tuple-element.59), channel_id=1, source_target_pairs={{0,1},{1,0},{2,3},{3,2},{4,5},{5,4},{6,7},{7,6},{8,9},{9,8},{10,11... | collective-permute-start | bytes 786440 | tf_op jit(solution)/shard_map/ppermute | solution.py:793
  15.3 25.8 %collective-permute-start.5 = (f32[3,512,128]{2,1,0:T(8,128)}, f32[3,512,128]{2,1,0:T(8,128)S(1)}, u32[]{:S(2)}, u32[]{:S(2)}) collective-permute-start(f32[3,512,128]{2,1,0:T(8,128)} %get-tuple-element.66), channel_id=1, source_target_pairs={{0,1},{1,0},{2,3},{3,2},{4,5},{5,4},{6,7},{7,6},{8,9},{9,8},{10,11... | collective-permute-start | bytes 2359304 | tf_op jit(solution)/shard_map/ppermute | solution.py:793
  17.2 1.3 copy-start.26
  29.6 9.7 %copy-start.38 = (s32[2,64,8]{1,2,0:T(8,128)S(1)}, s32[2,64,8]{1,2,0:T(8,128)}, u32[]{:S(2)}) copy-start(s32[2,64,8]{1,2,0:T(8,128)} %param.15) | copy-start | bytes 12292
  29.6 10.1 %copy-start.39 = (s32[1,1,8]{2,1,0:T(1,128)S(1)}, s32[1,1,8]{2,1,0:T(1,128)}, u32[]{:S(2)}) copy-start(s32[1,1,8]{2,1,0:T(1,128)} %param.18) | copy-start | bytes 100
  29.6 10.3 %copy-start.37 = (s32[8,512]{1,0:T(8,128)S(1)}, s32[8,512]{1,0:T(8,128)}, u32[]{:S(2)}) copy-start(s32[8,512]{1,0:T(8,128)} %mask.1) | copy-start | bytes 49156
  29.6 10.3 %copy-start.35 = (s32[2,64,64]{2,1,0:T(8,128)S(1)}, s32[2,64,64]{2,1,0:T(8,128)}, u32[]{:S(2)}) copy-start(s32[2,64,64]{2,1,0:T(8,128)} %param.16) | copy-start | bytes 98308
  29.6 11.3 %copy-start.40 = (s32[1,1,64]{2,1,0:T(1,128)S(1)}, s32[1,1,64]{2,1,0:T(1,128)}, u32[]{:S(2)}) copy-start(s32[1,1,64]{2,1,0:T(1,128)} %param.17) | copy-start | bytes 772
  29.6 30.9 %copy-start = (s32[2]{0:T(128)S(1)}, s32[2]{0:T(128)}, u32[]{:S(2)}) copy-start(s32[2]{0:T(128)} %pad_add_fusion.me) | copy-start | bytes 28
  36.3 22.3 %collective-permute-start.2 = (f32[3,512,128]{2,1,0:T(8,128)}, f32[3,512,128]{2,1,0:T(8,128)S(1)}, u32[]{:S(2)}, u32[]{:S(2)}) collective-permute-start(f32[3,512,128]{2,1,0:T(8,128)} %get-tuple-element.61.so), channel_id=1, source_target_pairs={{0,63},{1,2},{2,1},{3,4},{4,3},{5,6},{6,5},{7,8},{8,7},{9,10},{10,... | collective-permute-start | bytes 2359304 | tf_op jit(solution)/shard_map/ppermute | solution.py:790
  39.3 20.3 %collective-permute-start.3 = (f32[3,512,128]{2,1,0:T(8,128)}, f32[3,512,128]{2,1,0:T(8,128)S(1)}, u32[]{:S(2)}, u32[]{:S(2)}) collective-permute-start(f32[3,512,128]{2,1,0:T(8,128)} %get-tuple-element.62.si), channel_id=1, source_target_pairs={{0,1},{1,0},{2,3},{3,2},{4,5},{5,4},{6,7},{7,6},{8,9},{9,8},{10,11... | collective-permute-start | bytes 2359304 | tf_op jit(solution)/shard_map/ppermute | solution.py:793
  41.1 35.0 %copy-start.6 = (f32[3,512,128]{2,1,0:T(8,128)}, f32[3,512,128]{2,1,0:T(8,128)S(1)}, u32[]{:S(2)}) copy-start(f32[3,512,128]{2,1,0:T(8,128)S(1)} %collective-permute-done.5.di) | copy-start | bytes 2359300
  58.7 0.9 copy-start.13
  59.6 0.9 copy-start.15
  60.5 1.1 copy-start.11
  61.6 1.1 copy-start.12
  62.8 1.1 copy-start.14
  63.9 1.1 copy-start.16
  65.0 1.6 copy-start.25
  66.6 1.0 copy-start.29
  67.7 0.9 copy-start.32
  68.6 52.0 %copy-start.1 = (s32[2]{0:T(128)S(1)}, s32[2]{0:T(128)}, u32[]{:S(2)}) copy-start(s32[2]{0:T(128)} %pad_add_fusion.me) | copy-start | bytes 28
  76.2 0.8 copy-start.17
  77.0 0.7 copy-start.23
  77.7 56.0 %collective-permute-start.9 = (f32[4,512,128]{2,1,0:T(8,128)S(1)}, f32[4,512,128]{2,1,0:T(8,128)S(1)}, u32[]{:S(2)}, u32[]{:S(2)}) collective-permute-start(f32[4,512,128]{2,1,0:T(8,128)S(1)} %get-tuple-element.80.v2), channel_id=1, source_target_pairs={{0,1},{1,0},{2,3},{3,2},{4,5},{5,4},{6,7},{7,6},{8,9},{9,8},{10,11... | collective-permute-start | bytes 3145736 | tf_op jit(solution)/shard_map/ppermute | solution.py:793
  77.7 55.1 %collective-permute-start.6 = (f32[3,512,128]{2,1,0:T(8,128)}, f32[3,512,128]{2,1,0:T(8,128)S(1)}, u32[]{:S(2)}, u32[]{:S(2)}) collective-permute-start(f32[3,512,128]{2,1,0:T(8,128)} %get-tuple-element.78.v0), channel_id=1, source_target_pairs={{0,63},{1,2},{2,1},{3,4},{4,3},{5,6},{6,5},{7,8},{8,7},{9,10},{10,... | collective-permute-start | bytes 2359304 | tf_op jit(solution)/shard_map/ppermute | solution.py:790
  80.0 18.0 %collective-permute-start.7 = (f32[32,128]{1,0:T(8,128)S(1)}, f32[32,128]{1,0:T(8,128)S(1)}, u32[]{:S(2)}, u32[]{:S(2)}) collective-permute-start(f32[32,128]{1,0:T(8,128)S(1)} %get-tuple-element.82), channel_id=1, source_target_pairs={{0,64},{64,0},{1,65},{65,1},{2,66},{66,2},{3,67},{67,3},{4,68},{68... | collective-permute-start | bytes 49160 | tf_op jit(solution)/shard_map/ppermute | solution.py:796
  98.0 0.6 copy-start.36
  100.1 19.1 %all-to-all-start = ((f32[64,8,128]{2,1,0:T(8,128)}), f32[64,8,128]{2,1,0:T(8,128)S(1)}, u32[]{:S(2)}, u32[]{:S(2)}) async-start(f32[64,8,128]{2,1,0:T(8,128)} %bitcast.27), calls=%async_computation | async-start | bytes 524288 | tf_op jit(solution)/shard_map/all_to_all | solution.py:800
  108.4 21.7 %collective-permute-start.12 = (f32[1,512,128]{2,1,0:T(8,128)}, f32[1,512,128]{2,1,0:T(8,128)S(1)}, u32[]{:S(2)}, u32[]{:S(2)}) collective-permute-start(f32[1,512,128]{2,1,0:T(8,128)} %get-tuple-element.92), channel_id=1, source_target_pairs={{0,63},{1,2},{2,1},{3,4},{4,3},{5,6},{6,5},{7,8},{8,7},{9,10},{10,... | collective-permute-start | bytes 786440 | tf_op jit(solution)/shard_map/ppermute | solution.py:790
  119.2 13.5 %collective-permute-start.8 = (f32[1,512,128]{2,1,0:T(8,128)}, f32[1,512,128]{2,1,0:T(8,128)S(1)}, u32[]{:S(2)}, u32[]{:S(2)}) collective-permute-start(f32[1,512,128]{2,1,0:T(8,128)} %copy-done.23), channel_id=1, source_target_pairs={{0,63},{1,2},{2,1},{3,4},{4,3},{5,6},{6,5},{7,8},{8,7},{9,10},{10,... | collective-permute-start | bytes 786440 | tf_op jit(solution)/shard_map/ppermute | solution.py:790
  120.5 2.2 copy-start.3
  122.7 11.0 %copy-start.7 = (f32[3,512,128]{2,1,0:T(8,128)S(1)}, f32[3,512,128]{2,1,0:T(8,128)}, u32[]{:S(2)}) copy-start(f32[3,512,128]{2,1,0:T(8,128)} %copy-done.6) | copy-start | bytes 2359300
  122.7 11.0 %copy-start.18 = (f32[2,512,128]{2,1,0:T(8,128)S(1)}, f32[2,512,128]{2,1,0:T(8,128)}, u32[]{:S(2)}) copy-start(f32[2,512,128]{2,1,0:T(8,128)} %copy-done.17) | copy-start | bytes 1572868
  122.7 11.0 %copy-start.24 = (f32[1,512,128]{2,1,0:T(8,128)S(1)}, f32[1,512,128]{2,1,0:T(8,128)}, u32[]{:S(2)}) copy-start(f32[1,512,128]{2,1,0:T(8,128)} %copy-done.23) | copy-start | bytes 786436
  122.7 11.0 %copy-start.30 = (bf16[256,256]{1,0:T(8,128)(2,1)S(1)}, bf16[256,256]{1,0:T(8,128)(2,1)}, u32[]{:S(2)}) copy-start(bf16[256,256]{1,0:T(8,128)(2,1)} %get-tuple-element.94.w2b) | copy-start | bytes 393220
  122.7 11.0 %copy-start.33 = (bf16[256,256]{1,0:T(8,128)(2,1)S(1)}, bf16[256,256]{1,0:T(8,128)(2,1)}, u32[]{:S(2)}) copy-start(bf16[256,256]{1,0:T(8,128)(2,1)} %get-tuple-element.77.w2.w2f) | copy-start | bytes 393220
  125.1 7.7 %collective-permute-start.10 = (f32[16,128]{1,0:T(8,128)S(1)}, f32[16,128]{1,0:T(8,128)S(1)}, u32[]{:S(2)}, u32[]{:S(2)}) collective-permute-start(f32[16,128]{1,0:T(8,128)S(1)} %get-tuple-element.90), channel_id=1, source_target_pairs={{0,63},{1,2},{2,1},{3,4},{4,3},{5,6},{6,5},{7,8},{8,7},{9,10},{10,... | collective-permute-start | bytes 24584 | tf_op jit(solution)/shard_map/ppermute | solution.py:790
  130.1 0.7 copy-start.20
  130.8 1.9 collective-permute-start.11
  132.8 0.9 copy-start.9
  133.7 1.1 copy-start.10
  134.8 0.9 copy-start.21
  135.8 34.4 %copy-start.4 = (f32[1,64,128,128]{3,2,1,0:T(8,128)S(1)}, f32[1,64,128,128]{3,2,1,0:T(8,128)}, u32[]{:S(2)}) copy-start(f32[1,64,128,128]{3,2,1,0:T(8,128)} %param.19) | copy-start | bytes 12582916
  157.6 14.6 %copy-start.27 = (f32[8,512,128]{2,1,0:T(8,128)}, f32[8,512,128]{2,1,0:T(8,128)S(1)}, u32[]{:S(2)}) copy-start(f32[8,512,128]{2,1,0:T(8,128)S(1)} %get-tuple-element.95.x) | copy-start | bytes 6291460
  157.6 7.7 %collective-permute-start.13 = (f32[16,128]{1,0:T(8,128)S(1)}, f32[16,128]{1,0:T(8,128)S(1)}, u32[]{:S(2)}, u32[]{:S(2)}) collective-permute-start(f32[16,128]{1,0:T(8,128)S(1)} %get-tuple-element.99), channel_id=1, source_target_pairs={{0,63},{1,2},{2,1},{3,4},{4,3},{5,6},{6,5},{7,8},{8,7},{9,10},{10,... | collective-permute-start | bytes 24584 | tf_op jit(solution)/shard_map/ppermute | solution.py:790
  162.6 2.6 %collective-permute-start.14 = (f32[16,128]{1,0:T(8,128)S(1)}, f32[16,128]{1,0:T(8,128)S(1)}, u32[]{:S(2)}, u32[]{:S(2)}) collective-permute-start(f32[16,128]{1,0:T(8,128)S(1)} %get-tuple-element.100), channel_id=1, source_target_pairs={{0,1},{1,0},{2,3},{3,2},{4,5},{5,4},{6,7},{7,6},{8,9},{9,8},{10,11... | collective-permute-start | bytes 24584 | tf_op jit(solution)/shard_map/ppermute | solution.py:793
  165.2 41.5 %collective-permute-start.17 = (f32[4,512,128]{2,1,0:T(8,128)S(1)}, f32[4,512,128]{2,1,0:T(8,128)S(1)}, u32[]{:S(2)}, u32[]{:S(2)}) collective-permute-start(f32[4,512,128]{2,1,0:T(8,128)S(1)} %get-tuple-element.107), channel_id=1, source_target_pairs={{0,1},{1,0},{2,3},{3,2},{4,5},{5,4},{6,7},{7,6},{8,9},{9,8},{10,11... | collective-permute-start | bytes 3145736 | tf_op jit(solution)/shard_map/ppermute | solution.py:793
  165.2 41.5 %collective-permute-start.15 = (f32[3,512,128]{2,1,0:T(8,128)}, f32[3,512,128]{2,1,0:T(8,128)}, u32[]{:S(2)}, u32[]{:S(2)}) collective-permute-start(f32[3,512,128]{2,1,0:T(8,128)} %get-tuple-element.101), channel_id=1, source_target_pairs={{0,63},{1,2},{2,1},{3,4},{4,3},{5,6},{6,5},{7,8},{8,7},{9,10},{10,... | collective-permute-start | bytes 2359304 | tf_op jit(solution)/shard_map/ppermute | solution.py:790
  170.2 36.6 %copy-start.2 = (s32[2]{0:T(128)S(1)}, s32[2]{0:T(128)}, u32[]{:S(2)}) copy-start(s32[2]{0:T(128)} %pad_add_fusion.me) | copy-start | bytes 28
  170.2 36.6 %copy-start.8 = (f32[3,512,128]{2,1,0:T(8,128)S(1)}, f32[3,512,128]{2,1,0:T(8,128)}, u32[]{:S(2)}) copy-start(f32[3,512,128]{2,1,0:T(8,128)} %copy-done.6) | copy-start | bytes 2359300
  170.2 36.6 %copy-start.22 = (f32[1,512,128]{2,1,0:T(8,128)S(1)}, f32[1,512,128]{2,1,0:T(8,128)}, u32[]{:S(2)}) copy-start(f32[1,512,128]{2,1,0:T(8,128)} %copy-done.20) | copy-start | bytes 786436
  196.1 10.7 %collective-permute-start.16 = (f32[1,512,128]{2,1,0:T(8,128)}, f32[1,512,128]{2,1,0:T(8,128)S(1)}, u32[]{:S(2)}, u32[]{:S(2)}) collective-permute-start(f32[1,512,128]{2,1,0:T(8,128)} %get-tuple-element.106), channel_id=1, source_target_pairs={{0,63},{1,2},{2,1},{3,4},{4,3},{5,6},{6,5},{7,8},{8,7},{9,10},{10,... | collective-permute-start | bytes 786440 | tf_op jit(solution)/shard_map/ppermute | solution.py:790
  198.3 5.4 %collective-permute-start.18 = (f32[32,128]{1,0:T(8,128)}, f32[32,128]{1,0:T(8,128)S(1)}, u32[]{:S(2)}, u32[]{:S(2)}) collective-permute-start(f32[32,128]{1,0:T(8,128)} %collect.1), channel_id=1, source_target_pairs={{0,64},{64,0},{1,65},{65,1},{2,66},{66,2},{3,67},{67,3},{4,68},{68... | collective-permute-start | bytes 49160 | tf_op jit(solution)/shard_map/ppermute | solution.py:796
  206.8 1.0 copy-start.19
  207.8 0.9 copy-start.31
  208.7 1.6 copy-start.34
  210.3 14.5 %copy-start.28 = (f32[8,512,128]{2,1,0:T(8,128)S(1)}, f32[8,512,128]{2,1,0:T(8,128)}, u32[]{:S(2)}) copy-start(f32[8,512,128]{2,1,0:T(8,128)} %copy-done.27) | copy-start | bytes 6291460
  222.5 24.2 %collective-permute-start.19 = (f32[4,512,128]{2,1,0:T(8,128)S(1)}, f32[4,512,128]{2,1,0:T(8,128)S(1)}, u32[]{:S(2)}, u32[]{:S(2)}) collective-permute-start(f32[4,512,128]{2,1,0:T(8,128)S(1)} %get-tuple-element.110), channel_id=1, source_target_pairs={{0,63},{1,2},{2,1},{3,4},{4,3},{5,6},{6,5},{7,8},{8,7},{9,10},{10,... | collective-permute-start | bytes 3145736 | tf_op jit(solution)/shard_map/ppermute | solution.py:790
  224.9 21.8 %collective-permute-start.20 = (f32[4,512,128]{2,1,0:T(8,128)S(1)}, f32[4,512,128]{2,1,0:T(8,128)S(1)}, u32[]{:S(2)}, u32[]{:S(2)}) collective-permute-start(f32[4,512,128]{2,1,0:T(8,128)S(1)} %get-tuple-element.111), channel_id=1, source_target_pairs={{0,1},{1,0},{2,3},{3,2},{4,5},{5,4},{6,7},{7,6},{8,9},{9,8},{10,11... | collective-permute-start | bytes 3145736 | tf_op jit(solution)/shard_map/ppermute | solution.py:793

commit v6 on v5

--- a/solution.py
+++ b/solution.py
@@ -65,8 +65,8 @@
     return buf[j, pl.ds(r, 128, stride=8), :].T
 
 
-def start_in_kernel(me, x, outer, inner, full, buf, out, sems, osems):
-    odd = parity(me)
+def start_in_kernel(x, outer, inner, full, buf, out, sems, osems):
+    odd = lax.rem(lax.axis_index("tile"), 2)
     c = start_raw(x, buf, sems)
     todo = []
     for j in range(4):
@@ -81,17 +81,17 @@
         d.wait()
 
 
-def start_in(me, x):
+def start_in(x):
     return pl.pallas_call(
         start_in_kernel,
         out_shape=(sds(1, LON, LEV), sds(1, LON, LEV), sds(8, LON, LEV)),
-        in_specs=[SM, ANY],
+        in_specs=[ANY],
         out_specs=(ANY,) * 3,
         scratch_shapes=[RAW, ROWS, dma_sems(4), dma_sems(3, 4)],
         compiler_params=params(60),
         cost_estimate=cost(4),
         name="start_in",
-    )(me, x)
+    )(x)
 
 
 def diff_in_kernel(me, x, mask, outer, third, inner, full, buf, out, sems, osems):
@@ -374,16 +374,19 @@
 ]
 U_SCRATCH = pltpu.VMEM((NR, LON, 128), F32)
 COLS = pltpu.VMEM((128, 128), F32)
-PARTS = (sds(3, LON, LEV), sds(1, LON, LEV), sds(4, LON, LEV))
+
+
+def part_shapes(n):
+    return sds(n, LON, LEV), sds(4 - n, LON, LEV), sds(4, LON, LEV)
 
 
 def near_far(up, dn, odd):
     return up + (dn - up) * odd, dn + (up - dn) * odd
 
 
-def edge_refs(v, up, dn, odd, cut):
+def edge_refs(v, up, dn, odd, cut, n):
     outer, inner = near_far(up, dn, odd)
-    return cut(v, outer, 3), cut(v, outer + 3, 1), cut(v, inner, 4)
+    return cut(v, outer, n), cut(v, outer + n, 4 - n), cut(v, inner, 4)
 
 
 def diffusion_copies(d, odd, dt, do, dx, di):
@@ -479,7 +482,7 @@
     forward_step(va, vb, h, d, w2, 2)
     forward_step(vb, va, h, d, w2, 3)
     forward_step(va, vb, h, d, w2, 4, last=True)
-    c = copies(sems, list(zip(edge_refs(vb, 5, 9, odd, tile_rows), (o0, o1, o2))))
+    c = copies(sems, list(zip(edge_refs(vb, 5, 9, odd, tile_rows, 2), (o0, o1, o2))))
     o_surf[...] = gather_surface(lambda r, j: vb[r + 5, pl.ds(OFF + 128 * j, 128), :], 8)[0:32]
     wait(*c)
 
@@ -487,11 +490,11 @@
 def first_block(*args):
     return pl.pallas_call(
         first_kernel,
-        out_shape=PARTS + (sds(32, 128),),
+        out_shape=part_shapes(2) + (sds(32, 128),),
         in_specs=[SM] + [ANY] * 8 + [VM],
         out_specs=(ANY,) * 3 + (VM,),
         scratch_shapes=BLOCK_SCRATCH + [dma_sems(8)],
-        compiler_params=params(),
+        compiler_params=params(60),
         cost_estimate=cost(10),
         name="first_block",
     )(*args)
@@ -502,8 +505,8 @@
     o_final, o_adj, o0, o1, o2, o_s, o_so, o_si, va, vb, h, d, u, mm, cols, sems,
 ):
     odd = parity(me)
-    own = edge_refs(va, 5, 9, odd, tile_rows)
-    far = edge_refs(va, 1, 13, odd, tile_rows)
+    own = edge_refs(va, 5, 9, odd, tile_rows, 2)
+    far = edge_refs(va, 1, 13, odd, tile_rows, 2)
     c = copies(
         sems,
         [
@@ -565,7 +568,7 @@
     push_block(vb, va, u, h, d, w2b)
     out = copies(
         sems,
-        list(zip(edge_refs(u, 1, 13, odd, plain_rows), (o0, o1, o2)))
+        list(zip(edge_refs(u, 1, 13, odd, plain_rows, 3), (o0, o1, o2)))
         + [(u.at[pl.ds(5, 8)], o_adj)],
     )
     cols[...] = gather_surface(lambda r, j: u[r + 1, pl.ds(128 * j, 128), :], 16)
@@ -579,7 +582,7 @@
     return pl.pallas_call(
         middle_kernel,
         out_shape=(
-            sds(8, LON, LEV), sds(8, LON, LEV), *PARTS,
+            sds(8, LON, LEV), sds(8, LON, LEV), *part_shapes(3),
             sds(32, 128), sds(16, 128), sds(16, 128),
         ),
         in_specs=[SM] + [ANY] * 6 + [VM] * 3 + [ANY] * 5 + [VM] * 2,
@@ -597,7 +600,7 @@
     va, vb, h, d, u, got, base, cols, sems,
 ):
     odd = parity(me)
-    parts = edge_refs(got, 0, 4, odd, plain_rows)
+    parts = edge_refs(got, 0, 4, odd, plain_rows, 3)
     c = copies(
         sems,
         [
@@ -801,7 +804,7 @@
         return x.reshape(512, 128)
 
     me = jnp.stack([own_tile, component]).astype(jnp.int32)
-    e_o, e_i, start = start_in(me, starting_perturbation.reshape(1024, LON))
+    e_o, e_i, start = start_in(starting_perturbation.reshape(1024, LON))
     eo, ei = far(e_o), near(e_i)
     d_o, d_x, d_i, dt = diff_in(me, diffusion.reshape(1024, LON), ocean_mask)
     do, di = far(d_o), near(d_i)
@@ -846,7 +849,6 @@
         me, v0, v1, v2, h0, h1, h2, fix, fo, fi, dt, do, dx, di, measured, w2f, w2b
     )
     ro, ri = far(s0_o), near(s0_i)
-    a0, a2, ro, ri = lax.optimization_barrier((a0, a2, ro, ri))
     r0, r2 = far(a0), near(a2)
     offered = remap_back(me, ids, pick, dest, s0, ro, ri, weights, sea32)
     back = exchange(offered)

time: 253 us -> 248 us (0.980)
  waiting for transfers between devices: 84 us -> 96.7 us
  local copies, waits for them, and re-layouts: 23.9 us -> 11.6 us
  blocking collectives: 23.9 us -> 18.3 us
    ppermute x11, waiting for transfers between devices: 55.7 us -> 83.8 us  [far(): return lax.ppermute(x, 'tile', across)]
    ppermute x2, waiting for transfers between devices: 22.4 us -> 6.02 us  [swap(): return lax.ppermute(x, 'comp', [(0, 1), (1, 0)])]
    unnamed x82 -> x60, local copies, waits for them, and re-layouts: 22.8 us -> 10.5 us
    all_to_all x1, blocking collectives: 23.9 us -> 18.3 us  [exchange(): x = lax.all_to_all(x, 'tile', split_axis=0, concat_axis=0, tiled=True)]
    ppermute x11, starting transfers between devices: 35.2 us -> 31.5 us  [far(): return lax.ppermute(x, 'tile', across)]
    pallas_call x1, Pallas kernels: 7.59 us -> 10.6 us  [first_block(): pl.pallas_call(first_kernel, out_shape=part_shapes(2) + (sds(32, 128),),...]
  transfers between devices with their start and end apart: 22 -> 22, of which waited for: 9 -> 11; matrix products, arithmetic and copies ran while one was open for 1% -> 1% of each run, Pallas kernels for 9% -> 9%
where the time goes in v6:
time: 248 us; the launch traced here: 245 us
  waiting for transfers between devices  96.7 us (39%)
  Pallas kernels  72.6 us (29%)
  starting transfers between devices  43 us (17%)
  blocking collectives  18.3 us (7%)
  local copies, waits for them, and re-layouts  11.6 us (5%)
    ppermute x11, waiting for transfers between devices, far(): return lax.ppermute(x, 'tile', across)  83.8 us
    ppermute x11, starting transfers between devices, far(): return lax.ppermute(x, 'tile', across)  31.5 us
    pallas_call x1, Pallas kernels, middle_block(): pl.pallas_call(middle_kernel, out_shape=(sds(8, LON, LEV), sds(8, LON, LE...  21.5 us
    all_to_all x1, blocking collectives, exchange(): x = lax.all_to_all(x, 'tile', split_axis=0, concat_axis=0, tiled=True)  18.3 us
    pallas_call x1, Pallas kernels, last_block(): pl.pallas_call(last_kernel, out_shape=(sds(8, LON, LEV), sds(4, LON, LEV)...  12.2 us
    pallas_call x1, Pallas kernels, first_block(): pl.pallas_call(first_kernel, out_shape=part_shapes(2) + (sds(32, 128),),...  10.6 us
    unnamed x60, local copies, waits for them, and re-layouts  10.5 us
    all_to_all x1, starting transfers between devices, exchange(): x = lax.all_to_all(x, 'tile', split_axis=0, concat_axis=0, tiled=True)  8.56 us
  transfers between devices with their start and end apart: 22, of which 11 were waited for; matrix products, arithmetic and copies ran while one was open for 1% of the time, Pallas kernels for 9%

profile of v6, /device:TPU:8, one launch (start us, length us, event | category | flops | bytes accessed | tf_op | source)
XLA Modules:
  0.0 244.6 jit_solution(7473774685497026443)
XLA Ops:
  0.6 0.6 pad_add_fusion.me
  1.3 4.0 %diff_in.1 = (f32[2,512,128]{2,1,0:T(8,128)}, f32[1,512,128]{2,1,0:T(8,128)}, f32[3,512,128]{2,1,0:T(8,128)}, f32[8,512,128]{2,1,0:T(8,128)}) custom-call(s32[2]{0:T(128)} %pad_add_fusion.me, f32[1024,512]{1,0:T(8,128)} %bitcast.32, s32[8,512]{1,0:T(8,128)} %mask.1), custom_call_target="tpu_custom_call" | custom-call | flops 2000000000 | bytes 1048576 | tf_op jit(solution)/shard_map/diff_in/pallas_call | solution.py:116
  5.3 5.9 %collective-permute-start.4 = (f32[2,512,128]{2,1,0:T(8,128)}, f32[2,512,128]{2,1,0:T(8,128)}, u32[]{:S(2)}, u32[]{:S(2)}) collective-permute-start(f32[2,512,128]{2,1,0:T(8,128)} %get-tuple-element.60), channel_id=1, source_target_pairs={{0,63},{1,2},{2,1},{3,4},{4,3},{5,6},{6,5},{7,8},{8,7},{9,10},{10,... | collective-permute-start | bytes 1572872 | tf_op jit(solution)/shard_map/ppermute | solution.py:793
  11.2 3.0 %start_in.1 = (f32[1,512,128]{2,1,0:T(8,128)}, f32[1,512,128]{2,1,0:T(8,128)}, f32[8,512,128]{2,1,0:T(8,128)}) custom-call(f32[1024,512]{1,0:T(8,128)} %bitcast.33), custom_call_target="tpu_custom_call" | custom-call | flops 2000000000 | bytes 1048576 | tf_op jit(solution)/shard_map/start_in/pallas_call | solution.py:85
  14.2 0.5 collective-permute-start
  14.7 0.5 collective-permute-start.5
  15.2 1.3 to_rows.1.m
  16.5 1.4 copy-done.12
  17.9 11.6 %collective-permute-done.eo = f32[1,512,128]{2,1,0:T(8,128)S(1)} collective-permute-done((f32[1,512,128]{2,1,0:T(8,128)}, f32[1,512,128]{2,1,0:T(8,128)S(1)}, u32[]{:S(2)}, u32[]{:S(2)}) %collective-permute-start) | collective-permute-done | bytes 262176 | tf_op jit(solution)/shard_map/ppermute | solution.py:793
  29.5 0.7 copy-done.28
  30.2 0.1 copy-done.29
  30.3 6.8 %first_step.1 = (f32[3,512,128]{2,1,0:T(8,128)}, f32[3,512,128]{2,1,0:T(8,128)}, f32[2,512,128]{2,1,0:T(8,128)}, bf16[256,256]{1,0:T(8,128)(2,1)}, bf16[256,256]{1,0:T(8,128)(2,1)}) custom-call(s32[2]{0:T(128)} %pad_add_fusion.me, f32[8,512,128]{2,1,0:T(8,128)} %get-tuple-element.53.own, f32[1,512,128]{2,1,0:T(8,128)} %copy-done.28, ...), custom_call_target="tpu_custom_call" | custom-call | flops 2000000000 | bytes 1048576 | tf_op jit(solution)/shard_map/first_step/pallas_call | solution.py:448
  37.1 2.9 %collective-permute-start.2 = (f32[3,512,128]{2,1,0:T(8,128)}, f32[3,512,128]{2,1,0:T(8,128)S(1)}, u32[]{:S(2)}, u32[]{:S(2)}) collective-permute-start(f32[3,512,128]{2,1,0:T(8,128)} %get-tuple-element.57.so), channel_id=1, source_target_pairs={{0,63},{1,2},{2,1},{3,4},{4,3},{5,6},{6,5},{7,8},{8,7},{9,10},{10,... | collective-permute-start | bytes 2359304 | tf_op jit(solution)/shard_map/ppermute | solution.py:793
  40.0 0.2 multiply_reduce_fusion
  40.2 0.1 broadcast_in_dim.9
  40.3 0.1 mul.57
  40.4 0.1 broadcast_in_dim.8
  40.5 0.1 reshape.86
  40.6 0.1 copy.16
  40.7 0.1 copy.17
  40.8 0.7 reshape.87.send_rows
  41.4 0.1 convert_reduce_fusion
  41.6 0.2 select_reduce_fusion
  41.8 17.6 %collective-permute-done.2.ho = f32[3,512,128]{2,1,0:T(8,128)S(1)} collective-permute-done((f32[3,512,128]{2,1,0:T(8,128)}, f32[3,512,128]{2,1,0:T(8,128)S(1)}, u32[]{:S(2)}, u32[]{:S(2)}) %collective-permute-start.2) | collective-permute-done | bytes 786464 | tf_op jit(solution)/shard_map/ppermute | solution.py:793
  59.4 0.9 copy-done.25
  60.3 0.3 copy-done.26
  60.6 10.6 %first_block.1 = (f32[2,512,128]{2,1,0:T(8,128)}, f32[2,512,128]{2,1,0:T(8,128)}, f32[4,512,128]{2,1,0:T(8,128)}, f32[32,128]{1,0:T(8,128)}) custom-call(s32[2]{0:T(128)} %pad_add_fusion.me, f32[3,512,128]{2,1,0:T(8,128)} %get-tuple-element.57.so, f32[3,512,128]{2,1,0:T(8,128)} %get-tuple-element.58.si, f32[2,512,128]{2,1,0:T(8,128)} %get-tuple-element.59.mid, ...), custom_call_target="tpu_custom_call" | custom-call | flops 5000000000 | bytes 1048576 | tf_op jit(solution)/shard_map/first_block/pallas_call | solution.py:491
  71.2 0.1 collective-permute-start.9
  71.3 1.5 collective-permute-start.7
  72.8 2.5 %collective-permute-done.7.surf = f32[32,128]{1,0:T(8,128)S(1)} collective-permute-done((f32[32,128]{1,0:T(8,128)}, f32[32,128]{1,0:T(8,128)S(1)}, u32[]{:S(2)}, u32[]{:S(2)}) %collective-permute-start.7) | collective-permute-done | bytes 16416 | tf_op jit(solution)/shard_map/ppermute | solution.py:799
  75.3 0.6 copy-done.20
  75.9 1.6 offer.1
  77.6 8.6 %all-to-all-start = ((f32[64,8,128]{2,1,0:T(8,128)}), f32[64,8,128]{2,1,0:T(8,128)S(1)}, u32[]{:S(2)}, u32[]{:S(2)}) async-start(f32[64,8,128]{2,1,0:T(8,128)} %bitcast.27), calls=%async_computation | async-start | bytes 524288 | tf_op jit(solution)/shard_map/all_to_all | solution.py:803
  86.1 4.9 %collective-permute-start.6 = (f32[2,512,128]{2,1,0:T(8,128)}, f32[2,512,128]{2,1,0:T(8,128)S(1)}, u32[]{:S(2)}, u32[]{:S(2)}) collective-permute-start(f32[2,512,128]{2,1,0:T(8,128)} %get-tuple-element.74.v0), channel_id=1, source_target_pairs={{0,63},{1,2},{2,1},{3,4},{4,3},{5,6},{6,5},{7,8},{8,7},{9,10},{10,... | collective-permute-start | bytes 1572872 | tf_op jit(solution)/shard_map/ppermute | solution.py:793
  91.0 5.9 %all-to-all-done = f32[64,8,128]{2,1,0:T(8,128)S(1)} async-done(((f32[64,8,128]{2,1,0:T(8,128)}), f32[64,8,128]{2,1,0:T(8,128)S(1)}, u32[]{:S(2)}, u32[]{:S(2)}) %all-to-all-start) | async-done | bytes 262176 | tf_op jit(solution)/shard_map/all_to_all | solution.py:803
  96.9 1.3 collective-permute-start.8
  98.2 5.0 %collective-permute-start.12 = (f32[1,512,128]{2,1,0:T(8,128)S(1)}, f32[1,512,128]{2,1,0:T(8,128)S(1)}, u32[]{:S(2)}, u32[]{:S(2)}) collective-permute-start(f32[1,512,128]{2,1,0:T(8,128)S(1)} %copy-done.27), channel_id=1, source_target_pairs={{0,63},{1,2},{2,1},{3,4},{4,3},{5,6},{6,5},{7,8},{8,7},{9,10},{10,... | collective-permute-start | bytes 786440 | tf_op jit(solution)/shard_map/ppermute | solution.py:793
  103.2 2.2 copy-done.2
  105.4 2.4 remap.1
  107.8 1.4 collective-permute-start.10
  109.1 13.2 %collective-permute-done.12.dx = f32[1,512,128]{2,1,0:T(8,128)S(1)} collective-permute-done((f32[1,512,128]{2,1,0:T(8,128)S(1)}, f32[1,512,128]{2,1,0:T(8,128)S(1)}, u32[]{:S(2)}, u32[]{:S(2)}) %collective-permute-start.12) | collective-permute-done | bytes 262176 | tf_op jit(solution)/shard_map/ppermute | solution.py:793
  122.3 0.2 collective-permute-done.10.so
  122.5 1.0 collective-permute-done.11.si
  123.5 0.8 copy-done.10
  124.4 1.0 copy-done.11
  125.5 21.5 %middle_block.1 = (f32[8,512,128]{2,1,0:T(8,128)S(1)}, f32[8,512,128]{2,1,0:T(8,128)}, f32[3,512,128]{2,1,0:T(8,128)}, f32[1,512,128]{2,1,0:T(8,128)}, f32[4,512...) custom-call(s32[2]{0:T(128)S(1)} %copy-done, ...), custom_call_target="tpu_custom_call" | custom-call | flops 15000000512 | bytes 1048576 | tf_op jit(solution)/shard_map/middle_block/pallas_call | solution.py:582
  147.0 0.3 collective-permute-start.17
  147.3 2.1 collective-permute-start.13
  149.4 4.1 %collective-permute-start.14 = (f32[16,128]{1,0:T(8,128)S(1)}, f32[16,128]{1,0:T(8,128)S(1)}, u32[]{:S(2)}, u32[]{:S(2)}) collective-permute-start(f32[16,128]{1,0:T(8,128)S(1)} %get-tuple-element.96), channel_id=1, source_target_pairs={{0,63},{1,2},{2,1},{3,4},{4,3},{5,6},{6,5},{7,8},{8,7},{9,10},{10,... | collective-permute-start | bytes 24584 | tf_op jit(solution)/shard_map/ppermute | solution.py:793
  153.5 16.3 %collective-permute-done.14.so = f32[16,128]{1,0:T(8,128)S(1)} collective-permute-done((f32[16,128]{1,0:T(8,128)S(1)}, f32[16,128]{1,0:T(8,128)S(1)}, u32[]{:S(2)}, u32[]{:S(2)}) %collective-permute-start.14) | collective-permute-done | bytes 8224 | tf_op jit(solution)/shard_map/ppermute | solution.py:793
  169.9 2.0 remap_back.1
  171.8 18.3 %all_to_all.10 = f32[64,8,128]{2,1,0:T(8,128)} all-to-all(f32[64,8,128]{2,1,0:T(8,128)S(1)} %bitcast.23), channel_id=1, replica_groups=mesh['comp'=2,'tile'=64] {'tile'}, dimensions={0} | all-to-all | bytes 524288 | tf_op jit(solution)/shard_map/all_to_all | solution.py:803
  190.1 1.7 collective-permute-start.16
  191.9 2.2 collect.1
  194.1 0.6 collective-permute-start.18
  194.7 3.5 %collective-permute-done.18.s = f32[32,128]{1,0:T(8,128)S(1)} collective-permute-done((f32[32,128]{1,0:T(8,128)}, f32[32,128]{1,0:T(8,128)S(1)}, u32[]{:S(2)}, u32[]{:S(2)}) %collective-permute-start.18) | collective-permute-done | bytes 16416 | tf_op jit(solution)/shard_map/ppermute | solution.py:799
  198.2 3.6 %collective-permute-done.16.r1 = f32[1,512,128]{2,1,0:T(8,128)S(1)} collective-permute-done((f32[1,512,128]{2,1,0:T(8,128)}, f32[1,512,128]{2,1,0:T(8,128)S(1)}, u32[]{:S(2)}, u32[]{:S(2)}) %collective-permute-start.16) | collective-permute-done | bytes 262176 | tf_op jit(solution)/shard_map/ppermute | solution.py:793
  201.8 0.9 copy-done.16
  202.7 1.6 copy-done.18
  204.3 12.2 %last_block.1 = (f32[8,512,128]{2,1,0:T(8,128)S(1)}, f32[4,512,128]{2,1,0:T(8,128)S(1)}, f32[4,512,128]{2,1,0:T(8,128)S(1)}) custom-call(s32[2]{0:T(128)S(1)} %copy-done.1, f32[8,512,128]{2,1,0:T(8,128)S(1)} %copy-done.18, f32[3,512,128]{2,1,0:T(8,128)} %collective-permute-done.13.r0, f32[1,512,128]{2,1,0:T(8,128)S(1)} %collective-permute-done.16.r1, ...), custom_call_target="tpu_custom_call" | custom-call | flops 7500000256 | bytes 1048576 | tf_op jit(solution)/shard_map/last_block/pallas_call | solution.py:653
  216.5 1.7 collective-permute-start.19
  218.2 2.3 to_raw.1
  220.5 21.3 %collective-permute-done.19.outer = f32[4,512,128]{2,1,0:T(8,128)S(1)} collective-permute-done((f32[4,512,128]{2,1,0:T(8,128)S(1)}, f32[4,512,128]{2,1,0:T(8,128)S(1)}, u32[]{:S(2)}, u32[]{:S(2)}) %collective-permute-start.19) | collective-permute-done | bytes 1048608 | tf_op jit(solution)/shard_map/ppermute | solution.py:793
  241.8 2.6 %grad_out.1 = f32[1024,512]{1,0:T(8,128)} custom-call(s32[2]{0:T(128)S(1)} %copy-done.1, f32[8,512,128]{2,1,0:T(8,128)S(1)} %get-tuple-element.101.x, f32[4,512,128]{2,1,0:T(8,128)S(1)} %collective-permute-done.19.outer, f32[4,512,128]{2,1,0:T(8,128)S(1)} %collective-permute-done.20.inner), custom_call_target="tpu_custom_call" | custom-call | flops 2000000000 | bytes 1048576 | tf_op jit(solution)/shard_map/grad_out/pallas_call | solution.py:203
  (72 shorter events, 0.2 us)
Async XLA Ops:
  5.3 34.8 %collective-permute-start.4 = (f32[2,512,128]{2,1,0:T(8,128)}, f32[2,512,128]{2,1,0:T(8,128)}, u32[]{:S(2)}, u32[]{:S(2)}) collective-permute-start(f32[2,512,128]{2,1,0:T(8,128)} %get-tuple-element.60), channel_id=1, source_target_pairs={{0,63},{1,2},{2,1},{3,4},{4,3},{5,6},{6,5},{7,8},{8,7},{9,10},{10,... | collective-permute-start | bytes 1572872 | tf_op jit(solution)/shard_map/ppermute | solution.py:793
  11.2 4.0 %copy-start.4 = (f32[1,128,8,512]{3,2,1,0:T(8,128)S(1)}, f32[1,128,8,512]{3,2,1,0:T(8,128)}, u32[]{:S(2)}) copy-start(f32[1,128,8,512]{3,2,1,0:T(8,128)} %param.11) | copy-start | bytes 6291460
  14.2 15.3 %collective-permute-start = (f32[1,512,128]{2,1,0:T(8,128)}, f32[1,512,128]{2,1,0:T(8,128)S(1)}, u32[]{:S(2)}, u32[]{:S(2)}) collective-permute-start(f32[1,512,128]{2,1,0:T(8,128)} %get-tuple-element.54), channel_id=1, source_target_pairs={{0,63},{1,2},{2,1},{3,4},{4,3},{5,6},{6,5},{7,8},{8,7},{9,10},{10,... | collective-permute-start | bytes 786440 | tf_op jit(solution)/shard_map/ppermute | solution.py:793
  14.7 14.8 %collective-permute-start.1 = (f32[1,512,128]{2,1,0:T(8,128)}, f32[1,512,128]{2,1,0:T(8,128)S(1)}, u32[]{:S(2)}, u32[]{:S(2)}) collective-permute-start(f32[1,512,128]{2,1,0:T(8,128)} %get-tuple-element.55), channel_id=1, source_target_pairs={{0,1},{1,0},{2,3},{3,2},{4,5},{5,4},{6,7},{7,6},{8,9},{9,8},{10,11... | collective-permute-start | bytes 786440 | tf_op jit(solution)/shard_map/ppermute | solution.py:796
  14.7 27.1 %collective-permute-start.5 = (f32[3,512,128]{2,1,0:T(8,128)}, f32[3,512,128]{2,1,0:T(8,128)S(1)}, u32[]{:S(2)}, u32[]{:S(2)}) collective-permute-start(f32[3,512,128]{2,1,0:T(8,128)} %get-tuple-element.62), channel_id=1, source_target_pairs={{0,1},{1,0},{2,3},{3,2},{4,5},{5,4},{6,7},{7,6},{8,9},{9,8},{10,11... | collective-permute-start | bytes 2359304 | tf_op jit(solution)/shard_map/ppermute | solution.py:796
  16.5 1.4 copy-start.12
  29.5 0.7 copy-start.28
  29.5 0.8 copy-start.29
  30.3 9.8 %copy-start.22 = (s32[2,64,8]{1,2,0:T(8,128)S(1)}, s32[2,64,8]{1,2,0:T(8,128)}, u32[]{:S(2)}) copy-start(s32[2,64,8]{1,2,0:T(8,128)} %param.15) | copy-start | bytes 12292
  30.3 10.1 %copy-start.23 = (s32[1,1,8]{2,1,0:T(1,128)S(1)}, s32[1,1,8]{2,1,0:T(1,128)}, u32[]{:S(2)}) copy-start(s32[1,1,8]{2,1,0:T(1,128)} %param.18) | copy-start | bytes 100
  30.3 10.3 %copy-start.21 = (s32[8,512]{1,0:T(8,128)S(1)}, s32[8,512]{1,0:T(8,128)}, u32[]{:S(2)}) copy-start(s32[8,512]{1,0:T(8,128)} %mask.1) | copy-start | bytes 49156
  30.3 10.3 %copy-start.19 = (s32[2,64,64]{2,1,0:T(8,128)S(1)}, s32[2,64,64]{2,1,0:T(8,128)}, u32[]{:S(2)}) copy-start(s32[2,64,64]{2,1,0:T(8,128)} %param.16) | copy-start | bytes 98308
  30.3 11.3 %copy-start.24 = (s32[1,1,64]{2,1,0:T(1,128)S(1)}, s32[1,1,64]{2,1,0:T(1,128)}, u32[]{:S(2)}) copy-start(s32[1,1,64]{2,1,0:T(1,128)} %param.17) | copy-start | bytes 772
  37.1 22.4 %collective-permute-start.2 = (f32[3,512,128]{2,1,0:T(8,128)}, f32[3,512,128]{2,1,0:T(8,128)S(1)}, u32[]{:S(2)}, u32[]{:S(2)}) collective-permute-start(f32[3,512,128]{2,1,0:T(8,128)} %get-tuple-element.57.so), channel_id=1, source_target_pairs={{0,63},{1,2},{2,1},{3,4},{4,3},{5,6},{6,5},{7,8},{8,7},{9,10},{10,... | collective-permute-start | bytes 2359304 | tf_op jit(solution)/shard_map/ppermute | solution.py:793
  40.0 19.4 %collective-permute-start.3 = (f32[3,512,128]{2,1,0:T(8,128)}, f32[3,512,128]{2,1,0:T(8,128)S(1)}, u32[]{:S(2)}, u32[]{:S(2)}) collective-permute-start(f32[3,512,128]{2,1,0:T(8,128)} %get-tuple-element.58.si), channel_id=1, source_target_pairs={{0,1},{1,0},{2,3},{3,2},{4,5},{5,4},{6,7},{7,6},{8,9},{9,8},{10,11... | collective-permute-start | bytes 2359304 | tf_op jit(solution)/shard_map/ppermute | solution.py:796
  41.8 17.6 %copy-start.6 = (f32[3,512,128]{2,1,0:T(8,128)}, f32[3,512,128]{2,1,0:T(8,128)S(1)}, u32[]{:S(2)}) copy-start(f32[3,512,128]{2,1,0:T(8,128)S(1)} %collective-permute-done.5.di) | copy-start | bytes 2359300
  59.4 0.9 copy-start.25
  59.4 1.1 copy-start.26
  60.6 37.6 %copy-start.27 = (f32[1,512,128]{2,1,0:T(8,128)S(1)}, f32[1,512,128]{2,1,0:T(8,128)}, u32[]{:S(2)}) copy-start(f32[1,512,128]{2,1,0:T(8,128)} %get-tuple-element.88) | copy-start | bytes 786436
  60.6 42.6 %copy-start = (s32[2]{0:T(128)S(1)}, s32[2]{0:T(128)}, u32[]{:S(2)}) copy-start(s32[2]{0:T(128)} %pad_add_fusion.me) | copy-start | bytes 28
  71.2 53.1 %collective-permute-start.9 = (f32[4,512,128]{2,1,0:T(8,128)}, f32[4,512,128]{2,1,0:T(8,128)S(1)}, u32[]{:S(2)}, u32[]{:S(2)}) collective-permute-start(f32[4,512,128]{2,1,0:T(8,128)} %get-tuple-element.76.v2), channel_id=1, source_target_pairs={{0,1},{1,0},{2,3},{3,2},{4,5},{5,4},{6,7},{7,6},{8,9},{9,8},{10,11... | collective-permute-start | bytes 3145736 | tf_op jit(solution)/shard_map/ppermute | solution.py:796
  71.3 4.0 %collective-permute-start.7 = (f32[32,128]{1,0:T(8,128)}, f32[32,128]{1,0:T(8,128)S(1)}, u32[]{:S(2)}, u32[]{:S(2)}) collective-permute-start(f32[32,128]{1,0:T(8,128)} %get-tuple-element.78), channel_id=1, source_target_pairs={{0,64},{64,0},{1,65},{65,1},{2,66},{66,2},{3,67},{67,3},{4,68},{68... | collective-permute-start | bytes 49160 | tf_op jit(solution)/shard_map/ppermute | solution.py:799
  75.3 0.6 copy-start.20
  77.6 19.4 %all-to-all-start = ((f32[64,8,128]{2,1,0:T(8,128)}), f32[64,8,128]{2,1,0:T(8,128)S(1)}, u32[]{:S(2)}, u32[]{:S(2)}) async-start(f32[64,8,128]{2,1,0:T(8,128)} %bitcast.27), calls=%async_computation | async-start | bytes 524288 | tf_op jit(solution)/shard_map/all_to_all | solution.py:803
  86.1 37.4 %collective-permute-start.6 = (f32[2,512,128]{2,1,0:T(8,128)}, f32[2,512,128]{2,1,0:T(8,128)S(1)}, u32[]{:S(2)}, u32[]{:S(2)}) collective-permute-start(f32[2,512,128]{2,1,0:T(8,128)} %get-tuple-element.74.v0), channel_id=1, source_target_pairs={{0,63},{1,2},{2,1},{3,4},{4,3},{5,6},{6,5},{7,8},{8,7},{9,10},{10,... | collective-permute-start | bytes 1572872 | tf_op jit(solution)/shard_map/ppermute | solution.py:793
  96.9 27.4 %collective-permute-start.8 = (f32[2,512,128]{2,1,0:T(8,128)}, f32[2,512,128]{2,1,0:T(8,128)S(1)}, u32[]{:S(2)}, u32[]{:S(2)}) collective-permute-start(f32[2,512,128]{2,1,0:T(8,128)} %get-tuple-element.79.v1), channel_id=1, source_target_pairs={{0,63},{1,2},{2,1},{3,4},{4,3},{5,6},{6,5},{7,8},{8,7},{9,10},{10,... | collective-permute-start | bytes 1572872 | tf_op jit(solution)/shard_map/ppermute | solution.py:793
  98.2 24.1 %collective-permute-start.12 = (f32[1,512,128]{2,1,0:T(8,128)S(1)}, f32[1,512,128]{2,1,0:T(8,128)S(1)}, u32[]{:S(2)}, u32[]{:S(2)}) collective-permute-start(f32[1,512,128]{2,1,0:T(8,128)S(1)} %copy-done.27), channel_id=1, source_target_pairs={{0,63},{1,2},{2,1},{3,4},{4,3},{5,6},{6,5},{7,8},{8,7},{9,10},{10,... | collective-permute-start | bytes 786440 | tf_op jit(solution)/shard_map/ppermute | solution.py:793
  103.2 2.2 copy-start.2
  105.4 19.0 %copy-start.5 = (f32[4,512,128]{2,1,0:T(8,128)S(1)}, f32[4,512,128]{2,1,0:T(8,128)}, u32[]{:S(2)}) copy-start(f32[4,512,128]{2,1,0:T(8,128)} %get-tuple-element.76.v2) | copy-start | bytes 3145732
  105.4 19.0 %copy-start.7 = (f32[3,512,128]{2,1,0:T(8,128)S(1)}, f32[3,512,128]{2,1,0:T(8,128)}, u32[]{:S(2)}) copy-start(f32[3,512,128]{2,1,0:T(8,128)} %copy-done.6) | copy-start | bytes 2359300
  105.4 19.0 %copy-start.8 = (f32[2,512,128]{2,1,0:T(8,128)S(1)}, f32[2,512,128]{2,1,0:T(8,128)}, u32[]{:S(2)}) copy-start(f32[2,512,128]{2,1,0:T(8,128)} %get-tuple-element.74.v0) | copy-start | bytes 1572868
  105.4 19.0 %copy-start.9 = (f32[2,512,128]{2,1,0:T(8,128)S(1)}, f32[2,512,128]{2,1,0:T(8,128)}, u32[]{:S(2)}) copy-start(f32[2,512,128]{2,1,0:T(8,128)} %get-tuple-element.79.v1) | copy-start | bytes 1572868
  105.4 19.0 %copy-start.15 = (bf16[256,256]{1,0:T(8,128)(2,1)S(1)}, bf16[256,256]{1,0:T(8,128)(2,1)}, u32[]{:S(2)}) copy-start(bf16[256,256]{1,0:T(8,128)(2,1)} %get-tuple-element.90.w2b) | copy-start | bytes 393220
  105.4 19.0 %copy-start.17 = (bf16[256,256]{1,0:T(8,128)(2,1)S(1)}, bf16[256,256]{1,0:T(8,128)(2,1)}, u32[]{:S(2)}) copy-start(bf16[256,256]{1,0:T(8,128)(2,1)} %get-tuple-element.73.w2.w2f) | copy-start | bytes 393220
  107.8 14.7 %collective-permute-start.10 = (f32[16,128]{1,0:T(8,128)S(1)}, f32[16,128]{1,0:T(8,128)S(1)}, u32[]{:S(2)}, u32[]{:S(2)}) collective-permute-start(f32[16,128]{1,0:T(8,128)S(1)} %get-tuple-element.86), channel_id=1, source_target_pairs={{0,63},{1,2},{2,1},{3,4},{4,3},{5,6},{6,5},{7,8},{8,7},{9,10},{10,... | collective-permute-start | bytes 24584 | tf_op jit(solution)/shard_map/ppermute | solution.py:793
  122.3 1.2 collective-permute-start.11
  123.5 0.9 copy-start.10
  124.4 1.0 copy-start.11
  125.5 44.4 %copy-start.3 = (f32[1,64,128,128]{3,2,1,0:T(8,128)S(1)}, f32[1,64,128,128]{3,2,1,0:T(8,128)}, u32[]{:S(2)}) copy-start(f32[1,64,128,128]{3,2,1,0:T(8,128)} %param.19) | copy-start | bytes 12582916
  147.0 24.8 %copy-start.13 = (f32[8,512,128]{2,1,0:T(8,128)}, f32[8,512,128]{2,1,0:T(8,128)S(1)}, u32[]{:S(2)}) copy-start(f32[8,512,128]{2,1,0:T(8,128)S(1)} %get-tuple-element.91.x) | copy-start | bytes 6291460
  147.0 54.8 %collective-permute-start.17 = (f32[4,512,128]{2,1,0:T(8,128)S(1)}, f32[4,512,128]{2,1,0:T(8,128)S(1)}, u32[]{:S(2)}, u32[]{:S(2)}) collective-permute-start(f32[4,512,128]{2,1,0:T(8,128)S(1)} %get-tuple-element.99), channel_id=1, source_target_pairs={{0,1},{1,0},{2,3},{3,2},{4,5},{5,4},{6,7},{7,6},{8,9},{9,8},{10,11... | collective-permute-start | bytes 3145736 | tf_op jit(solution)/shard_map/ppermute | solution.py:796
  147.3 54.5 %collective-permute-start.13 = (f32[3,512,128]{2,1,0:T(8,128)}, f32[3,512,128]{2,1,0:T(8,128)}, u32[]{:S(2)}, u32[]{:S(2)}) collective-permute-start(f32[3,512,128]{2,1,0:T(8,128)} %get-tuple-element.93), channel_id=1, source_target_pairs={{0,63},{1,2},{2,1},{3,4},{4,3},{5,6},{6,5},{7,8},{8,7},{9,10},{10,... | collective-permute-start | bytes 2359304 | tf_op jit(solution)/shard_map/ppermute | solution.py:793
  149.4 20.4 %collective-permute-start.14 = (f32[16,128]{1,0:T(8,128)S(1)}, f32[16,128]{1,0:T(8,128)S(1)}, u32[]{:S(2)}, u32[]{:S(2)}) collective-permute-start(f32[16,128]{1,0:T(8,128)S(1)} %get-tuple-element.96), channel_id=1, source_target_pairs={{0,63},{1,2},{2,1},{3,4},{4,3},{5,6},{6,5},{7,8},{8,7},{9,10},{10,... | collective-permute-start | bytes 24584 | tf_op jit(solution)/shard_map/ppermute | solution.py:793
  153.5 16.3 %collective-permute-start.15 = (f32[16,128]{1,0:T(8,128)S(1)}, f32[16,128]{1,0:T(8,128)S(1)}, u32[]{:S(2)}, u32[]{:S(2)}) collective-permute-start(f32[16,128]{1,0:T(8,128)S(1)} %get-tuple-element.97), channel_id=1, source_target_pairs={{0,1},{1,0},{2,3},{3,2},{4,5},{5,4},{6,7},{7,6},{8,9},{9,8},{10,11... | collective-permute-start | bytes 24584 | tf_op jit(solution)/shard_map/ppermute | solution.py:796
  169.8 32.0 %copy-start.1 = (s32[2]{0:T(128)S(1)}, s32[2]{0:T(128)}, u32[]{:S(2)}) copy-start(s32[2]{0:T(128)} %pad_add_fusion.me) | copy-start | bytes 28
  190.1 11.7 %collective-permute-start.16 = (f32[1,512,128]{2,1,0:T(8,128)}, f32[1,512,128]{2,1,0:T(8,128)S(1)}, u32[]{:S(2)}, u32[]{:S(2)}) collective-permute-start(f32[1,512,128]{2,1,0:T(8,128)} %get-tuple-element.98), channel_id=1, source_target_pairs={{0,63},{1,2},{2,1},{3,4},{4,3},{5,6},{6,5},{7,8},{8,7},{9,10},{10,... | collective-permute-start | bytes 786440 | tf_op jit(solution)/shard_map/ppermute | solution.py:793
  194.1 4.1 %collective-permute-start.18 = (f32[32,128]{1,0:T(8,128)}, f32[32,128]{1,0:T(8,128)S(1)}, u32[]{:S(2)}, u32[]{:S(2)}) collective-permute-start(f32[32,128]{1,0:T(8,128)} %collect.1), channel_id=1, source_target_pairs={{0,64},{64,0},{1,65},{65,1},{2,66},{66,2},{3,67},{67,3},{4,68},{68... | collective-permute-start | bytes 49160 | tf_op jit(solution)/shard_map/ppermute | solution.py:799
  201.8 0.9 copy-start.16
  202.7 1.6 copy-start.18
  204.3 13.9 %copy-start.14 = (f32[8,512,128]{2,1,0:T(8,128)S(1)}, f32[8,512,128]{2,1,0:T(8,128)}, u32[]{:S(2)}) copy-start(f32[8,512,128]{2,1,0:T(8,128)} %copy-done.13) | copy-start | bytes 6291460
  216.5 25.3 %collective-permute-start.19 = (f32[4,512,128]{2,1,0:T(8,128)S(1)}, f32[4,512,128]{2,1,0:T(8,128)S(1)}, u32[]{:S(2)}, u32[]{:S(2)}) collective-permute-start(f32[4,512,128]{2,1,0:T(8,128)S(1)} %get-tuple-element.102), channel_id=1, source_target_pairs={{0,63},{1,2},{2,1},{3,4},{4,3},{5,6},{6,5},{7,8},{8,7},{9,10},{10,... | collective-permute-start | bytes 3145736 | tf_op jit(solution)/shard_map/ppermute | solution.py:793
  218.2 23.7 %collective-permute-start.20 = (f32[4,512,128]{2,1,0:T(8,128)S(1)}, f32[4,512,128]{2,1,0:T(8,128)S(1)}, u32[]{:S(2)}, u32[]{:S(2)}) collective-permute-start(f32[4,512,128]{2,1,0:T(8,128)S(1)} %get-tuple-element.103), channel_id=1, source_target_pairs={{0,1},{1,0},{2,3},{3,2},{4,5},{5,4},{6,7},{7,6},{8,9},{9,8},{10,11... | collective-permute-start | bytes 3145736 | tf_op jit(solution)/shard_map/ppermute | solution.py:796

commit v7 on v6

--- a/solution.py
+++ b/solution.py
@@ -482,7 +482,7 @@
     forward_step(va, vb, h, d, w2, 2)
     forward_step(vb, va, h, d, w2, 3)
     forward_step(va, vb, h, d, w2, 4, last=True)
-    c = copies(sems, list(zip(edge_refs(vb, 5, 9, odd, tile_rows, 2), (o0, o1, o2))))
+    c = copies(sems, list(zip(edge_refs(vb, 5, 9, odd, tile_rows, 3), (o0, o1, o2))))
     o_surf[...] = gather_surface(lambda r, j: vb[r + 5, pl.ds(OFF + 128 * j, 128), :], 8)[0:32]
     wait(*c)
 
@@ -490,7 +490,7 @@
 def first_block(*args):
     return pl.pallas_call(
         first_kernel,
-        out_shape=part_shapes(2) + (sds(32, 128),),
+        out_shape=part_shapes(3) + (sds(32, 128),),
         in_specs=[SM] + [ANY] * 8 + [VM],
         out_specs=(ANY,) * 3 + (VM,),
         scratch_shapes=BLOCK_SCRATCH + [dma_sems(8)],
@@ -505,8 +505,8 @@
     o_final, o_adj, o0, o1, o2, o_s, o_so, o_si, va, vb, h, d, u, mm, cols, sems,
 ):
     odd = parity(me)
-    own = edge_refs(va, 5, 9, odd, tile_rows, 2)
-    far = edge_refs(va, 1, 13, odd, tile_rows, 2)
+    own = edge_refs(va, 5, 9, odd, tile_rows, 3)
+    far = edge_refs(va, 1, 13, odd, tile_rows, 3)
     c = copies(
         sems,
         [
@@ -753,13 +753,16 @@
     )(me, ids, pick, dest, s, so, si, w, sea)
 
 
-def collect_kernel(me, send_rows, got, o):
-    o[...] = jnp.zeros((32, 128), F32)
+def collect_kernel(me, send_rows, got, o, *sums):
+    for acc in sums:
+        acc[...] = jnp.zeros((32, 128), F32)
     for off in OFFSETS:
         t = lax.rem(me[0] + (off + 64), 64) * 8
         for q in range(8):
+            acc = sums[q % 4]
             at = pl.ds(send_rows[t + q], 1)
-            o[at, :] = o[at, :] + got[pl.ds(t + q, 1), :]
+            acc[at, :] = acc[at, :] + got[pl.ds(t + q, 1), :]
+    o[...] = (sums[0][...] + sums[1][...]) + (sums[2][...] + sums[3][...])
 
 
 def collect(me, send_rows, got):
@@ -768,6 +771,7 @@
         out_shape=sds(32, 128),
         in_specs=[SM, SM, VM],
         out_specs=VM,
+        scratch_shapes=[pltpu.VMEM((32, 128), F32)] * 4,
         name="collect",
     )(me, send_rows, got)
 

time: 248 us -> 253 us (1.020)
  waiting for transfers between devices: 96.7 us -> 102 us
    ppermute x2, waiting for transfers between devices: 6.02 us -> 21.3 us  [swap(): return lax.ppermute(x, 'comp', [(0, 1), (1, 0)])]
    ppermute x11, waiting for transfers between devices: 83.8 us -> 74.6 us  [far(): return lax.ppermute(x, 'tile', across)]
  transfers between devices with their start and end apart: 22 -> 22, of which waited for: 11 -> 9; matrix products, arithmetic and copies ran while one was open for 1% -> 1% of each run, Pallas kernels for 9% -> 8%
where the time goes in v7:
time: 253 us; the launch traced here: 249 us
  waiting for transfers between devices  102 us (40%)
  Pallas kernels  72.1 us (28%)
  starting transfers between devices  42.8 us (17%)
  blocking collectives  18.6 us (7%)
  local copies, waits for them, and re-layouts  11.8 us (5%)
    ppermute x11, waiting for transfers between devices, far(): return lax.ppermute(x, 'tile', across)  74.6 us
    ppermute x11, starting transfers between devices, far(): return lax.ppermute(x, 'tile', across)  32.5 us
    pallas_call x1, Pallas kernels, middle_block(): pl.pallas_call(middle_kernel, out_shape=(sds(8, LON, LEV), sds(8, LON, LE...  21.6 us
    ppermute x2, waiting for transfers between devices, swap(): return lax.ppermute(x, 'comp', [(0, 1), (1, 0)])  21.3 us
    all_to_all x1, blocking collectives, exchange(): x = lax.all_to_all(x, 'tile', split_axis=0, concat_axis=0, tiled=True)  18.6 us
    pallas_call x1, Pallas kernels, last_block(): pl.pallas_call(last_kernel, out_shape=(sds(8, LON, LEV), sds(4, LON, LEV)...  12.2 us
    unnamed x60, local copies, waits for them, and re-layouts  10.7 us
    pallas_call x1, Pallas kernels, first_block(): pl.pallas_call(first_kernel, out_shape=part_shapes(3) + (sds(32, 128),),...  10.6 us
  transfers between devices with their start and end apart: 22, of which 9 were waited for; matrix products, arithmetic and copies ran while one was open for 1% of the time, Pallas kernels for 8%

profile of v7, /device:TPU:8, one launch (start us, length us, event | category | flops | bytes accessed | tf_op | source)
XLA Modules:
  0.0 249.4 jit_solution(16647314226873633677)
XLA Ops:
  0.6 0.6 pad_add_fusion.me
  1.3 4.0 %diff_in.1 = (f32[2,512,128]{2,1,0:T(8,128)}, f32[1,512,128]{2,1,0:T(8,128)}, f32[3,512,128]{2,1,0:T(8,128)}, f32[8,512,128]{2,1,0:T(8,128)}) custom-call(s32[2]{0:T(128)} %pad_add_fusion.me, f32[1024,512]{1,0:T(8,128)} %bitcast.32, s32[8,512]{1,0:T(8,128)} %mask.1), custom_call_target="tpu_custom_call" | custom-call | flops 2000000000 | bytes 1048576 | tf_op jit(solution)/shard_map/diff_in/pallas_call | solution.py:116
  5.3 5.9 %collective-permute-start.4 = (f32[2,512,128]{2,1,0:T(8,128)}, f32[2,512,128]{2,1,0:T(8,128)}, u32[]{:S(2)}, u32[]{:S(2)}) collective-permute-start(f32[2,512,128]{2,1,0:T(8,128)} %get-tuple-element.60), channel_id=1, source_target_pairs={{0,63},{1,2},{2,1},{3,4},{4,3},{5,6},{6,5},{7,8},{8,7},{9,10},{10,... | collective-permute-start | bytes 1572872 | tf_op jit(solution)/shard_map/ppermute | solution.py:797
  11.2 3.0 %start_in.1 = (f32[1,512,128]{2,1,0:T(8,128)}, f32[1,512,128]{2,1,0:T(8,128)}, f32[8,512,128]{2,1,0:T(8,128)}) custom-call(f32[1024,512]{1,0:T(8,128)} %bitcast.33), custom_call_target="tpu_custom_call" | custom-call | flops 2000000000 | bytes 1048576 | tf_op jit(solution)/shard_map/start_in/pallas_call | solution.py:85
  14.2 0.5 collective-permute-start
  14.7 0.0 collective-permute-start.1
  14.7 0.5 collective-permute-start.5
  15.2 1.3 to_rows.1.m
  16.5 1.4 copy-done.12
  17.9 11.6 %collective-permute-done.eo = f32[1,512,128]{2,1,0:T(8,128)S(1)} collective-permute-done((f32[1,512,128]{2,1,0:T(8,128)}, f32[1,512,128]{2,1,0:T(8,128)S(1)}, u32[]{:S(2)}, u32[]{:S(2)}) %collective-permute-start) | collective-permute-done | bytes 262176 | tf_op jit(solution)/shard_map/ppermute | solution.py:797
  29.5 0.7 copy-done.28
  30.2 0.1 copy-done.29
  30.3 0.0 copy-start.24
  30.3 6.7 %first_step.1 = (f32[3,512,128]{2,1,0:T(8,128)}, f32[3,512,128]{2,1,0:T(8,128)}, f32[2,512,128]{2,1,0:T(8,128)}, bf16[256,256]{1,0:T(8,128)(2,1)}, bf16[256,256]{1,0:T(8,128)(2,1)}) custom-call(s32[2]{0:T(128)} %pad_add_fusion.me, f32[8,512,128]{2,1,0:T(8,128)} %get-tuple-element.53.own, f32[1,512,128]{2,1,0:T(8,128)} %copy-done.28, ...), custom_call_target="tpu_custom_call" | custom-call | flops 2000000000 | bytes 1048576 | tf_op jit(solution)/shard_map/first_step/pallas_call | solution.py:448
  37.0 2.9 %collective-permute-start.2 = (f32[3,512,128]{2,1,0:T(8,128)}, f32[3,512,128]{2,1,0:T(8,128)S(1)}, u32[]{:S(2)}, u32[]{:S(2)}) collective-permute-start(f32[3,512,128]{2,1,0:T(8,128)} %get-tuple-element.57.so), channel_id=1, source_target_pairs={{0,63},{1,2},{2,1},{3,4},{4,3},{5,6},{6,5},{7,8},{8,7},{9,10},{10,... | collective-permute-start | bytes 2359304 | tf_op jit(solution)/shard_map/ppermute | solution.py:797
  40.0 0.2 multiply_reduce_fusion
  40.2 0.1 broadcast_in_dim.9
  40.3 0.1 mul.57
  40.4 0.1 broadcast_in_dim.8
  40.4 0.1 reshape.86
  40.5 0.1 copy.16
  40.7 0.1 copy.17
  40.7 0.7 reshape.87.send_rows
  41.4 0.1 convert_reduce_fusion
  41.6 0.2 select_reduce_fusion
  41.8 17.6 %collective-permute-done.2.ho = f32[3,512,128]{2,1,0:T(8,128)S(1)} collective-permute-done((f32[3,512,128]{2,1,0:T(8,128)}, f32[3,512,128]{2,1,0:T(8,128)S(1)}, u32[]{:S(2)}, u32[]{:S(2)}) %collective-permute-start.2) | collective-permute-done | bytes 786464 | tf_op jit(solution)/shard_map/ppermute | solution.py:797
  59.4 0.9 copy-done.25
  60.3 0.3 copy-done.26
  60.6 10.6 %first_block.1 = (f32[3,512,128]{2,1,0:T(8,128)}, f32[1,512,128]{2,1,0:T(8,128)}, f32[4,512,128]{2,1,0:T(8,128)}, f32[32,128]{1,0:T(8,128)}) custom-call(s32[2]{0:T(128)} %pad_add_fusion.me, f32[3,512,128]{2,1,0:T(8,128)} %get-tuple-element.57.so, f32[3,512,128]{2,1,0:T(8,128)} %get-tuple-element.58.si, f32[2,512,128]{2,1,0:T(8,128)} %get-tuple-element.59.mid, ...), custom_call_target="tpu_custom_call" | custom-call | flops 5000000000 | bytes 1048576 | tf_op jit(solution)/shard_map/first_block/pallas_call | solution.py:491
  71.2 0.1 collective-permute-start.9
  71.2 2.3 collective-permute-start.6
  73.5 0.6 collective-permute-start.7
  74.1 17.4 %collective-permute-done.7.surf = f32[32,128]{1,0:T(8,128)S(1)} collective-permute-done((f32[32,128]{1,0:T(8,128)}, f32[32,128]{1,0:T(8,128)S(1)}, u32[]{:S(2)}, u32[]{:S(2)}) %collective-permute-start.7) | collective-permute-done | bytes 16416 | tf_op jit(solution)/shard_map/ppermute | solution.py:803
  91.5 0.6 copy-done.20
  92.1 1.6 offer.1
  93.7 8.3 %all-to-all-start = ((f32[64,8,128]{2,1,0:T(8,128)}), f32[64,8,128]{2,1,0:T(8,128)S(1)}, u32[]{:S(2)}, u32[]{:S(2)}) async-start(f32[64,8,128]{2,1,0:T(8,128)} %bitcast.27), calls=%async_computation | async-start | bytes 524288 | tf_op jit(solution)/shard_map/all_to_all | solution.py:807
  102.0 4.9 %collective-permute-start.12 = (f32[1,512,128]{2,1,0:T(8,128)S(1)}, f32[1,512,128]{2,1,0:T(8,128)S(1)}, u32[]{:S(2)}, u32[]{:S(2)}) collective-permute-start(f32[1,512,128]{2,1,0:T(8,128)S(1)} %copy-done.27), channel_id=1, source_target_pairs={{0,63},{1,2},{2,1},{3,4},{4,3},{5,6},{6,5},{7,8},{8,7},{9,10},{10,... | collective-permute-start | bytes 786440 | tf_op jit(solution)/shard_map/ppermute | solution.py:797
  106.9 5.9 %all-to-all-done = f32[64,8,128]{2,1,0:T(8,128)S(1)} async-done(((f32[64,8,128]{2,1,0:T(8,128)}), f32[64,8,128]{2,1,0:T(8,128)S(1)}, u32[]{:S(2)}, u32[]{:S(2)}) %all-to-all-start) | async-done | bytes 262176 | tf_op jit(solution)/shard_map/all_to_all | solution.py:807
  112.8 1.3 collective-permute-start.8
  114.1 2.2 copy-done.2
  116.3 2.4 remap.1
  118.7 5.0 %collective-permute-start.10 = (f32[16,128]{1,0:T(8,128)S(1)}, f32[16,128]{1,0:T(8,128)S(1)}, u32[]{:S(2)}, u32[]{:S(2)}) collective-permute-start(f32[16,128]{1,0:T(8,128)S(1)} %get-tuple-element.86), channel_id=1, source_target_pairs={{0,63},{1,2},{2,1},{3,4},{4,3},{5,6},{6,5},{7,8},{8,7},{9,10},{10,... | collective-permute-start | bytes 24584 | tf_op jit(solution)/shard_map/ppermute | solution.py:797
  123.7 2.6 %collective-permute-done.10.so = f32[16,128]{1,0:T(8,128)S(1)} collective-permute-done((f32[16,128]{1,0:T(8,128)S(1)}, f32[16,128]{1,0:T(8,128)S(1)}, u32[]{:S(2)}, u32[]{:S(2)}) %collective-permute-start.10) | collective-permute-done | bytes 8224 | tf_op jit(solution)/shard_map/ppermute | solution.py:797
  126.4 0.9 copy-done.9
  127.3 1.1 copy-done.10
  128.5 21.6 %middle_block.1 = (f32[8,512,128]{2,1,0:T(8,128)S(1)}, f32[8,512,128]{2,1,0:T(8,128)}, f32[3,512,128]{2,1,0:T(8,128)}, f32[1,512,128]{2,1,0:T(8,128)}, f32[4,512...) custom-call(s32[2]{0:T(128)S(1)} %copy-done, ...), custom_call_target="tpu_custom_call" | custom-call | flops 15000000512 | bytes 1048576 | tf_op jit(solution)/shard_map/middle_block/pallas_call | solution.py:582
  150.1 0.1 collective-permute-start.17
  150.1 5.0 %collective-permute-start.13 = (f32[3,512,128]{2,1,0:T(8,128)}, f32[3,512,128]{2,1,0:T(8,128)}, u32[]{:S(2)}, u32[]{:S(2)}) collective-permute-start(f32[3,512,128]{2,1,0:T(8,128)} %get-tuple-element.93), channel_id=1, source_target_pairs={{0,63},{1,2},{2,1},{3,4},{4,3},{5,6},{6,5},{7,8},{8,7},{9,10},{10,... | collective-permute-start | bytes 2359304 | tf_op jit(solution)/shard_map/ppermute | solution.py:797
  155.2 1.3 collective-permute-start.14
  156.5 17.8 %collective-permute-done.14.so = f32[16,128]{1,0:T(8,128)S(1)} collective-permute-done((f32[16,128]{1,0:T(8,128)S(1)}, f32[16,128]{1,0:T(8,128)S(1)}, u32[]{:S(2)}, u32[]{:S(2)}) %collective-permute-start.14) | collective-permute-done | bytes 8224 | tf_op jit(solution)/shard_map/ppermute | solution.py:797
  174.3 2.0 remap_back.1
  176.3 18.6 %all_to_all.10 = f32[64,8,128]{2,1,0:T(8,128)} all-to-all(f32[64,8,128]{2,1,0:T(8,128)S(1)} %bitcast.23), channel_id=1, replica_groups=mesh['comp'=2,'tile'=64] {'tile'}, dimensions={0} | all-to-all | bytes 524288 | tf_op jit(solution)/shard_map/all_to_all | solution.py:807
  194.9 1.7 collective-permute-start.16
  196.6 1.8 collect.1
  198.4 0.7 collective-permute-start.18
  199.0 3.9 %collective-permute-done.18.s = f32[32,128]{1,0:T(8,128)S(1)} collective-permute-done((f32[32,128]{1,0:T(8,128)}, f32[32,128]{1,0:T(8,128)S(1)}, u32[]{:S(2)}, u32[]{:S(2)}) %collective-permute-start.18) | collective-permute-done | bytes 16416 | tf_op jit(solution)/shard_map/ppermute | solution.py:803
  203.0 3.6 %collective-permute-done.16.r1 = f32[1,512,128]{2,1,0:T(8,128)S(1)} collective-permute-done((f32[1,512,128]{2,1,0:T(8,128)}, f32[1,512,128]{2,1,0:T(8,128)S(1)}, u32[]{:S(2)}, u32[]{:S(2)}) %collective-permute-start.16) | collective-permute-done | bytes 262176 | tf_op jit(solution)/shard_map/ppermute | solution.py:797
  206.5 0.9 copy-done.16
  207.4 1.6 copy-done.18
  209.0 12.2 %last_block.1 = (f32[8,512,128]{2,1,0:T(8,128)S(1)}, f32[4,512,128]{2,1,0:T(8,128)S(1)}, f32[4,512,128]{2,1,0:T(8,128)S(1)}) custom-call(s32[2]{0:T(128)S(1)} %copy-done.1, f32[8,512,128]{2,1,0:T(8,128)S(1)} %copy-done.18, f32[3,512,128]{2,1,0:T(8,128)} %collective-permute-done.13.r0, f32[1,512,128]{2,1,0:T(8,128)S(1)} %collective-permute-done.16.r1, ...), custom_call_target="tpu_custom_call" | custom-call | flops 7500000256 | bytes 1048576 | tf_op jit(solution)/shard_map/last_block/pallas_call | solution.py:653
  221.3 1.6 collective-permute-start.19
  222.9 2.3 to_raw.1
  225.2 21.4 %collective-permute-done.19.outer = f32[4,512,128]{2,1,0:T(8,128)S(1)} collective-permute-done((f32[4,512,128]{2,1,0:T(8,128)S(1)}, f32[4,512,128]{2,1,0:T(8,128)S(1)}, u32[]{:S(2)}, u32[]{:S(2)}) %collective-permute-start.19) | collective-permute-done | bytes 1048608 | tf_op jit(solution)/shard_map/ppermute | solution.py:797
  246.6 2.6 %grad_out.1 = f32[1024,512]{1,0:T(8,128)} custom-call(s32[2]{0:T(128)S(1)} %copy-done.1, f32[8,512,128]{2,1,0:T(8,128)S(1)} %get-tuple-element.101.x, f32[4,512,128]{2,1,0:T(8,128)S(1)} %collective-permute-done.19.outer, f32[4,512,128]{2,1,0:T(8,128)S(1)} %collective-permute-done.20.inner), custom_call_target="tpu_custom_call" | custom-call | flops 2000000000 | bytes 1048576 | tf_op jit(solution)/shard_map/grad_out/pallas_call | solution.py:203
  (72 shorter events, 0.2 us)
Async XLA Ops:
  5.3 34.7 %collective-permute-start.4 = (f32[2,512,128]{2,1,0:T(8,128)}, f32[2,512,128]{2,1,0:T(8,128)}, u32[]{:S(2)}, u32[]{:S(2)}) collective-permute-start(f32[2,512,128]{2,1,0:T(8,128)} %get-tuple-element.60), channel_id=1, source_target_pairs={{0,63},{1,2},{2,1},{3,4},{4,3},{5,6},{6,5},{7,8},{8,7},{9,10},{10,... | collective-permute-start | bytes 1572872 | tf_op jit(solution)/shard_map/ppermute | solution.py:797
  11.2 4.0 %copy-start.4 = (f32[1,128,8,512]{3,2,1,0:T(8,128)S(1)}, f32[1,128,8,512]{3,2,1,0:T(8,128)}, u32[]{:S(2)}) copy-start(f32[1,128,8,512]{3,2,1,0:T(8,128)} %param.11) | copy-start | bytes 6291460
  14.2 15.3 %collective-permute-start = (f32[1,512,128]{2,1,0:T(8,128)}, f32[1,512,128]{2,1,0:T(8,128)S(1)}, u32[]{:S(2)}, u32[]{:S(2)}) collective-permute-start(f32[1,512,128]{2,1,0:T(8,128)} %get-tuple-element.54), channel_id=1, source_target_pairs={{0,63},{1,2},{2,1},{3,4},{4,3},{5,6},{6,5},{7,8},{8,7},{9,10},{10,... | collective-permute-start | bytes 786440 | tf_op jit(solution)/shard_map/ppermute | solution.py:797
  14.7 14.8 %collective-permute-start.1 = (f32[1,512,128]{2,1,0:T(8,128)}, f32[1,512,128]{2,1,0:T(8,128)S(1)}, u32[]{:S(2)}, u32[]{:S(2)}) collective-permute-start(f32[1,512,128]{2,1,0:T(8,128)} %get-tuple-element.55), channel_id=1, source_target_pairs={{0,1},{1,0},{2,3},{3,2},{4,5},{5,4},{6,7},{7,6},{8,9},{9,8},{10,11... | collective-permute-start | bytes 786440 | tf_op jit(solution)/shard_map/ppermute | solution.py:800
  14.7 27.1 %collective-permute-start.5 = (f32[3,512,128]{2,1,0:T(8,128)}, f32[3,512,128]{2,1,0:T(8,128)S(1)}, u32[]{:S(2)}, u32[]{:S(2)}) collective-permute-start(f32[3,512,128]{2,1,0:T(8,128)} %get-tuple-element.62), channel_id=1, source_target_pairs={{0,1},{1,0},{2,3},{3,2},{4,5},{5,4},{6,7},{7,6},{8,9},{9,8},{10,11... | collective-permute-start | bytes 2359304 | tf_op jit(solution)/shard_map/ppermute | solution.py:800
  16.5 1.4 copy-start.12
  29.5 0.7 copy-start.28
  29.5 0.8 copy-start.29
  30.3 9.7 %copy-start.22 = (s32[2,64,8]{1,2,0:T(8,128)S(1)}, s32[2,64,8]{1,2,0:T(8,128)}, u32[]{:S(2)}) copy-start(s32[2,64,8]{1,2,0:T(8,128)} %param.15) | copy-start | bytes 12292
  30.3 10.1 %copy-start.23 = (s32[1,1,8]{2,1,0:T(1,128)S(1)}, s32[1,1,8]{2,1,0:T(1,128)}, u32[]{:S(2)}) copy-start(s32[1,1,8]{2,1,0:T(1,128)} %param.18) | copy-start | bytes 100
  30.3 10.2 %copy-start.21 = (s32[8,512]{1,0:T(8,128)S(1)}, s32[8,512]{1,0:T(8,128)}, u32[]{:S(2)}) copy-start(s32[8,512]{1,0:T(8,128)} %mask.1) | copy-start | bytes 49156
  30.3 10.3 %copy-start.19 = (s32[2,64,64]{2,1,0:T(8,128)S(1)}, s32[2,64,64]{2,1,0:T(8,128)}, u32[]{:S(2)}) copy-start(s32[2,64,64]{2,1,0:T(8,128)} %param.16) | copy-start | bytes 98308
  30.3 11.3 %copy-start.24 = (s32[1,1,64]{2,1,0:T(1,128)S(1)}, s32[1,1,64]{2,1,0:T(1,128)}, u32[]{:S(2)}) copy-start(s32[1,1,64]{2,1,0:T(1,128)} %param.17) | copy-start | bytes 772
  37.0 22.4 %collective-permute-start.2 = (f32[3,512,128]{2,1,0:T(8,128)}, f32[3,512,128]{2,1,0:T(8,128)S(1)}, u32[]{:S(2)}, u32[]{:S(2)}) collective-permute-start(f32[3,512,128]{2,1,0:T(8,128)} %get-tuple-element.57.so), channel_id=1, source_target_pairs={{0,63},{1,2},{2,1},{3,4},{4,3},{5,6},{6,5},{7,8},{8,7},{9,10},{10,... | collective-permute-start | bytes 2359304 | tf_op jit(solution)/shard_map/ppermute | solution.py:797
  40.0 19.4 %collective-permute-start.3 = (f32[3,512,128]{2,1,0:T(8,128)}, f32[3,512,128]{2,1,0:T(8,128)S(1)}, u32[]{:S(2)}, u32[]{:S(2)}) collective-permute-start(f32[3,512,128]{2,1,0:T(8,128)} %get-tuple-element.58.si), channel_id=1, source_target_pairs={{0,1},{1,0},{2,3},{3,2},{4,5},{5,4},{6,7},{7,6},{8,9},{9,8},{10,11... | collective-permute-start | bytes 2359304 | tf_op jit(solution)/shard_map/ppermute | solution.py:800
  41.8 17.6 %copy-start.6 = (f32[3,512,128]{2,1,0:T(8,128)}, f32[3,512,128]{2,1,0:T(8,128)S(1)}, u32[]{:S(2)}) copy-start(f32[3,512,128]{2,1,0:T(8,128)S(1)} %collective-permute-done.5.di) | copy-start | bytes 2359300
  59.4 0.9 copy-start.25
  59.4 1.2 copy-start.26
  60.6 41.4 %copy-start.27 = (f32[1,512,128]{2,1,0:T(8,128)S(1)}, f32[1,512,128]{2,1,0:T(8,128)}, u32[]{:S(2)}) copy-start(f32[1,512,128]{2,1,0:T(8,128)} %get-tuple-element.88) | copy-start | bytes 786436
  60.6 53.5 %copy-start = (s32[2]{0:T(128)S(1)}, s32[2]{0:T(128)}, u32[]{:S(2)}) copy-start(s32[2]{0:T(128)} %pad_add_fusion.me) | copy-start | bytes 28
  71.2 56.1 %collective-permute-start.9 = (f32[4,512,128]{2,1,0:T(8,128)}, f32[4,512,128]{2,1,0:T(8,128)S(1)}, u32[]{:S(2)}, u32[]{:S(2)}) collective-permute-start(f32[4,512,128]{2,1,0:T(8,128)} %get-tuple-element.76.v2), channel_id=1, source_target_pairs={{0,1},{1,0},{2,3},{3,2},{4,5},{5,4},{6,7},{7,6},{8,9},{9,8},{10,11... | collective-permute-start | bytes 3145736 | tf_op jit(solution)/shard_map/ppermute | solution.py:800
  71.2 55.1 %collective-permute-start.6 = (f32[3,512,128]{2,1,0:T(8,128)}, f32[3,512,128]{2,1,0:T(8,128)S(1)}, u32[]{:S(2)}, u32[]{:S(2)}) collective-permute-start(f32[3,512,128]{2,1,0:T(8,128)} %get-tuple-element.74.v0), channel_id=1, source_target_pairs={{0,63},{1,2},{2,1},{3,4},{4,3},{5,6},{6,5},{7,8},{8,7},{9,10},{10,... | collective-permute-start | bytes 2359304 | tf_op jit(solution)/shard_map/ppermute | solution.py:797
  73.5 18.0 %collective-permute-start.7 = (f32[32,128]{1,0:T(8,128)}, f32[32,128]{1,0:T(8,128)S(1)}, u32[]{:S(2)}, u32[]{:S(2)}) collective-permute-start(f32[32,128]{1,0:T(8,128)} %get-tuple-element.78), channel_id=1, source_target_pairs={{0,64},{64,0},{1,65},{65,1},{2,66},{66,2},{3,67},{67,3},{4,68},{68... | collective-permute-start | bytes 49160 | tf_op jit(solution)/shard_map/ppermute | solution.py:803
  91.5 0.6 copy-start.20
  93.7 19.1 %all-to-all-start = ((f32[64,8,128]{2,1,0:T(8,128)}), f32[64,8,128]{2,1,0:T(8,128)S(1)}, u32[]{:S(2)}, u32[]{:S(2)}) async-start(f32[64,8,128]{2,1,0:T(8,128)} %bitcast.27), calls=%async_computation | async-start | bytes 524288 | tf_op jit(solution)/shard_map/all_to_all | solution.py:807
  102.0 21.7 %collective-permute-start.12 = (f32[1,512,128]{2,1,0:T(8,128)S(1)}, f32[1,512,128]{2,1,0:T(8,128)S(1)}, u32[]{:S(2)}, u32[]{:S(2)}) collective-permute-start(f32[1,512,128]{2,1,0:T(8,128)S(1)} %copy-done.27), channel_id=1, source_target_pairs={{0,63},{1,2},{2,1},{3,4},{4,3},{5,6},{6,5},{7,8},{8,7},{9,10},{10,... | collective-permute-start | bytes 786440 | tf_op jit(solution)/shard_map/ppermute | solution.py:797
  112.8 13.6 %collective-permute-start.8 = (f32[1,512,128]{2,1,0:T(8,128)}, f32[1,512,128]{2,1,0:T(8,128)S(1)}, u32[]{:S(2)}, u32[]{:S(2)}) collective-permute-start(f32[1,512,128]{2,1,0:T(8,128)} %get-tuple-element.79.v1), channel_id=1, source_target_pairs={{0,63},{1,2},{2,1},{3,4},{4,3},{5,6},{6,5},{7,8},{8,7},{9,10},{10,... | collective-permute-start | bytes 786440 | tf_op jit(solution)/shard_map/ppermute | solution.py:797
  114.1 2.2 copy-start.2
  116.3 11.0 %copy-start.5 = (f32[4,512,128]{2,1,0:T(8,128)S(1)}, f32[4,512,128]{2,1,0:T(8,128)}, u32[]{:S(2)}) copy-start(f32[4,512,128]{2,1,0:T(8,128)} %get-tuple-element.76.v2) | copy-start | bytes 3145732
  116.3 11.0 %copy-start.7 = (f32[3,512,128]{2,1,0:T(8,128)S(1)}, f32[3,512,128]{2,1,0:T(8,128)}, u32[]{:S(2)}) copy-start(f32[3,512,128]{2,1,0:T(8,128)} %copy-done.6) | copy-start | bytes 2359300
  116.3 11.0 %copy-start.8 = (f32[3,512,128]{2,1,0:T(8,128)S(1)}, f32[3,512,128]{2,1,0:T(8,128)}, u32[]{:S(2)}) copy-start(f32[3,512,128]{2,1,0:T(8,128)} %get-tuple-element.74.v0) | copy-start | bytes 2359300
  116.3 11.0 %copy-start.11 = (f32[1,512,128]{2,1,0:T(8,128)S(1)}, f32[1,512,128]{2,1,0:T(8,128)}, u32[]{:S(2)}) copy-start(f32[1,512,128]{2,1,0:T(8,128)} %get-tuple-element.79.v1) | copy-start | bytes 786436
  116.3 11.0 %copy-start.15 = (bf16[256,256]{1,0:T(8,128)(2,1)S(1)}, bf16[256,256]{1,0:T(8,128)(2,1)}, u32[]{:S(2)}) copy-start(bf16[256,256]{1,0:T(8,128)(2,1)} %get-tuple-element.90.w2b) | copy-start | bytes 393220
  116.3 11.0 %copy-start.17 = (bf16[256,256]{1,0:T(8,128)(2,1)S(1)}, bf16[256,256]{1,0:T(8,128)(2,1)}, u32[]{:S(2)}) copy-start(bf16[256,256]{1,0:T(8,128)(2,1)} %get-tuple-element.73.w2.w2f) | copy-start | bytes 393220
  118.7 7.7 %collective-permute-start.10 = (f32[16,128]{1,0:T(8,128)S(1)}, f32[16,128]{1,0:T(8,128)S(1)}, u32[]{:S(2)}, u32[]{:S(2)}) collective-permute-start(f32[16,128]{1,0:T(8,128)S(1)} %get-tuple-element.86), channel_id=1, source_target_pairs={{0,63},{1,2},{2,1},{3,4},{4,3},{5,6},{6,5},{7,8},{8,7},{9,10},{10,... | collective-permute-start | bytes 24584 | tf_op jit(solution)/shard_map/ppermute | solution.py:797
  123.7 2.6 %collective-permute-start.11 = (f32[16,128]{1,0:T(8,128)S(1)}, f32[16,128]{1,0:T(8,128)S(1)}, u32[]{:S(2)}, u32[]{:S(2)}) collective-permute-start(f32[16,128]{1,0:T(8,128)S(1)} %get-tuple-element.87), channel_id=1, source_target_pairs={{0,1},{1,0},{2,3},{3,2},{4,5},{5,4},{6,7},{7,6},{8,9},{9,8},{10,11... | collective-permute-start | bytes 24584 | tf_op jit(solution)/shard_map/ppermute | solution.py:800
  126.4 0.9 copy-start.9
  127.3 1.1 copy-start.10
  128.5 45.8 %copy-start.3 = (f32[1,64,128,128]{3,2,1,0:T(8,128)S(1)}, f32[1,64,128,128]{3,2,1,0:T(8,128)}, u32[]{:S(2)}) copy-start(f32[1,64,128,128]{3,2,1,0:T(8,128)} %param.19) | copy-start | bytes 12582916
  150.0 26.2 %copy-start.13 = (f32[8,512,128]{2,1,0:T(8,128)}, f32[8,512,128]{2,1,0:T(8,128)S(1)}, u32[]{:S(2)}) copy-start(f32[8,512,128]{2,1,0:T(8,128)S(1)} %get-tuple-element.91.x) | copy-start | bytes 6291460
  150.1 56.5 %collective-permute-start.17 = (f32[4,512,128]{2,1,0:T(8,128)S(1)}, f32[4,512,128]{2,1,0:T(8,128)S(1)}, u32[]{:S(2)}, u32[]{:S(2)}) collective-permute-start(f32[4,512,128]{2,1,0:T(8,128)S(1)} %get-tuple-element.99), channel_id=1, source_target_pairs={{0,1},{1,0},{2,3},{3,2},{4,5},{5,4},{6,7},{7,6},{8,9},{9,8},{10,11... | collective-permute-start | bytes 3145736 | tf_op jit(solution)/shard_map/ppermute | solution.py:800
  150.1 56.4 %collective-permute-start.13 = (f32[3,512,128]{2,1,0:T(8,128)}, f32[3,512,128]{2,1,0:T(8,128)}, u32[]{:S(2)}, u32[]{:S(2)}) collective-permute-start(f32[3,512,128]{2,1,0:T(8,128)} %get-tuple-element.93), channel_id=1, source_target_pairs={{0,63},{1,2},{2,1},{3,4},{4,3},{5,6},{6,5},{7,8},{8,7},{9,10},{10,... | collective-permute-start | bytes 2359304 | tf_op jit(solution)/shard_map/ppermute | solution.py:797
  155.2 19.1 %collective-permute-start.14 = (f32[16,128]{1,0:T(8,128)S(1)}, f32[16,128]{1,0:T(8,128)S(1)}, u32[]{:S(2)}, u32[]{:S(2)}) collective-permute-start(f32[16,128]{1,0:T(8,128)S(1)} %get-tuple-element.96), channel_id=1, source_target_pairs={{0,63},{1,2},{2,1},{3,4},{4,3},{5,6},{6,5},{7,8},{8,7},{9,10},{10,... | collective-permute-start | bytes 24584 | tf_op jit(solution)/shard_map/ppermute | solution.py:797
  156.5 17.8 %collective-permute-start.15 = (f32[16,128]{1,0:T(8,128)S(1)}, f32[16,128]{1,0:T(8,128)S(1)}, u32[]{:S(2)}, u32[]{:S(2)}) collective-permute-start(f32[16,128]{1,0:T(8,128)S(1)} %get-tuple-element.97), channel_id=1, source_target_pairs={{0,1},{1,0},{2,3},{3,2},{4,5},{5,4},{6,7},{7,6},{8,9},{9,8},{10,11... | collective-permute-start | bytes 24584 | tf_op jit(solution)/shard_map/ppermute | solution.py:800
  174.3 32.3 %copy-start.1 = (s32[2]{0:T(128)S(1)}, s32[2]{0:T(128)}, u32[]{:S(2)}) copy-start(s32[2]{0:T(128)} %pad_add_fusion.me) | copy-start | bytes 28
  194.9 11.7 %collective-permute-start.16 = (f32[1,512,128]{2,1,0:T(8,128)}, f32[1,512,128]{2,1,0:T(8,128)S(1)}, u32[]{:S(2)}, u32[]{:S(2)}) collective-permute-start(f32[1,512,128]{2,1,0:T(8,128)} %get-tuple-element.98), channel_id=1, source_target_pairs={{0,63},{1,2},{2,1},{3,4},{4,3},{5,6},{6,5},{7,8},{8,7},{9,10},{10,... | collective-permute-start | bytes 786440 | tf_op jit(solution)/shard_map/ppermute | solution.py:797
  198.4 4.6 %collective-permute-start.18 = (f32[32,128]{1,0:T(8,128)}, f32[32,128]{1,0:T(8,128)S(1)}, u32[]{:S(2)}, u32[]{:S(2)}) collective-permute-start(f32[32,128]{1,0:T(8,128)} %collect.1), channel_id=1, source_target_pairs={{0,64},{64,0},{1,65},{65,1},{2,66},{66,2},{3,67},{67,3},{4,68},{68... | collective-permute-start | bytes 49160 | tf_op jit(solution)/shard_map/ppermute | solution.py:803
  206.5 0.9 copy-start.16
  207.4 1.6 copy-start.18
  209.0 13.9 %copy-start.14 = (f32[8,512,128]{2,1,0:T(8,128)S(1)}, f32[8,512,128]{2,1,0:T(8,128)}, u32[]{:S(2)}) copy-start(f32[8,512,128]{2,1,0:T(8,128)} %copy-done.13) | copy-start | bytes 6291460
  221.3 25.3 %collective-permute-start.19 = (f32[4,512,128]{2,1,0:T(8,128)S(1)}, f32[4,512,128]{2,1,0:T(8,128)S(1)}, u32[]{:S(2)}, u32[]{:S(2)}) collective-permute-start(f32[4,512,128]{2,1,0:T(8,128)S(1)} %get-tuple-element.102), channel_id=1, source_target_pairs={{0,63},{1,2},{2,1},{3,4},{4,3},{5,6},{6,5},{7,8},{8,7},{9,10},{10,... | collective-permute-start | bytes 3145736 | tf_op jit(solution)/shard_map/ppermute | solution.py:797
  222.9 23.7 %collective-permute-start.20 = (f32[4,512,128]{2,1,0:T(8,128)S(1)}, f32[4,512,128]{2,1,0:T(8,128)S(1)}, u32[]{:S(2)}, u32[]{:S(2)}) collective-permute-start(f32[4,512,128]{2,1,0:T(8,128)S(1)} %get-tuple-element.103), channel_id=1, source_target_pairs={{0,1},{1,0},{2,3},{3,2},{4,5},{5,4},{6,7},{7,6},{8,9},{9,8},{10,11... | collective-permute-start | bytes 3145736 | tf_op jit(solution)/shard_map/ppermute | solution.py:800
